TPU v7x, 8 devices: a whole 2x2x1 slice. The times are simulated.
8 devices in a mesh: dp: 1 (over z), tp: 8 (over y, x, core).
Axes of the slice: x: 2, y: 2, z: 1, core: 2. Of those that a mesh axis runs over, the one named last changes fastest.
Arguments:
- tokens: int32 [1, 1024], P('dp')
- embed_table: bfloat16 [73448, 2560], P('tp')
- w_q: bfloat16 [2560, 40, 96], P(None, 'tp')
- w_dkv: bfloat16 [2560, 288], replicated
- g_kv: float32 [256], replicated
- w_uk: bfloat16 [256, 40, 64], P(None, 'tp')
- w_uv: bfloat16 [256, 40, 64], P(None, 'tp')
- w_o: bfloat16 [40, 64, 2560], P('tp')
- g_attn: float32 [2560], replicated
- g_mlp: float32 [2560], replicated
- w_gate: bfloat16 [2560, 6400], P(None, 'tp')
- w_up: bfloat16 [2560, 6400], P(None, 'tp')
- w_down: bfloat16 [6400, 2560], P('tp')
- d_out: bfloat16 [1, 1024, 2560], P('dp', 'tp')
Outputs:
- output 1: bfloat16 [1, 1024, 2560], P('dp', 'tp')
- output 2: bfloat16 [73448, 2560], P(('dp', 'tp'))
- output 3: float32 [2560, 40, 96], P('dp', 'tp')
- output 4: float32 [2560, 288], P('dp')
- output 5: float32 [256], P('dp')
- output 6: float32 [256, 40, 64], P('dp', 'tp')
- output 7: float32 [256, 40, 64], P('dp', 'tp')
- output 8: float32 [40, 64, 2560], P(('dp', 'tp'))
- output 9: float32 [2560], P('dp')
- output 10: float32 [2560], P('dp')
- output 11: float32 [2560, 6400], P('dp', 'tp')
- output 12: float32 [2560, 6400], P('dp', 'tp')
- output 13: float32 [6400, 2560], P(('dp', 'tp'))
All inputs are finite; a program needn't handle non-finite values.
Results may differ from a plain program's by a relative error of at most 0.02.
Values are sent between devices in bfloat16 or wider.
A program may use at most 1 GiB of HBM per device.

v0:
```python
import jax
import jax.numpy as jnp
from jax import lax
from jax.sharding import PartitionSpec as P

EPSILON = 1e-6
ROPE_BASE = 10000.0


def matmul_f32(form, lhs, rhs):
    return jnp.einsum(form, lhs, rhs, preferred_element_type=jnp.float32)


def rope_tables(seq_len, rope_dim):
    inv_freq = ROPE_BASE ** (-jnp.arange(0, rope_dim, 2, dtype=jnp.float32) / rope_dim)
    angles = jnp.arange(seq_len, dtype=jnp.float32)[:, None] * inv_freq[None, :]
    return jnp.cos(angles), jnp.sin(angles)


def apply_rope(x_in, cos_t, sin_t):
    half_dim = x_in.shape[-1] // 2
    x_lo = x_in[..., :half_dim]
    x_hi = x_in[..., half_dim:]
    return jnp.concatenate([x_lo * cos_t - x_hi * sin_t, x_hi * cos_t + x_lo * sin_t], axis=-1)


def rms_norm(x_in, gain):
    inv_rms = lax.rsqrt(jnp.mean(x_in * x_in, axis=-1, keepdims=True) + EPSILON)
    return (x_in * inv_rms * gain).astype(jnp.bfloat16)


def kv_prep(latent, g_kv):
    value_a7 = g_kv.shape[0]
    cos_t, sin_t = rope_tables(latent.shape[1], latent.shape[-1] - value_a7)
    k_pe = apply_rope(latent[..., value_a7:], cos_t, sin_t).astype(jnp.bfloat16)
    return rms_norm(latent[..., :value_a7], g_kv), k_pe


def attend(query, k_nope, k_pe, value):
    seq_len = query.shape[1]
    rope_dim = k_pe.shape[-1]
    nope_dim = query.shape[-1] - rope_dim
    cos_t, sin_t = rope_tables(seq_len, rope_dim)
    q_pe = apply_rope(query[..., nope_dim:].astype(jnp.float32), cos_t[:, None, :], sin_t[:, None, :]).astype(jnp.bfloat16)
    scores = matmul_f32('bqhn,bkhn->bhqk', query[..., :nope_dim], k_nope) + matmul_f32('bqhr,bkr->bhqk', q_pe, k_pe)
    causal = jnp.arange(seq_len)[:, None] >= jnp.arange(seq_len)[None, :]
    scores = jnp.where(causal, scores * query.shape[-1] ** -0.5, -1e30)
    attn_prob = jax.nn.softmax(scores, axis=-1).astype(jnp.bfloat16)
    return matmul_f32('bhqk,bkhv->bqhv', attn_prob, value).astype(jnp.bfloat16)


def layer_pass(embedded, d_out, w_q, w_dkv, g_kv, w_uk, w_uv, w_o, g_attn, g_mlp, w_gate, w_up, w_down):
    x_attn_loc, attn_norm_pull = jax.vjp(rms_norm, embedded.astype(jnp.float32), g_attn)
    x_attn = lax.all_gather(x_attn_loc, 'tp', axis=1, tiled=True)
    query = matmul_f32('bsd,dhe->bshe', x_attn, w_q).astype(jnp.bfloat16)
    latent = matmul_f32('bsd,dc->bsc', x_attn, w_dkv)
    (c_kv, k_pe), kv_pull = jax.vjp(kv_prep, latent, g_kv)
    k_nope = matmul_f32('bsc,che->bshe', c_kv, w_uk).astype(jnp.bfloat16)
    value = matmul_f32('bsc,chv->bshv', c_kv, w_uv).astype(jnp.bfloat16)
    attn_out, attend_pull = jax.vjp(attend, query, k_nope, k_pe, value)
    attn_part = matmul_f32('bshv,hvd->bsd', attn_out, w_o).astype(jnp.bfloat16)
    attn_loc = lax.psum_scatter(attn_part, 'tp', scatter_dimension=1, tiled=True)
    residual = (embedded.astype(jnp.float32) + attn_loc.astype(jnp.float32)).astype(jnp.bfloat16)
    x_mlp_loc, mlp_norm_pull = jax.vjp(rms_norm, residual.astype(jnp.float32), g_mlp)
    x_mlp = lax.all_gather(x_mlp_loc, 'tp', axis=1, tiled=True)
    gate = matmul_f32('bsd,df->bsf', x_mlp, w_gate)
    up_proj = matmul_f32('bsd,df->bsf', x_mlp, w_up)
    gate_sig = jax.nn.sigmoid(gate)
    hidden = (gate * gate_sig * up_proj).astype(jnp.bfloat16)
    mlp_part = matmul_f32('bsf,fd->bsd', hidden, w_down).astype(jnp.bfloat16)
    mlp_loc = lax.psum_scatter(mlp_part, 'tp', scatter_dimension=1, tiled=True)
    layer_out = (residual.astype(jnp.float32) + mlp_loc.astype(jnp.float32)).astype(jnp.bfloat16)

    dy_full = lax.all_gather(d_out, 'tp', axis=1, tiled=True)
    d_hidden = matmul_f32('bsd,fd->bsf', dy_full, w_down)
    dw_down = matmul_f32('bsf,bsd->fd', hidden, dy_full)
    d_up = (d_hidden * gate * gate_sig).astype(jnp.bfloat16)
    d_gate = (d_hidden * up_proj * gate_sig * (1.0 + gate * (1.0 - gate_sig))).astype(jnp.bfloat16)
    dw_gate = matmul_f32('bsd,bsf->df', x_mlp, d_gate)
    dw_up = matmul_f32('bsd,bsf->df', x_mlp, d_up)
    dx_mlp_part = (matmul_f32('bsf,df->bsd', d_gate, w_gate) + matmul_f32('bsf,df->bsd', d_up, w_up)).astype(jnp.bfloat16)
    dx_mlp = lax.psum_scatter(dx_mlp_part, 'tp', scatter_dimension=1, tiled=True)
    d_res_norm, dg_mlp_part = mlp_norm_pull(dx_mlp)
    d_residual = d_out.astype(jnp.float32) + d_res_norm
    d_attn_full = lax.all_gather(d_residual.astype(jnp.bfloat16), 'tp', axis=1, tiled=True)
    dw_o = matmul_f32('bshv,bsd->hvd', attn_out, d_attn_full)
    d_attn_out = matmul_f32('bsd,hvd->bshv', d_attn_full, w_o).astype(jnp.bfloat16)
    d_query, d_knope, d_kpe, d_value = attend_pull(d_attn_out)
    dw_uk = matmul_f32('bsc,bshe->che', c_kv, d_knope)
    dw_uv = matmul_f32('bsc,bshv->chv', c_kv, d_value)
    d_ckv = (matmul_f32('bshe,che->bsc', d_knope, w_uk) + matmul_f32('bshv,chv->bsc', d_value, w_uv)).astype(jnp.bfloat16)
    d_latent, dg_kv_part = kv_pull((d_ckv, d_kpe))
    d_latent = d_latent.astype(jnp.bfloat16)
    dw_q = matmul_f32('bsd,bshe->dhe', x_attn, d_query)
    dw_dkv_part = matmul_f32('bsd,bsc->dc', x_attn, d_latent)
    dx_attn_part = (matmul_f32('bshe,dhe->bsd', d_query, w_q) + matmul_f32('bsc,dc->bsd', d_latent, w_dkv)).astype(jnp.bfloat16)
    dx_attn = lax.psum_scatter(dx_attn_part, 'tp', scatter_dimension=1, tiled=True)
    d_emb_norm, dg_attn_part = attn_norm_pull(dx_attn)
    d_embed = (d_residual + d_emb_norm).astype(jnp.bfloat16)
    dw_dkv, dg_kv, dg_attn, dg_mlp = lax.psum((dw_dkv_part, dg_kv_part, dg_attn_part, dg_mlp_part), 'tp')
    return layer_out, d_embed, (dw_q, dw_dkv, dg_kv, dw_uk, dw_uv, dw_o, dg_attn, dg_mlp, dw_gate, dw_up, dw_down)


def solution(mesh):
    def device_step(tokens, embed_table, w_q, w_dkv, g_kv, w_uk, w_uv, w_o, g_attn, g_mlp, w_gate, w_up, w_down, d_out):
        vocab_local, model_dim = embed_table.shape
        local_ids = tokens - lax.axis_index('tp') * vocab_local
        owned = (local_ids >= 0) & (local_ids < vocab_local)
        rows = jnp.take(embed_table, jnp.where(owned, local_ids, 0), axis=0)
        rows = jnp.where(owned[..., None], rows, jnp.zeros((), rows.dtype))
        embedded = lax.psum_scatter(rows, 'tp', scatter_dimension=1, tiled=True)
        layer_out, d_embed, weight_grads = layer_pass(embedded, d_out, w_q, w_dkv, g_kv, w_uk, w_uv, w_o, g_attn, g_mlp, w_gate, w_up, w_down)
        de_full = lax.all_gather(d_embed, 'tp', axis=1, tiled=True)
        slot_ids = jnp.where(owned, local_ids, vocab_local)
        d_table = jax.ops.segment_sum(de_full.reshape(-1, model_dim).astype(jnp.float32), slot_ids.reshape(-1), num_segments=vocab_local)
        return (layer_out, d_table.astype(jnp.bfloat16)) + weight_grads

    row_spec = P('dp', 'tp', None)
    head_spec = P(None, 'tp', None)
    in_specs = (P('dp', None), P('tp', None), head_spec, P(None, None), P(None), head_spec, head_spec, P('tp', None, None), P(None), P(None), P(None, 'tp'), P(None, 'tp'), P('tp', None), row_spec)
    out_specs = (row_spec, P(('dp', 'tp'), None), P('dp', 'tp', None), P('dp', None), P('dp'), P('dp', 'tp', None), P('dp', 'tp', None), P(('dp', 'tp'), None, None), P('dp'), P('dp'), P('dp', 'tp'), P('dp', 'tp'), P(('dp', 'tp'), None))
    return jax.shard_map(device_step, mesh=mesh, in_specs=in_specs, out_specs=out_specs, check_vma=False)
```

profile of v0, /device:TPU:0, one launch (start us, length us, event | category | flops | bytes accessed | tf_op | source)
XLA Modules:
  0.0 1061.1 jit_solution(11492828910596668211)
XLA Ops:
  8.1 86.7 %gather_fusion = bf16[1024,2560]{1,0:T(8,128)(2,1)} fusion(bf16[9181,2560]{1,0:T(8,128)(2,1)} %param.15, s32[1024]{0:T(1024)S(1)} %broadcast_clamp_fusion), kind=kCustom, calls=%fused_computation | custom fusion | bytes 10489856 | tf_op jit(solution)/shard_map/jit(_take)/gather | solution.py:109
  94.9 6.2 fusion.48
  101.2 50.1 %reduce-scatter.6.cloned.1.call-done = bf16[1,128,2560]{2,1,0:T(8,128)(2,1)} async-done(((bf16[1,1024,2560]{2,1,0:T(8,128)(2,1)}), bf16[1,128,2560]{2,1,0:T(8,128)(2,1)}) %reduce-scatter.6.cloned.1.call-update) | async-done | bytes 655376 | tf_op jit(solution)/shard_map/reduce_scatter | solution.py:111
  157.3 33.9 %all-gather.6.cloned.1.call-done = bf16[1,1024,2560]{2,1,0:T(8,128)(2,1)} async-done(((bf16[1,128,2560]{2,1,0:T(8,128)(2,1)}), bf16[1,1024,2560]{2,1,0:T(8,128)(2,1)}) %all-gather.6.cloned.1.call-update) | async-done | bytes 5242896 | tf_op jit(solution)/shard_map/all_gather | solution.py:54
  191.2 4.8 fusion.57
  196.5 2.7 fusion.44
  200.5 9.6 fusion.132
  210.3 14.1 %fusion.163 = (f32[5,1024]{1,0:T(8,128)S(1)}, f32[1,5,1024,1024]{2,3,1,0:T(8,128)}) fusion(bf16[1024,5,16]{0,2,1:T(8,128)(2,1)S(1)} %get-tuple-element.34, bf16[1024,5,16]{0,2,1:T(8,128)(2,1)S(1)} %get-tuple-element.33, bf16[1024,16]{0,1:T(8,128)(2,1)S(1)} %get-tuple-element.30, bf16[1024,16]{0,1:T(8,128)(2,1)S(1)} %get-tuple-element.29, ...), kind=kOutput, calls=%fused_computation.199 | convolution fusion | flops 357297152 | bytes 43405312 | tf_op jit(solution)/shard_map/jvp(bqhr,bkr->bhqk)/dot_general | solution.py:11
  224.4 9.9 fusion.18
  234.4 3.1 copy-done.1
  237.5 3.5 divide_convert_fusion
  246.3 4.6 fusion.49
  251.0 47.8 %reduce-scatter.8.cloned.1.call-done = bf16[1,128,2560]{2,1,0:T(8,128)(2,1)} async-done(((bf16[1,1024,2560]{2,1,0:T(8,128)(2,1)}), bf16[1,128,2560]{2,1,0:T(8,128)(2,1)}) %reduce-scatter.8.cloned.1.call-update) | async-done | bytes 655376 | tf_op jit(solution)/shard_map/reduce_scatter | solution.py:62
  303.0 34.5 %all-gather.8.cloned.1.call-done = bf16[1,1024,2560]{2,1,0:T(8,128)(2,1)} async-done(((bf16[1,128,2560]{2,1,0:T(8,128)(2,1)}), bf16[1,1024,2560]{2,1,0:T(8,128)(2,1)}) %all-gather.8.cloned.1.call-update) | async-done | bytes 5242896 | tf_op jit(solution)/shard_map/all_gather | solution.py:65
  337.5 10.0 fusion.38
  347.5 6.1 fusion.36
  353.6 20.7 %all-gather.10.cloned.1.call-done = bf16[1,1024,2560]{2,1,0:T(8,128)(2,1)} async-done(((bf16[1,128,2560]{2,1,0:T(8,128)(2,1)}), bf16[1,1024,2560]{2,1,0:T(8,128)(2,1)}) %all-gather.10.cloned.1.call-update) | async-done | bytes 5242896 | tf_op jit(solution)/shard_map/all_gather | solution.py:74
  374.3 12.4 %multiply_convert_fusion = (bf16[1024,800]{0,1:T(8,128)(2,1)S(1)}, bf16[1024,800]{0,1:T(8,128)(2,1)S(1)}, bf16[1024,800]{0,1:T(8,128)(2,1)}) fusion(f32[1024,800]{0,1:T(8,128)} %fusion.38, f32[1024,800]{0,1:T(8,128)} %fusion.36, bf16[800,2560]{1,0:T(8,128)(2,1)} %param.26, bf16[1,1024,2560]{2,1,0:T(8,128)(2,1)} %all-gather.10.cloned.1.call-done), kind=kOutput, calls=%fused_computation.68 | convolution fusion | flops 4207411200 | bytes 20807680 | tf_op jit(solution)/shard_map/bsd,fd->bsf/dot_general | solution.py:11
  386.8 5.9 fusion.164
  392.7 7.8 fusion.50
  400.6 47.8 %reduce-scatter.12.cloned.1.call-done = bf16[1,128,2560]{2,1,0:T(8,128)(2,1)} async-done(((bf16[1,1024,2560]{2,1,0:T(8,128)(2,1)}), bf16[1,128,2560]{2,1,0:T(8,128)(2,1)}) %reduce-scatter.12.cloned.1.call-update) | async-done | bytes 655376 | tf_op jit(solution)/shard_map/reduce_scatter | solution.py:82
  450.8 2.6 fusion.140
  453.5 35.2 %all-gather.12.cloned.1.call-done = bf16[1,1024,2560]{2,1,0:T(8,128)(2,1)} async-done(((bf16[1,128,2560]{2,1,0:T(8,128)(2,1)}), bf16[1,1024,2560]{2,1,0:T(8,128)(2,1)}) %all-gather.12.cloned.1.call-update) | async-done | bytes 5242896 | tf_op jit(solution)/shard_map/all_gather | solution.py:85
  488.7 5.0 fusion.93
  493.7 11.9 %fusion.7 = (f32[5,1024]{1,0:T(8,128)S(1)}, bf16[5,1024,1024]{1,2,0:T(8,128)(2,1)}) fusion(f32[1,5,1024,1024]{2,3,1,0:T(8,128)} %get-tuple-element.43, f32[5,1024]{1,0:T(8,128)S(1)} %multiply_divide_fusion, f32[5,1024]{1,0:T(8,128)S(1)} %get-tuple-element.42, bf16[5,64,1024]{2,1,0:T(8,128)(2,1)S(1)} %fusion.93, f32[1024,5,64]{0,2,1:T(8,128)S(1)} %bitcast.298), kind=kOutput, calls=%fused_computation.11 | convolution fusion | flops 702868480 | bytes 33484800 | tf_op jit(solution)/shard_map/transpose(jvp(bhqk,bkhv->bqhv))/dot_general | solution.py:11
  505.7 13.8 %fusion.107 = f32[1,1024,5,32]{1,3,2,0:T(8,128)S(1)} fusion(bf16[1024,16]{0,1:T(8,128)(2,1)S(1)} %copy-done.50, bf16[1024,16]{0,1:T(8,128)(2,1)S(1)} %copy-done.48, bf16[5,1024,1024]{1,2,0:T(8,128)(2,1)} %get-tuple-element.45, f32[1,5,1024,1024]{2,3,1,0:T(8,128)} %get-tuple-element.43, f32[5,1024]{1,0:T(8,128)S(1)} %neg.57, f32[5,1024]{1,0:T(8,128)S(1)} %fusion.18, ...), kind=kOutput, calls=%fused_computation.125 | convolution fusion | flops 372703232 | bytes 33288192 | tf_op jit(solution)/shard_map/transpose(jvp(bqhr,bkr->bhqk))/dot_general | solution.py:11
  519.5 14.2 %fusion.90 = bf16[1,1024,5,64]{1,3,2,0:T(8,128)(2,1)} fusion(f32[1024,5,64]{0,2,1:T(8,128)S(1)} %bitcast.300, bf16[5,1024,1024]{1,2,0:T(8,128)(2,1)} %get-tuple-element.45, f32[1,5,1024,1024]{2,3,1,0:T(8,128)} %get-tuple-element.43, f32[5,1024]{1,0:T(8,128)S(1)} %neg.57, f32[5,1024]{1,0:T(8,128)S(1)} %fusion.18, f32[5,1024]{1,0:T(8,128)S(1)} %get-tuple-element.42, ...), kind=kOutput, calls=%fused_computation.118 | convolution fusion | flops 708444160 | bytes 34533376 | tf_op jit(solution)/shard_map/transpose(jvp(bqhn,bkhn->bhqk))/dot_general | solution.py:11
  533.7 15.0 %fusion.119 = f32[1,1024,32]{1,2,0:T(8,128)} fusion(bf16[1024,5,16]{0,2,1:T(8,128)(2,1)S(1)} %copy-done.32, bf16[1024,5,16]{0,2,1:T(8,128)(2,1)S(1)} %copy-done.30, bf16[5,1024,1024]{1,2,0:T(8,128)(2,1)} %get-tuple-element.45, f32[1,5,1024,1024]{2,3,1,0:T(8,128)} %get-tuple-element.43, f32[5,1024]{1,0:T(8,128)S(1)} %neg.57, f32[5,1024]{1,0:T(8,128)S(1)} %fusion.18, ...), kind=kOutput, calls=%fused_computation.130 | convolution fusion | flops 372965376 | bytes 33026048 | tf_op jit(solution)/shard_map/transpose(jvp(bqhr,bkr->bhqk))/dot_general | solution.py:11
  548.7 7.3 fusion.72
  556.2 13.9 %fusion.66 = bf16[5,1024,64]{1,2,0:T(8,128)(2,1)S(1)} fusion(bf16[1,1024,5,96]{1,3,2,0:T(8,128)(2,1)S(1)} %copy-done.18, bf16[5,1024,1024]{1,2,0:T(8,128)(2,1)} %get-tuple-element.45, f32[1,5,1024,1024]{2,3,1,0:T(8,128)} %get-tuple-element.43, f32[5,1024]{1,0:T(8,128)S(1)} %neg.57, f32[5,1024]{1,0:T(8,128)S(1)} %fusion.18, ...), kind=kOutput, calls=%fused_computation.98 | convolution fusion | flops 708116480 | bytes 33914880 | tf_op jit(solution)/shard_map/transpose(jvp(bqhn,bkhn->bhqk))/dot_general | solution.py:11
  573.1 2.9 fusion.127
  577.7 4.6 fusion.51
  582.4 9.4 fusion.52
  591.9 38.2 %reduce-scatter.14.cloned.1.call-done = bf16[1,128,2560]{2,1,0:T(8,128)(2,1)} async-done(((bf16[1,1024,2560]{2,1,0:T(8,128)(2,1)}), bf16[1,128,2560]{2,1,0:T(8,128)(2,1)}) %reduce-scatter.14.cloned.1.call-update) | async-done | bytes 655376 | tf_op jit(solution)/shard_map/reduce_scatter | solution.py:97
  632.0 49.8 %reduce-scatter.10.cloned.1.call-done = bf16[1,128,2560]{2,1,0:T(8,128)(2,1)} async-done(((bf16[1,1024,2560]{2,1,0:T(8,128)(2,1)}), bf16[1,128,2560]{2,1,0:T(8,128)(2,1)}) %reduce-scatter.10.cloned.1.call-update) | async-done | bytes 655376 | tf_op jit(solution)/shard_map/reduce_scatter | solution.py:71
  681.8 4.0 fusion.81
  686.1 10.9 %fusion.32 = f32[2560,800]{0,1:T(8,128)} fusion(bf16[1024,800]{0,1:T(8,128)(2,1)} %copy-done.77, bf16[1,1024,2560]{2,1,0:T(8,128)(2,1)} %all-gather.8.cloned.1.call-done), kind=kOutput, calls=%fused_computation.45 | convolution fusion | flops 4194304000 | bytes 15073280 | tf_op jit(solution)/shard_map/bsd,bsf->df/dot_general | solution.py:11
  696.9 9.2 fusion.34
  706.2 6.6 fusion.28
  713.8 3.3 fusion.42
  717.1 6.1 fusion.24
  723.3 7.0 fusion.40
  732.5 23.6 %all-reduce.8 = (f32[256]{0:T(256)}, f32[2560]{0:T(1024)}, f32[2560]{0:T(1024)}) all-reduce(f32[256]{0:T(256)S(1)} %get-tuple-element.13, f32[2560]{0:T(1024)S(1)} %get-tuple-element.17, f32[2560]{0:T(1024)S(1)} %copy-done.55), channel_id=1, replica_groups=mesh['dp'=1,'tp'=8] {'tp'}, use_global_device_ids=true, to_apply=%region_17.18 | all-reduce | flops 5376 | bytes 43008 | tf_op jit(solution)/shard_map/psum | solution.py:100
  756.1 8.0 bitcast_convert_fusion.1
  764.1 29.4 %broadcast_in_dim.93 = f32[9181,2560]{1,0:T(8,128)} broadcast(f32[]{:T(128)} %constant.24.clone.1), dimensions={} | broadcast | bytes 94013440 | tf_op jit(solution)/shard_map/broadcast_in_dim | solution.py:115
  793.5 211.4 %scatter_fusion = f32[9181,2560]{1,0:T(8,128)} fusion(f32[9181,2560]{1,0:T(8,128)} %broadcast_in_dim.93, s32[1024]{0:T(1024)S(1)} %bitcast.309, f32[1024,2560]{1,0:T(8,128)} %bitcast_convert_fusion.1), kind=kCustom, calls=%fused_computation.1 | custom fusion | flops 2621440 | bytes 31461376 | tf_op jit(solution)/shard_map/scatter-add | solution.py:115
  1004.9 45.8 %convert_element_type.265 = bf16[9181,2560]{1,0:T(8,128)(2,1)} convert(f32[9181,2560]{1,0:T(8,128)} %scatter_fusion) | non-fusion elementwise | flops 23503360 | bytes 141020160 | tf_op jit(solution)/shard_map/convert_element_type | solution.py:116
  1050.7 3.6 copy.53
  (234 shorter events, 30.8 us)
Async XLA Ops:
  7.2 189.3 %copy-start = (bf16[2560,5,96]{0,2,1:T(8,128)(2,1)S(1)}, bf16[2560,5,96]{0,2,1:T(8,128)(2,1)}, u32[]{:S(2)}) copy-start(bf16[2560,5,96]{0,2,1:T(8,128)(2,1)} %param.16) | copy-start | bytes 7372804
  7.2 144.1 %reduce-scatter.6.cloned.1.call-start = ((), (), s32[]{:S(2)}) async-start(), calls=%async_computation.5 | async-start | bytes 5898240 | tf_op jit(solution)/shard_map/reduce_scatter | solution.py:111
  101.1 52.6 %copy-start.51 = (f32[2560]{0:T(1024)S(1)}, f32[2560]{0:T(1024)}, u32[]{:S(2)}) copy-start(f32[2560]{0:T(1024)} %param.22) | copy-start | bytes 30724
  101.1 90.0 %all-gather.6.cloned.1.call-start = ((), (), s32[]{:S(2)}) async-start(), calls=%async_computation.6 | async-start | bytes 5898240 | tf_op jit(solution)/shard_map/all_gather | solution.py:54
  155.9 142.9 %reduce-scatter.8.cloned.1.call-start = ((), (), s32[]{:S(2)}) async-start(), calls=%async_computation.7 | async-start | bytes 5898240 | tf_op jit(solution)/shard_map/reduce_scatter | solution.py:62
  155.9 40.0 %copy-start.65 = (f32[16]{0:T(128)}, f32[16]{0:T(128)S(1)}, u32[]{:S(2)}) copy-start(f32[16]{0:T(128)S(1)} %multiply_power_fusion) | copy-start | bytes 196
  156.3 54.0 %copy-start.21 = (pred[1024,1024]{0,1:T(8,128)(4,1)}, pred[1024,1024]{0,1:T(8,128)(4,1)S(1)}, u32[]{:S(2)}) copy-start(pred[1024,1024]{0,1:T(8,128)(4,1)S(1)} %iota_compare_fusion) | copy-start | bytes 3145732
  196.3 14.0 %copy-start.47 = (bf16[1024,16]{0,1:T(8,128)(2,1)}, bf16[1024,16]{0,1:T(8,128)(2,1)S(1)}, u32[]{:S(2)}) copy-start(bf16[1024,16]{0,1:T(8,128)(2,1)S(1)} %get-tuple-element.29) | copy-start | bytes 98308
  196.3 14.0 %copy-start.49 = (bf16[1024,16]{0,1:T(8,128)(2,1)}, bf16[1024,16]{0,1:T(8,128)(2,1)S(1)}, u32[]{:S(2)}) copy-start(bf16[1024,16]{0,1:T(8,128)(2,1)S(1)} %get-tuple-element.30) | copy-start | bytes 98308
  199.6 41.4 %copy-start.11 = (bf16[1024,256]{0,1:T(8,128)(2,1)}, bf16[1024,256]{0,1:T(8,128)(2,1)S(1)}, u32[]{:S(2)}) copy-start(bf16[1024,256]{0,1:T(8,128)(2,1)S(1)} %fusion.133) | copy-start | bytes 1572868
  210.3 14.1 %copy-start.29 = (bf16[1024,5,16]{0,2,1:T(8,128)(2,1)}, bf16[1024,5,16]{0,2,1:T(8,128)(2,1)S(1)}, u32[]{:S(2)}) copy-start(bf16[1024,5,16]{0,2,1:T(8,128)(2,1)S(1)} %get-tuple-element.33) | copy-start | bytes 491524
  210.3 14.1 %copy-start.31 = (bf16[1024,5,16]{0,2,1:T(8,128)(2,1)}, bf16[1024,5,16]{0,2,1:T(8,128)(2,1)S(1)}, u32[]{:S(2)}) copy-start(bf16[1024,5,16]{0,2,1:T(8,128)(2,1)S(1)} %get-tuple-element.34) | copy-start | bytes 491524
  224.4 13.1 %copy-start.1 = (f32[1,5,1024,1024]{2,3,1,0:T(8,128)S(1)}, f32[1,5,1024,1024]{2,3,1,0:T(8,128)}, u32[]{:S(2)}) copy-start(f32[1,5,1024,1024]{2,3,1,0:T(8,128)} %get-tuple-element.43) | copy-start | bytes 62914564
  251.0 47.9 %copy-start.3 = (bf16[1,128,2560]{2,1,0:T(8,128)(2,1)S(1)}, bf16[1,128,2560]{2,1,0:T(8,128)(2,1)}, u32[]{:S(2)}) copy-start(bf16[1,128,2560]{2,1,0:T(8,128)(2,1)} %reduce-scatter.6.cloned.1.call-done) | copy-start | bytes 1966084
  251.0 50.1 %copy-start.45 = (f32[2560]{0:T(1024)S(1)}, f32[2560]{0:T(1024)}, u32[]{:S(2)}) copy-start(f32[2560]{0:T(1024)} %param.23) | copy-start | bytes 30724
  251.0 86.5 %all-gather.8.cloned.1.call-start = ((), (), s32[]{:S(2)}) async-start(), calls=%async_computation.8 | async-start | bytes 5898240 | tf_op jit(solution)/shard_map/all_gather | solution.py:65
  300.3 150.5 %copy-start.61 = (f32[128]{0:T(128)}, f32[128]{0:T(128)S(1)}, u32[]{:S(2)}) copy-start(f32[128]{0:T(128)S(1)} %fusion.151) | copy-start | bytes 1540
  302.2 72.1 %all-gather.10.cloned.1.call-start = ((), (), s32[]{:S(2)}) async-start(), calls=%async_computation.10 | async-start | bytes 5898240 | tf_op jit(solution)/shard_map/all_gather | solution.py:74
  302.8 145.6 %reduce-scatter.12.cloned.1.call-start = ((), (), s32[]{:S(2)}) async-start(), calls=%async_computation.11 | async-start | bytes 5898240 | tf_op jit(solution)/shard_map/reduce_scatter | solution.py:82
  374.3 12.5 %copy-start.73 = (bf16[2560,800]{0,1:T(8,128)(2,1)S(1)}, bf16[2560,800]{0,1:T(8,128)(2,1)}, u32[]{:S(2)}) copy-start(bf16[2560,800]{0,1:T(8,128)(2,1)} %param.24) | copy-start | bytes 12288004
  400.5 47.9 %copy-start.6 = (bf16[1,128,2560]{2,1,0:T(8,128)(2,1)S(1)}, bf16[1,128,2560]{2,1,0:T(8,128)(2,1)}, u32[]{:S(2)}) copy-start(bf16[1,128,2560]{2,1,0:T(8,128)(2,1)} %copy-done.5) | copy-start | bytes 1966084
  400.5 88.2 %all-gather.12.cloned.1.call-start = ((), (), s32[]{:S(2)}) async-start(), calls=%async_computation.12 | async-start | bytes 5898240 | tf_op jit(solution)/shard_map/all_gather | solution.py:85
  453.4 176.7 %reduce-scatter.14.cloned.1.call-start = ((), (), s32[]{:S(2)}) async-start(), calls=%async_computation.13 | async-start | bytes 5898240 | tf_op jit(solution)/shard_map/reduce_scatter | solution.py:97
  505.7 13.8 %copy-start.14 = (f32[1024,320]{0,1:S(1)}, f32[1024,320]{0,1}, u32[]{:S(2)}) copy-start(f32[1024,320]{0,1} %copy-done.13) | copy-start | bytes 3932164
  519.5 14.3 %copy-start.30 = (bf16[1024,5,16]{0,2,1:T(8,128)(2,1)S(1)}, bf16[1024,5,16]{0,2,1:T(8,128)(2,1)}, u32[]{:S(2)}) copy-start(bf16[1024,5,16]{0,2,1:T(8,128)(2,1)} %copy-done.29) | copy-start | bytes 491524
  519.5 14.2 %copy-start.32 = (bf16[1024,5,16]{0,2,1:T(8,128)(2,1)S(1)}, bf16[1024,5,16]{0,2,1:T(8,128)(2,1)}, u32[]{:S(2)}) copy-start(bf16[1024,5,16]{0,2,1:T(8,128)(2,1)} %copy-done.31) | copy-start | bytes 491524
  556.1 15.7 %copy-start.15 = (bf16[5,64,1024]{2,1,0:T(8,128)(2,1)}, bf16[5,64,1024]{2,1,0:T(8,128)(2,1)S(1)}, u32[]{:S(2)}) copy-start(bf16[5,64,1024]{2,1,0:T(8,128)(2,1)S(1)} %fusion.72) | copy-start | bytes 1966084
  556.1 14.0 %copy-start.40 = (f32[1024,16]{0,1:T(8,128)S(1)}, f32[1024,16]{0,1:T(8,128)}, u32[]{:S(2)}) copy-start(f32[1024,16]{0,1:T(8,128)} %get-tuple-element.40) | copy-start | bytes 196612
  556.1 14.0 %copy-start.42 = (f32[1024,16]{0,1:T(8,128)S(1)}, f32[1024,16]{0,1:T(8,128)}, u32[]{:S(2)}) copy-start(f32[1024,16]{0,1:T(8,128)} %get-tuple-element.41) | copy-start | bytes 196612
  556.1 14.1 %copy-start.66 = (f32[16]{0:T(128)S(1)}, f32[16]{0:T(128)}, u32[]{:S(2)}) copy-start(f32[16]{0:T(128)} %copy-done.65) | copy-start | bytes 196
  556.1 15.6 %copy-start.34 = (bf16[256,5,64]{0,2,1:T(8,128)(2,1)S(1)}, bf16[256,5,64]{0,2,1:T(8,128)(2,1)}, u32[]{:S(2)}) copy-start(bf16[256,5,64]{0,2,1:T(8,128)(2,1)} %param.20) | copy-start | bytes 491524
  556.1 16.1 %copy-start.8 = (f32[1,1024,288]{1,2,0:T(8,128)S(1)}, f32[1,1024,288]{1,2,0:T(8,128)}, u32[]{:S(2)}) copy-start(f32[1,1024,288]{1,2,0:T(8,128)} %copy-done.7) | copy-start | bytes 3538948
  556.1 16.1 %copy-start.36 = (bf16[256,5,64]{0,2,1:T(8,128)(2,1)S(1)}, bf16[256,5,64]{0,2,1:T(8,128)(2,1)}, u32[]{:S(2)}) copy-start(bf16[256,5,64]{0,2,1:T(8,128)(2,1)} %param.19) | copy-start | bytes 491524
  556.1 16.1 %copy-start.54 = (f32[1024]{0:T(1024)S(1)}, f32[1024]{0:T(1024)}, u32[]{:S(2)}) copy-start(f32[1024]{0:T(1024)} %copy-done.53) | copy-start | bytes 12292
  556.1 16.1 %copy-start.60 = (f32[256]{0:T(256)S(1)}, f32[256]{0:T(256)}, u32[]{:S(2)}) copy-start(f32[256]{0:T(256)} %param.18) | copy-start | bytes 3076
  582.3 99.4 %reduce-scatter.10.cloned.1.call-start = ((), (), s32[]{:S(2)}) async-start(), calls=%async_computation.9 | async-start | bytes 5898240 | tf_op jit(solution)/shard_map/reduce_scatter | solution.py:71
  591.8 38.3 %copy-start.4 = (bf16[1,128,2560]{2,1,0:T(8,128)(2,1)S(1)}, bf16[1,128,2560]{2,1,0:T(8,128)(2,1)}, u32[]{:S(2)}) copy-start(bf16[1,128,2560]{2,1,0:T(8,128)(2,1)} %reduce-scatter.6.cloned.1.call-done) | copy-start | bytes 1966084
  591.8 38.3 %copy-start.52 = (f32[2560]{0:T(1024)S(1)}, f32[2560]{0:T(1024)}, u32[]{:S(2)}) copy-start(f32[2560]{0:T(1024)} %param.22) | copy-start | bytes 30724
  591.8 38.3 %copy-start.64 = (f32[128]{0:T(128)S(1)}, f32[128]{0:T(128)}, u32[]{:S(2)}) copy-start(f32[128]{0:T(128)} %copy-done.63) | copy-start | bytes 1540
  591.8 40.1 %copy-start.70 = (f32[128]{0:T(128)S(1)}, f32[128]{0:T(128)}, u32[]{:S(2)}) copy-start(f32[128]{0:T(128)} %copy-done.69) | copy-start | bytes 1540
  591.8 89.9 %copy-start.46 = (f32[2560]{0:T(1024)S(1)}, f32[2560]{0:T(1024)}, u32[]{:S(2)}) copy-start(f32[2560]{0:T(1024)} %param.23) | copy-start | bytes 30724
  591.8 89.9 %copy-start.62 = (f32[128]{0:T(128)S(1)}, f32[128]{0:T(128)}, u32[]{:S(2)}) copy-start(f32[128]{0:T(128)} %copy-done.61) | copy-start | bytes 1540
  591.9 89.9 %copy-start.68 = (f32[128]{0:T(128)S(1)}, f32[128]{0:T(128)}, u32[]{:S(2)}) copy-start(f32[128]{0:T(128)} %copy-done.67) | copy-start | bytes 1540
  591.9 94.1 %copy-start.58 = (s32[1,1024]{1,0:T(1,128)S(1)}, s32[1,1024]{1,0:T(1,128)}, u32[]{:S(2)}) copy-start(s32[1,1024]{1,0:T(1,128)} %param.14) | copy-start | bytes 12292
  591.9 164.2 %all-gather.14.cloned.1.call-start = ((), (), s32[]{:S(2)}) async-start(), calls=%async_computation.14 | async-start | bytes 5898240 | tf_op jit(solution)/shard_map/all_gather | solution.py:113
  685.7 365.0 %all-reduce.11.cloned.1.call-start = ((), (), s32[]{:S(2)}) async-start(), calls=%async_computation.15 | async-start | bytes 5898240 | tf_op jit(solution)/shard_map/psum | solution.py:100
  686.0 20.1 %slice-start.2 = ((s8[5242880]{0:T(1024)(128)(4,1)}), s8[4194304]{0:T(1024)(128)(4,1)S(1)}, s32[]{:S(2)}) async-start(s8[5242880]{0:T(1024)(128)(4,1)} %bitcast.313), calls=%async_computation.18 | async-start | bytes 8388608
  696.9 16.9 %slice-start = ((s8[5242880]{0:T(1024)(128)(4,1)}), s8[4194304]{0:T(1024)(128)(4,1)S(1)}, s32[]{:S(2)}) async-start(s8[5242880]{0:T(1024)(128)(4,1)} %bitcast.311), calls=%async_computation.16 | async-start | bytes 8388608
  (48 other events, 291.9 us)
Sparse Core Ops, SparseCore 0:
  101.3 49.9 reduce-scatter.5
  156.0 35.1 all-gather.5
  251.1 47.6 reduce-scatter.7
  302.3 35.1 all-gather.7
  339.1 35.1 all-gather.9
  400.6 47.6 reduce-scatter.11
  453.5 35.1 all-gather.11
  582.4 47.6 reduce-scatter.13
  634.0 47.6 reduce-scatter.9
  685.9 35.1 all-gather.13
  724.9 56.8 all-reduce.10
where the time goes:
time: 1070 us; the launch traced here: 1060 us
  waiting for transfers between devices  359 us (34%)
  other arithmetic  308 us (29%)
  matrix products  225 us (21%)
  local copies, waits for them, and re-layouts  130 us (12%)
  blocking collectives  23.6 us (2%)
  between operations  15.2 us (1%)
    dot_general x27, matrix products, matmul_f32(): return jnp.einsum(form, lhs, rhs, preferred_element_type=jnp.float32)  213 us
    scatter-add x1, other arithmetic, device_step(): jax.ops.segment_sum(de_full.reshape(-1, model_dim).astype(jnp.float32), s...  211 us
    gather x1, local copies, waits for them, and re-layouts, device_step(): rows = jnp.take(embed_table, jnp.where(owned, local_ids, 0), axis=0)  86.7 us
    reduce_scatter x1, waiting for transfers between devices, device_step(): embedded = lax.psum_scatter(rows, 'tp', scatter_dimension=1, tiled=True)  50.1 us
    reduce_scatter x1, waiting for transfers between devices, layer_pass(): mlp_loc = lax.psum_scatter(mlp_part, 'tp', scatter_dimension=1, tiled=True)  49.8 us
    reduce_scatter x1, waiting for transfers between devices, layer_pass(): lax.psum_scatter(dx_mlp_part, 'tp', scatter_dimension=1, tiled=True)  47.8 us
    reduce_scatter x1, waiting for transfers between devices, layer_pass(): lax.psum_scatter(attn_part, 'tp', scatter_dimension=1, tiled=True)  47.8 us
    convert_element_type x1, other arithmetic, device_step(): return (layer_out, d_table.astype(jnp.bfloat16)) + weight_grads  45.8 us
  transfers between devices with their start and end apart: 11, of which 9 were waited for; matrix products, arithmetic and copies ran while one was open for 35% of the time, Pallas kernels for 0%

commit v1 on v0

v1 whole, which is shorter than its diff:
```python
import functools

import jax
import jax.numpy as jnp
from jax import lax
from jax.experimental import pallas as pl
from jax.experimental.pallas import tpu as pltpu
from jax.sharding import PartitionSpec as P

EPSILON = 1e-6
ROPE_BASE = 10000.0
F32, BF16 = jnp.float32, jnp.bfloat16
LOG2E = 1.4426950408889634
VM = pltpu.VMEM
GB = 64
QB = 256


def mm(lhs, rhs, lc, rc):
    return lax.dot_general(lhs, rhs, (((lc,), (rc,)), ((), ())), preferred_element_type=F32)


def rope_tables(seq_len, rope_dim):
    inv_freq = ROPE_BASE ** (-jnp.arange(0, rope_dim, 2, dtype=F32) / rope_dim)
    angles = jnp.arange(seq_len, dtype=F32)[:, None] * inv_freq[None, :]
    return jnp.cos(angles), jnp.sin(angles)


def apply_rope(x_in, cos_t, sin_t):
    half_dim = x_in.shape[-1] // 2
    x_lo, x_hi = x_in[..., :half_dim], x_in[..., half_dim:]
    return jnp.concatenate([x_lo * cos_t - x_hi * sin_t, x_hi * cos_t + x_lo * sin_t], axis=-1)


def rms_norm(x_in, gain):
    inv_rms = lax.rsqrt(jnp.mean(x_in * x_in, axis=-1, keepdims=True) + EPSILON)
    return (x_in * inv_rms * gain).astype(BF16)


def kv_prep(latent, g_kv):
    lora = g_kv.shape[0]
    cos_t, sin_t = rope_tables(latent.shape[0], latent.shape[-1] - lora)
    k_pe = apply_rope(latent[:, lora:], cos_t, sin_t).astype(BF16)
    return rms_norm(latent[:, :lora], g_kv), k_pe


def block_index(tokens, vocab_local):
    ids = tokens.reshape(-1) - lax.axis_index('tp') * vocab_local
    n = ids.shape[0]
    owned = (ids >= 0) & (ids < vocab_local)
    blk = jnp.where(owned, ids >> 3, -1)
    pos = jnp.arange(n, dtype=jnp.int32)
    eq = (blk[:, None] == blk[None, :])
    first = jnp.min(jnp.where(eq, pos[None, :], n), axis=1)
    isf = owned & (first == pos)
    slot = jnp.sum((isf[None, :] & (pos[None, :] < first[:, None])).astype(jnp.int32), axis=1)
    key = jnp.where(owned, slot * 8 + (ids & 7), -1)
    blocks = jnp.sum(jnp.where(isf[None, :] & (slot[None, :] == pos[:, None]), blk[None, :], 0), axis=1)
    count = jnp.sum(isf.astype(jnp.int32)).reshape(1)
    return key, blocks, count


def gather_body(count_ref, blocks_ref, key_ref, tail_ref, table_ref, out_ref, stage, sem):
    rows, width = out_ref.shape
    full = table_ref.shape[0] // 8
    stage[...] = jnp.zeros_like(stage)
    out_ref[...] = jnp.zeros_like(out_ref)
    count = count_ref[0]

    def fetch(b, i):
        return pltpu.make_async_copy(table_ref.at[pl.ds(pl.multiple_of(b * 8, 8), 8), :], stage.at[i], sem)

    def chunk(ci, carry):
        base = ci * GB
        n = jnp.minimum(GB, count - base)

        def start(i, c):
            b = blocks_ref[base + i]

            @pl.when(b < full)
            def _():
                fetch(b, i).start()

            @pl.when(b >= full)
            def _():
                stage[i] = tail_ref[...]
            return c

        def wait(i, c):
            b = blocks_ref[base + i]

            @pl.when(b < full)
            def _():
                fetch(b, i).wait()
            return c

        lax.fori_loop(0, n, start, 0)
        lax.fori_loop(0, n, wait, 0)
        cols = lax.broadcasted_iota(jnp.int32, (rows, GB * 8), 1) + base * 8
        hot = jnp.where(cols == key_ref[...], 1.0, 0.0).astype(BF16)
        for c in range(0, width, 512):
            got = mm(hot, stage[:, :, c:c + 512].reshape(GB * 8, 512), 1, 0)
            out_ref[:, c:c + 512] += got.astype(BF16)
        return carry

    lax.fori_loop(0, (count + GB - 1) // GB, chunk, 0)


def gather_rows(key, blocks, count, table):
    rows, (vocab, width) = key.shape[0], table.shape
    full = vocab // 8 * 8
    tail = jnp.pad(table[full:], ((0, 8 - (vocab - full)), (0, 0)))
    smem = pl.BlockSpec(memory_space=pltpu.SMEM)
    return pl.pallas_call(
        gather_body, out_shape=jax.ShapeDtypeStruct((rows, width), BF16),
        in_specs=[smem, smem, pl.BlockSpec(memory_space=VM), pl.BlockSpec(memory_space=VM), pl.BlockSpec(memory_space=pl.ANY)],
        out_specs=pl.BlockSpec(memory_space=VM),
        scratch_shapes=[VM((GB, 8, width), BF16), pltpu.SemaphoreType.DMA],
        compiler_params=pltpu.CompilerParams(vmem_limit_bytes=40 << 20), name='gather_rows',
    )(count, blocks, key[:, None], tail, table)


ZR = 248


def table_grad_body(count_ref, blocks_ref, key_ref, de_ref, out_ref, tail_ref, zero, stage, zsem, sem):
    rows, width = de_ref.shape
    vocab = out_ref.shape[0]
    full = vocab // 8
    zero[...] = jnp.zeros_like(zero)
    tail_ref[...] = jnp.zeros_like(tail_ref)
    fills = [(r, min(ZR, full * 8 - r)) for r in range(0, full * 8, ZR)]
    copies = [pltpu.make_async_copy(zero.at[pl.ds(0, n), :], out_ref.at[pl.ds(r, n), :], zsem) for r, n in fills]
    for cp in copies:
        cp.start()
    count = count_ref[0]

    def put(b, i):
        return pltpu.make_async_copy(stage.at[i], out_ref.at[pl.ds(pl.multiple_of(b * 8, 8), 8), :], sem)

    def sums(ci):
        ids = lax.broadcasted_iota(jnp.int32, (GB * 8, rows), 0) + ci * (GB * 8)
        hot = jnp.where(ids == key_ref[...], 1.0, 0.0).astype(BF16)
        for c in range(0, width, 512):
            got = mm(hot, de_ref[:, c:c + 512], 1, 0)
            stage[:, :, c:c + 512] = got.astype(BF16).reshape(GB, 8, 512)

    def move(ci, go):
        base = ci * GB

        def one(i, c):
            b = blocks_ref[base + i]

            @pl.when(b < full)
            def _():
                go(put(b, i))
            @pl.when(b >= full)
            def _():
                tail_ref[...] = stage[i]
            return c

        lax.fori_loop(0, jnp.minimum(GB, count - base), one, 0)

    sums(0)
    for cp in copies:
        cp.wait()

    def chunk(ci, carry):
        @pl.when(ci > 0)
        def _():
            sums(ci)
        move(ci, lambda cp: cp.start())
        move(ci, lambda cp: cp.wait())
        return carry

    lax.fori_loop(0, (count + GB - 1) // GB, chunk, 0)


def table_grad(key, blocks, count, de_full, vocab):
    width = de_full.shape[1]
    smem = pl.BlockSpec(memory_space=pltpu.SMEM)
    full = vocab // 8 * 8
    out, tail = pl.pallas_call(
        table_grad_body, out_shape=[jax.ShapeDtypeStruct((vocab, width), BF16), jax.ShapeDtypeStruct((8, width), BF16)],
        in_specs=[smem, smem, pl.BlockSpec(memory_space=VM), pl.BlockSpec(memory_space=VM)],
        out_specs=[pl.BlockSpec(memory_space=pl.ANY), pl.BlockSpec(memory_space=VM)],
        scratch_shapes=[VM((ZR, width), BF16), VM((GB, 8, width), BF16), pltpu.SemaphoreType.DMA, pltpu.SemaphoreType.DMA],
        compiler_params=pltpu.CompilerParams(vmem_limit_bytes=40 << 20), name='table_grad',
    )(count, blocks, key[None, :], de_full)
    return lax.dynamic_update_slice(out, tail[:vocab - full], (full, 0))


def heads_of(q_ref, kn_ref, kp_ref, cos_ref, sin_ref, nope, half):
    q_pe = q_ref[nope:, :].astype(F32)
    lo, hi, cos_t, sin_t = q_pe[:half], q_pe[half:], cos_ref[...], sin_ref[...]
    q_all = jnp.concatenate([q_ref[:nope, :], (lo * cos_t - hi * sin_t).astype(BF16), (hi * cos_t + lo * sin_t).astype(BF16)], axis=0)
    return q_all, jnp.concatenate([kn_ref[...], kp_ref[...]], axis=0)


def scores_of(k_all, q_all, ki, qi, scale):
    s = mm(k_all[:, ki * QB:(ki + 1) * QB], q_all[:, qi * QB:(qi + 1) * QB], 0, 0) * scale
    if ki == qi:
        keys = lax.broadcasted_iota(jnp.int32, (QB, QB), 0)
        s = jnp.where(keys <= lax.broadcasted_iota(jnp.int32, (QB, QB), 1), s, -1e30)
    return s


def attn_fwd_body(q_ref, kn_ref, kp_ref, v_ref, cos_ref, sin_ref, o_ref, lse_ref):
    nope, half = kn_ref.shape[0], cos_ref.shape[0]
    scale = q_ref.shape[0] ** -0.5 * LOG2E
    q_all, k_all = heads_of(q_ref, kn_ref, kp_ref, cos_ref, sin_ref, nope, half)
    for qi in range(q_ref.shape[1] // QB):
        lanes = slice(qi * QB, (qi + 1) * QB)
        s = [scores_of(k_all, q_all, ki, qi, scale) for ki in range(qi + 1)]
        top = functools.reduce(jnp.maximum, [jnp.max(x, axis=0, keepdims=True) for x in s])
        p = [jnp.exp2(x - top) for x in s]
        total = sum(jnp.sum(x, axis=0, keepdims=True) for x in p)
        inv = 1.0 / total
        o = sum(mm(v_ref[:, ki * QB:(ki + 1) * QB], (x * inv).astype(BF16), 1, 0) for ki, x in enumerate(p))
        o_ref[:, lanes] = o.astype(BF16)
        lse_ref[0, :, lanes] = top + jnp.log2(total)


def attn_bwd_body(q_ref, kn_ref, kp_ref, v_ref, cos_ref, sin_ref, lse_ref, do_ref, dq_ref, dkn_ref, dv_ref, dkp_ref, dk_acc, dv_acc):
    nope, half = kn_ref.shape[0], cos_ref.shape[0]
    raw = q_ref.shape[0] ** -0.5
    q_all, k_all = heads_of(q_ref, kn_ref, kp_ref, cos_ref, sin_ref, nope, half)
    dk_acc[...] = jnp.zeros_like(dk_acc)
    dv_acc[...] = jnp.zeros_like(dv_acc)
    for qi in range(q_ref.shape[1] // QB):
        lanes = slice(qi * QB, (qi + 1) * QB)
        q_b, do_b, lse = q_all[:, lanes], do_ref[:, lanes], lse_ref[0, :, lanes]
        p = [jnp.exp2(scores_of(k_all, q_all, ki, qi, raw * LOG2E) - lse) for ki in range(qi + 1)]
        dp = [mm(v_ref[:, ki * QB:(ki + 1) * QB], do_b, 0, 0) for ki in range(qi + 1)]
        delta = sum(jnp.sum(a * b, axis=0, keepdims=True) for a, b in zip(p, dp))
        dq = None
        for ki in range(qi + 1):
            keys = slice(ki * QB, (ki + 1) * QB)
            ds = (p[ki] * (dp[ki] - delta) * raw).astype(BF16)
            part = mm(k_all[:, keys], ds, 1, 0)
            dq = part if dq is None else dq + part
            dk_acc[:, keys] += mm(q_b, ds, 1, 1)
            dv_acc[:, keys] += mm(do_b, p[ki].astype(BF16), 1, 1)
        cos_t, sin_t = cos_ref[:, lanes], sin_ref[:, lanes]
        lo, hi = dq[nope:nope + half], dq[nope + half:]
        dq_ref[:nope, lanes] = dq[:nope].astype(BF16)
        dq_ref[nope:nope + half, lanes] = (lo * cos_t + hi * sin_t).astype(BF16)
        dq_ref[nope + half:, lanes] = (hi * cos_t - lo * sin_t).astype(BF16)
    dkn_ref[...] = dk_acc[:nope, :].astype(BF16)
    dv_ref[...] = dv_acc[...].astype(BF16)

    @pl.when(pl.program_id(0) == 0)
    def _():
        dkp_ref[...] = jnp.zeros_like(dkp_ref)
    dkp_ref[...] += dk_acc[nope:, :]


def attn_specs(heads, qd, nope, rope, vd, seq):
    per = lambda r: pl.BlockSpec((r, seq), lambda h: (h, 0))
    one = lambda r: pl.BlockSpec((r, seq), lambda h: (0, 0))
    return [per(qd), per(nope), one(rope), per(vd), one(rope // 2), one(rope // 2)], per, one, pl.BlockSpec((1, 1, seq), lambda h: (h, 0, 0))


def attend_fwd(q, kn, kp, v, cos_t, sin_t, heads):
    seq, qd, nope, vd, rope = q.shape[1], q.shape[0] // heads, kn.shape[0] // heads, v.shape[0] // heads, kp.shape[0]
    ins, per, one, lse = attn_specs(heads, qd, nope, rope, vd, seq)
    return pl.pallas_call(
        attn_fwd_body, grid=(heads,), in_specs=ins, out_specs=[per(vd), lse],
        out_shape=[jax.ShapeDtypeStruct((heads * vd, seq), BF16), jax.ShapeDtypeStruct((heads, 1, seq), F32)],
        compiler_params=pltpu.CompilerParams(vmem_limit_bytes=40 << 20), name='attend_fwd',
    )(q, kn, kp, v, cos_t, sin_t)


def attend_bwd(q, kn, kp, v, cos_t, sin_t, lse, do, heads):
    seq, qd, nope, vd, rope = q.shape[1], q.shape[0] // heads, kn.shape[0] // heads, v.shape[0] // heads, kp.shape[0]
    ins, per, one, lse_spec = attn_specs(heads, qd, nope, rope, vd, seq)
    return pl.pallas_call(
        attn_bwd_body, grid=(heads,), in_specs=ins + [lse_spec, per(vd)], out_specs=[per(qd), per(nope), per(vd), one(rope)],
        out_shape=[jax.ShapeDtypeStruct(q.shape, BF16), jax.ShapeDtypeStruct(kn.shape, BF16), jax.ShapeDtypeStruct(v.shape, BF16), jax.ShapeDtypeStruct(kp.shape, F32)],
        scratch_shapes=[VM((qd, seq), F32), VM((vd, seq), F32)],
        compiler_params=pltpu.CompilerParams(vmem_limit_bytes=40 << 20), name='attend_bwd',
    )(q, kn, kp, v, cos_t, sin_t, lse, do)


def gather(x):
    return lax.all_gather(x, 'tp', axis=0, tiled=True)


def scatter(x):
    return lax.psum_scatter(x, 'tp', scatter_dimension=0, tiled=True)


def layer_pass(embedded, d_out, w_q, w_dkv, g_kv, w_uk, w_uv, w_o, g_attn, g_mlp, w_gate, w_up, w_down):
    w_q, heads = w_q
    x_attn_loc, attn_norm_pull = jax.vjp(rms_norm, embedded.astype(F32), g_attn)
    x_attn = gather(x_attn_loc)
    seq = x_attn.shape[0]
    rope = w_dkv.shape[0] - g_kv.shape[0]
    cos_t, sin_t = (t.T for t in rope_tables(seq, rope))
    query = mm(w_q, x_attn, 1, 1).astype(BF16)
    latent = mm(x_attn, w_dkv, 1, 1)
    (c_kv, k_pe), kv_pull = jax.vjp(kv_prep, latent, g_kv)
    k_nope = mm(w_uk, c_kv, 1, 1).astype(BF16)
    value = mm(w_uv, c_kv, 1, 1).astype(BF16)
    k_pe_t = k_pe.T
    attn_out, lse = attend_fwd(query, k_nope, k_pe_t, value, cos_t, sin_t, heads)
    attn_part = mm(attn_out, w_o, 0, 0).astype(BF16)
    attn_loc = scatter(attn_part)
    residual = (embedded.astype(F32) + attn_loc.astype(F32)).astype(BF16)
    x_mlp_loc, mlp_norm_pull = jax.vjp(rms_norm, residual.astype(F32), g_mlp)
    x_mlp = gather(x_mlp_loc)
    gate = mm(x_mlp, w_gate, 1, 1)
    up_proj = mm(x_mlp, w_up, 1, 1)
    gate_sig = jax.nn.sigmoid(gate)
    hidden = (gate * gate_sig * up_proj).astype(BF16)
    mlp_loc = scatter(mm(hidden, w_down, 1, 0).astype(BF16))
    layer_out = (residual.astype(F32) + mlp_loc.astype(F32)).astype(BF16)

    dy_full = gather(d_out)
    d_hidden = mm(dy_full, w_down, 1, 1)
    dw_down = mm(hidden, dy_full, 0, 0)
    d_up = (d_hidden * gate * gate_sig).astype(BF16)
    d_gate = (d_hidden * up_proj * gate_sig * (1.0 + gate * (1.0 - gate_sig))).astype(BF16)
    dw_gate = mm(d_gate, x_mlp, 0, 0)
    dw_up = mm(d_up, x_mlp, 0, 0)
    dx_mlp = scatter((mm(d_gate, w_gate, 1, 0) + mm(d_up, w_up, 1, 0)).astype(BF16))
    d_res_norm, dg_mlp_part = mlp_norm_pull(dx_mlp)
    d_residual = d_out.astype(F32) + d_res_norm
    d_attn_full = gather(d_residual.astype(BF16))
    dw_o = mm(attn_out, d_attn_full, 1, 0)
    d_attn_out = mm(w_o, d_attn_full, 1, 1).astype(BF16)
    d_query, d_knope, d_value, d_kpe = attend_bwd(query, k_nope, k_pe_t, value, cos_t, sin_t, lse, d_attn_out, heads)
    dw_uk = mm(d_knope, c_kv, 1, 0)
    dw_uv = mm(d_value, c_kv, 1, 0)
    d_ckv = (mm(d_knope, w_uk, 0, 0) + mm(d_value, w_uv, 0, 0)).astype(BF16)
    d_latent, dg_kv_part = kv_pull((d_ckv, d_kpe.T.astype(BF16)))
    d_latent = d_latent.astype(BF16)
    dw_q = mm(d_query, x_attn, 1, 0)
    dw_dkv_part = mm(d_latent, x_attn, 0, 0)
    dx_attn = scatter((mm(d_query, w_q, 0, 0) + mm(d_latent, w_dkv, 1, 0)).astype(BF16))
    d_emb_norm, dg_attn_part = attn_norm_pull(dx_attn)
    d_embed = (d_residual + d_emb_norm).astype(BF16)
    dw_dkv, dg_kv, dg_attn, dg_mlp = lax.psum((dw_dkv_part, dg_kv_part, dg_attn_part, dg_mlp_part), 'tp')
    return layer_out, d_embed, (dw_q, dw_dkv, dg_kv, dw_uk, dw_uv, dw_o, dg_attn, dg_mlp, dw_gate, dw_up, dw_down)


def rows_of(w):
    return jnp.transpose(w, (1, 2, 0)).reshape(-1, w.shape[0])


def unrows(g, heads):
    return jnp.transpose(g.reshape(heads, -1, g.shape[1]), (2, 0, 1))


def solution(mesh):
    def device_step(tokens, embed_table, w_q, w_dkv, g_kv, w_uk, w_uv, w_o, g_attn, g_mlp, w_gate, w_up, w_down, d_out):
        vocab_local, model_dim = embed_table.shape
        heads = w_q.shape[1]
        key, blocks, count = block_index(tokens, vocab_local)
        rows = gather_rows(key, blocks, count, embed_table)
        embedded = scatter(rows)
        layer_out, d_embed, grads = layer_pass(
            embedded, d_out[0], (rows_of(w_q), heads), w_dkv.T, g_kv, rows_of(w_uk), rows_of(w_uv), w_o.reshape(-1, model_dim),
            g_attn, g_mlp, w_gate.T, w_up.T, w_down)
        de_full = gather(d_embed)
        d_table = table_grad(key, blocks, count, de_full, vocab_local)
        dw_q, dw_dkv, dg_kv, dw_uk, dw_uv, dw_o, dg_attn, dg_mlp, dw_gate, dw_up, dw_down = grads
        return (layer_out[None], d_table, unrows(dw_q, heads), dw_dkv.T, dg_kv, unrows(dw_uk, heads), unrows(dw_uv, heads),
                dw_o.reshape(w_o.shape), dg_attn, dg_mlp, dw_gate.T, dw_up.T, dw_down)

    row_spec = P('dp', 'tp', None)
    head_spec = P(None, 'tp', None)
    in_specs = (P('dp', None), P('tp', None), head_spec, P(None, None), P(None), head_spec, head_spec, P('tp', None, None), P(None), P(None), P(None, 'tp'), P(None, 'tp'), P('tp', None), row_spec)
    out_specs = (row_spec, P(('dp', 'tp'), None), P('dp', 'tp', None), P('dp', None), P('dp'), P('dp', 'tp', None), P('dp', 'tp', None), P(('dp', 'tp'), None, None), P('dp'), P('dp'), P('dp', 'tp'), P('dp', 'tp'), P(('dp', 'tp'), None))
    return jax.shard_map(device_step, mesh=mesh, in_specs=in_specs, out_specs=out_specs, check_vma=False)
```

time: 1070 us -> 625 us (0.58)
  other arithmetic: 308 us -> 24.6 us
  local copies, waits for them, and re-layouts: 130 us -> 19.3 us
  matrix products: 225 us -> 123 us
  Pallas kernels: 0 us -> 49.4 us
    scatter-add x1 -> x0, other arithmetic: 211 us -> none  [device_step(): jax.ops.segment_sum(de_full.reshape(-1, model_dim).astype(jnp.float32), s...]
    dot_general x27 -> x24, matrix products: 213 us -> 123 us  [mm(): lax.dot_general(lhs, rhs, (((lc,), (rc,)), ((), ())), preferred_element_t...]
    gather x1 -> x0, local copies, waits for them, and re-layouts: 86.7 us -> none  [device_step(): rows = jnp.take(embed_table, jnp.where(owned, local_ids, 0), axis=0)]
    convert_element_type x10 -> x6, other arithmetic: 67.3 us -> 10.1 us  [the longest x1 3.94 us: layer_pass(): d_embed = (d_residual + d_emb_norm).astype(BF16)]
    pallas_call x0 -> x4, Pallas kernels: none -> 49.4 us  [the longest x1 20 us: table_grad(): pl.pallas_call(table_grad_body, out_shape=[jax.ShapeDtypeStruct((vocab, w...]
    broadcast_in_dim x1 -> x0, local copies, waits for them, and re-layouts: 29.4 us -> none  [device_step(): jax.ops.segment_sum(de_full.reshape(-1, model_dim).astype(jnp.float32), s...]
    unnamed x6 -> x0, matrix products: 12.6 us -> none
  transfers between devices with their start and end apart: 11 -> 11, of which waited for: 9 -> 10; matrix products, arithmetic and copies ran while one was open for 35% -> 12% of each run, Pallas kernels for 0% -> 3%
where the time goes in v1:
time: 625 us; the launch traced here: 619 us
  waiting for transfers between devices  363 us (58%)
  matrix products  123 us (20%)
  Pallas kernels  49.4 us (8%)
  other arithmetic  24.6 us (4%)
  blocking collectives  23.6 us (4%)
  local copies, waits for them, and re-layouts  19.3 us (3%)
  between operations  15 us (2%)
    reduce_scatter x5, waiting for transfers between devices, scatter(): return lax.psum_scatter(x, 'tp', scatter_dimension=0, tiled=True)  234 us
    all_gather x5, waiting for transfers between devices, gather(): return lax.all_gather(x, 'tp', axis=0, tiled=True)  125 us
    dot_general x24, matrix products, mm(): lax.dot_general(lhs, rhs, (((lc,), (rc,)), ((), ())), preferred_element_t...  123 us
    psum x1, blocking collectives, layer_pass(): lax.psum((dw_dkv_part, dg_kv_part, dg_attn_part, dg_mlp_part), 'tp')  23.6 us
    pallas_call x1, Pallas kernels, table_grad(): pl.pallas_call(table_grad_body, out_shape=[jax.ShapeDtypeStruct((vocab, w...  20 us
    unnamed x109, local copies, waits for them, and re-layouts  16.5 us
    pallas_call x1, Pallas kernels, attend_bwd(): pl.pallas_call(attn_bwd_body, grid=(heads,), in_specs=ins + [lse_spec, pe...  13.9 us
  transfers between devices with their start and end apart: 11, of which 10 were waited for; matrix products, arithmetic and copies ran while one was open for 12% of the time, Pallas kernels for 3%

profile of v1, /device:TPU:0, one launch (start us, length us, event | category | flops | bytes accessed | tf_op | source)
XLA Modules:
  0.0 619.3 jit_solution(1478497592298055094)
XLA Ops:
  15.2 6.1 gather_rows.1
  21.3 2.3 copy-done.1
  23.8 50.6 %reduce-scatter.6.cloned.1.call-done = bf16[128,2560]{1,0:T(8,128)(2,1)} async-done(((bf16[1024,2560]{1,0:T(8,128)(2,1)}), bf16[128,2560]{1,0:T(8,128)(2,1)}) %reduce-scatter.6.cloned.1.call-update) | async-done | bytes 655376 | tf_op jit(solution)/shard_map/reduce_scatter | solution.py:290
  74.4 1.3 fusion.18
  76.7 2.1 fusion.12
  79.5 34.7 %all-gather.7.cloned.1.call-done = bf16[1024,2560]{1,0:T(8,128)(2,1)} async-done(((bf16[128,2560]{1,0:T(8,128)(2,1)}), bf16[1024,2560]{1,0:T(8,128)(2,1)}) %all-gather.7.cloned.1.call-update) | async-done | bytes 5242896 | tf_op jit(solution)/shard_map/all_gather | solution.py:286
  114.2 4.6 fusion.46
  120.7 1.6 copy-done.40
  122.4 2.7 fusion.10.q_ref
  125.1 9.4 %attend_fwd.1 = (bf16[320,1024]{1,0:T(8,128)(2,1)S(1)}, f32[5,1,1024]{2,1,0:T(1,128)S(1)}) custom-call(bf16[480,1024]{1,0:T(8,128)(2,1)S(1)} %fusion.10.q_ref, bf16[320,1024]{1,0:T(8,128)(2,1)S(1)} %fusion.25.kn_ref, bf16[32,1024]{1,0:T(8,128)(2,1)S(1)} %maximum_bitcast_fusion.kp_ref, bf16[320,1024]{1,0:T(8,128)(2,1)S(1)} %fusion.26.v_ref, ...), custom_call_target="tpu_custom_call" | custom-call | tf_op jit(solution)/shard_map/attend_fwd/pallas_call | solution.py:267
  135.4 4.6 convolution_convert_fusion
  140.1 47.8 %reduce-scatter.8.cloned.1.call-done = bf16[128,2560]{1,0:T(8,128)(2,1)} async-done(((bf16[1024,2560]{1,0:T(8,128)(2,1)}), bf16[128,2560]{1,0:T(8,128)(2,1)}) %reduce-scatter.8.cloned.1.call-update) | async-done | bytes 655376 | tf_op jit(solution)/shard_map/reduce_scatter | solution.py:290
  187.9 1.6 fusion.21
  190.4 1.1 fusion.11
  192.6 34.2 %all-gather.9.cloned.1.call-done = bf16[1024,2560]{1,0:T(8,128)(2,1)} async-done(((bf16[128,2560]{1,0:T(8,128)(2,1)}), bf16[1024,2560]{1,0:T(8,128)(2,1)}) %all-gather.9.cloned.1.call-update) | async-done | bytes 5242896 | tf_op jit(solution)/shard_map/all_gather | solution.py:286
  226.8 10.0 %fusion.47 = f32[1024,800]{0,1:T(8,128)} fusion(bf16[1024,2560]{1,0:T(8,128)(2,1)} %all-gather.9.cloned.1.call-done, bf16[2560,800]{0,1:T(8,128)(2,1)} %param.24), kind=kOutput, calls=%fused_computation.115 | convolution fusion | flops 4194304000 | bytes 12615680 | tf_op jit(solution)/shard_map/dot_general | solution.py:20
  236.8 6.1 fusion.48
  242.9 20.7 %all-gather.15.cloned.1.call-done = bf16[1,1024,2560]{2,1,0:T(8,128)(2,1)} async-done(((bf16[1,128,2560]{2,1,0:T(8,128)(2,1)}), bf16[1,1024,2560]{2,1,0:T(8,128)(2,1)}) %all-gather.15.cloned.1.call-update) | async-done | bytes 5242896 | tf_op jit(solution)/shard_map/all_gather | solution.py:286
  263.6 12.5 %multiply_convert_fusion = (bf16[1024,800]{0,1:T(8,128)(2,1)S(1)}, bf16[1024,800]{0,1:T(8,128)(2,1)S(1)}, bf16[1024,800]{0,1:T(8,128)(2,1)}) fusion(f32[1024,800]{0,1:T(8,128)} %fusion.47, f32[1024,800]{0,1:T(8,128)} %fusion.48, bf16[800,2560]{1,0:T(8,128)(2,1)} %param.26, bf16[1,1024,2560]{2,1,0:T(8,128)(2,1)} %all-gather.15.cloned.1.call-done), kind=kOutput, calls=%fused_computation.15 | convolution fusion | flops 4207411200 | bytes 20807680 | tf_op jit(solution)/shard_map/dot_general | solution.py:20
  276.1 5.9 fusion.49
  282.0 7.8 %add_convert_fusion.1 = bf16[1024,2560]{1,0:T(8,128)(2,1)} fusion(f32[1024,2560]{1,0:T(8,128)S(1)} %fusion.49, bf16[1024,800]{0,1:T(8,128)(2,1)S(1)} %get-tuple-element.42, bf16[2560,800]{0,1:T(8,128)(2,1)S(1)} %copy-done.44), kind=kOutput, calls=%fused_computation.1 | convolution fusion | flops 4199546880 | bytes 21463040 | tf_op jit(solution)/shard_map/dot_general | solution.py:20
  289.8 47.8 %reduce-scatter.12.cloned.1.call-done = bf16[128,2560]{1,0:T(8,128)(2,1)} async-done(((bf16[1024,2560]{1,0:T(8,128)(2,1)}), bf16[128,2560]{1,0:T(8,128)(2,1)}) %reduce-scatter.12.cloned.1.call-update) | async-done | bytes 655376 | tf_op jit(solution)/shard_map/reduce_scatter | solution.py:290
  337.6 2.0 fusion.13
  340.8 2.8 fusion.33
  343.7 35.2 %all-gather.11.cloned.1.call-done = bf16[1024,2560]{1,0:T(8,128)(2,1)} async-done(((bf16[128,2560]{1,0:T(8,128)(2,1)}), bf16[1024,2560]{1,0:T(8,128)(2,1)}) %all-gather.11.cloned.1.call-update) | async-done | bytes 5242896 | tf_op jit(solution)/shard_map/all_gather | solution.py:286
  378.9 5.0 fusion.27.do_ref
  384.0 13.9 %attend_bwd.1 = (bf16[480,1024]{1,0:T(8,128)(2,1)S(1)}, bf16[320,1024]{1,0:T(8,128)(2,1)S(1)}, bf16[320,1024]{1,0:T(8,128)(2,1)S(1)}, f32[32,1024]{1,0:T(8,128)S(1)}) custom-call(bf16[480,1024]{1,0:T(8,128)(2,1)S(1)} %copy-done.6, bf16[320,1024]{1,0:T(8,128)(2,1)S(1)} %fusion.25.kn_ref, bf16[32,1024]{1,0:T(8,128)(2,1)S(1)} %maximum_bitcast_fusion.kp_ref, ...), custom_call_target="tpu_custom_call" | custom-call | tf_op jit(solution)/shard_map/attend_bwd/pallas_call | solution.py:277
  399.5 2.9 fusion.50
  404.2 4.8 add_convert_fusion
  409.1 9.4 %convolution_convert_fusion.1 = bf16[1024,2560]{1,0:T(8,128)(2,1)} fusion(bf16[1024,800]{0,1:T(8,128)(2,1)} %get-tuple-element.44, bf16[800,2560]{1,0:T(8,128)(2,1)} %param.26), kind=kOutput, calls=%fused_computation.3 | convolution fusion | flops 4196925440 | bytes 10977280 | tf_op jit(solution)/shard_map/dot_general | solution.py:20
  418.8 38.1 %reduce-scatter.14.cloned.1.call-done = bf16[128,2560]{1,0:T(8,128)(2,1)} async-done(((bf16[1024,2560]{1,0:T(8,128)(2,1)}), bf16[128,2560]{1,0:T(8,128)(2,1)}) %reduce-scatter.14.cloned.1.call-update) | async-done | bytes 655376 | tf_op jit(solution)/shard_map/reduce_scatter | solution.py:290
  456.9 1.8 fusion.14
  458.7 49.8 %reduce-scatter.10.cloned.1.call-done = bf16[128,2560]{1,0:T(8,128)(2,1)} async-done(((bf16[1024,2560]{1,0:T(8,128)(2,1)}), bf16[128,2560]{1,0:T(8,128)(2,1)}) %reduce-scatter.10.cloned.1.call-update) | async-done | bytes 655376 | tf_op jit(solution)/shard_map/reduce_scatter | solution.py:290
  508.5 3.9 fusion.17
  512.5 10.8 %fusion.56 = f32[2560,800]{0,1:T(8,128)} fusion(bf16[1024,800]{0,1:T(8,128)(2,1)} %copy-done.46, bf16[1024,2560]{1,0:T(8,128)(2,1)} %all-gather.9.cloned.1.call-done), kind=kOutput, calls=%fused_computation.124 | convolution fusion | flops 4194304000 | bytes 15073280 | tf_op jit(solution)/shard_map/dot_general | solution.py:20
  523.4 9.2 %fusion.57 = f32[2560,800]{0,1:T(8,128)} fusion(bf16[1024,800]{0,1:T(8,128)(2,1)S(1)} %copy-done.49, bf16[1024,2560]{1,0:T(8,128)(2,1)} %all-gather.9.cloned.1.call-done), kind=kOutput, calls=%fused_computation.125 | convolution fusion | flops 4194304000 | bytes 15073280 | tf_op jit(solution)/shard_map/dot_general | solution.py:20
  532.6 6.6 %fusion = f32[800,2560]{1,0:T(8,128)} fusion(bf16[1024,800]{0,1:T(8,128)(2,1)S(1)} %copy-done.47, bf16[1,1024,2560]{2,1,0:T(8,128)(2,1)S(1)} %bitcast.119), kind=kOutput, calls=%fused_computation.4 | convolution fusion | flops 4194304000 | bytes 15073280 | tf_op jit(solution)/shard_map/dot_general | solution.py:20
  539.2 1.1 fusion.53
  540.3 3.3 fusion.34
  543.7 1.1 copy-done.14
  544.7 6.2 %fusion.55 = f32[320,2560]{1,0:T(8,128)} fusion(bf16[320,1024]{1,0:T(8,128)(2,1)S(1)} %copy-done.14, bf16[1024,2560]{1,0:T(8,128)(2,1)} %all-gather.11.cloned.1.call-done), kind=kOutput, calls=%fused_computation.123 | convolution fusion | flops 1677721600 | bytes 9175040 | tf_op jit(solution)/shard_map/dot_general | solution.py:20
  550.9 1.1 fusion.54
  552.0 6.8 %fusion.52 = f32[480,2560]{1,0:T(8,128)} fusion(bf16[480,1024]{1,0:T(8,128)(2,1)S(1)} %copy-done.12, bf16[1024,2560]{1,0:T(8,128)(2,1)} %all-gather.7.cloned.1.call-done), kind=kOutput, calls=%fused_computation.120 | convolution fusion | flops 2516582400 | bytes 11141120 | tf_op jit(solution)/shard_map/dot_general | solution.py:20
  558.9 23.6 %all-reduce.5 = (f32[256]{0:T(256)}, f32[2560]{0:T(1024)}, f32[2560]{0:T(1024)}) all-reduce(f32[256]{0:T(256)S(1)} %get-tuple-element.29, f32[2560]{0:T(1024)S(1)} %get-tuple-element.33, f32[2560]{0:T(1024)S(1)} %get-tuple-element.31), channel_id=1, replica_groups=mesh['dp'=1,'tp'=8] {'tp'}, use_global_device_ids=true, to_apply=%region_17.18 | all-reduce | flops 5376 | bytes 43008 | tf_op jit(solution)/shard_map/psum | solution.py:343
  582.5 2.5 copy-done.4
  585.0 20.0 %table_grad.1 = (bf16[9181,2560]{1,0:T(8,128)(2,1)}, bf16[8,2560]{1,0:T(8,128)(2,1)S(1)}) custom-call(s32[1]{0:T(128)} %bitcast.2.count_ref, s32[1024]{0:T(1024)S(1)} %select_reduce_fusion.blocks_ref, s32[1,1024]{1,0:T(1,128)S(1)} %get-tuple-element.51.key_ref, bf16[1024,2560]{1,0:T(8,128)(2,1)S(1)} %copy-done.4), custom_call_target="tpu_custom_call" | custom-call | tf_op jit(solution)/shard_map/table_grad/pallas_call | solution.py:183
  605.6 3.1 all-reduce.8.cloned.1.call-done
  608.7 3.6 copy.35
  (166 shorter events, 20.0 us)
Async XLA Ops:
  7.2 113.6 %copy-start = (bf16[2560,5,96]{0,2,1:T(8,128)(2,1)S(1)}, bf16[2560,5,96]{0,2,1:T(8,128)(2,1)}, u32[]{:S(2)}) copy-start(bf16[2560,5,96]{0,2,1:T(8,128)(2,1)} %param.16) | copy-start | bytes 7372804
  7.2 67.2 %reduce-scatter.6.cloned.1.call-start = ((), (), s32[]{:S(2)}) async-start(), calls=%async_computation.5 | async-start | bytes 5898240 | tf_op jit(solution)/shard_map/reduce_scatter | solution.py:290
  23.7 53.0 %copy-start.29 = (f32[2560]{0:T(1024)S(1)}, f32[2560]{0:T(1024)}, u32[]{:S(2)}) copy-start(f32[2560]{0:T(1024)} %param.22) | copy-start | bytes 30724
  23.7 90.5 %all-gather.7.cloned.1.call-start = ((), (), s32[]{:S(2)}) async-start(), calls=%async_computation.6 | async-start | bytes 5898240 | tf_op jit(solution)/shard_map/all_gather | solution.py:286
  78.9 109.0 %reduce-scatter.8.cloned.1.call-start = ((), (), s32[]{:S(2)}) async-start(), calls=%async_computation.7 | async-start | bytes 5898240 | tf_op jit(solution)/shard_map/reduce_scatter | solution.py:290
  79.2 39.7 %copy-start.33 = (f32[16]{0:T(128)}, f32[16]{0:T(128)S(1)}, u32[]{:S(2)}) copy-start(f32[16]{0:T(128)S(1)} %multiply_power_fusion) | copy-start | bytes 196
  79.5 39.8 %copy-start.30 = (f32[256]{0:T(256)S(1)}, f32[256]{0:T(256)}, u32[]{:S(2)}) copy-start(f32[256]{0:T(256)} %param.18) | copy-start | bytes 3076
  122.4 13.0 %copy-start.45 = (bf16[5,64,2560]{2,1,0:T(8,128)(2,1)S(1)}, bf16[5,64,2560]{2,1,0:T(8,128)(2,1)}, u32[]{:S(2)}) copy-start(bf16[5,64,2560]{2,1,0:T(8,128)(2,1)} %param.21) | copy-start | bytes 4915204
  125.1 9.4 %copy-start.5 = (bf16[480,1024]{1,0:T(8,128)(2,1)}, bf16[480,1024]{1,0:T(8,128)(2,1)S(1)}, u32[]{:S(2)}) copy-start(bf16[480,1024]{1,0:T(8,128)(2,1)S(1)} %fusion.10.q_ref) | copy-start | bytes 2949124
  140.1 50.3 %copy-start.28 = (f32[2560]{0:T(1024)S(1)}, f32[2560]{0:T(1024)}, u32[]{:S(2)}) copy-start(f32[2560]{0:T(1024)} %param.23) | copy-start | bytes 30724
  140.1 86.7 %all-gather.9.cloned.1.call-start = ((), (), s32[]{:S(2)}) async-start(), calls=%async_computation.8 | async-start | bytes 5898240 | tf_op jit(solution)/shard_map/all_gather | solution.py:286
  189.5 47.2 %copy-start.37 = (f32[128]{0:T(128)}, f32[128]{0:T(128)S(1)}, u32[]{:S(2)}) copy-start(f32[128]{0:T(128)S(1)} %get-tuple-element.38) | copy-start | bytes 1540
  191.5 72.1 %all-gather.15.cloned.1.call-start = ((), (), s32[]{:S(2)}) async-start(), calls=%async_computation.15 | async-start | bytes 5898240 | tf_op jit(solution)/shard_map/all_gather | solution.py:286
  192.1 145.5 %reduce-scatter.12.cloned.1.call-start = ((), (), s32[]{:S(2)}) async-start(), calls=%async_computation.10 | async-start | bytes 5898240 | tf_op jit(solution)/shard_map/reduce_scatter | solution.py:290
  226.8 10.0 %copy-start.41 = (bf16[1024,2560]{1,0:T(8,128)(2,1)S(1)}, bf16[1024,2560]{1,0:T(8,128)(2,1)}, u32[]{:S(2)}) copy-start(bf16[1024,2560]{1,0:T(8,128)(2,1)} %all-gather.9.cloned.1.call-done) | copy-start | bytes 15728644
  226.8 10.0 %copy-start.43 = (bf16[2560,800]{0,1:T(8,128)(2,1)S(1)}, bf16[2560,800]{0,1:T(8,128)(2,1)}, u32[]{:S(2)}) copy-start(bf16[2560,800]{0,1:T(8,128)(2,1)} %param.25) | copy-start | bytes 12288004
  263.6 12.5 %copy-start.42 = (bf16[2560,800]{0,1:T(8,128)(2,1)S(1)}, bf16[2560,800]{0,1:T(8,128)(2,1)}, u32[]{:S(2)}) copy-start(bf16[2560,800]{0,1:T(8,128)(2,1)} %param.24) | copy-start | bytes 12288004
  276.1 5.9 copy-start.46
  276.1 5.9 copy-start.48
  276.1 5.9 copy-start.44
  289.8 89.1 %all-gather.11.cloned.1.call-start = ((), (), s32[]{:S(2)}) async-start(), calls=%async_computation.11 | async-start | bytes 5898240 | tf_op jit(solution)/shard_map/all_gather | solution.py:286
  343.6 113.3 %reduce-scatter.14.cloned.1.call-start = ((), (), s32[]{:S(2)}) async-start(), calls=%async_computation.12 | async-start | bytes 5898240 | tf_op jit(solution)/shard_map/reduce_scatter | solution.py:290
  378.9 5.0 copy-start.3
  378.9 5.0 copy-start.6
  383.9 14.5 %copy-start.18 = (f32[1024,288]{0,1:T(8,128)S(1)}, f32[1024,288]{0,1:T(8,128)}, u32[]{:S(2)}) copy-start(f32[1024,288]{0,1:T(8,128)} %copy-done.17) | copy-start | bytes 3538948
  383.9 14.5 %copy-start.27 = (bf16[256,5,64]{0,2,1:T(8,128)(2,1)S(1)}, bf16[256,5,64]{0,2,1:T(8,128)(2,1)}, u32[]{:S(2)}) copy-start(bf16[256,5,64]{0,2,1:T(8,128)(2,1)} %param.20) | copy-start | bytes 491524
  397.8 4.6 copy-start.7
  397.9 4.6 copy-start.9
  397.9 4.6 copy-start.11
  409.0 99.5 %reduce-scatter.10.cloned.1.call-start = ((), (), s32[]{:S(2)}) async-start(), calls=%async_computation.9 | async-start | bytes 5898240 | tf_op jit(solution)/shard_map/reduce_scatter | solution.py:290
  418.5 38.4 %copy-start.15 = (bf16[128,2560]{1,0:T(8,128)(2,1)S(1)}, bf16[128,2560]{1,0:T(8,128)(2,1)}, u32[]{:S(2)}) copy-start(bf16[128,2560]{1,0:T(8,128)(2,1)} %reduce-scatter.6.cloned.1.call-done) | copy-start | bytes 1966084
  418.5 38.4 %copy-start.32 = (f32[128]{0:T(128)S(1)}, f32[128]{0:T(128)}, u32[]{:S(2)}) copy-start(f32[128]{0:T(128)} %copy-done.31) | copy-start | bytes 1540
  418.5 40.2 %copy-start.39 = (f32[128]{0:T(128)S(1)}, f32[128]{0:T(128)}, u32[]{:S(2)}) copy-start(f32[128]{0:T(128)} %copy-done.38) | copy-start | bytes 1540
  418.5 90.0 %copy-start.36 = (f32[128]{0:T(128)S(1)}, f32[128]{0:T(128)}, u32[]{:S(2)}) copy-start(f32[128]{0:T(128)} %copy-done.35) | copy-start | bytes 1540
  418.6 163.9 %all-gather.13.cloned.1.call-start = ((), (), s32[]{:S(2)}) async-start(), calls=%async_computation.13 | async-start | bytes 5898240 | tf_op jit(solution)/shard_map/all_gather | solution.py:286
  512.4 96.3 %all-reduce.8.cloned.1.call-start = ((), (), s32[]{:S(2)}) async-start(), calls=%async_computation.14 | async-start | bytes 5898240 | tf_op jit(solution)/shard_map/psum | solution.py:343
  512.5 10.9 %copy-start.49 = (bf16[1024,800]{0,1:T(8,128)(2,1)S(1)}, bf16[1024,800]{0,1:T(8,128)(2,1)}, u32[]{:S(2)}) copy-start(bf16[1024,800]{0,1:T(8,128)(2,1)} %copy-done.48) | copy-start | bytes 4915204
  512.5 20.1 %slice-start.2 = ((s8[5242880]{0:T(1024)(128)(4,1)}), s8[4194304]{0:T(1024)(128)(4,1)S(1)}, s32[]{:S(2)}) async-start(s8[5242880]{0:T(1024)(128)(4,1)} %bitcast.118), calls=%async_computation.18 | async-start | bytes 8388608
  523.4 9.2 %slice-start.3 = ((s8[5242880]{0:T(1024)(128)(4,1)}), s8[1048576]{0:T(1024)(128)(4,1)S(1)}, s32[]{:S(2)}) async-start(s8[5242880]{0:T(1024)(128)(4,1)} %bitcast.118), calls=%async_computation.19 | async-start | bytes 2097152
  523.4 9.2 %copy-start.47 = (bf16[1024,800]{0,1:T(8,128)(2,1)S(1)}, bf16[1024,800]{0,1:T(8,128)(2,1)}, u32[]{:S(2)}) copy-start(bf16[1024,800]{0,1:T(8,128)(2,1)} %get-tuple-element.44) | copy-start | bytes 4915204
  523.4 17.0 %slice-start = ((s8[5242880]{0:T(1024)(128)(4,1)}), s8[4194304]{0:T(1024)(128)(4,1)S(1)}, s32[]{:S(2)}) async-start(s8[5242880]{0:T(1024)(128)(4,1)} %bitcast.116), calls=%async_computation.16 | async-start | bytes 8388608
  532.6 6.6 %copy-start.8 = (bf16[320,1024]{1,0:T(8,128)(2,1)S(1)}, bf16[320,1024]{1,0:T(8,128)(2,1)}, u32[]{:S(2)}) copy-start(bf16[320,1024]{1,0:T(8,128)(2,1)} %copy-done.7) | copy-start | bytes 1966084
  532.6 6.6 %copy-start.20 = (bf16[1024,256]{0,1:T(8,128)(2,1)S(1)}, bf16[1024,256]{0,1:T(8,128)(2,1)}, u32[]{:S(2)}) copy-start(bf16[1024,256]{0,1:T(8,128)(2,1)} %copy-done.19) | copy-start | bytes 1572868
  532.6 7.7 %copy-start.23 = (f32[1024,256]{0,1:T(8,128)S(1)}, f32[1024,256]{0,1:T(8,128)}, u32[]{:S(2)}) copy-start(f32[1024,256]{0,1:T(8,128)} %copy-done.22) | copy-start | bytes 3145732
  532.6 7.7 %slice-start.1 = ((s8[5242880]{0:T(1024)(128)(4,1)}), s8[1048576]{0:T(1024)(128)(4,1)S(1)}, s32[]{:S(2)}) async-start(s8[5242880]{0:T(1024)(128)(4,1)} %bitcast.116), calls=%async_computation.17 | async-start | bytes 2097152
  544.7 6.2 %copy-start.10 = (bf16[320,1024]{1,0:T(8,128)(2,1)S(1)}, bf16[320,1024]{1,0:T(8,128)(2,1)}, u32[]{:S(2)}) copy-start(bf16[320,1024]{1,0:T(8,128)(2,1)} %copy-done.9) | copy-start | bytes 1966084
  544.7 6.2 %copy-start.21 = (bf16[1024,256]{0,1:T(8,128)(2,1)S(1)}, bf16[1024,256]{0,1:T(8,128)(2,1)}, u32[]{:S(2)}) copy-start(bf16[1024,256]{0,1:T(8,128)(2,1)} %copy-done.19) | copy-start | bytes 1572868
  544.7 7.3 %copy-start.12 = (bf16[480,1024]{1,0:T(8,128)(2,1)S(1)}, bf16[480,1024]{1,0:T(8,128)(2,1)}, u32[]{:S(2)}) copy-start(bf16[480,1024]{1,0:T(8,128)(2,1)} %copy-done.11) | copy-start | bytes 2949124
  (17 other events, 26.7 us)
Sparse Core Ops, SparseCore 0:
  23.8 50.5 reduce-scatter.5
  79.0 35.1 all-gather.6
  140.2 47.6 reduce-scatter.7
  191.6 35.1 all-gather.8
  228.4 35.1 all-gather.14
  289.9 47.6 reduce-scatter.11
  343.7 35.1 all-gather.10
  409.1 47.6 reduce-scatter.13
  460.8 47.6 reduce-scatter.9
  512.6 35.1 all-gather.12
  551.6 57.0 all-reduce.7

commit v2 on v1

--- a/solution.py
+++ b/solution.py
@@ -290,12 +290,284 @@
     return lax.psum_scatter(x, 'tp', scatter_dimension=0, tiled=True)
 
 
-def layer_pass(embedded, d_out, w_q, w_dkv, g_kv, w_uk, w_uv, w_o, g_attn, g_mlp, w_gate, w_up, w_down):
+class Exchange:
+    def __init__(self, widths, pieces):
+        self.widths, self.pieces = widths, pieces
+
+    def rs_scratch(self, rows):
+        n = len(self.pieces)
+        out = []
+        for w in self.widths:
+            out += [VM((4, rows, w), BF16), VM((2, rows, w), BF16), VM((2, rows, w), BF16), VM((rows, w), BF16), VM((rows, w), BF16)]
+        dma = pltpu.SemaphoreType.DMA
+        return out + [dma((4, n)), dma((4, n)), dma((n,)), dma((n,)), dma((n,)), dma((n,))]
+
+    def ag_scratch(self):
+        n = len(self.pieces)
+        dma = pltpu.SemaphoreType.DMA
+        return [dma((3, n)), dma((2, n)), dma((n,)), dma((n,)), dma((4, n)), dma((4, n))]
+
+    def place(self, rows):
+        me = lax.axis_index('tp')
+        core, x, y = me % 2, (me // 2) % 2, me // 4
+        dev = lambda yy, xx, cc: (yy * 2 + xx) * 2 + cc
+        self.me, self.rows = me, rows
+        self.pn, self.xn, self.yn = dev(y, x, 1 - core), dev(y, 1 - x, core), dev(1 - y, x, core)
+        chips = [(y, x), (y, 1 - x), (1 - y, x), (1 - y, 1 - x)]
+        at = lambda d: pl.ds(pl.multiple_of(d * rows, rows), rows)
+        self.mine = [at(dev(*ch, core)) for ch in chips]
+        self.theirs = [at(dev(*ch, 1 - core)) for ch in chips]
+        self.chip_rows = [pl.ds(pl.multiple_of((ch[0] * 2 + ch[1]) * 2 * rows, 2 * rows), 2 * rows) for ch in chips]
+
+    def enter(self):
+        sem = pltpu.get_barrier_semaphore()
+        for d in (self.pn, self.xn, self.yn):
+            pl.semaphore_signal(sem, inc=1, device_id={'tp': d}, device_id_type=pl.DeviceIdType.MESH)
+        pl.semaphore_wait(sem, 3)
+
+    def copy(self, src, dst, ssem, rsem, dev):
+        return pltpu.make_async_remote_copy(src_ref=src, dst_ref=dst, send_sem=ssem, recv_sem=rsem, device_id={'tp': dev}, device_id_type=pl.DeviceIdType.MESH)
+
+    def reduce_scatter(self, parts, accs, scratch, produce=None):
+        na = len(self.widths)
+        bufs = [scratch[5 * a:5 * a + 5] for a in range(na)]
+        ds, dr, s1, r1, s2, r2 = scratch[5 * na:]
+        order = range(len(self.pieces))
+        pair, hop1, hop2 = {}, {}, {}
+        for i, (h, a, c0, cn) in enumerate(self.pieces):
+            cols = pl.ds(c0, cn)
+            dbuf, sb1, rb1, sb2, rb2 = bufs[a]
+            for j in range(4):
+                pair[j, i] = self.copy(parts[a].at[self.theirs[j], cols], dbuf.at[j, :, cols], ds.at[j, i], dr.at[j, i], self.pn)
+            to1, to2 = (self.xn, self.yn) if h == 0 else (self.yn, self.xn)
+            hop1[i] = self.copy(sb1.at[:, :, cols], rb1.at[:, :, cols], s1.at[i], r1.at[i], to1)
+            hop2[i] = self.copy(sb2.at[:, cols], rb2.at[:, cols], s2.at[i], r2.at[i], to2)
+
+        def chip_sum(j, i):
+            h, a, c0, cn = self.pieces[i]
+            pair[j, i].wait_recv()
+            return parts[a][self.mine[j], c0:c0 + cn].astype(F32) + bufs[a][0][j, :, c0:c0 + cn].astype(F32)
+
+        if produce is None:
+            for i in order:
+                pair[3, i].start()
+                pair[1 if self.pieces[i][0] == 0 else 2, i].start()
+            for i in order:
+                pair[2 if self.pieces[i][0] == 0 else 1, i].start()
+                pair[0, i].start()
+            first = list(order)
+        else:
+            first = []
+            for j in (3, 1, 2, 0):
+                produce(j)
+                for i in order:
+                    pair[j, i].start()
+                if j in (1, 2):
+                    for i in order:
+                        if self.pieces[i][0] == j - 1:
+                            self.send1(i, chip_sum, bufs, hop1)
+        for i in first:
+            self.send1(i, chip_sum, bufs, hop1)
+        for i in order:
+            h, a, c0, cn = self.pieces[i]
+            hop1[i].wait_recv()
+            bufs[a][3][:, c0:c0 + cn] = (chip_sum(2 if h == 0 else 1, i) + bufs[a][2][1, :, c0:c0 + cn].astype(F32)).astype(BF16)
+            hop2[i].start()
+        for i in order:
+            h, a, c0, cn = self.pieces[i]
+            own = chip_sum(0, i) + bufs[a][2][0, :, c0:c0 + cn].astype(F32)
+            hop2[i].wait_recv()
+            accs[a][:, c0:c0 + cn] = own + bufs[a][4][:, c0:c0 + cn].astype(F32)
+        self.pending = list(pair.values()) + list(hop1.values()) + list(hop2.values())
+
+    def send1(self, i, chip_sum, bufs, hop1):
+        h, a, c0, cn = self.pieces[i]
+        bufs[a][1][0, :, c0:c0 + cn] = chip_sum(1 if h == 0 else 2, i).astype(BF16)
+        bufs[a][1][1, :, c0:c0 + cn] = chip_sum(3, i).astype(BF16)
+        hop1[i].start()
+
+    def drain(self):
+        for cp in self.pending:
+            cp.wait_send()
+        self.pending = []
+
+    def all_gather(self, fulls, scratch, consume=None):
+        os_, xr, fs, fr, ps, pr = scratch
+        half0 = [i for i, p in enumerate(self.pieces) if p[0] == 0]
+        half1 = [i for i, p in enumerate(self.pieces) if p[0] == 1]
+
+        def block(i, j):
+            h, a, c0, cn = self.pieces[i]
+            return fulls[a].at[self.mine[j], pl.ds(c0, cn)]
+
+        def to(i, j, ssem, rsem, dev):
+            return self.copy(block(i, j), block(i, j), ssem, rsem, dev)
+
+        own = [[to(i, 0, os_.at[k, i], xr.at[k, i], dev) for i in range(len(self.pieces))] for k, dev in enumerate((self.xn, self.yn))]
+        from_n = [[to(i, 1 + k, os_.at[k, i], xr.at[k, i], dev) for i in range(len(self.pieces))] for k, dev in enumerate((self.xn, self.yn))]
+        fwd = {i: to(i, 2 if self.pieces[i][0] == 0 else 1, fs.at[i], fr.at[i], self.xn if self.pieces[i][0] == 0 else self.yn) for i in half0 + half1}
+        diag = {i: to(i, 3, fs.at[i], fr.at[i], self.xn) for i in half0 + half1}
+        give = [[to(i, j, ps.at[j, i], pr.at[j, i], self.pn) for i in range(len(self.pieces))] for j in range(4)]
+        for a, b in zip(half1, half0):
+            own[0][a].start()
+            own[1][b].start()
+        for a, b in zip(half0, half1):
+            own[0][a].start()
+            own[1][b].start()
+        for i in half0 + half1:
+            give[0][i].start()
+        take = lambda j: [self.take(i, j, fulls, ps, pr).wait_recv() for i in range(len(self.pieces))]
+        take(0)
+        if consume is not None:
+            consume(0)
+        for a, b in zip(half1, half0):
+            from_n[1][b].wait_recv()
+            fwd[b].start()
+            give[2][b].start()
+            from_n[0][a].wait_recv()
+            fwd[a].start()
+            give[1][a].start()
+        for a, b in zip(half1, half0):
+            from_n[1][a].wait_recv()
+            give[2][a].start()
+            from_n[0][b].wait_recv()
+            give[1][b].start()
+        for j in (1, 2):
+            take(j)
+            if consume is not None:
+                consume(j)
+        for a, b in zip(half1, half0):
+            for i in (b, a):
+                diag[i].wait_recv()
+                give[3][i].start()
+        take(3)
+        if consume is not None:
+            consume(3)
+        for cp in own[0] + own[1] + list(fwd.values()) + [c for g in give for c in g]:
+            cp.wait_send()
+
+    def take(self, i, j, fulls, ps, pr):
+        h, a, c0, cn = self.pieces[i]
+        ref = fulls[a].at[self.theirs[j], pl.ds(c0, cn)]
+        return self.copy(ref, ref, ps.at[j, i], pr.at[j, i], self.pn)
+
+
+def halves(width, n):
+    step = width // (2 * n)
+    return [(h, 0, (h * n + k) * step, step) for k in range(n) for h in range(2)]
+
+
+MAIN = halves(2560, 2)
+
+
+def norm_rows(x, gain):
+    return x * lax.rsqrt(jnp.mean(x * x, axis=-1, keepdims=True) + EPSILON) * gain
+
+
+def norm_rows_vjp(x, gain, dy):
+    r = lax.rsqrt(jnp.mean(x * x, axis=-1, keepdims=True) + EPSILON)
+    gd = dy * gain
+    dot = jnp.mean(gd * x, axis=-1, keepdims=True)
+    return r * gd - x * (r * r * r * dot), jnp.sum(dy * x * r, axis=0, keepdims=True)
+
+
+def exchange_call(body, name, cid, ins, out_shape, scratch):
+    vmem = pl.BlockSpec(memory_space=VM)
+    return pl.pallas_call(
+        body, out_shape=out_shape, in_specs=[vmem] * len(ins), out_specs=[vmem] * len(out_shape), scratch_shapes=scratch,
+        compiler_params=pltpu.CompilerParams(vmem_limit_bytes=48 << 20, collective_id=cid, has_side_effects=True), name=name)(*ins)
+
+
+def shape(dims, dtype):
+    return jax.ShapeDtypeStruct(dims, dtype)
+
+
+def embed_body(part, gain, e_ref, full, acc, *scratch):
+    ex = Exchange([part.shape[1]], MAIN)
+    ex.place(acc.shape[0])
+    ex.enter()
+    ex.reduce_scatter([part], [acc], scratch[:11])
+    e = acc[...].astype(BF16)
+    e_ref[...] = e
+    full[ex.mine[0], :] = norm_rows(e.astype(F32), gain[...]).astype(BF16)
+    ex.all_gather([full], scratch[11:])
+    ex.drain()
+
+
+def attn_out_body(part, e_ref, gain, h_ref, full, acc, *scratch):
+    ex = Exchange([part.shape[1]], MAIN)
+    ex.place(acc.shape[0])
+    ex.enter()
+    ex.reduce_scatter([part], [acc], scratch[:11])
+    h = (e_ref[...].astype(F32) + acc[...].astype(BF16).astype(F32)).astype(BF16)
+    h_ref[...] = h
+    full[ex.mine[0], :] = norm_rows(h.astype(F32), gain[...]).astype(BF16)
+    ex.all_gather([full], scratch[11:])
+    ex.drain()
+
+
+def mlp_back_body(part, h_ref, dy_ref, gain, dres_ref, dg_ref, full, acc, *scratch):
+    ex = Exchange([part.shape[1]], MAIN)
+    ex.place(acc.shape[0])
+    ex.enter()
+    ex.reduce_scatter([part], [acc], scratch[:11])
+    dx, dg = norm_rows_vjp(h_ref[...].astype(F32), gain[...], acc[...])
+    dg_ref[...] = dg
+    dres = dy_ref[...].astype(F32) + dx
+    dres_ref[...] = dres
+    full[ex.mine[0], :] = dres.astype(BF16)
+    ex.all_gather([full], scratch[11:])
+    ex.drain()
+
+
+LAST = MAIN + [(0, 1, 0, 256), (1, 1, 256, 128)]
+
+
+def attn_back_body(part, lat, e_ref, dres_ref, gain, dgm_ref, dgk_ref, dg_ref, full, full_lat, acc, acc_lat, gsum, gs, gr, *scratch):
+    ex = Exchange([part.shape[1], lat.shape[1]], LAST)
+    ex.place(acc.shape[0])
+    width, lora = part.shape[1], dgk_ref.shape[1]
+    me = lax.axis_index('tp')
+    sem = pltpu.get_barrier_semaphore()
+    for k in range(1, 8):
+        pl.semaphore_signal(sem, inc=1, device_id={'tp': (me + k) % 8}, device_id_type=pl.DeviceIdType.MESH)
+    pl.semaphore_wait(sem, 7)
+    ex.reduce_scatter([part, lat], [acc, acc_lat], scratch[:16])
+    dx, dg = norm_rows_vjp(e_ref[...].astype(F32), gain[...], acc[...])
+    full[ex.mine[0], :] = (dres_ref[...] + dx).astype(BF16)
+    full_lat[ex.mine[0], :] = acc_lat[...].astype(BF16)
+    gsum[me, :, :width] = dg
+    gsum[me, :, width:2 * width] = dgm_ref[...]
+    gsum[me, :, 2 * width:] = dgk_ref[...]
+    sends = [ex.copy(gsum.at[me], gsum.at[me], gs.at[k - 1], gr.at[k - 1], (me + k) % 8) for k in range(1, 8)]
+    for cp in sends:
+        cp.start()
+    ex.all_gather([full, full_lat], scratch[16:])
+    for k in range(1, 8):
+        frm = (me + 8 - k) % 8
+        ex.copy(gsum.at[frm], gsum.at[frm], gs.at[k - 1], gr.at[k - 1], frm).wait_recv()
+    dg_ref[...] = jnp.sum(gsum[...], axis=0)
+    for cp in sends:
+        cp.wait_send()
+    ex.drain()
+
+
+def ex_scratch(widths, pieces, rows):
+    ex = Exchange(widths, pieces)
+    return ex.rs_scratch(rows) + ex.ag_scratch()
+
+
+def layer_pass(rows, d_out, w_q, w_dkv, g_kv, w_uk, w_uv, w_o, g_attn, g_mlp, w_gate, w_up, w_down):
     w_q, heads = w_q
-    x_attn_loc, attn_norm_pull = jax.vjp(rms_norm, embedded.astype(F32), g_attn)
-    x_attn = gather(x_attn_loc)
-    seq = x_attn.shape[0]
-    rope = w_dkv.shape[0] - g_kv.shape[0]
+    seq, width = rows.shape
+    local = d_out.shape[0]
+    lora = g_kv.shape[0]
+    rope = w_dkv.shape[0] - lora
+    main = [VM((local, width), F32)] + ex_scratch([width], MAIN, local)
+    loc, fullb = shape((local, width), BF16), shape((seq, width), BF16)
+    ga, gm = g_attn[None, :], g_mlp[None, :]
+    embedded, x_attn = exchange_call(embed_body, 'embed_exchange', 1, [rows, ga], [loc, fullb], main)
+    d_out_late, x_attn = lax.optimization_barrier((d_out, x_attn))
     cos_t, sin_t = (t.T for t in rope_tables(seq, rope))
     query = mm(w_q, x_attn, 1, 1).astype(BF16)
     latent = mm(x_attn, w_dkv, 1, 1)
@@ -305,28 +577,26 @@
     k_pe_t = k_pe.T
     attn_out, lse = attend_fwd(query, k_nope, k_pe_t, value, cos_t, sin_t, heads)
     attn_part = mm(attn_out, w_o, 0, 0).astype(BF16)
-    attn_loc = scatter(attn_part)
-    residual = (embedded.astype(F32) + attn_loc.astype(F32)).astype(BF16)
-    x_mlp_loc, mlp_norm_pull = jax.vjp(rms_norm, residual.astype(F32), g_mlp)
-    x_mlp = gather(x_mlp_loc)
+    dy_full = gather(d_out_late)
+    attn_part, dy_full = lax.optimization_barrier((attn_part, dy_full))
+    residual, x_mlp = exchange_call(attn_out_body, 'attn_exchange', 2, [attn_part, embedded, gm], [loc, fullb], main)
     gate = mm(x_mlp, w_gate, 1, 1)
     up_proj = mm(x_mlp, w_up, 1, 1)
     gate_sig = jax.nn.sigmoid(gate)
     hidden = (gate * gate_sig * up_proj).astype(BF16)
-    mlp_loc = scatter(mm(hidden, w_down, 1, 0).astype(BF16))
-    layer_out = (residual.astype(F32) + mlp_loc.astype(F32)).astype(BF16)
-
-    dy_full = gather(d_out)
+
     d_hidden = mm(dy_full, w_down, 1, 1)
     dw_down = mm(hidden, dy_full, 0, 0)
     d_up = (d_hidden * gate * gate_sig).astype(BF16)
     d_gate = (d_hidden * up_proj * gate_sig * (1.0 + gate * (1.0 - gate_sig))).astype(BF16)
     dw_gate = mm(d_gate, x_mlp, 0, 0)
     dw_up = mm(d_up, x_mlp, 0, 0)
-    dx_mlp = scatter((mm(d_gate, w_gate, 1, 0) + mm(d_up, w_up, 1, 0)).astype(BF16))
-    d_res_norm, dg_mlp_part = mlp_norm_pull(dx_mlp)
-    d_residual = d_out.astype(F32) + d_res_norm
-    d_attn_full = gather(d_residual.astype(BF16))
+    dx_part = (mm(d_gate, w_gate, 1, 0) + mm(d_up, w_up, 1, 0)).astype(BF16)
+    d_residual, dg_mlp_part, d_attn_full = exchange_call(
+        mlp_back_body, 'mlp_exchange', 3, [dx_part, residual, d_out, gm],
+        [shape((local, width), F32), shape((1, width), F32), fullb], main)
+    hidden_late, d_attn_full = lax.optimization_barrier((hidden, d_attn_full))
+    mlp_loc = scatter(mm(hidden_late, w_down, 1, 0).astype(BF16))
     dw_o = mm(attn_out, d_attn_full, 1, 0)
     d_attn_out = mm(w_o, d_attn_full, 1, 1).astype(BF16)
     d_query, d_knope, d_value, d_kpe = attend_bwd(query, k_nope, k_pe_t, value, cos_t, sin_t, lse, d_attn_out, heads)
@@ -336,12 +606,19 @@
     d_latent, dg_kv_part = kv_pull((d_ckv, d_kpe.T.astype(BF16)))
     d_latent = d_latent.astype(BF16)
     dw_q = mm(d_query, x_attn, 1, 0)
-    dw_dkv_part = mm(d_latent, x_attn, 0, 0)
-    dx_attn = scatter((mm(d_query, w_q, 0, 0) + mm(d_latent, w_dkv, 1, 0)).astype(BF16))
-    d_emb_norm, dg_attn_part = attn_norm_pull(dx_attn)
-    d_embed = (d_residual + d_emb_norm).astype(BF16)
-    dw_dkv, dg_kv, dg_attn, dg_mlp = lax.psum((dw_dkv_part, dg_kv_part, dg_attn_part, dg_mlp_part), 'tp')
-    return layer_out, d_embed, (dw_q, dw_dkv, dg_kv, dw_uk, dw_uv, dw_o, dg_attn, dg_mlp, dw_gate, dw_up, dw_down)
+    dx_part = (mm(d_query, w_q, 0, 0) + mm(d_latent, w_dkv, 1, 0)).astype(BF16)
+    dx_part, mlp_loc = lax.optimization_barrier((dx_part, mlp_loc))
+    layer_out = (residual.astype(F32) + mlp_loc.astype(F32)).astype(BF16)
+    lat_w = 384
+    lat_part = jnp.pad(d_latent, ((0, 0), (0, lat_w - d_latent.shape[1])))
+    dma = pltpu.SemaphoreType.DMA
+    dg, de_full, lat_full = exchange_call(
+        attn_back_body, 'back_exchange', 4, [dx_part, lat_part, embedded, d_residual, ga, dg_mlp_part, dg_kv_part[None, :]],
+        [shape((1, 2 * width + lora), F32), fullb, shape((seq, lat_w), BF16)],
+        [VM((local, width), F32), VM((local, lat_w), F32), VM((8, 1, 2 * width + lora), F32), dma((7,)), dma((7,))] + ex_scratch([width, lat_w], LAST, local))
+    dw_dkv = mm(lat_full[:, :lora + rope], x_attn, 0, 0)
+    dg_attn, dg_mlp, dg_kv = dg[0, :width], dg[0, width:2 * width], dg[0, 2 * width:]
+    return layer_out, de_full, (dw_q, dw_dkv, dg_kv, dw_uk, dw_uv, dw_o, dg_attn, dg_mlp, dw_gate, dw_up, dw_down)
 
 
 def rows_of(w):
@@ -358,11 +635,9 @@
         heads = w_q.shape[1]
         key, blocks, count = block_index(tokens, vocab_local)
         rows = gather_rows(key, blocks, count, embed_table)
-        embedded = scatter(rows)
-        layer_out, d_embed, grads = layer_pass(
-            embedded, d_out[0], (rows_of(w_q), heads), w_dkv.T, g_kv, rows_of(w_uk), rows_of(w_uv), w_o.reshape(-1, model_dim),
+        layer_out, de_full, grads = layer_pass(
+            rows, d_out[0], (rows_of(w_q), heads), w_dkv.T, g_kv, rows_of(w_uk), rows_of(w_uv), w_o.reshape(-1, model_dim),
             g_attn, g_mlp, w_gate.T, w_up.T, w_down)
-        de_full = gather(d_embed)
         d_table = table_grad(key, blocks, count, de_full, vocab_local)
         dw_q, dw_dkv, dg_kv, dw_uk, dw_uv, dw_o, dg_attn, dg_mlp, dw_gate, dw_up, dw_down = grads
         return (layer_out[None], d_table, unrows(dw_q, heads), dw_dkv.T, dg_kv, unrows(dw_uk, heads), unrows(dw_uv, heads),

time: 625 us -> 464 us (0.74)
  waiting for transfers between devices: 363 us -> 5.41 us
  Pallas kernels: 49.4 us -> 287 us
  blocking collectives: 23.6 us -> 0 us
  other arithmetic: 24.6 us -> 15.1 us
  matrix products: 123 us -> 115 us
    pallas_call x0 -> x4, Pallas kernels: none -> 237 us  [exchange_call(): pl.pallas_call(body, out_shape=out_shape, in_specs=[vmem] * len(ins), out...]
    reduce_scatter x5 -> x1, waiting for transfers between devices: 234 us -> 5.36 us  [scatter(): return lax.psum_scatter(x, 'tp', scatter_dimension=0, tiled=True)]
    all_gather x5 -> x1, waiting for transfers between devices: 125 us -> 0.02 us  [gather(): return lax.all_gather(x, 'tp', axis=0, tiled=True)]
    psum x1 -> x0, blocking collectives: 23.6 us -> none  [layer_pass(): lax.psum((dw_dkv_part, dg_kv_part, dg_attn_part, dg_mlp_part), 'tp')]
    dot_general x24, matrix products: 123 us -> 115 us  [mm(): lax.dot_general(lhs, rhs, (((lc,), (rc,)), ((), ())), preferred_element_t...]
    convert_element_type x2, other arithmetic: 6.73 us -> 0.11 us  [the longest x1 0.1 us: layer_pass(): d_latent = d_latent.astype(BF16)]
    unnamed x109 -> x114, local copies, waits for them, and re-layouts: 16.5 us -> 14.5 us
  transfers between devices with their start and end apart: 11 -> 2, of which waited for: 10 -> 1; matrix products, arithmetic and copies ran while one was open for 12% -> 14% of each run, Pallas kernels for 3% -> 2%
where the time goes in v2:
time: 464 us; the launch traced here: 458 us
  Pallas kernels  287 us (62%)
  matrix products  115 us (25%)
  local copies, waits for them, and re-layouts  19.7 us (4%)
  other arithmetic  15.1 us (3%)
  between operations  15.1 us (3%)
  waiting for transfers between devices  5.41 us (1%)
    pallas_call x4, Pallas kernels, exchange_call(): pl.pallas_call(body, out_shape=out_shape, in_specs=[vmem] * len(ins), out...  237 us
    dot_general x24, matrix products, mm(): lax.dot_general(lhs, rhs, (((lc,), (rc,)), ((), ())), preferred_element_t...  115 us
    pallas_call x1, Pallas kernels, table_grad(): pl.pallas_call(table_grad_body, out_shape=[jax.ShapeDtypeStruct((vocab, w...  20.1 us
    unnamed x114, local copies, waits for them, and re-layouts  14.5 us
    pallas_call x1, Pallas kernels, attend_bwd(): pl.pallas_call(attn_bwd_body, grid=(heads,), in_specs=ins + [lse_spec, pe...  14.3 us
    pallas_call x1, Pallas kernels, attend_fwd(): pl.pallas_call(attn_fwd_body, grid=(heads,), in_specs=ins, out_specs=[per...  9.39 us
  transfers between devices with their start and end apart: 2, of which 1 were waited for; matrix products, arithmetic and copies ran while one was open for 14% of the time, Pallas kernels for 2%

profile of v2, /device:TPU:0, one launch (start us, length us, event | category | flops | bytes accessed | tf_op | source)
XLA Modules:
  0.0 457.7 jit_solution(17792056202766834979)
XLA Ops:
  7.2 0.9 broadcast_select_fusion
  9.7 0.8 convert_reduce_fusion
  10.5 0.9 select_reduce_fusion.blocks_ref
  11.4 0.9 copy.70
  15.0 1.0 add_select_fusion.key_ref
  16.0 6.2 %gather_rows.1.part = bf16[1024,2560]{1,0:T(8,128)(2,1)S(1)} custom-call(s32[1]{0:T(128)} %bitcast.3.count_ref, s32[1024]{0:T(1024)S(1)} %select_reduce_fusion.blocks_ref, s32[1024,1]{1,0:T(8,128)S(1)} %add_select_fusion.key_ref, bf16[8,2560]{1,0:T(8,128)(2,1)S(1)} %pad.20.tail_ref, bf16[9181,2560]{1,0:T(8,128)(2,1)} %table_ref.1), custom_call_target="tpu_custom_call" | custom-call | tf_op jit(solution)/shard_map/gather_rows/pallas_call | solution.py:114
  22.2 2.3 copy-done.1
  24.5 56.6 %embed_exchange.1 = (bf16[128,2560]{1,0:T(8,128)(2,1)S(1)}, bf16[1024,2560]{1,0:T(8,128)(2,1)S(1)}) custom-call(bf16[1024,2560]{1,0:T(8,128)(2,1)} %copy-done.1, f32[1,2560]{1,0:T(1,128)S(1)} %broadcast_in_dim.67.gain), custom_call_target="tpu_custom_call" | custom-call | tf_op jit(solution)/shard_map/embed_exchange/pallas_call | solution.py:476
  82.0 2.4 copy-done.19
  84.8 5.3 %fusion.20 = f32[1024,288]{1,0:T(8,128)S(1)} fusion(bf16[1024,2560]{1,0:T(8,128)(2,1)} %copy-done.19, bf16[2560,288]{0,1:T(8,128)(2,1)} %param.17), kind=kOutput, calls=%fused_computation.72 | convolution fusion | flops 1509949440 | bytes 7897088 | tf_op jit(solution)/shard_map/dot_general | solution.py:20
  90.0 1.1 copy-done.26
  91.2 2.2 multiply_subtract_fusion
  93.6 1.4 multiply_reduce_fusion
  95.4 1.4 multiply_convert_fusion.3
  97.3 1.3 fusion.5.v_ref
  98.6 5.5 %fusion.2.q_ref = bf16[480,1024]{1,0:T(8,128)(2,1)S(1)} fusion(bf16[1024,2560]{1,0:T(8,128)(2,1)} %copy-done.19, bf16[480,2560]{1,0:T(8,128)(2,1)S(1)} %bitcast.93), kind=kOutput, calls=%fused_computation.19 | convolution fusion | flops 2517073920 | bytes 8683520 | tf_op jit(solution)/shard_map/dot_general | solution.py:20
  104.1 9.4 %attend_fwd.1 = (bf16[320,1024]{1,0:T(8,128)(2,1)S(1)}, f32[5,1,1024]{2,1,0:T(1,128)S(1)}) custom-call(bf16[480,1024]{1,0:T(8,128)(2,1)S(1)} %fusion.2.q_ref, bf16[320,1024]{1,0:T(8,128)(2,1)S(1)} %fusion.4.kn_ref, bf16[32,1024]{1,0:T(8,128)(2,1)S(1)} %maximum_bitcast_fusion.kp_ref, bf16[320,1024]{1,0:T(8,128)(2,1)S(1)} %fusion.5.v_ref, ...), custom_call_target="tpu_custom_call" | custom-call | tf_op jit(solution)/shard_map/attend_fwd/pallas_call | solution.py:267
  114.3 5.1 %convolution_convert_fusion.part = bf16[1024,2560]{1,0:T(8,128)(2,1)} fusion(bf16[320,1024]{1,0:T(8,128)(2,1)S(1)} %get-tuple-element.41, bf16[320,2560]{1,0:T(8,128)(2,1)S(1)} %bitcast.124), kind=kOutput, calls=%fused_computation.2 | convolution fusion | flops 1680343040 | bytes 7536640 | tf_op jit(solution)/shard_map/dot_general | solution.py:20
  119.5 1.1 copy-done.13
  120.6 57.3 %attn_exchange.1 = (bf16[128,2560]{1,0:T(8,128)(2,1)S(1)}, bf16[1024,2560]{1,0:T(8,128)(2,1)}) custom-call(bf16[1024,2560]{1,0:T(8,128)(2,1)} %convolution_convert_fusion.part, bf16[128,2560]{1,0:T(8,128)(2,1)S(1)} %copy-done.13, f32[1,2560]{1,0:T(1,128)S(1)} %broadcast_in_dim.68.gain), custom_call_target="tpu_custom_call" | custom-call | tf_op jit(solution)/shard_map/attn_exchange/pallas_call | solution.py:476
  178.0 8.9 %fusion.21 = f32[1024,800]{0,1:T(8,128)} fusion(bf16[1024,2560]{1,0:T(8,128)(2,1)} %get-tuple-element.47, bf16[2560,800]{0,1:T(8,128)(2,1)S(1)} %copy-done.36), kind=kOutput, calls=%fused_computation.73 | convolution fusion | flops 4194304000 | bytes 12615680 | tf_op jit(solution)/shard_map/dot_general | solution.py:20
  186.9 6.1 %fusion.22 = f32[1024,800]{0,1:T(8,128)} fusion(bf16[1024,2560]{1,0:T(8,128)(2,1)S(1)} %copy-done.35, bf16[2560,800]{0,1:T(8,128)(2,1)S(1)} %copy-done.37), kind=kOutput, calls=%fused_computation.74 | convolution fusion | flops 4194304000 | bytes 12615680 | tf_op jit(solution)/shard_map/dot_general | solution.py:20
  193.0 10.1 %multiply_convert_fusion = (bf16[1024,800]{0,1:T(8,128)(2,1)S(1)}, bf16[1024,800]{0,1:T(8,128)(2,1)S(1)}, bf16[1024,800]{0,1:T(8,128)(2,1)}) fusion(f32[1024,800]{0,1:T(8,128)} %fusion.21, f32[1024,800]{0,1:T(8,128)} %fusion.22, bf16[1024,2560]{1,0:T(8,128)(2,1)S(1)} %bitcast.117, bf16[800,2560]{1,0:T(8,128)(2,1)} %param.26), kind=kOutput, calls=%fused_computation.11 | convolution fusion | flops 4207411200 | bytes 20807680 | tf_op jit(solution)/shard_map/dot_general | solution.py:20
  203.1 5.8 %fusion.23 = f32[1024,2560]{1,0:T(8,128)S(1)} fusion(bf16[1024,800]{0,1:T(8,128)(2,1)S(1)} %get-tuple-element.72, bf16[2560,800]{0,1:T(8,128)(2,1)S(1)} %copy-done.36), kind=kOutput, calls=%fused_computation.75 | convolution fusion | flops 4194304000 | bytes 16220160 | tf_op jit(solution)/shard_map/dot_general | solution.py:20
  208.9 7.6 %add_convert_fusion.1.part = bf16[1024,2560]{1,0:T(8,128)(2,1)} fusion(f32[1024,2560]{1,0:T(8,128)S(1)} %fusion.23, bf16[1024,800]{0,1:T(8,128)(2,1)S(1)} %get-tuple-element.71, bf16[2560,800]{0,1:T(8,128)(2,1)S(1)} %copy-done.37), kind=kOutput, calls=%fused_computation.1 | convolution fusion | flops 4199546880 | bytes 21463040 | tf_op jit(solution)/shard_map/dot_general | solution.py:20
  216.6 56.6 %mlp_exchange.1 = (f32[128,2560]{1,0:T(8,128)S(1)}, f32[1,2560]{1,0:T(1,128)S(1)}, bf16[1024,2560]{1,0:T(8,128)(2,1)}) custom-call(bf16[1024,2560]{1,0:T(8,128)(2,1)} %add_convert_fusion.1.part, bf16[128,2560]{1,0:T(8,128)(2,1)S(1)} %get-tuple-element.45.h_ref, bf16[128,2560]{1,0:T(8,128)(2,1)S(1)} %bitcast.98, f32[1,2560]{1,0:T(1,128)S(1)} %broadcast_in_dim.68.gain), custom_call_target="tpu_custom_call" | custom-call | tf_op jit(solution)/shard_map/mlp_exchange/pallas_call | solution.py:476
  273.2 4.9 %fusion.6.do_ref = bf16[320,1024]{1,0:T(8,128)(2,1)S(1)} fusion(bf16[1024,2560]{1,0:T(8,128)(2,1)} %get-tuple-element.50, bf16[320,2560]{1,0:T(8,128)(2,1)S(1)} %bitcast.125), kind=kOutput, calls=%fused_computation.29 | convolution fusion | flops 1678049280 | bytes 7536640 | tf_op jit(solution)/shard_map/dot_general | solution.py:20
  278.1 14.3 %attend_bwd.1 = (bf16[480,1024]{1,0:T(8,128)(2,1)S(1)}, bf16[320,1024]{1,0:T(8,128)(2,1)S(1)}, bf16[320,1024]{1,0:T(8,128)(2,1)S(1)}, f32[32,1024]{1,0:T(8,128)S(1)}) custom-call(bf16[480,1024]{1,0:T(8,128)(2,1)S(1)} %copy-done.5, bf16[320,1024]{1,0:T(8,128)(2,1)S(1)} %fusion.4.kn_ref, bf16[32,1024]{1,0:T(8,128)(2,1)S(1)} %maximum_bitcast_fusion.kp_ref, ...), custom_call_target="tpu_custom_call" | custom-call | tf_op jit(solution)/shard_map/attend_bwd/pallas_call | solution.py:277
  293.2 0.8 copy-done.17
  294.1 0.9 copy-done.20
  295.2 9.5 %convolution_convert_fusion.1 = bf16[1024,2560]{1,0:T(8,128)(2,1)} fusion(bf16[1024,800]{0,1:T(8,128)(2,1)} %get-tuple-element.55, bf16[800,2560]{1,0:T(8,128)(2,1)} %param.26), kind=kOutput, calls=%fused_computation.3 | convolution fusion | flops 4196925440 | bytes 10977280 | tf_op jit(solution)/shard_map/dot_general | solution.py:20
  304.8 2.1 multiply_add_fusion.1
  309.7 1.1 fusion.27
  310.8 1.1 fusion.28
  311.9 3.6 fusion.29
  315.4 2.9 fusion.24
  318.4 4.4 fusion.26
  322.8 4.6 %add_convert_fusion.part = bf16[1024,2560]{1,0:T(8,128)(2,1)} fusion(f32[1024,2560]{1,0:T(8,128)S(1)} %fusion.24, bf16[1024,288]{1,0:T(8,128)(2,1)S(1)} %add_convert_fusion.2, bf16[2560,288]{0,1:T(8,128)(2,1)S(1)} %copy-done.28), kind=kOutput, calls=%fused_computation | convolution fusion | flops 1515192320 | bytes 17793024 | tf_op jit(solution)/shard_map/dot_general | solution.py:20
  327.5 6.6 %fusion.31 = f32[2560,800]{0,1:T(8,128)} fusion(bf16[1024,800]{0,1:T(8,128)(2,1)S(1)} %copy-done.41, bf16[1024,2560]{1,0:T(8,128)(2,1)S(1)} %bitcast.121), kind=kOutput, calls=%fused_computation.83 | convolution fusion | flops 4194304000 | bytes 15073280 | tf_op jit(solution)/shard_map/dot_general | solution.py:20
  334.0 6.6 %fusion.32 = f32[2560,800]{0,1:T(8,128)} fusion(bf16[1024,800]{0,1:T(8,128)(2,1)S(1)} %copy-done.44, bf16[1024,2560]{1,0:T(8,128)(2,1)S(1)} %bitcast.121), kind=kOutput, calls=%fused_computation.84 | convolution fusion | flops 4194304000 | bytes 15073280 | tf_op jit(solution)/shard_map/dot_general | solution.py:20
  340.6 6.8 %fusion.30 = f32[800,2560]{1,0:T(8,128)} fusion(bf16[1024,800]{0,1:T(8,128)(2,1)S(1)} %copy-done.42, bf16[1024,2560]{1,0:T(8,128)(2,1)S(1)} %bitcast.119), kind=kOutput, calls=%fused_computation.82 | convolution fusion | flops 4194304000 | bytes 15073280 | tf_op jit(solution)/shard_map/dot_general | solution.py:20
  347.4 5.4 %reduce-scatter.2.cloned.1.call-done = bf16[128,2560]{1,0:T(8,128)(2,1)} async-done(((bf16[1024,2560]{1,0:T(8,128)(2,1)}), bf16[128,2560]{1,0:T(8,128)(2,1)}) %reduce-scatter.2.cloned.1.call-update) | async-done | bytes 655376 | tf_op jit(solution)/shard_map/reduce_scatter | solution.py:290
  352.8 1.2 copy-done.14
  353.9 1.3 copy-done.16
  355.2 66.1 %back_exchange.1 = (f32[1,5376]{1,0:T(1,128)S(1)}, bf16[1024,2560]{1,0:T(8,128)(2,1)}, bf16[1024,384]{1,0:T(8,128)(2,1)S(1)}) custom-call(bf16[1024,2560]{1,0:T(8,128)(2,1)} %add_convert_fusion.part, bf16[1024,384]{1,0:T(8,128)(2,1)S(1)} %pad.25.lat, bf16[128,2560]{1,0:T(8,128)(2,1)S(1)} %copy-done.14, f32[128,2560]{1,0:T(8,128)S(1)} %copy-done.16, ...), custom_call_target="tpu_custom_call" | custom-call | tf_op jit(solution)/shard_map/back_exchange/pallas_call | solution.py:476
  422.6 1.0 fusion.13
  423.6 6.3 %fusion.11 = f32[2560,288]{0,1:T(8,128)} fusion(bf16[1024,2560]{1,0:T(8,128)(2,1)} %copy-done.19, bf16[1024,384]{1,0:T(8,128)(2,1)S(1)} %get-tuple-element.63), kind=kOutput, calls=%fused_computation.36 | convolution fusion | flops 1509949440 | bytes 8978432 | tf_op jit(solution)/shard_map/dot_general | solution.py:20
  429.9 20.1 %table_grad.1 = (bf16[9181,2560]{1,0:T(8,128)(2,1)}, bf16[8,2560]{1,0:T(8,128)(2,1)S(1)}) custom-call(s32[1]{0:T(128)} %bitcast.3.count_ref, s32[1024]{0:T(1024)S(1)} %select_reduce_fusion.blocks_ref, s32[1,1024]{1,0:T(1,128)S(1)} %get-tuple-element.78.key_ref, bf16[1024,2560]{1,0:T(8,128)(2,1)S(1)} %bitcast.96), custom_call_target="tpu_custom_call" | custom-call | tf_op jit(solution)/shard_map/table_grad/pallas_call | solution.py:183
  (150 shorter events, 13.0 us)
Async XLA Ops:
  7.2 91.4 %copy-start = (bf16[2560,5,96]{0,2,1:T(8,128)(2,1)S(1)}, bf16[2560,5,96]{0,2,1:T(8,128)(2,1)}, u32[]{:S(2)}) copy-start(bf16[2560,5,96]{0,2,1:T(8,128)(2,1)} %param.16) | copy-start | bytes 7372804
  7.2 112.3 %all-gather.2.cloned.1.call-start = ((), (), s32[]{:S(2)}) async-start(), calls=%async_computation.1 | async-start | bytes 5898240 | tf_op jit(solution)/shard_map/all_gather | solution.py:286
  22.2 2.4 copy-start.1
  82.0 2.4 copy-start.19
  84.4 268.4 %reduce-scatter.2.cloned.1.call-start = ((), (), s32[]{:S(2)}) async-start(), calls=%async_computation.2 | async-start | bytes 5898240 | tf_op jit(solution)/shard_map/reduce_scatter | solution.py:290
  84.7 8.9 %copy-start.33 = (f32[2560]{0:T(1024)S(1)}, f32[2560]{0:T(1024)}, u32[]{:S(2)}) copy-start(f32[2560]{0:T(1024)} %param.23) | copy-start | bytes 30724
  84.8 10.7 %copy-start.34 = (f32[256]{0:T(256)S(1)}, f32[256]{0:T(256)}, u32[]{:S(2)}) copy-start(f32[256]{0:T(256)} %param.18) | copy-start | bytes 3076
  91.2 5.7 %copy-start.29 = (bf16[256,5,64]{0,2,1:T(8,128)(2,1)S(1)}, bf16[256,5,64]{0,2,1:T(8,128)(2,1)}, u32[]{:S(2)}) copy-start(bf16[256,5,64]{0,2,1:T(8,128)(2,1)} %param.19) | copy-start | bytes 491524
  96.9 1.7 copy-start.24
  98.6 5.5 %copy-start.2 = (bf16[320,1024]{1,0:T(8,128)(2,1)}, bf16[320,1024]{1,0:T(8,128)(2,1)S(1)}, u32[]{:S(2)}) copy-start(bf16[320,1024]{1,0:T(8,128)(2,1)S(1)} %fusion.5.v_ref) | copy-start | bytes 1966084
  98.6 15.8 %copy-start.38 = (bf16[5,64,2560]{2,1,0:T(8,128)(2,1)S(1)}, bf16[5,64,2560]{2,1,0:T(8,128)(2,1)}, u32[]{:S(2)}) copy-start(bf16[5,64,2560]{2,1,0:T(8,128)(2,1)} %param.21) | copy-start | bytes 4915204
  104.1 9.4 %copy-start.4 = (bf16[480,1024]{1,0:T(8,128)(2,1)}, bf16[480,1024]{1,0:T(8,128)(2,1)S(1)}, u32[]{:S(2)}) copy-start(bf16[480,1024]{1,0:T(8,128)(2,1)S(1)} %fusion.2.q_ref) | copy-start | bytes 2949124
  120.6 57.4 %copy-start.36 = (bf16[2560,800]{0,1:T(8,128)(2,1)S(1)}, bf16[2560,800]{0,1:T(8,128)(2,1)}, u32[]{:S(2)}) copy-start(bf16[2560,800]{0,1:T(8,128)(2,1)} %param.24) | copy-start | bytes 12288004
  178.0 38.6 %copy-start.10 = (bf16[128,2560]{1,0:T(8,128)(2,1)}, bf16[128,2560]{1,0:T(8,128)(2,1)S(1)}, u32[]{:S(2)}) copy-start(bf16[128,2560]{1,0:T(8,128)(2,1)S(1)} %get-tuple-element.45.h_ref) | copy-start | bytes 1966084
  178.0 8.9 %copy-start.35 = (bf16[1024,2560]{1,0:T(8,128)(2,1)S(1)}, bf16[1024,2560]{1,0:T(8,128)(2,1)}, u32[]{:S(2)}) copy-start(bf16[1024,2560]{1,0:T(8,128)(2,1)} %get-tuple-element.47) | copy-start | bytes 15728644
  178.0 8.9 %copy-start.37 = (bf16[2560,800]{0,1:T(8,128)(2,1)S(1)}, bf16[2560,800]{0,1:T(8,128)(2,1)}, u32[]{:S(2)}) copy-start(bf16[2560,800]{0,1:T(8,128)(2,1)} %param.25) | copy-start | bytes 12288004
  178.0 15.0 %slice-start.4 = ((s8[5242880]{0:T(1024)(128)(4,1)}), s8[4194304]{0:T(1024)(128)(4,1)S(1)}, s32[]{:S(2)}) async-start(s8[5242880]{0:T(1024)(128)(4,1)} %bitcast.116), calls=%async_computation.7 | async-start | bytes 8388608
  186.9 6.1 %slice-start.5 = ((s8[5242880]{0:T(1024)(128)(4,1)}), s8[1048576]{0:T(1024)(128)(4,1)S(1)}, s32[]{:S(2)}) async-start(s8[5242880]{0:T(1024)(128)(4,1)} %bitcast.116), calls=%async_computation.8 | async-start | bytes 2097152
  203.1 5.8 %copy-start.40 = (bf16[1024,800]{0,1:T(8,128)(2,1)}, bf16[1024,800]{0,1:T(8,128)(2,1)S(1)}, u32[]{:S(2)}) copy-start(bf16[1024,800]{0,1:T(8,128)(2,1)S(1)} %get-tuple-element.72) | copy-start | bytes 4915204
  203.1 5.8 %copy-start.43 = (bf16[1024,800]{0,1:T(8,128)(2,1)}, bf16[1024,800]{0,1:T(8,128)(2,1)S(1)}, u32[]{:S(2)}) copy-start(bf16[1024,800]{0,1:T(8,128)(2,1)S(1)} %get-tuple-element.71) | copy-start | bytes 4915204
  208.9 7.7 %copy-start.6 = (bf16[1,128,2560]{2,1,0:T(8,128)(2,1)S(1)}, bf16[1,128,2560]{2,1,0:T(8,128)(2,1)}, u32[]{:S(2)}) copy-start(bf16[1,128,2560]{2,1,0:T(8,128)(2,1)} %param.27) | copy-start | bytes 1966084
  216.6 56.6 %copy-start.39 = (bf16[5,64,2560]{2,1,0:T(8,128)(2,1)S(1)}, bf16[5,64,2560]{2,1,0:T(8,128)(2,1)}, u32[]{:S(2)}) copy-start(bf16[5,64,2560]{2,1,0:T(8,128)(2,1)} %param.21) | copy-start | bytes 4915204
  273.2 4.9 %copy-start.15 = (f32[128,2560]{1,0:T(8,128)}, f32[128,2560]{1,0:T(8,128)S(1)}, u32[]{:S(2)}) copy-start(f32[128,2560]{1,0:T(8,128)S(1)} %get-tuple-element.58.dres_ref) | copy-start | bytes 3932164
  273.2 4.9 %copy-start.3 = (bf16[320,1024]{1,0:T(8,128)(2,1)S(1)}, bf16[320,1024]{1,0:T(8,128)(2,1)}, u32[]{:S(2)}) copy-start(bf16[320,1024]{1,0:T(8,128)(2,1)} %copy-done.2) | copy-start | bytes 1966084
  273.2 4.9 %copy-start.5 = (bf16[480,1024]{1,0:T(8,128)(2,1)S(1)}, bf16[480,1024]{1,0:T(8,128)(2,1)}, u32[]{:S(2)}) copy-start(bf16[480,1024]{1,0:T(8,128)(2,1)} %copy-done.4) | copy-start | bytes 2949124
  304.7 2.5 copy-start.8
  304.7 2.5 copy-start.30
  304.7 3.0 copy-start.18
  304.7 3.0 copy-start.27
  304.7 3.0 copy-start.32
  307.2 4.7 %slice-start.10 = ((s8[5242880]{0:T(1024)(128)(4,1)}), s8[4194304]{0:T(1024)(128)(4,1)S(1)}, s32[]{:S(2)}) async-start(s8[5242880]{0:T(1024)(128)(4,1)} %bitcast.122), calls=%async_computation.13 | async-start | bytes 8388608
  308.5 3.4 slice-start.11
  308.8 3.0 copy-start.23
  311.8 3.6 copy-start.21
  311.8 6.6 %slice-start.2 = ((s8[5242880]{0:T(1024)(128)(4,1)}), s8[4194304]{0:T(1024)(128)(4,1)S(1)}, s32[]{:S(2)}) async-start(s8[5242880]{0:T(1024)(128)(4,1)} %bitcast.100), calls=%async_computation.5 | async-start | bytes 8388608
  315.4 3.0 slice-start.3
  315.4 12.0 %slice-start.8 = ((s8[5242880]{0:T(1024)(128)(4,1)}), s8[4194304]{0:T(1024)(128)(4,1)S(1)}, s32[]{:S(2)}) async-start(s8[5242880]{0:T(1024)(128)(4,1)} %bitcast.120), calls=%async_computation.11 | async-start | bytes 8388608
  318.4 4.4 copy-start.28
  318.4 9.0 %slice-start.9 = ((s8[5242880]{0:T(1024)(128)(4,1)}), s8[1048576]{0:T(1024)(128)(4,1)S(1)}, s32[]{:S(2)}) async-start(s8[5242880]{0:T(1024)(128)(4,1)} %bitcast.120), calls=%async_computation.12 | async-start | bytes 2097152
  322.8 4.6 %copy-start.41 = (bf16[1024,800]{0,1:T(8,128)(2,1)S(1)}, bf16[1024,800]{0,1:T(8,128)(2,1)}, u32[]{:S(2)}) copy-start(bf16[1024,800]{0,1:T(8,128)(2,1)} %copy-done.40) | copy-start | bytes 4915204
  327.4 6.6 %copy-start.44 = (bf16[1024,800]{0,1:T(8,128)(2,1)S(1)}, bf16[1024,800]{0,1:T(8,128)(2,1)}, u32[]{:S(2)}) copy-start(bf16[1024,800]{0,1:T(8,128)(2,1)} %copy-done.43) | copy-start | bytes 4915204
  327.4 13.2 %slice-start.6 = ((s8[5242880]{0:T(1024)(128)(4,1)}), s8[4194304]{0:T(1024)(128)(4,1)S(1)}, s32[]{:S(2)}) async-start(s8[5242880]{0:T(1024)(128)(4,1)} %bitcast.118), calls=%async_computation.9 | async-start | bytes 8388608
  334.0 6.6 %slice-start.7 = ((s8[5242880]{0:T(1024)(128)(4,1)}), s8[1048576]{0:T(1024)(128)(4,1)S(1)}, s32[]{:S(2)}) async-start(s8[5242880]{0:T(1024)(128)(4,1)} %bitcast.118), calls=%async_computation.10 | async-start | bytes 2097152
  334.0 6.6 %copy-start.42 = (bf16[1024,800]{0,1:T(8,128)(2,1)S(1)}, bf16[1024,800]{0,1:T(8,128)(2,1)}, u32[]{:S(2)}) copy-start(bf16[1024,800]{0,1:T(8,128)(2,1)} %get-tuple-element.55) | copy-start | bytes 4915204
  352.7 69.8 %copy-start.11 = (bf16[128,2560]{1,0:T(8,128)(2,1)S(1)}, bf16[128,2560]{1,0:T(8,128)(2,1)}, u32[]{:S(2)}) copy-start(bf16[128,2560]{1,0:T(8,128)(2,1)} %copy-done.10) | copy-start | bytes 1966084
  355.2 67.4 %copy-start.31 = (bf16[128,2560]{1,0:T(8,128)(2,1)S(1)}, bf16[128,2560]{1,0:T(8,128)(2,1)}, u32[]{:S(2)}) copy-start(bf16[128,2560]{1,0:T(8,128)(2,1)} %reduce-scatter.2.cloned.1.call-done) | copy-start | bytes 1966084
  422.6 7.3 %slice-start = ((s8[5242880]{0:T(1024)(128)(4,1)}), s8[4194304]{0:T(1024)(128)(4,1)S(1)}, s32[]{:S(2)}) async-start(s8[5242880]{0:T(1024)(128)(4,1)} %bitcast.95), calls=%async_computation.3 | async-start | bytes 8388608
  423.6 6.3 %slice-start.1 = ((s8[5242880]{0:T(1024)(128)(4,1)}), s8[1048576]{0:T(1024)(128)(4,1)S(1)}, s32[]{:S(2)}) async-start(s8[5242880]{0:T(1024)(128)(4,1)} %bitcast.95), calls=%async_computation.4 | async-start | bytes 2097152
  (11 other events, 11.4 us)
Sparse Core Ops, SparseCore 0:
  84.5 34.9 all-gather.1
  304.8 47.8 reduce-scatter.1

commit v3 on v1

--- a/solution.py
+++ b/solution.py
@@ -12,12 +12,25 @@
 F32, BF16 = jnp.float32, jnp.bfloat16
 LOG2E = 1.4426950408889634
 VM = pltpu.VMEM
+ZR = 248
 GB = 64
 QB = 256
 
 
 def mm(lhs, rhs, lc, rc):
     return lax.dot_general(lhs, rhs, (((lc,), (rc,)), ((), ())), preferred_element_type=F32)
+
+
+def nn(a, b):
+    return mm(a, b, 1, 0)
+
+
+def nt(a, b):
+    return mm(a, b, 1, 1)
+
+
+def tn(a, b):
+    return mm(a, b, 0, 0)
 
 
 def rope_tables(seq_len, rope_dim):
@@ -99,7 +112,7 @@
         cols = lax.broadcasted_iota(jnp.int32, (rows, GB * 8), 1) + base * 8
         hot = jnp.where(cols == key_ref[...], 1.0, 0.0).astype(BF16)
         for c in range(0, width, 512):
-            got = mm(hot, stage[:, :, c:c + 512].reshape(GB * 8, 512), 1, 0)
+            got = nn(hot, stage[:, :, c:c + 512].reshape(GB * 8, 512))
             out_ref[:, c:c + 512] += got.astype(BF16)
         return carry
 
@@ -120,19 +133,11 @@
     )(count, blocks, key[:, None], tail, table)
 
 
-ZR = 248
-
-
-def table_grad_body(count_ref, blocks_ref, key_ref, de_ref, out_ref, tail_ref, zero, stage, zsem, sem):
+def table_grad_body(count_ref, blocks_ref, key_ref, de_ref, zeros_ref, out_ref, tail_ref, stage, sem):
     rows, width = de_ref.shape
     vocab = out_ref.shape[0]
     full = vocab // 8
-    zero[...] = jnp.zeros_like(zero)
     tail_ref[...] = jnp.zeros_like(tail_ref)
-    fills = [(r, min(ZR, full * 8 - r)) for r in range(0, full * 8, ZR)]
-    copies = [pltpu.make_async_copy(zero.at[pl.ds(0, n), :], out_ref.at[pl.ds(r, n), :], zsem) for r, n in fills]
-    for cp in copies:
-        cp.start()
     count = count_ref[0]
 
     def put(b, i):
@@ -142,7 +147,7 @@
         ids = lax.broadcasted_iota(jnp.int32, (GB * 8, rows), 0) + ci * (GB * 8)
         hot = jnp.where(ids == key_ref[...], 1.0, 0.0).astype(BF16)
         for c in range(0, width, 512):
-            got = mm(hot, de_ref[:, c:c + 512], 1, 0)
+            got = nn(hot, de_ref[:, c:c + 512])
             stage[:, :, c:c + 512] = got.astype(BF16).reshape(GB, 8, 512)
 
     def move(ci, go):
@@ -161,14 +166,8 @@
 
         lax.fori_loop(0, jnp.minimum(GB, count - base), one, 0)
 
-    sums(0)
-    for cp in copies:
-        cp.wait()
-
     def chunk(ci, carry):
-        @pl.when(ci > 0)
-        def _():
-            sums(ci)
+        sums(ci)
         move(ci, lambda cp: cp.start())
         move(ci, lambda cp: cp.wait())
         return carry
@@ -176,17 +175,17 @@
     lax.fori_loop(0, (count + GB - 1) // GB, chunk, 0)
 
 
-def table_grad(key, blocks, count, de_full, vocab):
-    width = de_full.shape[1]
+def table_grad(key, blocks, count, de_full, table):
+    vocab, width = table.shape
     smem = pl.BlockSpec(memory_space=pltpu.SMEM)
     full = vocab // 8 * 8
     out, tail = pl.pallas_call(
         table_grad_body, out_shape=[jax.ShapeDtypeStruct((vocab, width), BF16), jax.ShapeDtypeStruct((8, width), BF16)],
-        in_specs=[smem, smem, pl.BlockSpec(memory_space=VM), pl.BlockSpec(memory_space=VM)],
+        in_specs=[smem, smem, pl.BlockSpec(memory_space=VM), pl.BlockSpec(memory_space=VM), pl.BlockSpec(memory_space=pl.ANY)], input_output_aliases={4: 0},
         out_specs=[pl.BlockSpec(memory_space=pl.ANY), pl.BlockSpec(memory_space=VM)],
-        scratch_shapes=[VM((ZR, width), BF16), VM((GB, 8, width), BF16), pltpu.SemaphoreType.DMA, pltpu.SemaphoreType.DMA],
+        scratch_shapes=[VM((GB, 8, width), BF16), pltpu.SemaphoreType.DMA],
         compiler_params=pltpu.CompilerParams(vmem_limit_bytes=40 << 20), name='table_grad',
-    )(count, blocks, key[None, :], de_full)
+    )(count, blocks, key[None, :], de_full, table)
     return lax.dynamic_update_slice(out, tail[:vocab - full], (full, 0))
 
 
@@ -198,7 +197,7 @@
 
 
 def scores_of(k_all, q_all, ki, qi, scale):
-    s = mm(k_all[:, ki * QB:(ki + 1) * QB], q_all[:, qi * QB:(qi + 1) * QB], 0, 0) * scale
+    s = tn(k_all[:, ki * QB:(ki + 1) * QB], q_all[:, qi * QB:(qi + 1) * QB]) * scale
     if ki == qi:
         keys = lax.broadcasted_iota(jnp.int32, (QB, QB), 0)
         s = jnp.where(keys <= lax.broadcasted_iota(jnp.int32, (QB, QB), 1), s, -1e30)
@@ -216,12 +215,22 @@
         p = [jnp.exp2(x - top) for x in s]
         total = sum(jnp.sum(x, axis=0, keepdims=True) for x in p)
         inv = 1.0 / total
-        o = sum(mm(v_ref[:, ki * QB:(ki + 1) * QB], (x * inv).astype(BF16), 1, 0) for ki, x in enumerate(p))
+        o = sum(nn(v_ref[:, ki * QB:(ki + 1) * QB], (x * inv).astype(BF16)) for ki, x in enumerate(p))
         o_ref[:, lanes] = o.astype(BF16)
         lse_ref[0, :, lanes] = top + jnp.log2(total)
 
 
-def attn_bwd_body(q_ref, kn_ref, kp_ref, v_ref, cos_ref, sin_ref, lse_ref, do_ref, dq_ref, dkn_ref, dv_ref, dkp_ref, dk_acc, dv_acc):
+def attn_bwd_body(q_ref, kn_ref, kp_ref, v_ref, cos_ref, sin_ref, lse_ref, do_ref, dq_ref, dkn_ref, dv_ref, dkp_ref, table_ref, dk_acc, dv_acc, zero, zsem):
+    full = table_ref.shape[0] // 8 * 8
+    fills = [pltpu.make_async_copy(zero.at[pl.ds(0, n), :], table_ref.at[pl.ds(r, n), :], zsem.at[k])
+             for k, (r, n) in enumerate((r, min(ZR, full - r)) for r in range(0, full, ZR))]
+
+    @pl.when(pl.program_id(0) == 0)
+    def _():
+        zero[...] = jnp.zeros_like(zero)
+        for cp in fills:
+            cp.start()
+
     nope, half = kn_ref.shape[0], cos_ref.shape[0]
     raw = q_ref.shape[0] ** -0.5
     q_all, k_all = heads_of(q_ref, kn_ref, kp_ref, cos_ref, sin_ref, nope, half)
@@ -231,16 +240,16 @@
         lanes = slice(qi * QB, (qi + 1) * QB)
         q_b, do_b, lse = q_all[:, lanes], do_ref[:, lanes], lse_ref[0, :, lanes]
         p = [jnp.exp2(scores_of(k_all, q_all, ki, qi, raw * LOG2E) - lse) for ki in range(qi + 1)]
-        dp = [mm(v_ref[:, ki * QB:(ki + 1) * QB], do_b, 0, 0) for ki in range(qi + 1)]
+        dp = [tn(v_ref[:, ki * QB:(ki + 1) * QB], do_b) for ki in range(qi + 1)]
         delta = sum(jnp.sum(a * b, axis=0, keepdims=True) for a, b in zip(p, dp))
         dq = None
         for ki in range(qi + 1):
             keys = slice(ki * QB, (ki + 1) * QB)
             ds = (p[ki] * (dp[ki] - delta) * raw).astype(BF16)
-            part = mm(k_all[:, keys], ds, 1, 0)
+            part = nn(k_all[:, keys], ds)
             dq = part if dq is None else dq + part
-            dk_acc[:, keys] += mm(q_b, ds, 1, 1)
-            dv_acc[:, keys] += mm(do_b, p[ki].astype(BF16), 1, 1)
+            dk_acc[:, keys] += nt(q_b, ds)
+            dv_acc[:, keys] += nt(do_b, p[ki].astype(BF16))
         cos_t, sin_t = cos_ref[:, lanes], sin_ref[:, lanes]
         lo, hi = dq[nope:nope + half], dq[nope + half:]
         dq_ref[:nope, lanes] = dq[:nope].astype(BF16)
@@ -253,6 +262,11 @@
     def _():
         dkp_ref[...] = jnp.zeros_like(dkp_ref)
     dkp_ref[...] += dk_acc[nope:, :]
+
+    @pl.when(pl.program_id(0) == pl.num_programs(0) - 1)
+    def _():
+        for cp in fills:
+            cp.wait()
 
 
 def attn_specs(heads, qd, nope, rope, vd, seq):
@@ -271,77 +285,413 @@
     )(q, kn, kp, v, cos_t, sin_t)
 
 
-def attend_bwd(q, kn, kp, v, cos_t, sin_t, lse, do, heads):
+def attend_bwd(q, kn, kp, v, cos_t, sin_t, lse, do, heads, table):
     seq, qd, nope, vd, rope = q.shape[1], q.shape[0] // heads, kn.shape[0] // heads, v.shape[0] // heads, kp.shape[0]
     ins, per, one, lse_spec = attn_specs(heads, qd, nope, rope, vd, seq)
     return pl.pallas_call(
-        attn_bwd_body, grid=(heads,), in_specs=ins + [lse_spec, per(vd)], out_specs=[per(qd), per(nope), per(vd), one(rope)],
-        out_shape=[jax.ShapeDtypeStruct(q.shape, BF16), jax.ShapeDtypeStruct(kn.shape, BF16), jax.ShapeDtypeStruct(v.shape, BF16), jax.ShapeDtypeStruct(kp.shape, F32)],
-        scratch_shapes=[VM((qd, seq), F32), VM((vd, seq), F32)],
+        attn_bwd_body, grid=(heads,), in_specs=ins + [lse_spec, per(vd)], out_specs=[per(qd), per(nope), per(vd), one(rope), pl.BlockSpec(memory_space=pl.ANY)],
+        out_shape=[jax.ShapeDtypeStruct(q.shape, BF16), jax.ShapeDtypeStruct(kn.shape, BF16), jax.ShapeDtypeStruct(v.shape, BF16), jax.ShapeDtypeStruct(kp.shape, F32), jax.ShapeDtypeStruct(table, BF16)],
+        scratch_shapes=[VM((qd, seq), F32), VM((vd, seq), F32), VM((ZR, table[1]), BF16), pltpu.SemaphoreType.DMA((-(-table[0] // ZR),))],
         compiler_params=pltpu.CompilerParams(vmem_limit_bytes=40 << 20), name='attend_bwd',
     )(q, kn, kp, v, cos_t, sin_t, lse, do)
 
 
-def gather(x):
-    return lax.all_gather(x, 'tp', axis=0, tiled=True)
-
-
-def scatter(x):
-    return lax.psum_scatter(x, 'tp', scatter_dimension=0, tiled=True)
-
-
-def layer_pass(embedded, d_out, w_q, w_dkv, g_kv, w_uk, w_uv, w_o, g_attn, g_mlp, w_gate, w_up, w_down):
+def shift(x, bit):
+    return lax.ppermute(x, 'tp', [(d, d ^ bit) for d in range(8)])
+
+
+PAIR, XBIT, YBIT = 1, 2, 4
+
+
+def coords():
+    me = lax.axis_index('tp')
+    return me // YBIT, (me // XBIT) % 2, me % 2
+
+
+def pick(x, i, axis):
+    return lax.dynamic_index_in_dim(x, i, axis, keepdims=False)
+
+
+def added(a, b):
+    return (a.astype(F32) + b.astype(F32)).astype(BF16)
+
+
+def scatter_hops(part, local):
+    y, x, core = coords()
+    half = part.shape[1] // 2
+    p = part.reshape(2, 2, 2, local, part.shape[1])
+    q = added(pick(p, core, 2), shift(pick(p, 1 - core, 2), PAIR))
+    a, b = q[..., :half], q[..., half:]
+    a = added(pick(a, x, 1), shift(pick(a, 1 - x, 1), XBIT))
+    b = added(pick(b, y, 0), shift(pick(b, 1 - y, 0), YBIT))
+    a = pick(a, y, 0).astype(F32) + shift(pick(a, 1 - y, 0), YBIT).astype(F32)
+    b = pick(b, x, 0).astype(F32) + shift(pick(b, 1 - x, 0), XBIT).astype(F32)
+    return jnp.concatenate([a, b], axis=1)
+
+
+def gather_hops(blk):
+    half = blk.shape[1] // 2
+    bx, by = shift(blk, XBIT), shift(blk, YBIT)
+    near = jnp.concatenate([blk, bx, by])
+    diag = jnp.concatenate([shift(by[:, :half], XBIT), shift(bx[:, half:], YBIT)], axis=1)
+    return jnp.concatenate([near, diag, shift(near, PAIR), shift(diag, PAIR)])
+
+
+def hop_order():
+    me = lax.axis_index('tp')
+    flip = lambda v, bit: v + bit - 2 * bit * ((v // bit) % 2)
+    own = [me, flip(me, XBIT), flip(me, YBIT), flip(flip(me, XBIT), YBIT)]
+    return own + [flip(d, PAIR) for d in own]
+
+
+def to_hop_order(x, axis):
+    n = x.shape[axis] // 8
+    return jnp.concatenate([lax.dynamic_slice_in_dim(x, d * n, n, axis) for d in hop_order()], axis=axis)
+
+
+def from_hop_order(x):
+    n = x.shape[0] // 8
+    out = jnp.zeros_like(x)
+    for k, d in enumerate(hop_order()):
+        out = lax.dynamic_update_slice_in_dim(out, x[k * n:(k + 1) * n], d * n, 0)
+    return out
+
+
+def sum_hops(x):
+    for bit in (PAIR, XBIT, YBIT):
+        x = x + shift(x, bit)
+    return x
+
+
+class Exchange:
+    def __init__(self, widths, pieces):
+        self.widths, self.pieces = widths, pieces
+        self.order = range(len(pieces))
+
+    def rs_scratch(self, rows):
+        n = len(self.pieces)
+        out = []
+        for w in self.widths:
+            out += [VM((4, rows, w), BF16), VM((2, rows, w), BF16), VM((2, rows, w), BF16), VM((rows, w), BF16), VM((rows, w), BF16)]
+        dma = pltpu.SemaphoreType.DMA
+        return out + [dma((4, n)), dma((4, n)), dma((2, n)), dma((2, n)), dma((n,)), dma((n,))]
+
+    def ag_scratch(self):
+        n = len(self.pieces)
+        dma = pltpu.SemaphoreType.DMA
+        return [dma((2, n)), dma((2, n)), dma((n,)), dma((n,)), dma((4, n)), dma((4, n))]
+
+    def place(self, rows):
+        me = lax.axis_index('tp')
+        core, x, y = me % 2, (me // 2) % 2, me // 4
+        dev = lambda yy, xx, cc: (yy * 2 + xx) * 2 + cc
+        self.me, self.rows = me, rows
+        self.pn, self.xn, self.yn = dev(y, x, 1 - core), dev(y, 1 - x, core), dev(1 - y, x, core)
+        chips = [(y, x), (y, 1 - x), (1 - y, x), (1 - y, 1 - x)]
+        at = lambda d: pl.ds(pl.multiple_of(d * rows, rows), rows)
+        self.mine = [at(dev(*ch, core)) for ch in chips]
+        self.theirs = [at(dev(*ch, 1 - core)) for ch in chips]
+        self.chip = [pl.ds(pl.multiple_of(dev(*ch, 0) * rows, 2 * rows), 2 * rows) for ch in chips]
+
+    def enter(self):
+        sem = pltpu.get_barrier_semaphore()
+        near = (self.pn, self.xn, self.yn)
+        for d in near:
+            pl.semaphore_signal(sem, inc=1, device_id={'tp': d}, device_id_type=pl.DeviceIdType.MESH)
+        pl.semaphore_wait(sem, len(near))
+
+    def copy(self, src, dst, ssem, rsem, dev):
+        return pltpu.make_async_remote_copy(src_ref=src, dst_ref=dst, send_sem=ssem, recv_sem=rsem, device_id={'tp': dev}, device_id_type=pl.DeviceIdType.MESH)
+
+    def rs_begin(self, parts, scratch):
+        na = len(self.widths)
+        self.parts = parts
+        self.bufs = [scratch[5 * a:5 * a + 5] for a in range(na)]
+        ds, dr, s1, r1, s2, r2 = scratch[5 * na:5 * na + 6]
+        self.pair, self.hop1, self.hop2 = {}, {}, {}
+        for i, (h, a, c0, cn) in enumerate(self.pieces):
+            cols = pl.ds(c0, cn)
+            dbuf, sb1, rb1, sb2, rb2 = self.bufs[a]
+            for j in range(4):
+                self.pair[j, i] = self.copy(parts[a].at[self.theirs[j], cols], dbuf.at[j, :, cols], ds.at[j, i], dr.at[j, i], self.pn)
+            to1, to2 = (self.xn, self.yn) if h == 0 else (self.yn, self.xn)
+            for k in range(2):
+                self.hop1[k, i] = self.copy(sb1.at[k, :, cols], rb1.at[k, :, cols], s1.at[k, i], r1.at[k, i], to1)
+            self.hop2[i] = self.copy(sb2.at[:, cols], rb2.at[:, cols], s2.at[i], r2.at[i], to2)
+
+    def ready(self, j):
+        for i in self.order:
+            self.pair[j, i].start()
+
+    def chip_sum(self, j, i):
+        h, a, c0, cn = self.pieces[i]
+        self.pair[j, i].wait_recv()
+        return self.parts[a][self.mine[j], c0:c0 + cn].astype(F32) + self.bufs[a][0][j, :, c0:c0 + cn].astype(F32)
+
+    def push(self, j):
+        for i in self.order:
+            h, a, c0, cn = self.pieces[i]
+            if j == 3 or j == 1 + h:
+                k = 1 if j == 3 else 0
+                self.bufs[a][1][k, :, c0:c0 + cn] = self.chip_sum(j, i).astype(BF16)
+                self.hop1[k, i].start()
+
+    def relay(self):
+        for i in self.order:
+            h, a, c0, cn = self.pieces[i]
+            own = self.chip_sum(2 - h, i)
+            self.hop1[1, i].wait_recv()
+            self.bufs[a][3][:, c0:c0 + cn] = (own + self.bufs[a][2][1, :, c0:c0 + cn].astype(F32)).astype(BF16)
+            self.hop2[i].start()
+
+    def land(self, accs):
+        for i in self.order:
+            h, a, c0, cn = self.pieces[i]
+            own = self.chip_sum(0, i)
+            self.hop1[0, i].wait_recv()
+            own = own + self.bufs[a][2][0, :, c0:c0 + cn].astype(F32)
+            self.hop2[i].wait_recv()
+            accs[a][:, c0:c0 + cn] = own + self.bufs[a][4][:, c0:c0 + cn].astype(F32)
+
+    def drain(self):
+        for cp in list(self.pair.values()) + list(self.hop1.values()) + list(self.hop2.values()):
+            cp.wait_send()
+
+    def reduce_scatter(self, accs, produce):
+        late = None
+        for j in (3, 1, 2, 0):
+            produce(j)
+            self.ready(j)
+            if late:
+                self.push(late)
+            late = j
+        self.relay()
+        self.land(accs)
+
+    def all_gather(self, fulls, scratch, arrive):
+        os_, xr, fs, fr, ps, pr = scratch
+        half0 = [i for i in self.order if self.pieces[i][0] == 0]
+        half1 = [i for i in self.order if self.pieces[i][0] == 1]
+
+        def to(i, j, ssem, rsem, dev, rows=None):
+            h, a, c0, cn = self.pieces[i]
+            ref = fulls[a].at[(rows or self.mine)[j], pl.ds(c0, cn)]
+            return self.copy(ref, ref, ssem, rsem, dev)
+
+        near = (self.xn, self.yn)
+        own = [[to(i, 0, os_.at[k, i], xr.at[k, i], dev) for i in self.order] for k, dev in enumerate(near)]
+        from_n = [[to(i, 1 + k, os_.at[k, i], xr.at[k, i], dev) for i in self.order] for k, dev in enumerate(near)]
+        fwd = [to(i, 2 - self.pieces[i][0], fs.at[i], fr.at[i], near[self.pieces[i][0]]) for i in self.order]
+        diag = [to(i, 3, fs.at[i], fr.at[i], self.xn) for i in self.order]
+        give = [[to(i, j, ps.at[j, i], pr.at[j, i], self.pn) for i in self.order] for j in range(4)]
+        take = [[to(i, j, ps.at[j, i], pr.at[j, i], self.pn, self.theirs) for i in self.order] for j in range(4)]
+        for i0, i1 in zip(half0, half1):
+            own[0][i1].start()
+            own[1][i0].start()
+        for i0, i1 in zip(half0, half1):
+            own[0][i0].start()
+            own[1][i1].start()
+        for cp in give[0]:
+            cp.start()
+        for cp in take[0]:
+            cp.wait_recv()
+        arrive(0)
+        for i0, i1 in zip(half0, half1):
+            from_n[1][i0].wait_recv()
+            fwd[i0].start()
+            give[2][i0].start()
+            from_n[0][i1].wait_recv()
+            fwd[i1].start()
+            give[1][i1].start()
+        for i0, i1 in zip(half0, half1):
+            from_n[1][i1].wait_recv()
+            give[2][i1].start()
+            from_n[0][i0].wait_recv()
+            give[1][i0].start()
+        for j in (1, 2):
+            for cp in take[j]:
+                cp.wait_recv()
+            arrive(j)
+        for i in self.order:
+            diag[i].wait_recv()
+            give[3][i].start()
+        for cp in take[3]:
+            cp.wait_recv()
+        arrive(3)
+        for cp in own[0] + own[1] + fwd + [c for g in give for c in g]:
+            cp.wait_send()
+
+
+def halves(width, n):
+    step = width // (2 * n)
+    return [(h, 0, (h * n + k) * step, step) for k in range(n) for h in range(2)]
+
+
+MAIN = halves(2560, 2)
+LAST = MAIN + [(0, 1, 0, 256), (1, 1, 256, 128)]
+NRS = 11
+
+
+def norm_rows(x, gain):
+    return x * lax.rsqrt(jnp.mean(x * x, axis=-1, keepdims=True) + EPSILON) * gain
+
+
+def norm_rows_vjp(x, gain, dy):
+    r = lax.rsqrt(jnp.mean(x * x, axis=-1, keepdims=True) + EPSILON)
+    gd = dy * gain
+    dot = jnp.mean(gd * x, axis=-1, keepdims=True)
+    return r * gd - x * (r * r * r * dot), jnp.sum(dy * x * r, axis=0, keepdims=True)
+
+
+def exchange_call(body, name, cid, ins, out_shape, scratch):
+    vmem = pl.BlockSpec(memory_space=VM)
+    return pl.pallas_call(
+        body, out_shape=out_shape, in_specs=[vmem] * len(ins), out_specs=[vmem] * len(out_shape), scratch_shapes=scratch,
+        compiler_params=pltpu.CompilerParams(vmem_limit_bytes=50 << 20, collective_id=cid, has_side_effects=True), name=name)(*ins)
+
+
+def shape(dims, dtype):
+    return jax.ShapeDtypeStruct(dims, dtype)
+
+
+def idle(j):
+    pass
+
+
+def embed_body(part, gain, wq, wdkv, e_ref, full, q_ref, lat_ref, acc, *scratch):
+    ex = Exchange([part.shape[1]], MAIN)
+    ex.place(acc.shape[0])
+    ex.enter()
+    ex.rs_begin([part], scratch)
+    ex.reduce_scatter([acc], idle)
+    e = acc[...].astype(BF16)
+    e_ref[...] = e
+    full[ex.mine[0], :] = norm_rows(e.astype(F32), gain[...]).astype(BF16)
+
+    def arrive(j):
+        u = full[ex.chip[j], :]
+        q_ref[:, ex.chip[j]] = nt(wq[...], u).astype(BF16)
+        lat_ref[ex.chip[j], :] = nt(u, wdkv[...])
+
+    ex.all_gather([full], scratch[NRS:], arrive)
+    ex.drain()
+
+
+def attn_out_body(o_ref, wo, e_ref, gain, h_ref, full, part, acc, *scratch):
+    ex = Exchange([part.shape[1]], MAIN)
+    ex.place(acc.shape[0])
+    ex.enter()
+    ex.rs_begin([part], scratch)
+
+    def produce(j):
+        part[ex.chip[j], :] = tn(o_ref[:, ex.chip[j]], wo[...]).astype(BF16)
+
+    ex.reduce_scatter([acc], produce)
+    h = (e_ref[...].astype(F32) + acc[...].astype(BF16).astype(F32)).astype(BF16)
+    h_ref[...] = h
+    full[ex.mine[0], :] = norm_rows(h.astype(F32), gain[...]).astype(BF16)
+    ex.all_gather([full], scratch[NRS:], idle)
+    ex.drain()
+
+
+def mlp_back_body(part, h_ref, dy_ref, gain, wo, dres_ref, dg_ref, full, do_ref, acc, *scratch):
+    ex = Exchange([part.shape[1]], MAIN)
+    ex.place(acc.shape[0])
+    ex.enter()
+    ex.rs_begin([part], scratch)
+    ex.reduce_scatter([acc], idle)
+    dx, dg = norm_rows_vjp(h_ref[...].astype(F32), gain[...], acc[...])
+    dg_ref[...] = dg
+    dres = dy_ref[...].astype(F32) + dx
+    dres_ref[...] = dres
+    full[ex.mine[0], :] = dres.astype(BF16)
+
+    def arrive(j):
+        do_ref[:, ex.chip[j]] = nt(wo[...], full[ex.chip[j], :]).astype(BF16)
+
+    ex.all_gather([full], scratch[NRS:], arrive)
+    ex.drain()
+
+
+def attn_back_body(dq_ref, lat, wq, wdkv, e_ref, dres_ref, gain, de_ref, dlat_ref, dg_ref, part, acc, acc_lat, *scratch):
+    ex = Exchange([part.shape[1], lat.shape[1]], LAST)
+    ex.place(acc.shape[0])
+    ex.enter()
+    ex.rs_begin([part, lat], scratch)
+    lw = wdkv.shape[0]
+
+    def produce(j):
+        rows = ex.chip[j]
+        part[rows, :] = (tn(dq_ref[:, rows], wq[...]) + nn(lat[rows, :lw], wdkv[...])).astype(BF16)
+
+    ex.reduce_scatter([acc, acc_lat], produce)
+    dx, dg_ref[...] = norm_rows_vjp(e_ref[...].astype(F32), gain[...], acc[...])
+    de_ref[...] = (dres_ref[...] + dx).astype(BF16)
+    dlat_ref[...] = acc_lat[...].astype(BF16)
+    ex.drain()
+
+
+def layer_pass(rows, d_out, w_q, w_dkv, g_kv, w_uk, w_uv, w_o, g_attn, g_mlp, w_gate, w_up, w_down, vocab):
     w_q, heads = w_q
-    x_attn_loc, attn_norm_pull = jax.vjp(rms_norm, embedded.astype(F32), g_attn)
-    x_attn = gather(x_attn_loc)
-    seq = x_attn.shape[0]
-    rope = w_dkv.shape[0] - g_kv.shape[0]
-    cos_t, sin_t = (t.T for t in rope_tables(seq, rope))
-    query = mm(w_q, x_attn, 1, 1).astype(BF16)
-    latent = mm(x_attn, w_dkv, 1, 1)
+    seq, width = rows.shape
+    local = d_out.shape[0]
+    lora = g_kv.shape[0]
+    latw = w_dkv.shape[0]
+    one = Exchange([width], MAIN)
+    main = [VM((local, width), F32)] + one.rs_scratch(local) + one.ag_scratch()
+    partb = [VM((seq, width), BF16)]
+    loc, fullb = shape((local, width), BF16), shape((seq, width), BF16)
+    ga, gm = g_attn[None, :], g_mlp[None, :]
+    embedded, x_attn, query, latent = exchange_call(
+        embed_body, 'embed_exchange', 1, [rows, ga, w_q, w_dkv], [loc, fullb, shape((w_q.shape[0], seq), BF16), shape((seq, latw), F32)], main)
+    d_out_late, latent = lax.optimization_barrier((d_out, latent))
+    dy_full = from_hop_order(gather_hops(d_out_late))
+    cos_t, sin_t = (t.T for t in rope_tables(seq, latw - lora))
     (c_kv, k_pe), kv_pull = jax.vjp(kv_prep, latent, g_kv)
-    k_nope = mm(w_uk, c_kv, 1, 1).astype(BF16)
-    value = mm(w_uv, c_kv, 1, 1).astype(BF16)
+    k_nope = nt(w_uk, c_kv).astype(BF16)
+    value = nt(w_uv, c_kv).astype(BF16)
     k_pe_t = k_pe.T
     attn_out, lse = attend_fwd(query, k_nope, k_pe_t, value, cos_t, sin_t, heads)
-    attn_part = mm(attn_out, w_o, 0, 0).astype(BF16)
-    attn_loc = scatter(attn_part)
-    residual = (embedded.astype(F32) + attn_loc.astype(F32)).astype(BF16)
-    x_mlp_loc, mlp_norm_pull = jax.vjp(rms_norm, residual.astype(F32), g_mlp)
-    x_mlp = gather(x_mlp_loc)
-    gate = mm(x_mlp, w_gate, 1, 1)
-    up_proj = mm(x_mlp, w_up, 1, 1)
+    residual, x_mlp = exchange_call(attn_out_body, 'attn_exchange', 2, [attn_out, w_o, embedded, gm], [loc, fullb], partb + main)
+    gate = nt(x_mlp, w_gate)
+    up_proj = nt(x_mlp, w_up)
     gate_sig = jax.nn.sigmoid(gate)
     hidden = (gate * gate_sig * up_proj).astype(BF16)
-    mlp_loc = scatter(mm(hidden, w_down, 1, 0).astype(BF16))
-    layer_out = (residual.astype(F32) + mlp_loc.astype(F32)).astype(BF16)
-
-    dy_full = gather(d_out)
-    d_hidden = mm(dy_full, w_down, 1, 1)
-    dw_down = mm(hidden, dy_full, 0, 0)
+
+    d_hidden = nt(dy_full, w_down)
     d_up = (d_hidden * gate * gate_sig).astype(BF16)
     d_gate = (d_hidden * up_proj * gate_sig * (1.0 + gate * (1.0 - gate_sig))).astype(BF16)
-    dw_gate = mm(d_gate, x_mlp, 0, 0)
-    dw_up = mm(d_up, x_mlp, 0, 0)
-    dx_mlp = scatter((mm(d_gate, w_gate, 1, 0) + mm(d_up, w_up, 1, 0)).astype(BF16))
-    d_res_norm, dg_mlp_part = mlp_norm_pull(dx_mlp)
-    d_residual = d_out.astype(F32) + d_res_norm
-    d_attn_full = gather(d_residual.astype(BF16))
-    dw_o = mm(attn_out, d_attn_full, 1, 0)
-    d_attn_out = mm(w_o, d_attn_full, 1, 1).astype(BF16)
-    d_query, d_knope, d_value, d_kpe = attend_bwd(query, k_nope, k_pe_t, value, cos_t, sin_t, lse, d_attn_out, heads)
-    dw_uk = mm(d_knope, c_kv, 1, 0)
-    dw_uv = mm(d_value, c_kv, 1, 0)
-    d_ckv = (mm(d_knope, w_uk, 0, 0) + mm(d_value, w_uv, 0, 0)).astype(BF16)
-    d_latent, dg_kv_part = kv_pull((d_ckv, d_kpe.T.astype(BF16)))
-    d_latent = d_latent.astype(BF16)
-    dw_q = mm(d_query, x_attn, 1, 0)
-    dw_dkv_part = mm(d_latent, x_attn, 0, 0)
-    dx_attn = scatter((mm(d_query, w_q, 0, 0) + mm(d_latent, w_dkv, 1, 0)).astype(BF16))
-    d_emb_norm, dg_attn_part = attn_norm_pull(dx_attn)
-    d_embed = (d_residual + d_emb_norm).astype(BF16)
-    dw_dkv, dg_kv, dg_attn, dg_mlp = lax.psum((dw_dkv_part, dg_kv_part, dg_attn_part, dg_mlp_part), 'tp')
-    return layer_out, d_embed, (dw_q, dw_dkv, dg_kv, dw_uk, dw_uv, dw_o, dg_attn, dg_mlp, dw_gate, dw_up, dw_down)
+    dx_part = (nn(d_gate, w_gate) + nn(d_up, w_up)).astype(BF16)
+    d_residual, dg_mlp, d_attn_full, d_attn_out = exchange_call(
+        mlp_back_body, 'mlp_exchange', 3, [dx_part, residual, d_out, gm, w_o],
+        [shape((local, width), F32), shape((1, width), F32), fullb, shape((w_o.shape[0], seq), BF16)], main)
+    hidden_late, d_attn_full = lax.optimization_barrier((hidden, d_attn_full))
+    mlp_loc = scatter_hops(nn(hidden_late, w_down).astype(BF16), local)
+    layer_out = (residual.astype(F32) + mlp_loc.astype(BF16).astype(F32)).astype(BF16)
+    d_query, d_knope, d_value, d_kpe, table0 = attend_bwd(query, k_nope, k_pe_t, value, cos_t, sin_t, lse, d_attn_out, heads, (vocab, width))
+    d_ckv = (tn(d_knope, w_uk) + tn(d_value, w_uv)).astype(BF16)
+    d_latent, dg_kv = kv_pull((d_ckv, d_kpe.T.astype(BF16)))
+    lat_part = jnp.pad(d_latent.astype(BF16), ((0, 0), (0, -latw % 128)))
+    padw = lat_part.shape[1]
+    two = Exchange([width, padw], LAST)
+    de, dlat, dg_attn = exchange_call(
+        attn_back_body, 'back_exchange', 4, [d_query, lat_part, w_q, w_dkv, embedded, d_residual, ga],
+        [loc, shape((local, padw), BF16), shape((1, width), F32)],
+        partb + [VM((local, width), F32), VM((local, padw), F32)] + two.rs_scratch(local))
+    hidden, d_gate, d_up, d_query_l, d_knope, d_value, attn_out, de = lax.optimization_barrier((hidden, d_gate, d_up, d_query, d_knope, d_value, attn_out, de))
+    de_full = gather_hops(de)
+    lat_full = from_hop_order(gather_hops(dlat))
+    dw_down = tn(hidden, dy_full)
+    dw_gate = tn(d_gate, x_mlp)
+    dw_up = tn(d_up, x_mlp)
+    dw_o = nn(attn_out, d_attn_full)
+    dw_uk = nn(d_knope, c_kv)
+    dw_uv = nn(d_value, c_kv)
+    dw_q = nn(d_query_l, x_attn)
+    dw_dkv = tn(lat_full[:, :latw], x_attn)
+    dg = sum_hops(jnp.concatenate([dg_attn[0], dg_mlp[0], dg_kv]))
+    dg_attn, dg_mlp, dg_kv = dg[:width], dg[width:2 * width], dg[2 * width:]
+    return layer_out, de_full, table0, (dw_q, dw_dkv, dg_kv, dw_uk, dw_uv, dw_o, dg_attn, dg_mlp, dw_gate, dw_up, dw_down)
 
 
 def rows_of(w):
@@ -358,12 +708,10 @@
         heads = w_q.shape[1]
         key, blocks, count = block_index(tokens, vocab_local)
         rows = gather_rows(key, blocks, count, embed_table)
-        embedded = scatter(rows)
-        layer_out, d_embed, grads = layer_pass(
-            embedded, d_out[0], (rows_of(w_q), heads), w_dkv.T, g_kv, rows_of(w_uk), rows_of(w_uv), w_o.reshape(-1, model_dim),
-            g_attn, g_mlp, w_gate.T, w_up.T, w_down)
-        de_full = gather(d_embed)
-        d_table = table_grad(key, blocks, count, de_full, vocab_local)
+        layer_out, de_full, table0, grads = layer_pass(
+            rows, d_out[0], (rows_of(w_q), heads), w_dkv.T, g_kv, rows_of(w_uk), rows_of(w_uv), w_o.reshape(-1, model_dim),
+            g_attn, g_mlp, w_gate.T, w_up.T, w_down, vocab_local)
+        d_table = table_grad(to_hop_order(key, 0), blocks, count, de_full, table0)
         dw_q, dw_dkv, dg_kv, dw_uk, dw_uv, dw_o, dg_attn, dg_mlp, dw_gate, dw_up, dw_down = grads
         return (layer_out[None], d_table, unrows(dw_q, heads), dw_dkv.T, dg_kv, unrows(dw_uk, heads), unrows(dw_uv, heads),
                 dw_o.reshape(w_o.shape), dg_attn, dg_mlp, dw_gate.T, dw_up.T, dw_down)

time: 625 us -> 443 us (0.71)
  waiting for transfers between devices: 363 us -> 41 us
  Pallas kernels: 49.4 us -> 246 us
  matrix products: 123 us -> 82.6 us
  blocking collectives: 23.6 us -> 0 us
  starting transfers between devices: 1.35 us -> 18.9 us
  between operations: 15 us -> 2.12 us
  local copies, waits for them, and re-layouts: 19.3 us -> 27.1 us
    reduce_scatter x5 -> x0, waiting for transfers between devices: 234 us -> none  [scatter(): return lax.psum_scatter(x, 'tp', scatter_dimension=0, tiled=True)]
    pallas_call x0 -> x4, Pallas kernels: none -> 209 us  [exchange_call(): pl.pallas_call(body, out_shape=out_shape, in_specs=[vmem] * len(ins), out...]
    all_gather x5 -> x0, waiting for transfers between devices: 125 us -> none  [gather(): return lax.all_gather(x, 'tp', axis=0, tiled=True)]
    ppermute x0 -> x26, waiting for transfers between devices: none -> 41 us  [shift(): return lax.ppermute(x, 'tp', [(d, d ^ bit) for d in range(8)])]
    dot_general x24 -> x18, matrix products: 123 us -> 82.6 us  [mm(): lax.dot_general(lhs, rhs, (((lc,), (rc,)), ((), ())), preferred_element_t...]
    psum x1 -> x0, blocking collectives: 23.6 us -> none  [layer_pass(): lax.psum((dw_dkv_part, dg_kv_part, dg_attn_part, dg_mlp_part), 'tp')]
    ppermute x0 -> x26, starting transfers between devices: none -> 18.9 us  [shift(): return lax.ppermute(x, 'tp', [(d, d ^ bit) for d in range(8)])]
    pallas_call x1, Pallas kernels: 20 us -> 5.26 us  [table_grad(): pl.pallas_call(table_grad_body, out_shape=[jax.ShapeDtypeStruct((vocab, w...]
  transfers between devices with their start and end apart: 11 -> 26, of which waited for: 10 -> 13; matrix products, arithmetic and copies ran while one was open for 12% -> 19% of each run, Pallas kernels for 3% -> 16%
where the time goes in v3:
time: 443 us; the launch traced here: 437 us
  Pallas kernels  246 us (56%)
  matrix products  82.6 us (19%)
  waiting for transfers between devices  41 us (9%)
  local copies, waits for them, and re-layouts  27.1 us (6%)
  other arithmetic  19.6 us (4%)
  starting transfers between devices  18.9 us (4%)
    pallas_call x4, Pallas kernels, exchange_call(): pl.pallas_call(body, out_shape=out_shape, in_specs=[vmem] * len(ins), out...  209 us
    dot_general x18, matrix products, mm(): lax.dot_general(lhs, rhs, (((lc,), (rc,)), ((), ())), preferred_element_t...  82.6 us
    ppermute x26, waiting for transfers between devices, shift(): return lax.ppermute(x, 'tp', [(d, d ^ bit) for d in range(8)])  41 us
    ppermute x26, starting transfers between devices, shift(): return lax.ppermute(x, 'tp', [(d, d ^ bit) for d in range(8)])  18.9 us
    pallas_call x1, Pallas kernels, attend_bwd(): pl.pallas_call(attn_bwd_body, grid=(heads,), in_specs=ins + [lse_spec, pe...  15.3 us
    unnamed x108, local copies, waits for them, and re-layouts  13.6 us
    pallas_call x1, Pallas kernels, attend_fwd(): pl.pallas_call(attn_fwd_body, grid=(heads,), in_specs=ins, out_specs=[per...  9.35 us
  transfers between devices with their start and end apart: 26, of which 13 were waited for; matrix products, arithmetic and copies ran while one was open for 19% of the time, Pallas kernels for 16%

profile of v3, /device:TPU:0, one launch (start us, length us, event | category | flops | bytes accessed | tf_op | source)
XLA Modules:
  0.0 437.1 jit_solution(14388352825995212002)
XLA Ops:
  7.1 6.8 %gather_rows.1.part = bf16[1024,2560]{1,0:T(8,128)(2,1)S(1)} custom-call(s32[1]{0:T(128)} %bitcast.2.count_ref, s32[1024]{0:T(1024)S(1)} %select_reduce_fusion.blocks_ref, s32[1024,1]{1,0:T(8,128)S(1)} %add_select_fusion.key_ref, bf16[8,2560]{1,0:T(8,128)(2,1)S(1)} %pad.20.tail_ref, bf16[9181,2560]{1,0:T(8,128)(2,1)} %table_ref.1), custom_call_target="tpu_custom_call" | custom-call | tf_op jit(solution)/shard_map/gather_rows/pallas_call | solution.py:127
  13.9 2.3 copy-done.2
  16.2 60.5 %embed_exchange.1 = (bf16[128,2560]{1,0:T(8,128)(2,1)S(1)}, bf16[1024,2560]{1,0:T(8,128)(2,1)}, bf16[480,1024]{1,0:T(8,128)(2,1)S(1)}, f32[1024,288]{1,0:T(8,128)}) custom-call(bf16[1024,2560]{1,0:T(8,128)(2,1)} %copy-done.2, f32[1,2560]{1,0:T(1,128)S(1)} %broadcast_in_dim.74.gain, bf16[480,2560]{1,0:T(8,128)(2,1)} %bitcast.113, bf16[288,2560]{1,0:T(8,128)(2,1)S(1)} %bitcast.111), custom_call_target="tpu_custom_call" | custom-call | tf_op jit(solution)/shard_map/embed_exchange/pallas_call | solution.py:548
  77.7 1.3 collective-permute-start.1
  80.2 1.4 multiply_reduce_fusion
  81.6 3.7 multiply_subtract_fusion
  85.7 1.6 multiply_convert_fusion.3
  89.1 1.2 copy-done.6
  90.3 9.3 %attend_fwd.1 = (bf16[320,1024]{1,0:T(8,128)(2,1)S(1)}, f32[5,1,1024]{2,1,0:T(1,128)S(1)}) custom-call(bf16[480,1024]{1,0:T(8,128)(2,1)S(1)} %copy-done.6, bf16[320,1024]{1,0:T(8,128)(2,1)S(1)} %fusion.6.kn_ref, bf16[32,1024]{1,0:T(8,128)(2,1)S(1)} %maximum_bitcast_fusion.kp_ref, bf16[320,1024]{1,0:T(8,128)(2,1)S(1)} %fusion.7.v_ref, ...), custom_call_target="tpu_custom_call" | custom-call | tf_op jit(solution)/shard_map/attend_fwd/pallas_call | solution.py:281
  99.7 1.3 copy-done.9
  101.0 54.6 %attn_exchange.1 = (bf16[128,2560]{1,0:T(8,128)(2,1)S(1)}, bf16[1024,2560]{1,0:T(8,128)(2,1)}) custom-call(bf16[320,1024]{1,0:T(8,128)(2,1)S(1)} %get-tuple-element.76.o_ref, bf16[320,2560]{1,0:T(8,128)(2,1)S(1)} %bitcast.109, bf16[128,2560]{1,0:T(8,128)(2,1)S(1)} %copy-done.9, f32[1,2560]{1,0:T(1,128)S(1)} %broadcast_in_dim.75.gain), custom_call_target="tpu_custom_call" | custom-call | tf_op jit(solution)/shard_map/attn_exchange/pallas_call | solution.py:548
  155.7 8.1 %fusion.26 = f32[1024,800]{0,1:T(8,128)S(1)} fusion(bf16[1024,2560]{1,0:T(8,128)(2,1)} %get-tuple-element.53, bf16[2560,800]{0,1:T(8,128)(2,1)} %param.25), kind=kOutput, calls=%fused_computation.121 | convolution fusion | flops 4194304000 | bytes 12615680 | tf_op jit(solution)/shard_map/dot_general | solution.py:21
  163.8 4.4 %fusion.25 = f32[1024,800]{0,1:T(8,128)S(1)} fusion(bf16[1024,2560]{1,0:T(8,128)(2,1)S(1)} %copy-done.27, bf16[2560,800]{0,1:T(8,128)(2,1)S(1)} %copy-done.28), kind=kOutput, calls=%fused_computation.120 | convolution fusion | flops 4194304000 | bytes 12615680 | tf_op jit(solution)/shard_map/dot_general | solution.py:21
  168.2 1.6 pad_maximum_fusion
  174.7 1.2 collective-permute-start.3
  178.2 4.4 %collective-permute-done.2 = bf16[128,1280]{1,0:T(8,128)(2,1)S(1)} collective-permute-done((bf16[128,1280]{1,0:T(8,128)(2,1)S(1)}, bf16[128,1280]{1,0:T(8,128)(2,1)S(1)}, u32[]{:S(2)}, u32[]{:S(2)}) %collective-permute-start.2) | collective-permute-done | bytes 327712 | tf_op jit(solution)/shard_map/ppermute | solution.py:300
  182.6 1.6 collective-permute-done.3
  184.5 1.8 collective-permute-done.5
  186.4 6.7 %multiply_convert_fusion = (bf16[1024,800]{0,1:T(8,128)(2,1)S(1)}, bf16[1024,800]{0,1:T(8,128)(2,1)S(1)}, bf16[1024,800]{0,1:T(8,128)(2,1)}) fusion(f32[1024,800]{0,1:T(8,128)S(1)} %fusion.25, f32[1024,800]{0,1:T(8,128)S(1)} %fusion.26, bf16[1024,2560]{1,0:T(8,128)(2,1)S(1)} %constant_dynamic-update-slice_fusion.15, bf16[800,2560]{1,0:T(8,128)(2,1)S(1)} %copy-done.30), kind=kOutput, calls=%fused_computation.11 | convolution fusion | flops 4207411200 | bytes 20807680 | tf_op jit(solution)/shard_map/dot_general | solution.py:21
  193.1 5.7 %fusion.27 = f32[1024,2560]{1,0:T(8,128)S(1)} fusion(bf16[1024,800]{0,1:T(8,128)(2,1)S(1)} %get-tuple-element.78, bf16[2560,800]{0,1:T(8,128)(2,1)S(1)} %copy-done.28), kind=kOutput, calls=%fused_computation.122 | convolution fusion | flops 4194304000 | bytes 16220160 | tf_op jit(solution)/shard_map/dot_general | solution.py:21
  198.9 8.2 %add_convert_fusion.part = bf16[1024,2560]{1,0:T(8,128)(2,1)} fusion(f32[1024,2560]{1,0:T(8,128)S(1)} %fusion.27, bf16[1024,800]{0,1:T(8,128)(2,1)S(1)} %get-tuple-element.79, bf16[2560,800]{0,1:T(8,128)(2,1)S(1)} %copy-done.29), kind=kOutput, calls=%fused_computation | convolution fusion | flops 4199546880 | bytes 21463040 | tf_op jit(solution)/shard_map/dot_general | solution.py:21
  207.1 58.1 %mlp_exchange.1 = (f32[128,2560]{1,0:T(8,128)S(1)}, f32[1,2560]{1,0:T(1,128)S(1)}, bf16[1024,2560]{1,0:T(8,128)(2,1)}, bf16[320,1024]{1,0:T(8,128)(2,1)S(1)}) custom-call(bf16[1024,2560]{1,0:T(8,128)(2,1)} %add_convert_fusion.part, bf16[128,2560]{1,0:T(8,128)(2,1)S(1)} %get-tuple-element.52.h_ref, bf16[128,2560]{1,0:T(8,128)(2,1)} %bitcast.10.dy_ref, ...), custom_call_target="tpu_custom_call" | custom-call | tf_op jit(solution)/shard_map/mlp_exchange/pallas_call | solution.py:548
  265.2 15.3 %attend_bwd.1 = (bf16[480,1024]{1,0:T(8,128)(2,1)S(1)}, bf16[320,1024]{1,0:T(8,128)(2,1)S(1)}, bf16[320,1024]{1,0:T(8,128)(2,1)S(1)}, f32[32,1024]{1,0:T(8,128)S(1)}, bf16[9181,2560]{1,0:T(8,128)(2,1)}) custom-call(bf16[480,1024]{1,0:T(8,128)(2,1)S(1)} %copy-done.7, bf16[320,1024]{1,0:T(8,128)(2,1)S(1)} %fusion.6.kn_ref, ...), custom_call_target="tpu_custom_call" | custom-call | tf_op jit(solution)/shard_map/attend_bwd/pallas_call | solution.py:291
  282.6 2.3 multiply_add_fusion.1
  284.9 1.4 fusion.28
  286.4 1.9 fusion.11
  289.7 35.7 %back_exchange.1 = (bf16[128,2560]{1,0:T(8,128)(2,1)S(1)}, bf16[128,384]{1,0:T(8,128)(2,1)S(1)}, f32[1,2560]{1,0:T(1,128)S(1)}) custom-call(bf16[480,1024]{1,0:T(8,128)(2,1)S(1)} %copy-done.15, bf16[1024,384]{1,0:T(8,128)(2,1)S(1)} %pad.25.lat, bf16[480,2560]{1,0:T(8,128)(2,1)} %bitcast.114, bf16[288,2560]{1,0:T(8,128)(2,1)} %bitcast.110, ...), custom_call_target="tpu_custom_call" | custom-call | tf_op jit(solution)/shard_map/back_exchange/pallas_call | solution.py:548
  330.4 7.8 %convolution_convert_fusion = bf16[1024,2560]{1,0:T(8,128)(2,1)} fusion(bf16[1024,800]{0,1:T(8,128)(2,1)S(1)} %copy-done.36, bf16[800,2560]{1,0:T(8,128)(2,1)S(1)} %copy-done.31), kind=kOutput, calls=%fused_computation.1 | convolution fusion | flops 4196925440 | bytes 10977280 | tf_op jit(solution)/shard_map/dot_general | solution.py:21
  338.4 10.8 %fusion.33 = f32[800,2560]{1,0:T(8,128)} fusion(bf16[1024,800]{0,1:T(8,128)(2,1)} %get-tuple-element.80, bf16[1024,2560]{1,0:T(8,128)(2,1)} %copy-done.23), kind=kOutput, calls=%fused_computation.128 | convolution fusion | flops 4194304000 | bytes 15073280 | tf_op jit(solution)/shard_map/dot_general | solution.py:21
  349.3 6.6 %fusion.34 = f32[2560,800]{0,1:T(8,128)} fusion(bf16[1024,800]{0,1:T(8,128)(2,1)S(1)} %copy-done.33, bf16[1024,2560]{1,0:T(8,128)(2,1)S(1)} %bitcast.134), kind=kOutput, calls=%fused_computation.129 | convolution fusion | flops 4194304000 | bytes 15073280 | tf_op jit(solution)/shard_map/dot_general | solution.py:21
  355.9 6.6 %fusion.35 = f32[2560,800]{0,1:T(8,128)} fusion(bf16[1024,800]{0,1:T(8,128)(2,1)S(1)} %copy-done.35, bf16[1024,2560]{1,0:T(8,128)(2,1)S(1)} %bitcast.134), kind=kOutput, calls=%fused_computation.130 | convolution fusion | flops 4194304000 | bytes 15073280 | tf_op jit(solution)/shard_map/dot_general | solution.py:21
  363.5 3.6 fusion.32
  367.1 4.6 %fusion.29 = f32[480,2560]{1,0:T(8,128)} fusion(bf16[480,1024]{1,0:T(8,128)(2,1)S(1)} %copy-done.15, bf16[1024,2560]{1,0:T(8,128)(2,1)S(1)} %bitcast.132), kind=kOutput, calls=%fused_computation.124 | convolution fusion | flops 2516582400 | bytes 11141120 | tf_op jit(solution)/shard_map/dot_general | solution.py:21
  374.8 1.9 collective-permute-done.24
  377.7 2.9 collective-permute-done.25
  382.7 1.2 collective-permute-start.20
  384.0 2.0 collective-permute-done.19
  387.2 3.9 collective-permute-done.22
  391.1 3.4 fusion.12
  397.3 1.2 collective-permute-start.14
  398.6 1.4 pad_maximum_fusion.1
  402.3 3.0 collective-permute-done.13
  405.3 1.6 collective-permute-done.14
  407.9 1.2 collective-permute-start.9
  410.2 5.3 %table_grad.1 = (bf16[9181,2560]{1,0:T(8,128)(2,1)}, bf16[8,2560]{1,0:T(8,128)(2,1)S(1)}) custom-call(s32[1]{0:T(128)} %bitcast.2.count_ref, s32[1024]{0:T(1024)S(1)} %select_reduce_fusion.blocks_ref, s32[1,1024]{1,0:T(1,128)S(1)} %bitcast.112, bf16[1024,2560]{1,0:T(8,128)(2,1)S(1)} %constant_dynamic-update-slice_fusion.3.de_ref, ...), custom_call_target="tpu_custom_call", output_to_operand_aliasing={{0}: (4, {})} | custom-call | tf_op jit(solution)/shard_map/table_grad/pallas_call | solution.py:182
  416.1 8.9 %collective-permute-done.9 = bf16[2,128,1280]{2,1,0:T(8,128)(2,1)S(1)} collective-permute-done((bf16[2,128,1280]{2,1,0:T(8,128)(2,1)S(1)}, bf16[2,128,1280]{2,1,0:T(8,128)(2,1)S(1)}, u32[]{:S(2)}, u32[]{:S(2)}) %collective-permute-start.9) | collective-permute-done | bytes 655392 | tf_op jit(solution)/shard_map/ppermute | solution.py:300
  425.3 1.2 collective-permute-start.10
  427.6 7.0 %collective-permute-done.10 = bf16[128,1280]{1,0:T(8,128)(2,1)S(1)} collective-permute-done((bf16[128,1280]{1,0:T(8,128)(2,1)S(1)}, bf16[128,1280]{1,0:T(8,128)(2,1)S(1)}, u32[]{:S(2)}, u32[]{:S(2)}) %collective-permute-start.10) | collective-permute-done | bytes 327712 | tf_op jit(solution)/shard_map/ppermute | solution.py:300
  (230 shorter events, 46.3 us)
Async XLA Ops:
  0.6 86.6 %copy-start = (bf16[256,5,64]{0,2,1:T(8,128)(2,1)S(1)}, bf16[256,5,64]{0,2,1:T(8,128)(2,1)}, u32[]{:S(2)}) copy-start(bf16[256,5,64]{0,2,1:T(8,128)(2,1)} %param.20) | copy-start | bytes 491524
  7.1 9.2 %copy-start.4 = (bf16[2560,288]{0,1:T(8,128)(2,1)S(1)}, bf16[2560,288]{0,1:T(8,128)(2,1)}, u32[]{:S(2)}) copy-start(bf16[2560,288]{0,1:T(8,128)(2,1)} %param.17) | copy-start | bytes 4423684
  16.2 69.2 %copy-start.25 = (f32[2560]{0:T(1024)S(1)}, f32[2560]{0:T(1024)}, u32[]{:S(2)}) copy-start(f32[2560]{0:T(1024)} %param.23) | copy-start | bytes 30724
  16.2 69.4 %copy-start.26 = (f32[256]{0:T(256)S(1)}, f32[256]{0:T(256)}, u32[]{:S(2)}) copy-start(f32[256]{0:T(256)} %param.18) | copy-start | bytes 3076
  77.7 10.4 %copy-start.24 = (bf16[256,5,64]{0,2,1:T(8,128)(2,1)S(1)}, bf16[256,5,64]{0,2,1:T(8,128)(2,1)}, u32[]{:S(2)}) copy-start(bf16[256,5,64]{0,2,1:T(8,128)(2,1)} %param.19) | copy-start | bytes 491524
  77.7 90.5 %collective-permute-start.1 = (bf16[128,2560]{1,0:T(8,128)(2,1)}, bf16[128,2560]{1,0:T(8,128)(2,1)}, u32[]{:S(2)}, u32[]{:S(2)}) collective-permute-start(bf16[128,2560]{1,0:T(8,128)(2,1)} %bitcast.10.dy_ref), channel_id=1, source_target_pairs={{0,4},{1,5},{2,6},{3,7},{4,0},{5,1},{6,2},{7,3}} | collective-permute-start | bytes 1966088 | tf_op jit(solution)/shard_map/ppermute | solution.py:300
  79.0 89.3 %collective-permute-start = (bf16[128,2560]{1,0:T(8,128)(2,1)}, bf16[128,2560]{1,0:T(8,128)(2,1)}, u32[]{:S(2)}, u32[]{:S(2)}) collective-permute-start(bf16[128,2560]{1,0:T(8,128)(2,1)} %bitcast.10.dy_ref), channel_id=1, source_target_pairs={{0,2},{1,3},{2,0},{3,1},{4,6},{5,7},{6,4},{7,5}} | collective-permute-start | bytes 1966088 | tf_op jit(solution)/shard_map/ppermute | solution.py:300
  85.4 14.3 %copy-start.3 = (bf16[5,64,2560]{2,1,0:T(8,128)(2,1)S(1)}, bf16[5,64,2560]{2,1,0:T(8,128)(2,1)}, u32[]{:S(2)}) copy-start(bf16[5,64,2560]{2,1,0:T(8,128)(2,1)} %param.21) | copy-start | bytes 4915204
  99.7 64.1 %copy-start.16 = (bf16[320,1024]{1,0:T(8,128)(2,1)}, bf16[320,1024]{1,0:T(8,128)(2,1)S(1)}, u32[]{:S(2)}) copy-start(bf16[320,1024]{1,0:T(8,128)(2,1)S(1)} %get-tuple-element.76.o_ref) | copy-start | bytes 1966084
  155.6 51.4 %copy-start.11 = (bf16[128,2560]{1,0:T(8,128)(2,1)}, bf16[128,2560]{1,0:T(8,128)(2,1)S(1)}, u32[]{:S(2)}) copy-start(bf16[128,2560]{1,0:T(8,128)(2,1)S(1)} %get-tuple-element.52.h_ref) | copy-start | bytes 1966084
  169.8 14.5 %collective-permute-start.4 = (bf16[384,2560]{1,0:T(8,128)(2,1)S(1)}, bf16[384,2560]{1,0:T(8,128)(2,1)S(1)}, u32[]{:S(2)}, u32[]{:S(2)}) collective-permute-start(bf16[384,2560]{1,0:T(8,128)(2,1)S(1)} %pad_maximum_fusion), channel_id=1, source_target_pairs={{0,1},{1,0},{2,3},{3,2},{4,5},{5,4},{6,7},{7,6}} | collective-permute-start | bytes 5898248 | tf_op jit(solution)/shard_map/ppermute | solution.py:300
  172.8 9.7 %collective-permute-start.2 = (bf16[128,1280]{1,0:T(8,128)(2,1)S(1)}, bf16[128,1280]{1,0:T(8,128)(2,1)S(1)}, u32[]{:S(2)}, u32[]{:S(2)}) collective-permute-start(bf16[128,1280]{1,0:T(8,128)(2,1)S(1)} %slice.95), channel_id=1, source_target_pairs={{0,2},{1,3},{2,0},{3,1},{4,6},{5,7},{6,4},{7,5}} | collective-permute-start | bytes 983048 | tf_op jit(solution)/shard_map/ppermute | solution.py:300
  174.7 9.5 %collective-permute-start.3 = (bf16[128,1280]{1,0:T(8,128)(2,1)S(1)}, bf16[128,1280]{1,0:T(8,128)(2,1)S(1)}, u32[]{:S(2)}, u32[]{:S(2)}) collective-permute-start(bf16[128,1280]{1,0:T(8,128)(2,1)S(1)} %slice.96), channel_id=1, source_target_pairs={{0,4},{1,5},{2,6},{3,7},{4,0},{5,1},{6,2},{7,3}} | collective-permute-start | bytes 983048 | tf_op jit(solution)/shard_map/ppermute | solution.py:300
  178.2 8.2 %copy-start.30 = (bf16[800,2560]{1,0:T(8,128)(2,1)S(1)}, bf16[800,2560]{1,0:T(8,128)(2,1)}, u32[]{:S(2)}) copy-start(bf16[800,2560]{1,0:T(8,128)(2,1)} %param.26) | copy-start | bytes 12288004
  184.2 2.1 collective-permute-start.5
  207.0 58.2 %copy-start.7 = (bf16[480,1024]{1,0:T(8,128)(2,1)S(1)}, bf16[480,1024]{1,0:T(8,128)(2,1)}, u32[]{:S(2)}) copy-start(bf16[480,1024]{1,0:T(8,128)(2,1)} %copy-done.5) | copy-start | bytes 2949124
  265.2 15.4 %copy-start.13 = (f32[128,2560]{1,0:T(8,128)}, f32[128,2560]{1,0:T(8,128)S(1)}, u32[]{:S(2)}) copy-start(f32[128,2560]{1,0:T(8,128)S(1)} %get-tuple-element.63.dres_ref) | copy-start | bytes 3932164
  289.7 40.7 %copy-start.31 = (bf16[800,2560]{1,0:T(8,128)(2,1)S(1)}, bf16[800,2560]{1,0:T(8,128)(2,1)}, u32[]{:S(2)}) copy-start(bf16[800,2560]{1,0:T(8,128)(2,1)} %param.26) | copy-start | bytes 12288004
  289.7 40.7 %copy-start.36 = (bf16[1024,800]{0,1:T(8,128)(2,1)S(1)}, bf16[1024,800]{0,1:T(8,128)(2,1)}, u32[]{:S(2)}) copy-start(bf16[1024,800]{0,1:T(8,128)(2,1)} %get-tuple-element.80) | copy-start | bytes 4915204
  325.5 56.3 %collective-permute-start.18 = (bf16[128,384]{1,0:T(8,128)(2,1)S(1)}, bf16[128,384]{1,0:T(8,128)(2,1)S(1)}, u32[]{:S(2)}, u32[]{:S(2)}) collective-permute-start(bf16[128,384]{1,0:T(8,128)(2,1)S(1)} %get-tuple-element.71), channel_id=1, source_target_pairs={{0,4},{1,5},{2,6},{3,7},{4,0},{5,1},{6,2},{7,3}} | collective-permute-start | bytes 294920 | tf_op jit(solution)/shard_map/ppermute | solution.py:300
  326.4 56.2 %collective-permute-start.17 = (bf16[128,384]{1,0:T(8,128)(2,1)S(1)}, bf16[128,384]{1,0:T(8,128)(2,1)S(1)}, u32[]{:S(2)}, u32[]{:S(2)}) collective-permute-start(bf16[128,384]{1,0:T(8,128)(2,1)S(1)} %get-tuple-element.71), channel_id=1, source_target_pairs={{0,2},{1,3},{2,0},{3,1},{4,6},{5,7},{6,4},{7,5}} | collective-permute-start | bytes 294920 | tf_op jit(solution)/shard_map/ppermute | solution.py:300
  327.5 67.0 %collective-permute-start.12 = (bf16[128,2560]{1,0:T(8,128)(2,1)S(1)}, bf16[128,2560]{1,0:T(8,128)(2,1)}, u32[]{:S(2)}, u32[]{:S(2)}) collective-permute-start(bf16[128,2560]{1,0:T(8,128)(2,1)S(1)} %get-tuple-element.65), channel_id=1, source_target_pairs={{0,4},{1,5},{2,6},{3,7},{4,0},{5,1},{6,2},{7,3}} | collective-permute-start | bytes 1966088 | tf_op jit(solution)/shard_map/ppermute | solution.py:300
  328.4 68.0 %collective-permute-start.11 = (bf16[128,2560]{1,0:T(8,128)(2,1)S(1)}, bf16[128,2560]{1,0:T(8,128)(2,1)}, u32[]{:S(2)}, u32[]{:S(2)}) collective-permute-start(bf16[128,2560]{1,0:T(8,128)(2,1)S(1)} %get-tuple-element.65), channel_id=1, source_target_pairs={{0,2},{1,3},{2,0},{3,1},{4,6},{5,7},{6,4},{7,5}} | collective-permute-start | bytes 1966088 | tf_op jit(solution)/shard_map/ppermute | solution.py:300
  338.3 10.9 %slice-start.6 = ((s8[5242880]{0:T(1024)(128)(4,1)}), s8[4194304]{0:T(1024)(128)(4,1)S(1)}, s32[]{:S(2)}) async-start(s8[5242880]{0:T(1024)(128)(4,1)} %bitcast.133), calls=%async_computation.6 | async-start | bytes 8388608
  338.3 10.9 %slice-start.7 = ((s8[5242880]{0:T(1024)(128)(4,1)}), s8[1048576]{0:T(1024)(128)(4,1)S(1)}, s32[]{:S(2)}) async-start(s8[5242880]{0:T(1024)(128)(4,1)} %bitcast.133), calls=%async_computation.7 | async-start | bytes 2097152
  338.3 10.9 %copy-start.33 = (bf16[1024,800]{0,1:T(8,128)(2,1)S(1)}, bf16[1024,800]{0,1:T(8,128)(2,1)}, u32[]{:S(2)}) copy-start(bf16[1024,800]{0,1:T(8,128)(2,1)} %copy-done.32) | copy-start | bytes 4915204
  338.3 34.5 %collective-permute-start.23 = (f32[5376]{0:T(1024)S(1)}, f32[5376]{0:T(1024)S(1)}, u32[]{:S(2)}, u32[]{:S(2)}) collective-permute-start(f32[5376]{0:T(1024)S(1)} %pad_maximum_fusion.5), channel_id=1, source_target_pairs={{0,1},{1,0},{2,3},{3,2},{4,5},{5,4},{6,7},{7,6}} | collective-permute-start | bytes 64520 | tf_op jit(solution)/shard_map/ppermute | solution.py:300
  349.3 13.2 %slice-start.2 = ((s8[5242880]{0:T(1024)(128)(4,1)}), s8[4194304]{0:T(1024)(128)(4,1)S(1)}, s32[]{:S(2)}) async-start(s8[5242880]{0:T(1024)(128)(4,1)} %bitcast.115), calls=%async_computation.2 | async-start | bytes 8388608
  349.3 13.4 %slice-start.8 = ((s8[5242880]{0:T(1024)(128)(4,1)}), s8[4194304]{0:T(1024)(128)(4,1)S(1)}, s32[]{:S(2)}) async-start(s8[5242880]{0:T(1024)(128)(4,1)} %bitcast.135), calls=%async_computation.8 | async-start | bytes 8388608
  372.8 3.9 collective-permute-start.24
  376.7 3.8 collective-permute-start.25
  381.7 4.3 collective-permute-start.19
  382.7 4.3 collective-permute-start.20
  383.9 3.2 collective-permute-start.21
  386.0 21.0 %collective-permute-start.6 = (bf16[2,2,128,2560]{3,2,1,0:T(8,128)(2,1)S(1)}, bf16[2,2,128,2560]{3,2,1,0:T(8,128)(2,1)S(1)}, u32[]{:S(2)}, u32[]{:S(2)}) collective-permute-start(bf16[2,2,128,2560]{3,2,1,0:T(8,128)(2,1)S(1)} %dynamic-slice_bitcast_fusion), channel_id=1, source_target_pairs={{0,1},{1,0},{2,3},{3,2},{4,5},{5,4},{6,7},{7,6}} | collective-permute-start | bytes 7864328 | tf_op jit(solution)/shard_map/ppermute | solution.py:300
  387.1 4.0 collective-permute-start.22
  391.1 8.9 %slice-start = ((s8[5242880]{0:T(1024)(128)(4,1)}), s8[4194304]{0:T(1024)(128)(4,1)S(1)}, s32[]{:S(2)}) async-start(s8[5242880]{0:T(1024)(128)(4,1)} %bitcast.106), calls=%async_computation | async-start | bytes 8388608
  391.1 8.9 %slice-start.1 = ((s8[5242880]{0:T(1024)(128)(4,1)}), s8[1048576]{0:T(1024)(128)(4,1)S(1)}, s32[]{:S(2)}) async-start(s8[5242880]{0:T(1024)(128)(4,1)} %bitcast.106), calls=%async_computation.1 | async-start | bytes 2097152
  395.5 9.8 %collective-permute-start.13 = (bf16[128,1280]{1,0:T(8,128)(2,1)S(1)}, bf16[128,1280]{1,0:T(8,128)(2,1)S(1)}, u32[]{:S(2)}, u32[]{:S(2)}) collective-permute-start(bf16[128,1280]{1,0:T(8,128)(2,1)S(1)} %slice.102), channel_id=1, source_target_pairs={{0,2},{1,3},{2,0},{3,1},{4,6},{5,7},{6,4},{7,5}} | collective-permute-start | bytes 983048 | tf_op jit(solution)/shard_map/ppermute | solution.py:300
  397.3 9.5 %collective-permute-start.14 = (bf16[128,1280]{1,0:T(8,128)(2,1)S(1)}, bf16[128,1280]{1,0:T(8,128)(2,1)S(1)}, u32[]{:S(2)}, u32[]{:S(2)}) collective-permute-start(bf16[128,1280]{1,0:T(8,128)(2,1)S(1)} %slice.103), channel_id=1, source_target_pairs={{0,4},{1,5},{2,6},{3,7},{4,0},{5,1},{6,2},{7,3}} | collective-permute-start | bytes 983048 | tf_op jit(solution)/shard_map/ppermute | solution.py:300
  400.0 10.1 %collective-permute-start.15 = (bf16[384,2560]{1,0:T(8,128)(2,1)S(1)}, bf16[384,2560]{1,0:T(8,128)(2,1)S(1)}, u32[]{:S(2)}, u32[]{:S(2)}) collective-permute-start(bf16[384,2560]{1,0:T(8,128)(2,1)S(1)} %pad_maximum_fusion.1), channel_id=1, source_target_pairs={{0,1},{1,0},{2,3},{3,2},{4,5},{5,4},{6,7},{7,6}} | collective-permute-start | bytes 5898248 | tf_op jit(solution)/shard_map/ppermute | solution.py:300
  406.9 3.3 collective-permute-start.16
  407.9 17.1 %collective-permute-start.9 = (bf16[2,128,1280]{2,1,0:T(8,128)(2,1)S(1)}, bf16[2,128,1280]{2,1,0:T(8,128)(2,1)S(1)}, u32[]{:S(2)}, u32[]{:S(2)}) collective-permute-start(bf16[2,128,1280]{2,1,0:T(8,128)(2,1)S(1)} %dynamic-slice_bitcast_fusion.1), channel_id=1, source_target_pairs={{0,4},{1,5},{2,6},{3,7},{4,0},{5,1},{6,2},{7,3}} | collective-permute-start | bytes 1966088 | tf_op jit(solution)/shard_map/ppermute | solution.py:300
  409.2 17.3 %collective-permute-start.7 = (bf16[2,128,1280]{2,1,0:T(8,128)(2,1)S(1)}, bf16[2,128,1280]{2,1,0:T(8,128)(2,1)S(1)}, u32[]{:S(2)}, u32[]{:S(2)}) collective-permute-start(bf16[2,128,1280]{2,1,0:T(8,128)(2,1)S(1)} %dynamic-slice_bitcast_fusion.2), channel_id=1, source_target_pairs={{0,2},{1,3},{2,0},{3,1},{4,6},{5,7},{6,4},{7,5}} | collective-permute-start | bytes 1966088 | tf_op jit(solution)/shard_map/ppermute | solution.py:300
  415.5 20.3 %copy-start.12 = (bf16[128,2560]{1,0:T(8,128)(2,1)S(1)}, bf16[128,2560]{1,0:T(8,128)(2,1)}, u32[]{:S(2)}) copy-start(bf16[128,2560]{1,0:T(8,128)(2,1)} %copy-done.11) | copy-start | bytes 1966084
  425.1 11.7 %copy-start.1 = (bf16[256,5,64]{0,2,1:T(8,128)(2,1)S(1)}, bf16[256,5,64]{0,2,1:T(8,128)(2,1)}, u32[]{:S(2)}) copy-start(bf16[256,5,64]{0,2,1:T(8,128)(2,1)} %param.20) | copy-start | bytes 491524
  425.3 9.3 %collective-permute-start.10 = (bf16[128,1280]{1,0:T(8,128)(2,1)S(1)}, bf16[128,1280]{1,0:T(8,128)(2,1)S(1)}, u32[]{:S(2)}, u32[]{:S(2)}) collective-permute-start(bf16[128,1280]{1,0:T(8,128)(2,1)S(1)} %dynamic-slice_bitcast_fusion.3), channel_id=1, source_target_pairs={{0,2},{1,3},{2,0},{3,1},{4,6},{5,7},{6,4},{7,5}} | collective-permute-start | bytes 983048 | tf_op jit(solution)/shard_map/ppermute | solution.py:300
  426.7 9.0 %collective-permute-start.8 = (bf16[128,1280]{1,0:T(8,128)(2,1)S(1)}, bf16[128,1280]{1,0:T(8,128)(2,1)S(1)}, u32[]{:S(2)}, u32[]{:S(2)}) collective-permute-start(bf16[128,1280]{1,0:T(8,128)(2,1)S(1)} %dynamic-slice_bitcast_fusion.4), channel_id=1, source_target_pairs={{0,4},{1,5},{2,6},{3,7},{4,0},{5,1},{6,2},{7,3}} | collective-permute-start | bytes 983048 | tf_op jit(solution)/shard_map/ppermute | solution.py:300
  (25 other events, 98.9 us)

commit v4 on v3

--- a/solution.py
+++ b/solution.py
@@ -33,6 +33,10 @@
     return mm(a, b, 0, 0)
 
 
+mean_last = functools.partial(jnp.mean, axis=-1, keepdims=True)
+sum_rows = functools.partial(jnp.sum, axis=0, keepdims=True)
+
+
 def rope_tables(seq_len, rope_dim):
     inv_freq = ROPE_BASE ** (-jnp.arange(0, rope_dim, 2, dtype=F32) / rope_dim)
     angles = jnp.arange(seq_len, dtype=F32)[:, None] * inv_freq[None, :]
@@ -46,7 +50,7 @@
 
 
 def rms_norm(x_in, gain):
-    inv_rms = lax.rsqrt(jnp.mean(x_in * x_in, axis=-1, keepdims=True) + EPSILON)
+    inv_rms = lax.rsqrt(mean_last(x_in * x_in) + EPSILON)
     return (x_in * inv_rms * gain).astype(BF16)
 
 
@@ -213,7 +217,7 @@
         s = [scores_of(k_all, q_all, ki, qi, scale) for ki in range(qi + 1)]
         top = functools.reduce(jnp.maximum, [jnp.max(x, axis=0, keepdims=True) for x in s])
         p = [jnp.exp2(x - top) for x in s]
-        total = sum(jnp.sum(x, axis=0, keepdims=True) for x in p)
+        total = sum(sum_rows(x) for x in p)
         inv = 1.0 / total
         o = sum(nn(v_ref[:, ki * QB:(ki + 1) * QB], (x * inv).astype(BF16)) for ki, x in enumerate(p))
         o_ref[:, lanes] = o.astype(BF16)
@@ -241,7 +245,7 @@
         q_b, do_b, lse = q_all[:, lanes], do_ref[:, lanes], lse_ref[0, :, lanes]
         p = [jnp.exp2(scores_of(k_all, q_all, ki, qi, raw * LOG2E) - lse) for ki in range(qi + 1)]
         dp = [tn(v_ref[:, ki * QB:(ki + 1) * QB], do_b) for ki in range(qi + 1)]
-        delta = sum(jnp.sum(a * b, axis=0, keepdims=True) for a, b in zip(p, dp))
+        delta = sum(sum_rows(a * b) for a, b in zip(p, dp))
         dq = None
         for ki in range(qi + 1):
             keys = slice(ki * QB, (ki + 1) * QB)
@@ -275,16 +279,6 @@
     return [per(qd), per(nope), one(rope), per(vd), one(rope // 2), one(rope // 2)], per, one, pl.BlockSpec((1, 1, seq), lambda h: (h, 0, 0))
 
 
-def attend_fwd(q, kn, kp, v, cos_t, sin_t, heads):
-    seq, qd, nope, vd, rope = q.shape[1], q.shape[0] // heads, kn.shape[0] // heads, v.shape[0] // heads, kp.shape[0]
-    ins, per, one, lse = attn_specs(heads, qd, nope, rope, vd, seq)
-    return pl.pallas_call(
-        attn_fwd_body, grid=(heads,), in_specs=ins, out_specs=[per(vd), lse],
-        out_shape=[jax.ShapeDtypeStruct((heads * vd, seq), BF16), jax.ShapeDtypeStruct((heads, 1, seq), F32)],
-        compiler_params=pltpu.CompilerParams(vmem_limit_bytes=40 << 20), name='attend_fwd',
-    )(q, kn, kp, v, cos_t, sin_t)
-
-
 def attend_bwd(q, kn, kp, v, cos_t, sin_t, lse, do, heads, table):
     seq, qd, nope, vd, rope = q.shape[1], q.shape[0] // heads, kn.shape[0] // heads, v.shape[0] // heads, kp.shape[0]
     ins, per, one, lse_spec = attn_specs(heads, qd, nope, rope, vd, seq)
@@ -468,7 +462,7 @@
         self.relay()
         self.land(accs)
 
-    def all_gather(self, fulls, scratch, arrive):
+    def all_gather(self, fulls, scratch, arrive, slow=False):
         os_, xr, fs, fr, ps, pr = scratch
         half0 = [i for i in self.order if self.pieces[i][0] == 0]
         half1 = [i for i in self.order if self.pieces[i][0] == 1]
@@ -508,13 +502,17 @@
             give[2][i1].start()
             from_n[0][i0].wait_recv()
             give[1][i0].start()
+        def diagonal():
+            for i in self.order:
+                diag[i].wait_recv()
+                give[3][i].start()
+
         for j in (1, 2):
             for cp in take[j]:
                 cp.wait_recv()
             arrive(j)
-        for i in self.order:
-            diag[i].wait_recv()
-            give[3][i].start()
+            if slow == (j == 1):
+                diagonal()
         for cp in take[3]:
             cp.wait_recv()
         arrive(3)
@@ -529,25 +527,26 @@
 
 MAIN = halves(2560, 2)
 LAST = MAIN + [(0, 1, 0, 256), (1, 1, 256, 128)]
-NRS = 11
+NRS, NAG = 11, 6
+COLS = 512
 
 
 def norm_rows(x, gain):
-    return x * lax.rsqrt(jnp.mean(x * x, axis=-1, keepdims=True) + EPSILON) * gain
+    return x * lax.rsqrt(mean_last(x * x) + EPSILON) * gain
 
 
 def norm_rows_vjp(x, gain, dy):
-    r = lax.rsqrt(jnp.mean(x * x, axis=-1, keepdims=True) + EPSILON)
+    r = lax.rsqrt(mean_last(x * x) + EPSILON)
     gd = dy * gain
-    dot = jnp.mean(gd * x, axis=-1, keepdims=True)
-    return r * gd - x * (r * r * r * dot), jnp.sum(dy * x * r, axis=0, keepdims=True)
-
-
-def exchange_call(body, name, cid, ins, out_shape, scratch):
-    vmem = pl.BlockSpec(memory_space=VM)
+    dot = mean_last(gd * x)
+    return r * gd - x * (r * r * r * dot), sum_rows(dy * x * r)
+
+
+def exchange_call(body, name, cid, ins, out_shape, scratch, far=0, limit=50):
+    vmem, hbm = pl.BlockSpec(memory_space=VM), pl.BlockSpec(memory_space=pltpu.HBM)
     return pl.pallas_call(
-        body, out_shape=out_shape, in_specs=[vmem] * len(ins), out_specs=[vmem] * len(out_shape), scratch_shapes=scratch,
-        compiler_params=pltpu.CompilerParams(vmem_limit_bytes=50 << 20, collective_id=cid, has_side_effects=True), name=name)(*ins)
+        body, out_shape=out_shape, in_specs=[vmem] * (len(ins) - far) + [hbm] * far, out_specs=[vmem] * len(out_shape), scratch_shapes=scratch,
+        compiler_params=pltpu.CompilerParams(vmem_limit_bytes=limit << 20, collective_id=cid, has_side_effects=True), name=name)(*ins)
 
 
 def shape(dims, dtype):
@@ -577,39 +576,94 @@
     ex.drain()
 
 
-def attn_out_body(o_ref, wo, e_ref, gain, h_ref, full, part, acc, *scratch):
+def attn_body(lat, g_kv, wuk, wuv, q_ref, cos_ref, sin_ref, dy_ref, c_ref, kn_ref, kp_ref, v_ref, o_ref, lse_ref, dyf, *scratch):
+    ex = Exchange([dyf.shape[1]], MAIN)
+    ex.place(dy_ref.shape[0])
+    ex.enter()
+    dyf[ex.mine[0], :] = dy_ref[...]
+    lora, half, heads = c_ref.shape[1], cos_ref.shape[0], lse_ref.shape[0]
+    per = lambda ref, h: ref.at[pl.ds(h * (ref.shape[0] // heads), ref.shape[0] // heads), :]
+
+    def arrive(j):
+        if j:
+            return
+        c = norm_rows(lat[:, :lora], g_kv[...]).astype(BF16)
+        c_ref[...] = c
+        pe = lat[:, lora:].T
+        lo, hi, cos_t, sin_t = pe[:half], pe[half:], cos_ref[...], sin_ref[...]
+        kp_ref[...] = jnp.concatenate([lo * cos_t - hi * sin_t, hi * cos_t + lo * sin_t], axis=0).astype(BF16)
+        kn_ref[...] = nt(wuk[...], c).astype(BF16)
+        v_ref[...] = nt(wuv[...], c).astype(BF16)
+        for h in range(heads):
+            attn_fwd_body(per(q_ref, h), per(kn_ref, h), kp_ref, per(v_ref, h), cos_ref, sin_ref, per(o_ref, h), lse_ref.at[pl.ds(h, 1)])
+
+    ex.all_gather([dyf], scratch, arrive)
+
+
+def middle_body(o_ref, wo, e_ref, gain, dyl_ref, dy_hbm, wg_hbm, wu_hbm, wd_hbm,
+                h_ref, z, y_ref, hid_ref, dgate_ref, dup_ref, dres_ref, dgain_ref, dfull, do_ref,
+                wg, wu, wd, dyb, part, acc, wsem, dsem, *scratch):
     ex = Exchange([part.shape[1]], MAIN)
     ex.place(acc.shape[0])
     ex.enter()
+    loads = [pltpu.make_async_copy(a, b, wsem.at[k]) for k, (a, b) in enumerate(((wg_hbm, wg), (wu_hbm, wu), (wd_hbm, wd)))]
+    dy_in = [pltpu.make_async_copy(dy_hbm.at[ex.chip[j], :], dyb.at[j % 2], dsem.at[j % 2]) for j in range(4)]
+    for cp in loads + dy_in[:2]:
+        cp.start()
     ex.rs_begin([part], scratch)
-
-    def produce(j):
+    width = part.shape[1]
+
+    def attn_part(j):
         part[ex.chip[j], :] = tn(o_ref[:, ex.chip[j]], wo[...]).astype(BF16)
 
-    ex.reduce_scatter([acc], produce)
+    ex.reduce_scatter([acc], attn_part)
     h = (e_ref[...].astype(F32) + acc[...].astype(BF16).astype(F32)).astype(BF16)
     h_ref[...] = h
-    full[ex.mine[0], :] = norm_rows(h.astype(F32), gain[...]).astype(BF16)
-    ex.all_gather([full], scratch[NRS:], idle)
-    ex.drain()
-
-
-def mlp_back_body(part, h_ref, dy_ref, gain, wo, dres_ref, dg_ref, full, do_ref, acc, *scratch):
-    ex = Exchange([part.shape[1]], MAIN)
-    ex.place(acc.shape[0])
-    ex.enter()
-    ex.rs_begin([part], scratch)
-    ex.reduce_scatter([acc], idle)
-    dx, dg = norm_rows_vjp(h_ref[...].astype(F32), gain[...], acc[...])
-    dg_ref[...] = dg
-    dres = dy_ref[...].astype(F32) + dx
+    z[ex.mine[0], :] = norm_rows(h.astype(F32), gain[...]).astype(BF16)
+
+    def mlp(j):
+        rows = ex.chip[j]
+        gate, up = nt(z[rows, :], wg[...]), nt(z[rows, :], wu[...])
+        sig = jax.nn.sigmoid(gate)
+        hid = (gate * sig * up).astype(BF16)
+        hid_ref[rows, :] = hid
+        dh = nt(dyb[j % 2], wd[...])
+        dup = (dh * gate * sig).astype(BF16)
+        dgate = (dh * up * sig * (1.0 + gate * (1.0 - sig))).astype(BF16)
+        dup_ref[rows, :] = dup
+        dgate_ref[rows, :] = dgate
+        for c in range(0, width, COLS):
+            part[rows, c:c + COLS] = (nn(dgate, wg[:, c:c + COLS]) + nn(dup, wu[:, c:c + COLS])).astype(BF16)
+            y_ref[rows, c:c + COLS] = nn(hid, wd[:, c:c + COLS]).astype(BF16)
+
+    def arrive_z(j):
+        if j == 0:
+            ex.drain()
+            for cp in loads:
+                cp.wait()
+        dy_in[j].wait()
+        mlp(j)
+        if j < 2:
+            dy_in[j + 2].start()
+        ex.ready(j)
+        if j == 2:
+            ex.push(1)
+        if j == 3:
+            ex.push(2)
+            ex.push(3)
+
+    ex.all_gather([z], scratch[NRS:NRS + NAG], arrive_z, slow=True)
+    ex.relay()
+    ex.land([acc])
+    dx, dgain_ref[...] = norm_rows_vjp(h_ref[...].astype(F32), gain[...], acc[...])
+    dres = dyl_ref[...].astype(F32) + dx
     dres_ref[...] = dres
-    full[ex.mine[0], :] = dres.astype(BF16)
-
-    def arrive(j):
-        do_ref[:, ex.chip[j]] = nt(wo[...], full[ex.chip[j], :]).astype(BF16)
-
-    ex.all_gather([full], scratch[NRS:], arrive)
+    dfull[ex.mine[0], :] = dres.astype(BF16)
+
+    def arrive_d(j):
+        do_ref[:, ex.chip[j]] = nt(wo[...], dfull[ex.chip[j], :]).astype(BF16)
+
+    ex.all_gather([dfull], scratch[NRS + NAG:], arrive_d)
     ex.drain()
 
 
@@ -644,29 +698,22 @@
     ga, gm = g_attn[None, :], g_mlp[None, :]
     embedded, x_attn, query, latent = exchange_call(
         embed_body, 'embed_exchange', 1, [rows, ga, w_q, w_dkv], [loc, fullb, shape((w_q.shape[0], seq), BF16), shape((seq, latw), F32)], main)
-    d_out_late, latent = lax.optimization_barrier((d_out, latent))
-    dy_full = from_hop_order(gather_hops(d_out_late))
     cos_t, sin_t = (t.T for t in rope_tables(seq, latw - lora))
-    (c_kv, k_pe), kv_pull = jax.vjp(kv_prep, latent, g_kv)
-    k_nope = nt(w_uk, c_kv).astype(BF16)
-    value = nt(w_uv, c_kv).astype(BF16)
-    k_pe_t = k_pe.T
-    attn_out, lse = attend_fwd(query, k_nope, k_pe_t, value, cos_t, sin_t, heads)
-    residual, x_mlp = exchange_call(attn_out_body, 'attn_exchange', 2, [attn_out, w_o, embedded, gm], [loc, fullb], partb + main)
-    gate = nt(x_mlp, w_gate)
-    up_proj = nt(x_mlp, w_up)
-    gate_sig = jax.nn.sigmoid(gate)
-    hidden = (gate * gate_sig * up_proj).astype(BF16)
-
-    d_hidden = nt(dy_full, w_down)
-    d_up = (d_hidden * gate * gate_sig).astype(BF16)
-    d_gate = (d_hidden * up_proj * gate_sig * (1.0 + gate * (1.0 - gate_sig))).astype(BF16)
-    dx_part = (nn(d_gate, w_gate) + nn(d_up, w_up)).astype(BF16)
-    d_residual, dg_mlp, d_attn_full, d_attn_out = exchange_call(
-        mlp_back_body, 'mlp_exchange', 3, [dx_part, residual, d_out, gm, w_o],
-        [shape((local, width), F32), shape((1, width), F32), fullb, shape((w_o.shape[0], seq), BF16)], main)
-    hidden_late, d_attn_full = lax.optimization_barrier((hidden, d_attn_full))
-    mlp_loc = scatter_hops(nn(hidden_late, w_down).astype(BF16), local)
+    nq, nk, nv = w_q.shape[0], w_uk.shape[0], w_uv.shape[0]
+    c_kv, k_nope, k_pe_t, value, attn_out, lse, dy_full = exchange_call(
+        attn_body, 'attend_fwd', 2, [latent, g_kv[None, :], w_uk, w_uv, query, cos_t, sin_t, d_out],
+        [shape((seq, lora), BF16), shape((nk, seq), BF16), shape((latw - lora, seq), BF16), shape((nv, seq), BF16), shape((nv, seq), BF16),
+         shape((heads, 1, seq), F32), fullb], one.ag_scratch())
+    kv_pull = jax.vjp(kv_prep, latent, g_kv)[1]
+    ffn = w_gate.shape[0]
+    dma = pltpu.SemaphoreType.DMA
+    act, wide = shape((seq, ffn), BF16), VM((ffn, width), BF16)
+    residual, x_mlp, y_part, hidden, d_gate, d_up, d_residual, dg_mlp, d_attn_full, d_attn_out = exchange_call(
+        middle_body, 'middle', 3, [attn_out, w_o, embedded, gm, d_out, dy_full, w_gate, w_up, w_down],
+        [loc, fullb, fullb, act, act, act, shape((local, width), F32), shape((1, width), F32), fullb, shape((w_o.shape[0], seq), BF16)],
+        [wide, wide, wide, VM((2, seq // 4, width), BF16)] + partb + [VM((local, width), F32), dma((3,)), dma((2,))] + one.rs_scratch(local) + one.ag_scratch() + one.ag_scratch(),
+        far=4, limit=63)
+    mlp_loc = scatter_hops(y_part, local)
     layer_out = (residual.astype(F32) + mlp_loc.astype(BF16).astype(F32)).astype(BF16)
     d_query, d_knope, d_value, d_kpe, table0 = attend_bwd(query, k_nope, k_pe_t, value, cos_t, sin_t, lse, d_attn_out, heads, (vocab, width))
     d_ckv = (tn(d_knope, w_uk) + tn(d_value, w_uv)).astype(BF16)

time: 443 us -> 443 us (level)
  Pallas kernels: 246 us -> 285 us
  matrix products: 82.6 us -> 46.8 us
  local copies, waits for them, and re-layouts: 27.1 us -> 41.3 us
  waiting for transfers between devices: 41 us -> 29.5 us
    pallas_call x5 -> x4, Pallas kernels: 218 us -> 258 us  [exchange_call(): pl.pallas_call(body, out_shape=out_shape, in_specs=[vmem] * (len(ins) - f...]
    dot_general x18 -> x10, matrix products: 82.6 us -> 46.8 us  [mm(): lax.dot_general(lhs, rhs, (((lc,), (rc,)), ((), ())), preferred_element_t...]
    ppermute x26 -> x20, waiting for transfers between devices: 41 us -> 29.5 us  [shift(): return lax.ppermute(x, 'tp', [(d, d ^ bit) for d in range(8)])]
    unnamed x108 -> x129, local copies, waits for them, and re-layouts: 13.6 us -> 21.2 us
    ppermute x26 -> x20, starting transfers between devices: 18.9 us -> 14.8 us  [shift(): return lax.ppermute(x, 'tp', [(d, d ^ bit) for d in range(8)])]
  transfers between devices with their start and end apart: 26 -> 20, of which waited for: 13 -> 8; matrix products, arithmetic and copies ran while one was open for 19% -> 16% of each run, Pallas kernels for 16% -> 1%
where the time goes in v4:
time: 443 us; the launch traced here: 437 us
  Pallas kernels  285 us (64%)
  matrix products  46.8 us (11%)
  local copies, waits for them, and re-layouts  41.3 us (9%)
  waiting for transfers between devices  29.5 us (7%)
  other arithmetic  17 us (4%)
  starting transfers between devices  14.8 us (3%)
    pallas_call x4, Pallas kernels, exchange_call(): pl.pallas_call(body, out_shape=out_shape, in_specs=[vmem] * (len(ins) - f...  258 us
    dot_general x10, matrix products, mm(): lax.dot_general(lhs, rhs, (((lc,), (rc,)), ((), ())), preferred_element_t...  46.8 us
    ppermute x20, waiting for transfers between devices, shift(): return lax.ppermute(x, 'tp', [(d, d ^ bit) for d in range(8)])  29.5 us
    unnamed x129, local copies, waits for them, and re-layouts  21.2 us
    pallas_call x1, Pallas kernels, attend_bwd(): pl.pallas_call(attn_bwd_body, grid=(heads,), in_specs=ins + [lse_spec, pe...  15.3 us
    ppermute x20, starting transfers between devices, shift(): return lax.ppermute(x, 'tp', [(d, d ^ bit) for d in range(8)])  14.8 us
  transfers between devices with their start and end apart: 20, of which 8 were waited for; matrix products, arithmetic and copies ran while one was open for 16% of the time, Pallas kernels for 1%

profile of v4, /device:TPU:0, one launch (start us, length us, event | category | flops | bytes accessed | tf_op | source)
XLA Modules:
  0.0 436.7 jit_solution(11158408113985907980)
XLA Ops:
  1.4 1.3 broadcast_in_dim.76.gain
  6.0 1.3 add_select_fusion.1
  9.3 6.6 %gather_rows.1.part = bf16[1024,2560]{1,0:T(8,128)(2,1)S(1)} custom-call(s32[1]{0:T(128)} %bitcast.2.count_ref, s32[1024]{0:T(1024)S(1)} %select_reduce_fusion.blocks_ref, s32[1024,1]{1,0:T(8,128)S(1)} %add_select_fusion.key_ref, bf16[8,2560]{1,0:T(8,128)(2,1)S(1)} %pad.20.tail_ref, bf16[9181,2560]{1,0:T(8,128)(2,1)} %table_ref.1), custom_call_target="tpu_custom_call" | custom-call | tf_op jit(solution)/shard_map/gather_rows/pallas_call | solution.py:131
  16.0 2.3 copy-done
  18.3 60.6 %embed_exchange.1 = (bf16[128,2560]{1,0:T(8,128)(2,1)S(1)}, bf16[1024,2560]{1,0:T(8,128)(2,1)}, bf16[480,1024]{1,0:T(8,128)(2,1)S(1)}, f32[1024,288]{1,0:T(8,128)}) custom-call(bf16[1024,2560]{1,0:T(8,128)(2,1)} %copy-done, f32[1,2560]{1,0:T(1,128)S(1)} %broadcast_in_dim.74.gain, bf16[480,2560]{1,0:T(8,128)(2,1)} %bitcast.97, bf16[288,2560]{1,0:T(8,128)(2,1)S(1)} %bitcast.88), custom_call_target="tpu_custom_call" | custom-call | tf_op jit(solution)/shard_map/embed_exchange/pallas_call | solution.py:547
  80.7 1.4 multiply_reduce_fusion
  82.8 30.6 %attend_fwd.1 = (bf16[1024,256]{1,0:T(8,128)(2,1)S(1)}, bf16[320,1024]{1,0:T(8,128)(2,1)S(1)}, bf16[32,1024]{1,0:T(8,128)(2,1)S(1)}, bf16[320,1024]{1,0:T(8,128)...) custom-call(f32[1024,288]{1,0:T(8,128)} %get-tuple-element.52.lat, ...), custom_call_target="tpu_custom_call" | custom-call | tf_op jit(solution)/shard_map/attend_fwd/pallas_call | solution.py:547
  117.9 131.5 %middle.1 = (bf16[128,2560]{1,0:T(8,128)(2,1)}, bf16[1024,2560]{1,0:T(8,128)(2,1)}, bf16[1024,2560]{1,0:T(8,128)(2,1)}, bf16[1024,800]{1,0:T(8,128)(2,1)}, bf16[...) custom-call(bf16[320,1024]{1,0:T(8,128)(2,1)} %copy-done.11, ...), custom_call_target="tpu_custom_call" | custom-call | tf_op jit(solution)/shard_map/middle/pallas_call | solution.py:547
  249.4 1.1 copy-done.16
  250.5 1.1 copy-done.18
  251.6 1.1 copy-done.19
  255.9 15.3 %attend_bwd.1 = (bf16[480,1024]{1,0:T(8,128)(2,1)S(1)}, bf16[320,1024]{1,0:T(8,128)(2,1)S(1)}, bf16[320,1024]{1,0:T(8,128)(2,1)S(1)}, f32[32,1024]{1,0:T(8,128)S(1)}, bf16[9181,2560]{1,0:T(8,128)(2,1)}) custom-call(bf16[480,1024]{1,0:T(8,128)(2,1)S(1)} %copy-done.3, bf16[320,1024]{1,0:T(8,128)(2,1)S(1)} %copy-done.16, bf16[32,1024]{1,0:T(8,128)(2,1)S(1)} %copy-done.31, ...), custom_call_target="tpu_custom_call" | custom-call | tf_op jit(solution)/shard_map/attend_bwd/pallas_call | solution.py:285
  272.5 3.1 multiply_add_fusion.1
  276.1 1.9 fusion.9
  279.5 35.7 %back_exchange.1 = (bf16[128,2560]{1,0:T(8,128)(2,1)S(1)}, bf16[128,384]{1,0:T(8,128)(2,1)}, f32[1,2560]{1,0:T(1,128)S(1)}) custom-call(bf16[480,1024]{1,0:T(8,128)(2,1)S(1)} %copy-done.10, bf16[1024,384]{1,0:T(8,128)(2,1)S(1)} %pad.25.lat, bf16[480,2560]{1,0:T(8,128)(2,1)} %bitcast.98, bf16[288,2560]{1,0:T(8,128)(2,1)} %bitcast.87, ...), custom_call_target="tpu_custom_call" | custom-call | tf_op jit(solution)/shard_map/back_exchange/pallas_call | solution.py:547
  316.1 1.1 collective-permute-start.11
  318.1 1.1 collective-permute-start.5
  320.4 1.1 fusion.25
  321.5 1.1 fusion.26
  322.5 11.6 %fusion.30 = f32[800,2560]{1,0:T(8,128)} fusion(bf16[1024,800]{1,0:T(8,128)(2,1)} %get-tuple-element.90, bf16[1024,2560]{1,0:T(8,128)(2,1)} %get-tuple-element.56.dy_hbm), kind=kOutput, calls=%fused_computation.102 | convolution fusion | flops 4194304000 | bytes 15073280 | tf_op jit(solution)/shard_map/dot_general | solution.py:21
  334.2 6.8 %fusion.28 = f32[2560,800]{0,1:T(8,128)} fusion(bf16[1024,2560]{1,0:T(8,128)(2,1)S(1)} %bitcast.119, bf16[1024,800]{1,0:T(8,128)(2,1)S(1)} %copy-done.49), kind=kOutput, calls=%fused_computation.100 | convolution fusion | flops 4194304000 | bytes 15073280 | tf_op jit(solution)/shard_map/dot_general | solution.py:21
  341.0 6.8 %fusion.29 = f32[2560,800]{0,1:T(8,128)} fusion(bf16[1024,2560]{1,0:T(8,128)(2,1)S(1)} %bitcast.119, bf16[1024,800]{1,0:T(8,128)(2,1)S(1)} %copy-done.48), kind=kOutput, calls=%fused_computation.101 | convolution fusion | flops 4194304000 | bytes 15073280 | tf_op jit(solution)/shard_map/dot_general | solution.py:21
  347.9 1.0 constant_dynamic-update-slice_fusion.16
  349.7 3.5 dynamic-slice_bitcast_fusion
  353.2 6.2 %fusion.27 = f32[320,2560]{1,0:T(8,128)} fusion(bf16[320,1024]{1,0:T(8,128)(2,1)S(1)} %copy-done.12, bf16[1024,2560]{1,0:T(8,128)(2,1)} %get-tuple-element.86), kind=kOutput, calls=%fused_computation.99 | convolution fusion | flops 1677721600 | bytes 9175040 | tf_op jit(solution)/shard_map/dot_general | solution.py:21
  359.4 4.5 %fusion.24 = f32[480,2560]{1,0:T(8,128)} fusion(bf16[480,1024]{1,0:T(8,128)(2,1)S(1)} %copy-done.10, bf16[1024,2560]{1,0:T(8,128)(2,1)S(1)} %bitcast.117), kind=kOutput, calls=%fused_computation.96 | convolution fusion | flops 2516582400 | bytes 11141120 | tf_op jit(solution)/shard_map/dot_general | solution.py:21
  365.8 2.8 collective-permute-done.18
  369.6 2.8 collective-permute-done.19
  376.3 1.1 collective-permute-start.14
  377.5 1.0 pad_maximum_fusion.2
  378.5 1.5 constant_dynamic-update-slice_fusion.15
  380.1 1.5 constant_dynamic-update-slice_fusion.14
  384.8 2.0 collective-permute-done.16
  387.4 6.4 %fusion.10 = f32[2560,288]{0,1:T(8,128)} fusion(bf16[1024,2560]{1,0:T(8,128)(2,1)} %get-tuple-element.78, bf16[1024,384]{1,0:T(8,128)(2,1)} %constant_dynamic-update-slice_fusion.17), kind=kOutput, calls=%fused_computation.27 | convolution fusion | flops 1509949440 | bytes 8978432 | tf_op jit(solution)/shard_map/dot_general | solution.py:21
  393.8 1.1 slice.66
  395.9 1.0 slice.67
  396.9 1.2 collective-permute-start.8
  398.0 1.4 pad_maximum_fusion
  399.5 1.1 constant_dynamic-update-slice_fusion.5
  400.6 1.1 constant_dynamic-update-slice_fusion.4
  401.8 3.2 collective-permute-done.7
  404.9 1.7 collective-permute-done.8
  407.8 1.1 collective-permute-start.3
  410.1 5.2 %table_grad.1 = (bf16[9181,2560]{1,0:T(8,128)(2,1)}, bf16[8,2560]{1,0:T(8,128)(2,1)S(1)}) custom-call(s32[1]{0:T(128)} %bitcast.2.count_ref, s32[1024]{0:T(1024)S(1)} %copy-done.35, s32[1,1024]{1,0:T(1,128)S(1)} %bitcast.95, bf16[1024,2560]{1,0:T(8,128)(2,1)S(1)} %constant_dynamic-update-slice_fusion.1.de_ref, ...), custom_call_target="tpu_custom_call", output_to_operand_aliasing={{0}: (4, {})} | custom-call | tf_op jit(solution)/shard_map/table_grad/pallas_call | solution.py:186
  415.9 9.0 %collective-permute-done.3 = bf16[2,128,1280]{2,1,0:T(8,128)(2,1)S(1)} collective-permute-done((bf16[2,128,1280]{2,1,0:T(8,128)(2,1)S(1)}, bf16[2,128,1280]{2,1,0:T(8,128)(2,1)S(1)}, u32[]{:S(2)}, u32[]{:S(2)}) %collective-permute-start.3) | collective-permute-done | bytes 655392 | tf_op jit(solution)/shard_map/ppermute | solution.py:294
  425.1 1.1 collective-permute-start.4
  427.4 7.0 %collective-permute-done.4 = bf16[128,1280]{1,0:T(8,128)(2,1)S(1)} collective-permute-done((bf16[128,1280]{1,0:T(8,128)(2,1)S(1)}, bf16[128,1280]{1,0:T(8,128)(2,1)S(1)}, u32[]{:S(2)}, u32[]{:S(2)}) %collective-permute-start.4) | collective-permute-done | bytes 327712 | tf_op jit(solution)/shard_map/ppermute | solution.py:294
  435.6 1.0 fusion.12
  (211 shorter events, 39.8 us)
Async XLA Ops:
  0.7 8.3 %copy-start.47 = (f32[16]{0:T(128)}, f32[16]{0:T(128)S(1)}, u32[]{:S(2)}) copy-start(f32[16]{0:T(128)S(1)} %multiply_power_fusion) | copy-start | bytes 196
  1.4 16.9 %copy-start.28 = (f32[1,2560]{1,0:T(1,128)}, f32[1,2560]{1,0:T(1,128)S(1)}, u32[]{:S(2)}) copy-start(f32[1,2560]{1,0:T(1,128)S(1)} %broadcast_in_dim.74.gain) | copy-start | bytes 30724
  6.0 9.9 %copy-start.34 = (s32[1024]{0:T(1024)}, s32[1024]{0:T(1024)S(1)}, u32[]{:S(2)}) copy-start(s32[1024]{0:T(1024)S(1)} %select_reduce_fusion.blocks_ref) | copy-start | bytes 12292
  8.7 74.1 %copy-start.22 = (f32[16,1024]{1,0:T(8,128)}, f32[16,1024]{1,0:T(8,128)S(1)}, u32[]{:S(2)}) copy-start(f32[16,1024]{1,0:T(8,128)S(1)} %get-tuple-element.108.sin_ref) | copy-start | bytes 196612
  8.7 74.1 %copy-start.24 = (f32[16,1024]{1,0:T(8,128)}, f32[16,1024]{1,0:T(8,128)S(1)}, u32[]{:S(2)}) copy-start(f32[16,1024]{1,0:T(8,128)S(1)} %get-tuple-element.109.cos_ref) | copy-start | bytes 196612
  9.3 9.0 %copy-start.1 = (bf16[2560,288]{0,1:T(8,128)(2,1)S(1)}, bf16[2560,288]{0,1:T(8,128)(2,1)}, u32[]{:S(2)}) copy-start(bf16[2560,288]{0,1:T(8,128)(2,1)} %param.17) | copy-start | bytes 4423684
  18.3 64.4 %copy-start.6 = (bf16[1,128,2560]{2,1,0:T(8,128)(2,1)S(1)}, bf16[1,128,2560]{2,1,0:T(8,128)(2,1)}, u32[]{:S(2)}) copy-start(bf16[1,128,2560]{2,1,0:T(8,128)(2,1)} %param.27) | copy-start | bytes 1966084
  18.3 64.4 %copy-start.20 = (bf16[256,5,64]{0,2,1:T(8,128)(2,1)S(1)}, bf16[256,5,64]{0,2,1:T(8,128)(2,1)}, u32[]{:S(2)}) copy-start(bf16[256,5,64]{0,2,1:T(8,128)(2,1)} %param.19) | copy-start | bytes 491524
  18.3 64.4 %copy-start.26 = (bf16[256,5,64]{0,2,1:T(8,128)(2,1)S(1)}, bf16[256,5,64]{0,2,1:T(8,128)(2,1)}, u32[]{:S(2)}) copy-start(bf16[256,5,64]{0,2,1:T(8,128)(2,1)} %param.20) | copy-start | bytes 491524
  18.3 64.4 %copy-start.36 = (f32[256]{0:T(256)S(1)}, f32[256]{0:T(256)}, u32[]{:S(2)}) copy-start(f32[256]{0:T(256)} %param.18) | copy-start | bytes 3076
  82.1 35.8 %copy-start.42 = (f32[1024]{0:T(1024)}, f32[1024]{0:T(1024)S(1)}, u32[]{:S(2)}) copy-start(f32[1024]{0:T(1024)S(1)} %multiply_reduce_fusion) | copy-start | bytes 12292
  117.9 131.5 %copy-start.3 = (bf16[480,1024]{1,0:T(8,128)(2,1)S(1)}, bf16[480,1024]{1,0:T(8,128)(2,1)}, u32[]{:S(2)}) copy-start(bf16[480,1024]{1,0:T(8,128)(2,1)} %copy-done.2) | copy-start | bytes 2949124
  255.9 19.7 %copy-start.21 = (bf16[256,5,64]{0,2,1:T(8,128)(2,1)S(1)}, bf16[256,5,64]{0,2,1:T(8,128)(2,1)}, u32[]{:S(2)}) copy-start(bf16[256,5,64]{0,2,1:T(8,128)(2,1)} %param.19) | copy-start | bytes 491524
  255.9 20.2 %copy-start.27 = (bf16[256,5,64]{0,2,1:T(8,128)(2,1)S(1)}, bf16[256,5,64]{0,2,1:T(8,128)(2,1)}, u32[]{:S(2)}) copy-start(bf16[256,5,64]{0,2,1:T(8,128)(2,1)} %param.20) | copy-start | bytes 491524
  255.9 20.2 %copy-start.37 = (f32[256]{0:T(256)S(1)}, f32[256]{0:T(256)}, u32[]{:S(2)}) copy-start(f32[256]{0:T(256)} %param.18) | copy-start | bytes 3076
  278.9 40.4 %copy-start.45 = (f32[1,2560]{1,0:T(1,128)S(1)}, f32[1,2560]{1,0:T(1,128)}, u32[]{:S(2)}) copy-start(f32[1,2560]{1,0:T(1,128)} %get-tuple-element.81) | copy-start | bytes 30724
  279.5 41.0 %copy-start.8 = (bf16[1024,256]{1,0:T(8,128)(2,1)S(1)}, bf16[1024,256]{1,0:T(8,128)(2,1)}, u32[]{:S(2)}) copy-start(bf16[1024,256]{1,0:T(8,128)(2,1)} %copy-done.7) | copy-start | bytes 1572868
  279.5 42.0 %copy-start.14 = (bf16[320,1024]{1,0:T(8,128)(2,1)S(1)}, bf16[320,1024]{1,0:T(8,128)(2,1)}, u32[]{:S(2)}) copy-start(bf16[320,1024]{1,0:T(8,128)(2,1)} %copy-done.13) | copy-start | bytes 1966084
  315.2 58.4 %collective-permute-start.12 = (bf16[128,384]{1,0:T(8,128)(2,1)}, bf16[128,384]{1,0:T(8,128)(2,1)}, u32[]{:S(2)}, u32[]{:S(2)}) collective-permute-start(bf16[128,384]{1,0:T(8,128)(2,1)} %get-tuple-element.79), channel_id=1, source_target_pairs={{0,4},{1,5},{2,6},{3,7},{4,0},{5,1},{6,2},{7,3}} | collective-permute-start | bytes 294920 | tf_op jit(solution)/shard_map/ppermute | solution.py:294
  316.1 59.3 %collective-permute-start.11 = (bf16[128,384]{1,0:T(8,128)(2,1)}, bf16[128,384]{1,0:T(8,128)(2,1)}, u32[]{:S(2)}, u32[]{:S(2)}) collective-permute-start(bf16[128,384]{1,0:T(8,128)(2,1)} %get-tuple-element.79), channel_id=1, source_target_pairs={{0,2},{1,3},{2,0},{3,1},{4,6},{5,7},{6,4},{7,5}} | collective-permute-start | bytes 294920 | tf_op jit(solution)/shard_map/ppermute | solution.py:294
  317.2 76.5 %collective-permute-start.6 = (bf16[128,2560]{1,0:T(8,128)(2,1)S(1)}, bf16[128,2560]{1,0:T(8,128)(2,1)}, u32[]{:S(2)}, u32[]{:S(2)}) collective-permute-start(bf16[128,2560]{1,0:T(8,128)(2,1)S(1)} %get-tuple-element.73), channel_id=1, source_target_pairs={{0,4},{1,5},{2,6},{3,7},{4,0},{5,1},{6,2},{7,3}} | collective-permute-start | bytes 1966088 | tf_op jit(solution)/shard_map/ppermute | solution.py:294
  318.1 77.7 %collective-permute-start.5 = (bf16[128,2560]{1,0:T(8,128)(2,1)S(1)}, bf16[128,2560]{1,0:T(8,128)(2,1)}, u32[]{:S(2)}, u32[]{:S(2)}) collective-permute-start(bf16[128,2560]{1,0:T(8,128)(2,1)S(1)} %get-tuple-element.73), channel_id=1, source_target_pairs={{0,2},{1,3},{2,0},{3,1},{4,6},{5,7},{6,4},{7,5}} | collective-permute-start | bytes 1966088 | tf_op jit(solution)/shard_map/ppermute | solution.py:294
  319.3 44.7 %collective-permute-start.17 = (f32[5376]{0:T(1024)S(1)}, f32[5376]{0:T(1024)}, u32[]{:S(2)}, u32[]{:S(2)}) collective-permute-start(f32[5376]{0:T(1024)S(1)} %pad_maximum_fusion.4), channel_id=1, source_target_pairs={{0,1},{1,0},{2,3},{3,2},{4,5},{5,4},{6,7},{7,6}} | collective-permute-start | bytes 64520 | tf_op jit(solution)/shard_map/ppermute | solution.py:294
  321.5 12.6 %slice-start.6 = ((s8[5242880]{0:T(1024)(128)(4,1)}), s8[4194304]{0:T(1024)(128)(4,1)S(1)}, s32[]{:S(2)}) async-start(s8[5242880]{0:T(1024)(128)(4,1)} %bitcast.118), calls=%async_computation.6 | async-start | bytes 8388608
  322.5 11.6 %slice-start.7 = ((s8[5242880]{0:T(1024)(128)(4,1)}), s8[1048576]{0:T(1024)(128)(4,1)S(1)}, s32[]{:S(2)}) async-start(s8[5242880]{0:T(1024)(128)(4,1)} %bitcast.118), calls=%async_computation.7 | async-start | bytes 2097152
  322.5 11.6 %copy-start.49 = (bf16[1024,800]{1,0:T(8,128)(2,1)S(1)}, bf16[1024,800]{1,0:T(8,128)(2,1)}, u32[]{:S(2)}) copy-start(bf16[1024,800]{1,0:T(8,128)(2,1)} %get-tuple-element.88) | copy-start | bytes 4915204
  341.0 7.9 %copy-start.46 = (s32[1024]{0:T(1024)S(1)}, s32[1024]{0:T(1024)}, u32[]{:S(2)}) copy-start(s32[1024]{0:T(1024)} %get-tuple-element.104) | copy-start | bytes 12292
  349.7 9.7 %slice-start.4 = ((s8[5242880]{0:T(1024)(128)(4,1)}), s8[1048576]{0:T(1024)(128)(4,1)S(1)}, s32[]{:S(2)}) async-start(s8[5242880]{0:T(1024)(128)(4,1)} %bitcast.116), calls=%async_computation.4 | async-start | bytes 2097152
  364.8 3.8 collective-permute-start.18
  368.6 3.8 collective-permute-start.19
  374.5 7.1 %collective-permute-start.13 = (bf16[128,192]{1,0:T(8,128)(2,1)S(1)}, bf16[128,192]{1,0:T(8,128)(2,1)S(1)}, u32[]{:S(2)}, u32[]{:S(2)}) collective-permute-start(bf16[128,192]{1,0:T(8,128)(2,1)S(1)} %slice.68), channel_id=1, source_target_pairs={{0,2},{1,3},{2,0},{3,1},{4,6},{5,7},{6,4},{7,5}} | collective-permute-start | bytes 147464 | tf_op jit(solution)/shard_map/ppermute | solution.py:294
  376.3 5.8 %collective-permute-start.14 = (bf16[128,192]{1,0:T(8,128)(2,1)S(1)}, bf16[128,192]{1,0:T(8,128)(2,1)S(1)}, u32[]{:S(2)}, u32[]{:S(2)}) collective-permute-start(bf16[128,192]{1,0:T(8,128)(2,1)S(1)} %slice.69), channel_id=1, source_target_pairs={{0,4},{1,5},{2,6},{3,7},{4,0},{5,1},{6,2},{7,3}} | collective-permute-start | bytes 147464 | tf_op jit(solution)/shard_map/ppermute | solution.py:294
  378.5 4.4 collective-permute-start.15
  381.6 25.2 %collective-permute-start = (bf16[2,2,128,2560]{3,2,1,0:T(8,128)(2,1)}, bf16[2,2,128,2560]{3,2,1,0:T(8,128)(2,1)S(1)}, u32[]{:S(2)}, u32[]{:S(2)}) collective-permute-start(bf16[2,2,128,2560]{3,2,1,0:T(8,128)(2,1)} %dynamic-slice_bitcast_fusion), channel_id=1, source_target_pairs={{0,1},{1,0},{2,3},{3,2},{4,5},{5,4},{6,7},{7,6}} | collective-permute-start | bytes 7864328 | tf_op jit(solution)/shard_map/ppermute | solution.py:294
  382.8 4.0 collective-permute-start.16
  386.8 12.7 %slice-start = ((s8[5242880]{0:T(1024)(128)(4,1)}), s8[4194304]{0:T(1024)(128)(4,1)S(1)}, s32[]{:S(2)}) async-start(s8[5242880]{0:T(1024)(128)(4,1)} %bitcast.85), calls=%async_computation | async-start | bytes 8388608
  387.4 12.1 %slice-start.1 = ((s8[5242880]{0:T(1024)(128)(4,1)}), s8[1048576]{0:T(1024)(128)(4,1)S(1)}, s32[]{:S(2)}) async-start(s8[5242880]{0:T(1024)(128)(4,1)} %bitcast.85), calls=%async_computation.1 | async-start | bytes 2097152
  393.8 13.0 %slice-start.2 = ((s8[5242880]{0:T(1024)(128)(4,1)}), s8[4194304]{0:T(1024)(128)(4,1)S(1)}, s32[]{:S(2)}) async-start(s8[5242880]{0:T(1024)(128)(4,1)} %bitcast.100), calls=%async_computation.2 | async-start | bytes 8388608
  394.9 10.0 %collective-permute-start.7 = (bf16[128,1280]{1,0:T(8,128)(2,1)S(1)}, bf16[128,1280]{1,0:T(8,128)(2,1)S(1)}, u32[]{:S(2)}, u32[]{:S(2)}) collective-permute-start(bf16[128,1280]{1,0:T(8,128)(2,1)S(1)} %slice.66), channel_id=1, source_target_pairs={{0,2},{1,3},{2,0},{3,1},{4,6},{5,7},{6,4},{7,5}} | collective-permute-start | bytes 983048 | tf_op jit(solution)/shard_map/ppermute | solution.py:294
  396.9 9.9 %slice-start.3 = ((s8[5242880]{0:T(1024)(128)(4,1)}), s8[1048576]{0:T(1024)(128)(4,1)S(1)}, s32[]{:S(2)}) async-start(s8[5242880]{0:T(1024)(128)(4,1)} %bitcast.100), calls=%async_computation.3 | async-start | bytes 2097152
  396.9 9.7 %collective-permute-start.8 = (bf16[128,1280]{1,0:T(8,128)(2,1)S(1)}, bf16[128,1280]{1,0:T(8,128)(2,1)S(1)}, u32[]{:S(2)}, u32[]{:S(2)}) collective-permute-start(bf16[128,1280]{1,0:T(8,128)(2,1)S(1)} %slice.67), channel_id=1, source_target_pairs={{0,4},{1,5},{2,6},{3,7},{4,0},{5,1},{6,2},{7,3}} | collective-permute-start | bytes 983048 | tf_op jit(solution)/shard_map/ppermute | solution.py:294
  399.4 10.4 %collective-permute-start.9 = (bf16[384,2560]{1,0:T(8,128)(2,1)S(1)}, bf16[384,2560]{1,0:T(8,128)(2,1)S(1)}, u32[]{:S(2)}, u32[]{:S(2)}) collective-permute-start(bf16[384,2560]{1,0:T(8,128)(2,1)S(1)} %pad_maximum_fusion), channel_id=1, source_target_pairs={{0,1},{1,0},{2,3},{3,2},{4,5},{5,4},{6,7},{7,6}} | collective-permute-start | bytes 5898248 | tf_op jit(solution)/shard_map/ppermute | solution.py:294
  406.7 3.4 collective-permute-start.10
  407.8 17.1 %collective-permute-start.3 = (bf16[2,128,1280]{2,1,0:T(8,128)(2,1)S(1)}, bf16[2,128,1280]{2,1,0:T(8,128)(2,1)S(1)}, u32[]{:S(2)}, u32[]{:S(2)}) collective-permute-start(bf16[2,128,1280]{2,1,0:T(8,128)(2,1)S(1)} %dynamic-slice_bitcast_fusion.1), channel_id=1, source_target_pairs={{0,4},{1,5},{2,6},{3,7},{4,0},{5,1},{6,2},{7,3}} | collective-permute-start | bytes 1966088 | tf_op jit(solution)/shard_map/ppermute | solution.py:294
  408.9 17.3 %collective-permute-start.1 = (bf16[2,128,1280]{2,1,0:T(8,128)(2,1)S(1)}, bf16[2,128,1280]{2,1,0:T(8,128)(2,1)S(1)}, u32[]{:S(2)}, u32[]{:S(2)}) collective-permute-start(bf16[2,128,1280]{2,1,0:T(8,128)(2,1)S(1)} %dynamic-slice_bitcast_fusion.2), channel_id=1, source_target_pairs={{0,2},{1,3},{2,0},{3,1},{4,6},{5,7},{6,4},{7,5}} | collective-permute-start | bytes 1966088 | tf_op jit(solution)/shard_map/ppermute | solution.py:294
  415.3 20.3 %copy-start.41 = (bf16[128,2560]{1,0:T(8,128)(2,1)S(1)}, bf16[128,2560]{1,0:T(8,128)(2,1)}, u32[]{:S(2)}) copy-start(bf16[128,2560]{1,0:T(8,128)(2,1)} %get-tuple-element.57) | copy-start | bytes 1966084
  425.1 9.3 %collective-permute-start.4 = (bf16[128,1280]{1,0:T(8,128)(2,1)S(1)}, bf16[128,1280]{1,0:T(8,128)(2,1)S(1)}, u32[]{:S(2)}, u32[]{:S(2)}) collective-permute-start(bf16[128,1280]{1,0:T(8,128)(2,1)S(1)} %dynamic-slice_bitcast_fusion.3), channel_id=1, source_target_pairs={{0,2},{1,3},{2,0},{3,1},{4,6},{5,7},{6,4},{7,5}} | collective-permute-start | bytes 983048 | tf_op jit(solution)/shard_map/ppermute | solution.py:294
  426.5 9.0 %collective-permute-start.2 = (bf16[128,1280]{1,0:T(8,128)(2,1)S(1)}, bf16[128,1280]{1,0:T(8,128)(2,1)S(1)}, u32[]{:S(2)}, u32[]{:S(2)}) collective-permute-start(bf16[128,1280]{1,0:T(8,128)(2,1)S(1)} %dynamic-slice_bitcast_fusion.4), channel_id=1, source_target_pairs={{0,4},{1,5},{2,6},{3,7},{4,0},{5,1},{6,2},{7,3}} | collective-permute-start | bytes 983048 | tf_op jit(solution)/shard_map/ppermute | solution.py:294
  (30 other events, 69.0 us)

commit v5 on v4

--- a/solution.py
+++ b/solution.py
@@ -14,6 +14,8 @@
 VM = pltpu.VMEM
 ZR = 248
 GB = 64
+GR = GB * 8
+LIMIT = 40 << 20
 QB = 256
 
 
@@ -113,11 +115,11 @@
 
         lax.fori_loop(0, n, start, 0)
         lax.fori_loop(0, n, wait, 0)
-        cols = lax.broadcasted_iota(jnp.int32, (rows, GB * 8), 1) + base * 8
+        cols = lax.broadcasted_iota(jnp.int32, (rows, GR), 1) + base * 8
         hot = jnp.where(cols == key_ref[...], 1.0, 0.0).astype(BF16)
-        for c in range(0, width, 512):
-            got = nn(hot, stage[:, :, c:c + 512].reshape(GB * 8, 512))
-            out_ref[:, c:c + 512] += got.astype(BF16)
+        for c in range(0, width, COLS):
+            got = nn(hot, stage[:, :, c:c + COLS].reshape(GR, COLS))
+            out_ref[:, c:c + COLS] += got.astype(BF16)
         return carry
 
     lax.fori_loop(0, (count + GB - 1) // GB, chunk, 0)
@@ -133,14 +135,18 @@
         in_specs=[smem, smem, pl.BlockSpec(memory_space=VM), pl.BlockSpec(memory_space=VM), pl.BlockSpec(memory_space=pl.ANY)],
         out_specs=pl.BlockSpec(memory_space=VM),
         scratch_shapes=[VM((GB, 8, width), BF16), pltpu.SemaphoreType.DMA],
-        compiler_params=pltpu.CompilerParams(vmem_limit_bytes=40 << 20), name='gather_rows',
+        compiler_params=pltpu.CompilerParams(vmem_limit_bytes=LIMIT), name='gather_rows',
     )(count, blocks, key[:, None], tail, table)
 
 
-def table_grad_body(count_ref, blocks_ref, key_ref, de_ref, zeros_ref, out_ref, tail_ref, stage, sem):
+def table_grad_body(count_ref, blocks_ref, key_ref, zeros_ref, *refs):
+    pieces, (out_ref, tail_ref, lat_ref, de_ref, stage, sem) = refs[:-6], refs[-6:]
     rows, width = de_ref.shape
-    vocab = out_ref.shape[0]
-    full = vocab // 8
+    local = rows // len(pieces)
+    for k, (piece, d) in enumerate(zip(pieces, hop_order())):
+        de_ref[k * local:(k + 1) * local, :] = piece[:, :width]
+        lat_ref[pl.ds(pl.multiple_of(d * local, local), local), :] = piece[:, width:]
+    full = out_ref.shape[0] // 8
     tail_ref[...] = jnp.zeros_like(tail_ref)
     count = count_ref[0]
 
@@ -148,11 +154,11 @@
         return pltpu.make_async_copy(stage.at[i], out_ref.at[pl.ds(pl.multiple_of(b * 8, 8), 8), :], sem)
 
     def sums(ci):
-        ids = lax.broadcasted_iota(jnp.int32, (GB * 8, rows), 0) + ci * (GB * 8)
+        ids = lax.broadcasted_iota(jnp.int32, (GR, rows), 0) + ci * GR
         hot = jnp.where(ids == key_ref[...], 1.0, 0.0).astype(BF16)
-        for c in range(0, width, 512):
-            got = nn(hot, de_ref[:, c:c + 512])
-            stage[:, :, c:c + 512] = got.astype(BF16).reshape(GB, 8, 512)
+        for c in range(0, width, COLS):
+            got = nn(hot, de_ref[:, c:c + COLS])
+            stage[:, :, c:c + COLS] = got.astype(BF16).reshape(GB, 8, COLS)
 
     def move(ci, go):
         base = ci * GB
@@ -179,18 +185,19 @@
     lax.fori_loop(0, (count + GB - 1) // GB, chunk, 0)
 
 
-def table_grad(key, blocks, count, de_full, table):
-    vocab, width = table.shape
-    smem = pl.BlockSpec(memory_space=pltpu.SMEM)
+def table_grad(key, blocks, count, pieces, table):
+    (vocab, width), rows = table.shape, key.shape[0]
+    latw = pieces[0].shape[1] - width
+    smem, vmem, anym = (pl.BlockSpec(memory_space=m) for m in (pltpu.SMEM, VM, pl.ANY))
     full = vocab // 8 * 8
-    out, tail = pl.pallas_call(
-        table_grad_body, out_shape=[jax.ShapeDtypeStruct((vocab, width), BF16), jax.ShapeDtypeStruct((8, width), BF16)],
-        in_specs=[smem, smem, pl.BlockSpec(memory_space=VM), pl.BlockSpec(memory_space=VM), pl.BlockSpec(memory_space=pl.ANY)], input_output_aliases={4: 0},
-        out_specs=[pl.BlockSpec(memory_space=pl.ANY), pl.BlockSpec(memory_space=VM)],
-        scratch_shapes=[VM((GB, 8, width), BF16), pltpu.SemaphoreType.DMA],
-        compiler_params=pltpu.CompilerParams(vmem_limit_bytes=40 << 20), name='table_grad',
-    )(count, blocks, key[None, :], de_full, table)
-    return lax.dynamic_update_slice(out, tail[:vocab - full], (full, 0))
+    out, tail, lat = pl.pallas_call(
+        table_grad_body, out_shape=[shape((vocab, width), BF16), shape((8, width), BF16), shape((rows, latw), BF16)],
+        in_specs=[smem, smem, vmem, anym] + [vmem] * len(pieces), input_output_aliases={3: 0},
+        out_specs=[anym, vmem, vmem],
+        scratch_shapes=[VM((rows, width), BF16), VM((GB, 8, width), BF16), pltpu.SemaphoreType.DMA],
+        compiler_params=pltpu.CompilerParams(vmem_limit_bytes=LIMIT), name='table_grad',
+    )(count, blocks, key[None, :], table, *pieces)
+    return lax.dynamic_update_slice(out, tail[:vocab - full], (full, 0)), lat
 
 
 def heads_of(q_ref, kn_ref, kp_ref, cos_ref, sin_ref, nope, half):
@@ -286,7 +293,7 @@
         attn_bwd_body, grid=(heads,), in_specs=ins + [lse_spec, per(vd)], out_specs=[per(qd), per(nope), per(vd), one(rope), pl.BlockSpec(memory_space=pl.ANY)],
         out_shape=[jax.ShapeDtypeStruct(q.shape, BF16), jax.ShapeDtypeStruct(kn.shape, BF16), jax.ShapeDtypeStruct(v.shape, BF16), jax.ShapeDtypeStruct(kp.shape, F32), jax.ShapeDtypeStruct(table, BF16)],
         scratch_shapes=[VM((qd, seq), F32), VM((vd, seq), F32), VM((ZR, table[1]), BF16), pltpu.SemaphoreType.DMA((-(-table[0] // ZR),))],
-        compiler_params=pltpu.CompilerParams(vmem_limit_bytes=40 << 20), name='attend_bwd',
+        compiler_params=pltpu.CompilerParams(vmem_limit_bytes=LIMIT), name='attend_bwd',
     )(q, kn, kp, v, cos_t, sin_t, lse, do)
 
 
@@ -295,40 +302,6 @@
 
 
 PAIR, XBIT, YBIT = 1, 2, 4
-
-
-def coords():
-    me = lax.axis_index('tp')
-    return me // YBIT, (me // XBIT) % 2, me % 2
-
-
-def pick(x, i, axis):
-    return lax.dynamic_index_in_dim(x, i, axis, keepdims=False)
-
-
-def added(a, b):
-    return (a.astype(F32) + b.astype(F32)).astype(BF16)
-
-
-def scatter_hops(part, local):
-    y, x, core = coords()
-    half = part.shape[1] // 2
-    p = part.reshape(2, 2, 2, local, part.shape[1])
-    q = added(pick(p, core, 2), shift(pick(p, 1 - core, 2), PAIR))
-    a, b = q[..., :half], q[..., half:]
-    a = added(pick(a, x, 1), shift(pick(a, 1 - x, 1), XBIT))
-    b = added(pick(b, y, 0), shift(pick(b, 1 - y, 0), YBIT))
-    a = pick(a, y, 0).astype(F32) + shift(pick(a, 1 - y, 0), YBIT).astype(F32)
-    b = pick(b, x, 0).astype(F32) + shift(pick(b, 1 - x, 0), XBIT).astype(F32)
-    return jnp.concatenate([a, b], axis=1)
-
-
-def gather_hops(blk):
-    half = blk.shape[1] // 2
-    bx, by = shift(blk, XBIT), shift(blk, YBIT)
-    near = jnp.concatenate([blk, bx, by])
-    diag = jnp.concatenate([shift(by[:, :half], XBIT), shift(bx[:, half:], YBIT)], axis=1)
-    return jnp.concatenate([near, diag, shift(near, PAIR), shift(diag, PAIR)])
 
 
 def hop_order():
@@ -341,20 +314,6 @@
 def to_hop_order(x, axis):
     n = x.shape[axis] // 8
     return jnp.concatenate([lax.dynamic_slice_in_dim(x, d * n, n, axis) for d in hop_order()], axis=axis)
-
-
-def from_hop_order(x):
-    n = x.shape[0] // 8
-    out = jnp.zeros_like(x)
-    for k, d in enumerate(hop_order()):
-        out = lax.dynamic_update_slice_in_dim(out, x[k * n:(k + 1) * n], d * n, 0)
-    return out
-
-
-def sum_hops(x):
-    for bit in (PAIR, XBIT, YBIT):
-        x = x + shift(x, bit)
-    return x
 
 
 class Exchange:
@@ -396,6 +355,9 @@
 
     def copy(self, src, dst, ssem, rsem, dev):
         return pltpu.make_async_remote_copy(src_ref=src, dst_ref=dst, send_sem=ssem, recv_sem=rsem, device_id={'tp': dev}, device_id_type=pl.DeviceIdType.MESH)
+
+    def saver(self, src, dst, sem):
+        return [pltpu.make_async_copy(src.at[rows, :], dst.at[rows, :], sem.at[j]) for j, rows in enumerate(self.chip)]
 
     def rs_begin(self, parts, scratch):
         na = len(self.widths)
@@ -542,10 +504,10 @@
     return r * gd - x * (r * r * r * dot), sum_rows(dy * x * r)
 
 
-def exchange_call(body, name, cid, ins, out_shape, scratch, far=0, limit=50):
+def exchange_call(body, name, cid, ins, out_shape, scratch, far=0, out=0, limit=50):
     vmem, hbm = pl.BlockSpec(memory_space=VM), pl.BlockSpec(memory_space=pltpu.HBM)
     return pl.pallas_call(
-        body, out_shape=out_shape, in_specs=[vmem] * (len(ins) - far) + [hbm] * far, out_specs=[vmem] * len(out_shape), scratch_shapes=scratch,
+        body, out_shape=out_shape, in_specs=[vmem] * (len(ins) - far) + [hbm] * far, out_specs=[vmem] * (len(out_shape) - out) + [hbm] * out, scratch_shapes=scratch,
         compiler_params=pltpu.CompilerParams(vmem_limit_bytes=limit << 20, collective_id=cid, has_side_effects=True), name=name)(*ins)
 
 
@@ -557,7 +519,7 @@
     pass
 
 
-def embed_body(part, gain, wq, wdkv, e_ref, full, q_ref, lat_ref, acc, *scratch):
+def embed_body(part, gain, wq, wdkv, e_ref, q_ref, lat_ref, u_out, full, usem, acc, *scratch):
     ex = Exchange([part.shape[1]], MAIN)
     ex.place(acc.shape[0])
     ex.enter()
@@ -571,12 +533,16 @@
         u = full[ex.chip[j], :]
         q_ref[:, ex.chip[j]] = nt(wq[...], u).astype(BF16)
         lat_ref[ex.chip[j], :] = nt(u, wdkv[...])
-
+        save[j].start()
+
+    save = ex.saver(full, u_out, usem)
     ex.all_gather([full], scratch[NRS:], arrive)
     ex.drain()
-
-
-def attn_body(lat, g_kv, wuk, wuv, q_ref, cos_ref, sin_ref, dy_ref, c_ref, kn_ref, kp_ref, v_ref, o_ref, lse_ref, dyf, *scratch):
+    for cp in save:
+        cp.wait()
+
+
+def attn_body(lat, g_kv, wuk, wuv, q_ref, cos_ref, sin_ref, dy_ref, c_ref, kn_ref, kp_ref, v_ref, o_ref, lse_ref, dy_out, dyf, dsem, *scratch):
     ex = Exchange([dyf.shape[1]], MAIN)
     ex.place(dy_ref.shape[0])
     ex.enter()
@@ -584,7 +550,10 @@
     lora, half, heads = c_ref.shape[1], cos_ref.shape[0], lse_ref.shape[0]
     per = lambda ref, h: ref.at[pl.ds(h * (ref.shape[0] // heads), ref.shape[0] // heads), :]
 
+    save = ex.saver(dyf, dy_out, dsem)
+
     def arrive(j):
+        save[j].start()
         if j:
             return
         c = norm_rows(lat[:, :lora], g_kv[...]).astype(BF16)
@@ -598,19 +567,27 @@
             attn_fwd_body(per(q_ref, h), per(kn_ref, h), kp_ref, per(v_ref, h), cos_ref, sin_ref, per(o_ref, h), lse_ref.at[pl.ds(h, 1)])
 
     ex.all_gather([dyf], scratch, arrive)
+    for cp in save:
+        cp.wait()
 
 
 def middle_body(o_ref, wo, e_ref, gain, dyl_ref, dy_hbm, wg_hbm, wu_hbm, wd_hbm,
-                h_ref, z, y_ref, hid_ref, dgate_ref, dup_ref, dres_ref, dgain_ref, dfull, do_ref,
-                wg, wu, wd, dyb, part, acc, wsem, dsem, *scratch):
-    ex = Exchange([part.shape[1]], MAIN)
-    ex.place(acc.shape[0])
+                h_ref, y_ref, dres_ref, dgain_ref, do_ref, z_out, hid_out, dgate_out, dup_out, dfull_out,
+                wall, dyb, act, part, ypart, z, acc, wsem, dsem, asem, zsem, fsem, *scratch):
+    ex, ey = Exchange([part.shape[1]], MAIN), Exchange([part.shape[1]], MAIN)
+    for e in (ex, ey):
+        e.place(acc.shape[0])
     ex.enter()
+    ffn = wd_hbm.shape[0]
+    wg, wu, wd = (wall.at[pl.ds(k * ffn, ffn), :] for k in range(3))
+    dfull = wall.at[pl.ds(0, part.shape[0]), :]
     loads = [pltpu.make_async_copy(a, b, wsem.at[k]) for k, (a, b) in enumerate(((wg_hbm, wg), (wu_hbm, wu), (wd_hbm, wd)))]
     dy_in = [pltpu.make_async_copy(dy_hbm.at[ex.chip[j], :], dyb.at[j % 2], dsem.at[j % 2]) for j in range(4)]
     for cp in loads + dy_in[:2]:
         cp.start()
+    rs = 2 * NRS
     ex.rs_begin([part], scratch)
+    ey.rs_begin([ypart], scratch[NRS:])
     width = part.shape[1]
 
     def attn_part(j):
@@ -620,41 +597,55 @@
     h = (e_ref[...].astype(F32) + acc[...].astype(BF16).astype(F32)).astype(BF16)
     h_ref[...] = h
     z[ex.mine[0], :] = norm_rows(h.astype(F32), gain[...]).astype(BF16)
+    save_z, save_d = ex.saver(z, z_out, zsem), ex.saver(dfull, dfull_out, fsem)
+    save_a = [[pltpu.make_async_copy(act.at[j % 2, k], dst.at[ex.chip[j], :], asem.at[j % 2, k]) for k, dst in enumerate((hid_out, dgate_out, dup_out))]
+              for j in range(4)]
 
     def mlp(j):
         rows = ex.chip[j]
         gate, up = nt(z[rows, :], wg[...]), nt(z[rows, :], wu[...])
         sig = jax.nn.sigmoid(gate)
         hid = (gate * sig * up).astype(BF16)
-        hid_ref[rows, :] = hid
         dh = nt(dyb[j % 2], wd[...])
         dup = (dh * gate * sig).astype(BF16)
         dgate = (dh * up * sig * (1.0 + gate * (1.0 - sig))).astype(BF16)
-        dup_ref[rows, :] = dup
-        dgate_ref[rows, :] = dgate
+        if j > 1:
+            for cp in save_a[j - 2]:
+                cp.wait()
+        for k, value in enumerate((hid, dgate, dup)):
+            act[j % 2, k] = value
         for c in range(0, width, COLS):
-            part[rows, c:c + COLS] = (nn(dgate, wg[:, c:c + COLS]) + nn(dup, wu[:, c:c + COLS])).astype(BF16)
-            y_ref[rows, c:c + COLS] = nn(hid, wd[:, c:c + COLS]).astype(BF16)
+            cols = slice(c, c + COLS)
+            part[rows, cols] = (nn(dgate, wg[:, cols]) + nn(dup, wu[:, cols])).astype(BF16)
+            ypart[rows, cols] = nn(hid, wd[:, cols]).astype(BF16)
+        for cp in save_a[j]:
+            cp.start()
 
     def arrive_z(j):
         if j == 0:
             ex.drain()
             for cp in loads:
                 cp.wait()
+        save_z[j].start()
         dy_in[j].wait()
         mlp(j)
         if j < 2:
             dy_in[j + 2].start()
         ex.ready(j)
+        ey.ready(j)
         if j == 2:
             ex.push(1)
+            ey.push(1)
         if j == 3:
             ex.push(2)
             ex.push(3)
 
-    ex.all_gather([z], scratch[NRS:NRS + NAG], arrive_z, slow=True)
+    ex.all_gather([z], scratch[rs:rs + NAG], arrive_z, slow=True)
     ex.relay()
+    ey.push(2)
+    ey.push(3)
     ex.land([acc])
+    ey.relay()
     dx, dgain_ref[...] = norm_rows_vjp(h_ref[...].astype(F32), gain[...], acc[...])
     dres = dyl_ref[...].astype(F32) + dx
     dres_ref[...] = dres
@@ -662,12 +653,19 @@
 
     def arrive_d(j):
         do_ref[:, ex.chip[j]] = nt(wo[...], dfull[ex.chip[j], :]).astype(BF16)
-
-    ex.all_gather([dfull], scratch[NRS + NAG:], arrive_d)
+        save_d[j].start()
+        if j == 2:
+            ey.land([acc])
+            y_ref[...] = (h_ref[...].astype(F32) + acc[...].astype(BF16).astype(F32)).astype(BF16)
+
+    ex.all_gather([dfull], scratch[rs + NAG:], arrive_d)
     ex.drain()
-
-
-def attn_back_body(dq_ref, lat, wq, wdkv, e_ref, dres_ref, gain, de_ref, dlat_ref, dg_ref, part, acc, acc_lat, *scratch):
+    ey.drain()
+    for cp in save_z + save_d + save_a[2] + save_a[3]:
+        cp.wait()
+
+
+def attn_back_body(dq_ref, lat, wq, wdkv, e_ref, dres_ref, gain, de_ref, dg_ref, part, acc, acc_lat, *scratch):
     ex = Exchange([part.shape[1], lat.shape[1]], LAST)
     ex.place(acc.shape[0])
     ex.enter()
@@ -680,12 +678,12 @@
 
     ex.reduce_scatter([acc, acc_lat], produce)
     dx, dg_ref[...] = norm_rows_vjp(e_ref[...].astype(F32), gain[...], acc[...])
-    de_ref[...] = (dres_ref[...] + dx).astype(BF16)
-    dlat_ref[...] = acc_lat[...].astype(BF16)
+    de_ref[:, :dx.shape[1]] = (dres_ref[...] + dx).astype(BF16)
+    de_ref[:, dx.shape[1]:] = acc_lat[...].astype(BF16)
     ex.drain()
 
 
-def layer_pass(rows, d_out, w_q, w_dkv, g_kv, w_uk, w_uv, w_o, g_attn, g_mlp, w_gate, w_up, w_down, vocab):
+def layer_pass(rows, d_out, w_q, w_dkv, g_kv, w_uk, w_uv, w_o, g_attn, g_mlp, w_gate, w_up, w_down, vocab, key, blocks, count):
     w_q, heads = w_q
     seq, width = rows.shape
     local = d_out.shape[0]
@@ -694,51 +692,55 @@
     one = Exchange([width], MAIN)
     main = [VM((local, width), F32)] + one.rs_scratch(local) + one.ag_scratch()
     partb = [VM((seq, width), BF16)]
+    dma = pltpu.SemaphoreType.DMA
+    saved = partb + [dma((4,))]
     loc, fullb = shape((local, width), BF16), shape((seq, width), BF16)
     ga, gm = g_attn[None, :], g_mlp[None, :]
-    embedded, x_attn, query, latent = exchange_call(
-        embed_body, 'embed_exchange', 1, [rows, ga, w_q, w_dkv], [loc, fullb, shape((w_q.shape[0], seq), BF16), shape((seq, latw), F32)], main)
+    embedded, query, latent, x_attn = exchange_call(
+        embed_body, 'embed_exchange', 1, [rows, ga, w_q, w_dkv], [loc, shape((w_q.shape[0], seq), BF16), shape((seq, latw), F32), fullb], saved + main, out=1)
     cos_t, sin_t = (t.T for t in rope_tables(seq, latw - lora))
     nq, nk, nv = w_q.shape[0], w_uk.shape[0], w_uv.shape[0]
     c_kv, k_nope, k_pe_t, value, attn_out, lse, dy_full = exchange_call(
         attn_body, 'attend_fwd', 2, [latent, g_kv[None, :], w_uk, w_uv, query, cos_t, sin_t, d_out],
         [shape((seq, lora), BF16), shape((nk, seq), BF16), shape((latw - lora, seq), BF16), shape((nv, seq), BF16), shape((nv, seq), BF16),
-         shape((heads, 1, seq), F32), fullb], one.ag_scratch())
+         shape((heads, 1, seq), F32), fullb], saved + one.ag_scratch(), out=1)
     kv_pull = jax.vjp(kv_prep, latent, g_kv)[1]
     ffn = w_gate.shape[0]
-    dma = pltpu.SemaphoreType.DMA
-    act, wide = shape((seq, ffn), BF16), VM((ffn, width), BF16)
-    residual, x_mlp, y_part, hidden, d_gate, d_up, d_residual, dg_mlp, d_attn_full, d_attn_out = exchange_call(
+    act = shape((seq, ffn), BF16)
+    residual, layer_out, d_residual, dg_mlp, d_attn_out, x_mlp, hidden, d_gate, d_up, d_attn_full = exchange_call(
         middle_body, 'middle', 3, [attn_out, w_o, embedded, gm, d_out, dy_full, w_gate, w_up, w_down],
-        [loc, fullb, fullb, act, act, act, shape((local, width), F32), shape((1, width), F32), fullb, shape((w_o.shape[0], seq), BF16)],
-        [wide, wide, wide, VM((2, seq // 4, width), BF16)] + partb + [VM((local, width), F32), dma((3,)), dma((2,))] + one.rs_scratch(local) + one.ag_scratch() + one.ag_scratch(),
-        far=4, limit=63)
-    mlp_loc = scatter_hops(y_part, local)
-    layer_out = (residual.astype(F32) + mlp_loc.astype(BF16).astype(F32)).astype(BF16)
+        [loc, loc, shape((local, width), F32), shape((1, width), F32), shape((w_o.shape[0], seq), BF16), fullb, act, act, act, fullb],
+        [VM((3 * ffn, width), BF16), VM((2, seq // 4, width), BF16), VM((2, 3, seq // 4, ffn), BF16)] + partb * 3
+        + [VM((local, width), F32), dma((3,)), dma((2,)), dma((2, 3)), dma((4,)), dma((4,))]
+        + one.rs_scratch(local) * 2 + one.ag_scratch() * 2, far=4, out=5, limit=63)
     d_query, d_knope, d_value, d_kpe, table0 = attend_bwd(query, k_nope, k_pe_t, value, cos_t, sin_t, lse, d_attn_out, heads, (vocab, width))
     d_ckv = (tn(d_knope, w_uk) + tn(d_value, w_uv)).astype(BF16)
     d_latent, dg_kv = kv_pull((d_ckv, d_kpe.T.astype(BF16)))
     lat_part = jnp.pad(d_latent.astype(BF16), ((0, 0), (0, -latw % 128)))
     padw = lat_part.shape[1]
     two = Exchange([width, padw], LAST)
-    de, dlat, dg_attn = exchange_call(
+    de, dg_attn = exchange_call(
         attn_back_body, 'back_exchange', 4, [d_query, lat_part, w_q, w_dkv, embedded, d_residual, ga],
-        [loc, shape((local, padw), BF16), shape((1, width), F32)],
+        [shape((local, width + padw), BF16), shape((1, width), F32)],
         partb + [VM((local, width), F32), VM((local, padw), F32)] + two.rs_scratch(local))
-    hidden, d_gate, d_up, d_query_l, d_knope, d_value, attn_out, de = lax.optimization_barrier((hidden, d_gate, d_up, d_query, d_knope, d_value, attn_out, de))
-    de_full = gather_hops(de)
-    lat_full = from_hop_order(gather_hops(dlat))
-    dw_down = tn(hidden, dy_full)
-    dw_gate = tn(d_gate, x_mlp)
-    dw_up = tn(d_up, x_mlp)
+    later = lax.optimization_barrier
+    dg = jnp.concatenate([dg_attn[0], dg_mlp[0], dg_kv])
+    hidden, d_gate, d_up, d_query, de, dg = later((hidden, d_gate, d_up, d_query, de, dg))
+    near = [shift(de, XBIT), shift(de, YBIT), shift(de, XBIT + YBIT)]
+    pair = shift(de, PAIR)
+    dg = dg + shift(dg, PAIR)
+    dw_down, dw_gate, dw_up, dw_q = tn(hidden, dy_full), tn(d_gate, x_mlp), tn(d_up, x_mlp), nn(d_query, x_attn)
+    dw_down, dw_gate, dw_up, dw_q, near, pair, dg, attn_out = later((dw_down, dw_gate, dw_up, dw_q, near, pair, dg, attn_out))
+    far = [shift(b, PAIR) for b in near]
+    dg = dg + shift(dg, XBIT)
     dw_o = nn(attn_out, d_attn_full)
-    dw_uk = nn(d_knope, c_kv)
-    dw_uv = nn(d_value, c_kv)
-    dw_q = nn(d_query_l, x_attn)
+    dw_o, far, dg, d_knope, d_value = later((dw_o, far, dg, d_knope, d_value))
+    dg = dg + shift(dg, YBIT)
+    dw_uk, dw_uv = nn(d_knope, c_kv), nn(d_value, c_kv)
+    d_table, lat_full = table_grad(to_hop_order(key, 0), blocks, count, [de, *near, pair, *far], table0)
     dw_dkv = tn(lat_full[:, :latw], x_attn)
-    dg = sum_hops(jnp.concatenate([dg_attn[0], dg_mlp[0], dg_kv]))
     dg_attn, dg_mlp, dg_kv = dg[:width], dg[width:2 * width], dg[2 * width:]
-    return layer_out, de_full, table0, (dw_q, dw_dkv, dg_kv, dw_uk, dw_uv, dw_o, dg_attn, dg_mlp, dw_gate, dw_up, dw_down)
+    return layer_out, d_table, (dw_q, dw_dkv, dg_kv, dw_uk, dw_uv, dw_o, dg_attn, dg_mlp, dw_gate, dw_up, dw_down)
 
 
 def rows_of(w):
@@ -755,10 +757,9 @@
         heads = w_q.shape[1]
         key, blocks, count = block_index(tokens, vocab_local)
         rows = gather_rows(key, blocks, count, embed_table)
-        layer_out, de_full, table0, grads = layer_pass(
+        layer_out, d_table, grads = layer_pass(
             rows, d_out[0], (rows_of(w_q), heads), w_dkv.T, g_kv, rows_of(w_uk), rows_of(w_uv), w_o.reshape(-1, model_dim),
-            g_attn, g_mlp, w_gate.T, w_up.T, w_down, vocab_local)
-        d_table = table_grad(to_hop_order(key, 0), blocks, count, de_full, table0)
+            g_attn, g_mlp, w_gate.T, w_up.T, w_down, vocab_local, key, blocks, count)
         dw_q, dw_dkv, dg_kv, dw_uk, dw_uv, dw_o, dg_attn, dg_mlp, dw_gate, dw_up, dw_down = grads
         return (layer_out[None], d_table, unrows(dw_q, heads), dw_dkv.T, dg_kv, unrows(dw_uk, heads), unrows(dw_uv, heads),
                 dw_o.reshape(w_o.shape), dg_attn, dg_mlp, dw_gate.T, dw_up.T, dw_down)

time: 443 us -> 396 us (0.89)
  waiting for transfers between devices: 29.5 us -> 0.17 us
  local copies, waits for them, and re-layouts: 41.3 us -> 24.7 us
  Pallas kernels: 285 us -> 297 us
  starting transfers between devices: 14.8 us -> 6.59 us
  other arithmetic: 17 us -> 11 us
    ppermute x20 -> x10, waiting for transfers between devices: 29.5 us -> 0.17 us  [shift(): return lax.ppermute(x, 'tp', [(d, d ^ bit) for d in range(8)])]
    pallas_call x4, Pallas kernels: 258 us -> 268 us  [exchange_call(): pl.pallas_call(body, out_shape=out_shape, in_specs=[vmem] * (len(ins) - f...]
    ppermute x20 -> x10, starting transfers between devices: 14.8 us -> 6.59 us  [shift(): return lax.ppermute(x, 'tp', [(d, d ^ bit) for d in range(8)])]
    dynamic_update_slice x8 -> x1, local copies, waits for them, and re-layouts: 7.25 us -> 0.62 us  [table_grad(): return (lax.dynamic_update_slice(out, tail[:vocab - full], (full, 0)), lat)]
    unnamed x129 -> x118, local copies, waits for them, and re-layouts: 21.2 us -> 19 us
  transfers between devices with their start and end apart: 20 -> 10, of which waited for: 8 -> 1; matrix products, arithmetic and copies ran while one was open for 16% -> 11% of each run, Pallas kernels for 1% -> 0%
where the time goes in v5:
time: 396 us; the launch traced here: 390 us
  Pallas kernels  297 us (75%)
  matrix products  49.3 us (12%)
  local copies, waits for them, and re-layouts  24.7 us (6%)
  other arithmetic  11 us (3%)
  starting transfers between devices  6.59 us (2%)
    pallas_call x4, Pallas kernels, exchange_call(): pl.pallas_call(body, out_shape=out_shape, in_specs=[vmem] * (len(ins) - f...  268 us
    dot_general x10, matrix products, mm(): lax.dot_general(lhs, rhs, (((lc,), (rc,)), ((), ())), preferred_element_t...  49.3 us
    unnamed x118, local copies, waits for them, and re-layouts  19 us
    pallas_call x1, Pallas kernels, attend_bwd(): pl.pallas_call(attn_bwd_body, grid=(heads,), in_specs=ins + [lse_spec, pe...  15.3 us
  transfers between devices with their start and end apart: 10, of which 1 were waited for; matrix products, arithmetic and copies ran while one was open for 11% of the time, Pallas kernels for 0%

profile of v5, /device:TPU:0, one launch (start us, length us, event | category | flops | bytes accessed | tf_op | source)
XLA Modules:
  0.0 390.1 jit_solution(18025216540498304211)
XLA Ops:
  0.7 0.7 broadcast_in_dim.71.gain
  1.4 1.3 broadcast_in_dim.73.gain
  2.7 0.7 broadcast_select_fusion
  3.5 0.8 select_reduce_fusion.1
  4.3 0.8 convert_reduce_fusion
  5.1 0.9 select_reduce_fusion.blocks_ref
  6.0 1.2 add_select_fusion.1
  7.3 0.8 slice.21
  9.3 6.7 %gather_rows.1.part = bf16[1024,2560]{1,0:T(8,128)(2,1)S(1)} custom-call(s32[1]{0:T(128)} %bitcast.2.count_ref, s32[1024]{0:T(1024)S(1)} %select_reduce_fusion.blocks_ref, s32[1024,1]{1,0:T(8,128)S(1)} %add_select_fusion.key_ref, bf16[8,2560]{1,0:T(8,128)(2,1)S(1)} %pad.20.tail_ref, bf16[9181,2560]{1,0:T(8,128)(2,1)} %table_ref.1), custom_call_target="tpu_custom_call" | custom-call | tf_op jit(solution)/shard_map/gather_rows/pallas_call | solution.py:133
  16.0 2.3 copy-done
  18.3 59.8 %embed_exchange.1 = (bf16[128,2560]{1,0:T(8,128)(2,1)S(1)}, bf16[480,1024]{1,0:T(8,128)(2,1)S(1)}, f32[1024,288]{1,0:T(8,128)}, bf16[1024,2560]{1,0:T(8,128)(2,1)}) custom-call(bf16[1024,2560]{1,0:T(8,128)(2,1)} %copy-done, f32[1,2560]{1,0:T(1,128)S(1)} %broadcast_in_dim.71.gain, bf16[480,2560]{1,0:T(8,128)(2,1)} %bitcast.68, bf16[288,2560]{1,0:T(8,128)(2,1)S(1)} %bitcast.59), custom_call_target="tpu_custom_call" | custom-call | tf_op jit(solution)/shard_map/embed_exchange/pallas_call | solution.py:509
  78.2 0.9 copy-done.2
  79.1 0.8 copy-done.4
  79.9 1.4 multiply_reduce_fusion
  82.0 29.3 %attend_fwd.1 = (bf16[1024,256]{1,0:T(8,128)(2,1)S(1)}, bf16[320,1024]{1,0:T(8,128)(2,1)S(1)}, bf16[32,1024]{1,0:T(8,128)(2,1)S(1)}, bf16[320,1024]{1,0:T(8,128)...) custom-call(f32[1024,288]{1,0:T(8,128)} %get-tuple-element.66.lat, ...), custom_call_target="tpu_custom_call" | custom-call | tf_op jit(solution)/shard_map/attend_fwd/pallas_call | solution.py:509
  111.3 0.8 copy-done.7
  112.1 0.8 copy-done.13
  113.0 0.8 copy-done.17
  113.8 0.8 copy-done.19
  115.9 144.3 %middle.1 = (bf16[128,2560]{1,0:T(8,128)(2,1)}, bf16[128,2560]{1,0:T(8,128)(2,1)}, f32[128,2560]{1,0:T(8,128)}, f32[1,2560]{1,0:T(1,128)}, bf16[320,1024]{1,0:T(...) custom-call(bf16[320,1024]{1,0:T(8,128)(2,1)} %copy-done.13, ...), custom_call_target="tpu_custom_call" | custom-call | tf_op jit(solution)/shard_map/middle/pallas_call | solution.py:509
  260.2 1.1 copy-done.18
  261.3 1.1 copy-done.20
  262.4 1.1 copy-done.21
  263.5 0.8 copy-done.25
  264.3 0.8 copy-done.27
  265.2 0.8 copy-done.33
  266.0 0.7 copy-done.35
  266.7 15.3 %attend_bwd.1 = (bf16[480,1024]{1,0:T(8,128)(2,1)S(1)}, bf16[320,1024]{1,0:T(8,128)(2,1)S(1)}, bf16[320,1024]{1,0:T(8,128)(2,1)S(1)}, f32[32,1024]{1,0:T(8,128)S(1)}, bf16[9181,2560]{1,0:T(8,128)(2,1)}) custom-call(bf16[480,1024]{1,0:T(8,128)(2,1)S(1)} %copy-done.3, bf16[320,1024]{1,0:T(8,128)(2,1)S(1)} %copy-done.18, bf16[32,1024]{1,0:T(8,128)(2,1)S(1)} %copy-done.33, ...), custom_call_target="tpu_custom_call" | custom-call | tf_op jit(solution)/shard_map/attend_bwd/pallas_call | solution.py:292
  282.1 0.9 copy-done.9
  283.3 3.3 multiply_add_fusion.1
  287.1 1.9 fusion.6
  290.4 34.7 %back_exchange.1 = (bf16[128,2944]{1,0:T(8,128)(2,1)S(1)}, f32[1,2560]{1,0:T(1,128)S(1)}) custom-call(bf16[480,1024]{1,0:T(8,128)(2,1)S(1)} %copy-done.10, bf16[1024,384]{1,0:T(8,128)(2,1)S(1)} %pad.25.lat, bf16[480,2560]{1,0:T(8,128)(2,1)} %bitcast.69, bf16[288,2560]{1,0:T(8,128)(2,1)} %bitcast.58, bf16[128,2560]{1,0:T(8,128)(2,1)S(1)} %copy-done.5, ...), custom_call_target="tpu_custom_call" | custom-call | tf_op jit(solution)/shard_map/back_exchange/pallas_call | solution.py:509
  325.2 0.9 copy-done.11
  326.1 1.5 collective-permute-start.2
  327.6 1.1 collective-permute-start.1
  328.7 0.9 collective-permute-start
  329.6 11.2 %fusion.17 = f32[800,2560]{1,0:T(8,128)} fusion(bf16[1024,800]{1,0:T(8,128)(2,1)} %get-tuple-element.90, bf16[1024,2560]{1,0:T(8,128)(2,1)} %get-tuple-element.70.dy_hbm), kind=kOutput, calls=%fused_computation.59 | convolution fusion | flops 4194304000 | bytes 15073280 | tf_op jit(solution)/shard_map/dot_general | solution.py:23
  340.8 10.4 %fusion.18 = f32[800,2560]{1,0:T(8,128)} fusion(bf16[1024,800]{1,0:T(8,128)(2,1)S(1)} %copy-done.50, bf16[1024,2560]{1,0:T(8,128)(2,1)} %get-tuple-element.92), kind=kOutput, calls=%fused_computation.60 | convolution fusion | flops 4194304000 | bytes 15073280 | tf_op jit(solution)/shard_map/dot_general | solution.py:23
  351.3 6.7 %fusion.19 = f32[800,2560]{1,0:T(8,128)} fusion(bf16[1024,800]{1,0:T(8,128)(2,1)S(1)} %copy-done.49, bf16[1024,2560]{1,0:T(8,128)(2,1)S(1)} %bitcast.87), kind=kOutput, calls=%fused_computation.61 | convolution fusion | flops 4194304000 | bytes 15073280 | tf_op jit(solution)/shard_map/dot_general | solution.py:23
  358.4 6.9 %fusion.20 = f32[480,2560]{1,0:T(8,128)} fusion(bf16[480,1024]{1,0:T(8,128)(2,1)S(1)} %copy-done.10, bf16[1024,2560]{1,0:T(8,128)(2,1)} %get-tuple-element.95), kind=kOutput, calls=%fused_computation.62 | convolution fusion | flops 2516582400 | bytes 11141120 | tf_op jit(solution)/shard_map/dot_general | solution.py:23
  366.6 1.1 collective-permute-start.8
  367.7 6.2 %fusion.21 = f32[320,2560]{1,0:T(8,128)} fusion(bf16[320,1024]{1,0:T(8,128)(2,1)S(1)} %copy-done.14, bf16[1024,2560]{1,0:T(8,128)(2,1)} %get-tuple-element.102), kind=kOutput, calls=%fused_computation.63 | convolution fusion | flops 1677721600 | bytes 9175040 | tf_op jit(solution)/shard_map/dot_general | solution.py:23
  374.0 6.7 %table_grad.1 = (bf16[9181,2560]{1,0:T(8,128)(2,1)}, bf16[8,2560]{1,0:T(8,128)(2,1)S(1)}, bf16[1024,384]{1,0:T(8,128)(2,1)S(1)}) custom-call(s32[1]{0:T(128)} %bitcast.2.count_ref, s32[1024]{0:T(1024)S(1)} %copy-done.37, s32[1,1024]{1,0:T(1,128)S(1)} %bitcast.67, bf16[9181,2560]{1,0:T(8,128)(2,1)} %get-tuple-element.77.zeros_ref, ...), custom_call_target="tpu_custom_call", output_to_operand_aliasing={{0}: (3, {})} | custom-call | tf_op jit(solution)/shard_map/table_grad/pallas_call | solution.py:193
  380.7 3.4 fusion.7
  384.1 0.9 collective-permute-start.9
  385.6 1.1 fusion.22
  386.7 1.1 fusion.23
  389.1 0.8 copy.63
  (149 shorter events, 8.9 us)
Async XLA Ops:
  0.7 8.2 %copy-start.48 = (f32[16]{0:T(128)}, f32[16]{0:T(128)S(1)}, u32[]{:S(2)}) copy-start(f32[16]{0:T(128)S(1)} %multiply_power_fusion) | copy-start | bytes 196
  1.4 16.9 %copy-start.30 = (f32[1,2560]{1,0:T(1,128)}, f32[1,2560]{1,0:T(1,128)S(1)}, u32[]{:S(2)}) copy-start(f32[1,2560]{1,0:T(1,128)S(1)} %broadcast_in_dim.71.gain) | copy-start | bytes 30724
  6.0 9.9 %copy-start.36 = (s32[1024]{0:T(1024)}, s32[1024]{0:T(1024)S(1)}, u32[]{:S(2)}) copy-start(s32[1024]{0:T(1024)S(1)} %select_reduce_fusion.blocks_ref) | copy-start | bytes 12292
  8.7 73.3 %copy-start.24 = (f32[16,1024]{1,0:T(8,128)}, f32[16,1024]{1,0:T(8,128)S(1)}, u32[]{:S(2)}) copy-start(f32[16,1024]{1,0:T(8,128)S(1)} %get-tuple-element.132.sin_ref) | copy-start | bytes 196612
  8.7 73.3 %copy-start.26 = (f32[16,1024]{1,0:T(8,128)}, f32[16,1024]{1,0:T(8,128)S(1)}, u32[]{:S(2)}) copy-start(f32[16,1024]{1,0:T(8,128)S(1)} %get-tuple-element.133.cos_ref) | copy-start | bytes 196612
  9.2 9.1 %copy-start.1 = (bf16[2560,288]{0,1:T(8,128)(2,1)S(1)}, bf16[2560,288]{0,1:T(8,128)(2,1)}, u32[]{:S(2)}) copy-start(bf16[2560,288]{0,1:T(8,128)(2,1)} %param.17) | copy-start | bytes 4423684
  15.9 2.4 copy-start
  18.3 63.7 %copy-start.6 = (bf16[1,128,2560]{2,1,0:T(8,128)(2,1)S(1)}, bf16[1,128,2560]{2,1,0:T(8,128)(2,1)}, u32[]{:S(2)}) copy-start(bf16[1,128,2560]{2,1,0:T(8,128)(2,1)} %param.27) | copy-start | bytes 1966084
  18.3 63.7 %copy-start.22 = (bf16[256,5,64]{0,2,1:T(8,128)(2,1)S(1)}, bf16[256,5,64]{0,2,1:T(8,128)(2,1)}, u32[]{:S(2)}) copy-start(bf16[256,5,64]{0,2,1:T(8,128)(2,1)} %param.19) | copy-start | bytes 491524
  18.3 63.7 %copy-start.28 = (bf16[256,5,64]{0,2,1:T(8,128)(2,1)S(1)}, bf16[256,5,64]{0,2,1:T(8,128)(2,1)}, u32[]{:S(2)}) copy-start(bf16[256,5,64]{0,2,1:T(8,128)(2,1)} %param.20) | copy-start | bytes 491524
  18.3 63.7 %copy-start.38 = (f32[256]{0:T(256)S(1)}, f32[256]{0:T(256)}, u32[]{:S(2)}) copy-start(f32[256]{0:T(256)} %param.18) | copy-start | bytes 3076
  81.4 34.5 %copy-start.43 = (f32[1024]{0:T(1024)}, f32[1024]{0:T(1024)S(1)}, u32[]{:S(2)}) copy-start(f32[1024]{0:T(1024)S(1)} %multiply_reduce_fusion) | copy-start | bytes 12292
  115.9 144.3 %copy-start.3 = (bf16[480,1024]{1,0:T(8,128)(2,1)S(1)}, bf16[480,1024]{1,0:T(8,128)(2,1)}, u32[]{:S(2)}) copy-start(bf16[480,1024]{1,0:T(8,128)(2,1)} %copy-done.2) | copy-start | bytes 2949124
  260.2 1.1 copy-start.18
  266.7 19.8 %copy-start.23 = (bf16[256,5,64]{0,2,1:T(8,128)(2,1)S(1)}, bf16[256,5,64]{0,2,1:T(8,128)(2,1)}, u32[]{:S(2)}) copy-start(bf16[256,5,64]{0,2,1:T(8,128)(2,1)} %param.19) | copy-start | bytes 491524
  266.7 20.3 %copy-start.29 = (bf16[256,5,64]{0,2,1:T(8,128)(2,1)S(1)}, bf16[256,5,64]{0,2,1:T(8,128)(2,1)}, u32[]{:S(2)}) copy-start(bf16[256,5,64]{0,2,1:T(8,128)(2,1)} %param.20) | copy-start | bytes 491524
  266.7 20.4 %copy-start.39 = (f32[256]{0:T(256)S(1)}, f32[256]{0:T(256)}, u32[]{:S(2)}) copy-start(f32[256]{0:T(256)} %param.18) | copy-start | bytes 3076
  283.0 6.0 %copy-start.15 = (bf16[320,1024]{1,0:T(8,128)(2,1)}, bf16[320,1024]{1,0:T(8,128)(2,1)S(1)}, u32[]{:S(2)}) copy-start(bf16[320,1024]{1,0:T(8,128)(2,1)S(1)} %get-tuple-element.114) | copy-start | bytes 1966084
  283.0 4.1 %copy-start.45 = (f32[1024]{0:T(1024)S(1)}, f32[1024]{0:T(1024)}, u32[]{:S(2)}) copy-start(f32[1024]{0:T(1024)} %fusion.14) | copy-start | bytes 12292
  283.2 5.8 %copy-start.44 = (f32[1024]{0:T(1024)S(1)}, f32[1024]{0:T(1024)}, u32[]{:S(2)}) copy-start(f32[1024]{0:T(1024)} %copy-done.43) | copy-start | bytes 12292
  283.3 6.0 %copy-start.40 = (f32[256]{0:T(256)S(1)}, f32[256]{0:T(256)}, u32[]{:S(2)}) copy-start(f32[256]{0:T(256)} %param.18) | copy-start | bytes 3076
  283.3 6.0 %copy-start.41 = (f32[1024,288]{1,0:T(8,128)S(1)}, f32[1024,288]{1,0:T(8,128)}, u32[]{:S(2)}) copy-start(f32[1024,288]{1,0:T(8,128)} %get-tuple-element.66.lat) | copy-start | bytes 3538948
  289.0 1.1 copy-start.5
  289.0 1.4 copy-start.10
  289.0 1.4 copy-start.31
  326.1 39.3 %collective-permute-start.3 = (bf16[128,2944]{1,0:T(8,128)(2,1)}, bf16[128,2944]{1,0:T(8,128)(2,1)S(1)}, u32[]{:S(2)}, u32[]{:S(2)}) collective-permute-start(bf16[128,2944]{1,0:T(8,128)(2,1)} %copy-done.11), channel_id=1, source_target_pairs={{0,1},{1,0},{2,3},{3,2},{4,5},{5,4},{6,7},{7,6}} | collective-permute-start | bytes 2261000 | tf_op jit(solution)/shard_map/ppermute | solution.py:301
  326.1 39.3 %collective-permute-start.2 = (bf16[128,2944]{1,0:T(8,128)(2,1)}, bf16[128,2944]{1,0:T(8,128)(2,1)}, u32[]{:S(2)}, u32[]{:S(2)}) collective-permute-start(bf16[128,2944]{1,0:T(8,128)(2,1)} %copy-done.11), channel_id=1, source_target_pairs={{0,6},{1,7},{2,4},{3,5},{4,2},{5,3},{6,0},{7,1}} | collective-permute-start | bytes 2261000 | tf_op jit(solution)/shard_map/ppermute | solution.py:301
  327.6 37.8 %collective-permute-start.1 = (bf16[128,2944]{1,0:T(8,128)(2,1)}, bf16[128,2944]{1,0:T(8,128)(2,1)}, u32[]{:S(2)}, u32[]{:S(2)}) collective-permute-start(bf16[128,2944]{1,0:T(8,128)(2,1)} %copy-done.11), channel_id=1, source_target_pairs={{0,4},{1,5},{2,6},{3,7},{4,0},{5,1},{6,2},{7,3}} | collective-permute-start | bytes 2261000 | tf_op jit(solution)/shard_map/ppermute | solution.py:301
  328.7 36.7 %collective-permute-start = (bf16[128,2944]{1,0:T(8,128)(2,1)}, bf16[128,2944]{1,0:T(8,128)(2,1)}, u32[]{:S(2)}, u32[]{:S(2)}) collective-permute-start(bf16[128,2944]{1,0:T(8,128)(2,1)} %copy-done.11), channel_id=1, source_target_pairs={{0,2},{1,3},{2,0},{3,1},{4,6},{5,7},{6,4},{7,5}} | collective-permute-start | bytes 2261000 | tf_op jit(solution)/shard_map/ppermute | solution.py:301
  329.6 35.7 %collective-permute-start.4 = (f32[5376]{0:T(1024)S(1)}, f32[5376]{0:T(1024)S(1)}, u32[]{:S(2)}, u32[]{:S(2)}) collective-permute-start(f32[5376]{0:T(1024)S(1)} %pad_maximum_fusion), channel_id=1, source_target_pairs={{0,1},{1,0},{2,3},{3,2},{4,5},{5,4},{6,7},{7,6}} | collective-permute-start | bytes 64520 | tf_op jit(solution)/shard_map/ppermute | solution.py:301
  329.6 11.2 %copy-start.50 = (bf16[1024,800]{1,0:T(8,128)(2,1)S(1)}, bf16[1024,800]{1,0:T(8,128)(2,1)}, u32[]{:S(2)}) copy-start(bf16[1024,800]{1,0:T(8,128)(2,1)} %get-tuple-element.91) | copy-start | bytes 4915204
  329.6 21.6 %slice-start.2 = ((s8[5242880]{0:T(1024)(128)(4,1)}), s8[4194304]{0:T(1024)(128)(4,1)S(1)}, s32[]{:S(2)}) async-start(s8[5242880]{0:T(1024)(128)(4,1)} %bitcast.86), calls=%async_computation.2 | async-start | bytes 8388608
  340.8 10.4 %slice-start.3 = ((s8[5242880]{0:T(1024)(128)(4,1)}), s8[1048576]{0:T(1024)(128)(4,1)S(1)}, s32[]{:S(2)}) async-start(s8[5242880]{0:T(1024)(128)(4,1)} %bitcast.86), calls=%async_computation.3 | async-start | bytes 2097152
  340.8 10.4 %copy-start.49 = (bf16[1024,800]{1,0:T(8,128)(2,1)S(1)}, bf16[1024,800]{1,0:T(8,128)(2,1)}, u32[]{:S(2)}) copy-start(bf16[1024,800]{1,0:T(8,128)(2,1)} %get-tuple-element.93) | copy-start | bytes 4915204
  351.3 6.7 %copy-start.47 = (s32[1024]{0:T(1024)S(1)}, s32[1024]{0:T(1024)}, u32[]{:S(2)}) copy-start(s32[1024]{0:T(1024)} %get-tuple-element.128) | copy-start | bytes 12292
  358.4 9.3 %copy-start.14 = (bf16[320,1024]{1,0:T(8,128)(2,1)S(1)}, bf16[320,1024]{1,0:T(8,128)(2,1)}, u32[]{:S(2)}) copy-start(bf16[320,1024]{1,0:T(8,128)(2,1)} %copy-done.13) | copy-start | bytes 1966084
  365.4 8.5 %collective-permute-start.5 = (bf16[128,2944]{1,0:T(8,128)(2,1)}, bf16[128,2944]{1,0:T(8,128)(2,1)S(1)}, u32[]{:S(2)}, u32[]{:S(2)}) collective-permute-start(bf16[128,2944]{1,0:T(8,128)(2,1)} %collective-permute-done.refs_1_), channel_id=1, source_target_pairs={{0,1},{1,0},{2,3},{3,2},{4,5},{5,4},{6,7},{7,6}} | collective-permute-start | bytes 2261000 | tf_op jit(solution)/shard_map/ppermute | solution.py:301
  365.9 8.0 %collective-permute-start.6 = (bf16[128,2944]{1,0:T(8,128)(2,1)}, bf16[128,2944]{1,0:T(8,128)(2,1)S(1)}, u32[]{:S(2)}, u32[]{:S(2)}) collective-permute-start(bf16[128,2944]{1,0:T(8,128)(2,1)} %collective-permute-done.1.refs_2_), channel_id=1, source_target_pairs={{0,1},{1,0},{2,3},{3,2},{4,5},{5,4},{6,7},{7,6}} | collective-permute-start | bytes 2261000 | tf_op jit(solution)/shard_map/ppermute | solution.py:301
  365.9 8.0 %collective-permute-start.7 = (bf16[128,2944]{1,0:T(8,128)(2,1)}, bf16[128,2944]{1,0:T(8,128)(2,1)S(1)}, u32[]{:S(2)}, u32[]{:S(2)}) collective-permute-start(bf16[128,2944]{1,0:T(8,128)(2,1)} %collective-permute-done.2.refs_3_), channel_id=1, source_target_pairs={{0,1},{1,0},{2,3},{3,2},{4,5},{5,4},{6,7},{7,6}} | collective-permute-start | bytes 2261000 | tf_op jit(solution)/shard_map/ppermute | solution.py:301
  366.6 7.3 %collective-permute-start.8 = (f32[5376]{0:T(1024)S(1)}, f32[5376]{0:T(1024)S(1)}, u32[]{:S(2)}, u32[]{:S(2)}) collective-permute-start(f32[5376]{0:T(1024)S(1)} %add.152), channel_id=1, source_target_pairs={{0,2},{1,3},{2,0},{3,1},{4,6},{5,7},{6,4},{7,5}} | collective-permute-start | bytes 64520 | tf_op jit(solution)/shard_map/ppermute | solution.py:301
  367.7 6.3 %copy-start.12 = (bf16[128,2944]{1,0:T(8,128)(2,1)S(1)}, bf16[128,2944]{1,0:T(8,128)(2,1)}, u32[]{:S(2)}) copy-start(bf16[128,2944]{1,0:T(8,128)(2,1)} %copy-done.11) | copy-start | bytes 2260996
  367.7 6.3 %copy-start.37 = (s32[1024]{0:T(1024)S(1)}, s32[1024]{0:T(1024)}, u32[]{:S(2)}) copy-start(s32[1024]{0:T(1024)} %copy-done.36) | copy-start | bytes 12292
  367.7 13.0 %slice-start = ((s8[5242880]{0:T(1024)(128)(4,1)}), s8[4194304]{0:T(1024)(128)(4,1)S(1)}, s32[]{:S(2)}) async-start(s8[5242880]{0:T(1024)(128)(4,1)} %bitcast.84), calls=%async_computation | async-start | bytes 8388608
  374.0 6.7 %slice-start.1 = ((s8[5242880]{0:T(1024)(128)(4,1)}), s8[1048576]{0:T(1024)(128)(4,1)S(1)}, s32[]{:S(2)}) async-start(s8[5242880]{0:T(1024)(128)(4,1)} %bitcast.84), calls=%async_computation.1 | async-start | bytes 2097152
  380.7 5.0 %copy-start.8 = (bf16[1024,256]{1,0:T(8,128)(2,1)S(1)}, bf16[1024,256]{1,0:T(8,128)(2,1)}, u32[]{:S(2)}) copy-start(bf16[1024,256]{1,0:T(8,128)(2,1)} %copy-done.7) | copy-start | bytes 1572868
  380.7 6.0 %copy-start.16 = (bf16[320,1024]{1,0:T(8,128)(2,1)S(1)}, bf16[320,1024]{1,0:T(8,128)(2,1)}, u32[]{:S(2)}) copy-start(bf16[320,1024]{1,0:T(8,128)(2,1)} %copy-done.15) | copy-start | bytes 1966084
  380.7 8.4 %copy-start.42 = (bf16[128,2560]{1,0:T(8,128)(2,1)S(1)}, bf16[128,2560]{1,0:T(8,128)(2,1)}, u32[]{:S(2)}) copy-start(bf16[128,2560]{1,0:T(8,128)(2,1)} %get-tuple-element.71) | copy-start | bytes 1966084
  384.1 3.8 collective-permute-start.9
  (17 other events, 14.4 us)

commit v6 on v5

--- a/solution.py
+++ b/solution.py
@@ -16,6 +16,7 @@
 GB = 64
 GR = GB * 8
 LIMIT = 40 << 20
+ALL = 63
 QB = 256
 
 
@@ -293,7 +294,7 @@
         attn_bwd_body, grid=(heads,), in_specs=ins + [lse_spec, per(vd)], out_specs=[per(qd), per(nope), per(vd), one(rope), pl.BlockSpec(memory_space=pl.ANY)],
         out_shape=[jax.ShapeDtypeStruct(q.shape, BF16), jax.ShapeDtypeStruct(kn.shape, BF16), jax.ShapeDtypeStruct(v.shape, BF16), jax.ShapeDtypeStruct(kp.shape, F32), jax.ShapeDtypeStruct(table, BF16)],
         scratch_shapes=[VM((qd, seq), F32), VM((vd, seq), F32), VM((ZR, table[1]), BF16), pltpu.SemaphoreType.DMA((-(-table[0] // ZR),))],
-        compiler_params=pltpu.CompilerParams(vmem_limit_bytes=LIMIT), name='attend_bwd',
+        compiler_params=pltpu.CompilerParams(vmem_limit_bytes=ALL << 20), name='attend_bwd',
     )(q, kn, kp, v, cos_t, sin_t, lse, do)
 
 
@@ -392,9 +393,11 @@
                 self.bufs[a][1][k, :, c0:c0 + cn] = self.chip_sum(j, i).astype(BF16)
                 self.hop1[k, i].start()
 
-    def relay(self):
+    def relay(self, halves=(0, 1)):
         for i in self.order:
             h, a, c0, cn = self.pieces[i]
+            if h not in halves:
+                continue
             own = self.chip_sum(2 - h, i)
             self.hop1[1, i].wait_recv()
             self.bufs[a][3][:, c0:c0 + cn] = (own + self.bufs[a][2][1, :, c0:c0 + cn].astype(F32)).astype(BF16)
@@ -424,7 +427,7 @@
         self.relay()
         self.land(accs)
 
-    def all_gather(self, fulls, scratch, arrive, slow=False):
+    def all_gather(self, fulls, scratch, arrive, blocks=(1, 2, 3), known=False):
         os_, xr, fs, fr, ps, pr = scratch
         half0 = [i for i in self.order if self.pieces[i][0] == 0]
         half1 = [i for i in self.order if self.pieces[i][0] == 1]
@@ -441,44 +444,47 @@
         diag = [to(i, 3, fs.at[i], fr.at[i], self.xn) for i in self.order]
         give = [[to(i, j, ps.at[j, i], pr.at[j, i], self.pn) for i in self.order] for j in range(4)]
         take = [[to(i, j, ps.at[j, i], pr.at[j, i], self.pn, self.theirs) for i in self.order] for j in range(4)]
-        for i0, i1 in zip(half0, half1):
-            own[0][i1].start()
-            own[1][i0].start()
-        for i0, i1 in zip(half0, half1):
-            own[0][i0].start()
-            own[1][i1].start()
-        for cp in give[0]:
-            cp.start()
-        for cp in take[0]:
-            cp.wait_recv()
+        pairs = list(zip(half0, half1))
+        sent = fwd + [cp for g in give for cp in g]
+
+        def start(copies):
+            for cp in copies:
+                cp.start()
+
+        def landed(copies):
+            for cp in copies:
+                cp.wait_recv()
+
+        if not known:
+            sent += own[0] + own[1]
+            for i0, i1 in pairs:
+                start((own[0][i1], own[1][i0]))
+            for i0, i1 in pairs:
+                start((own[0][i0], own[1][i1]))
+        start(give[0])
+        if known:
+            start(fwd + give[1] + give[2])
+        landed(take[0])
         arrive(0)
-        for i0, i1 in zip(half0, half1):
-            from_n[1][i0].wait_recv()
-            fwd[i0].start()
-            give[2][i0].start()
-            from_n[0][i1].wait_recv()
-            fwd[i1].start()
-            give[1][i1].start()
-        for i0, i1 in zip(half0, half1):
-            from_n[1][i1].wait_recv()
-            give[2][i1].start()
-            from_n[0][i0].wait_recv()
-            give[1][i0].start()
-        def diagonal():
-            for i in self.order:
-                diag[i].wait_recv()
-                give[3][i].start()
-
-        for j in (1, 2):
-            for cp in take[j]:
-                cp.wait_recv()
+        if not known:
+            for i0, i1 in pairs:
+                from_n[1][i0].wait_recv()
+                start((fwd[i0], give[2][i0]))
+                from_n[0][i1].wait_recv()
+                start((fwd[i1], give[1][i1]))
+            for i0, i1 in pairs:
+                from_n[1][i1].wait_recv()
+                give[2][i1].start()
+                from_n[0][i0].wait_recv()
+                give[1][i0].start()
+        for j in blocks:
+            if j == 3:
+                for i in self.order:
+                    diag[i].wait_recv()
+                    give[3][i].start()
+            landed(take[j])
             arrive(j)
-            if slow == (j == 1):
-                diagonal()
-        for cp in take[3]:
-            cp.wait_recv()
-        arrive(3)
-        for cp in own[0] + own[1] + fwd + [c for g in give for c in g]:
+        for cp in sent:
             cp.wait_send()
 
 
@@ -542,11 +548,12 @@
         cp.wait()
 
 
-def attn_body(lat, g_kv, wuk, wuv, q_ref, cos_ref, sin_ref, dy_ref, c_ref, kn_ref, kp_ref, v_ref, o_ref, lse_ref, dy_out, dyf, dsem, *scratch):
+def attn_body(lat, g_kv, wuk, wuv, q_ref, cos_ref, sin_ref, dy_ref, dyx_ref, dyy_ref, c_ref, kn_ref, kp_ref, v_ref, o_ref, lse_ref, dy_out, dyf, dsem, *scratch):
     ex = Exchange([dyf.shape[1]], MAIN)
     ex.place(dy_ref.shape[0])
     ex.enter()
-    dyf[ex.mine[0], :] = dy_ref[...]
+    for rows, ref in zip(ex.mine, (dy_ref, dyx_ref, dyy_ref)):
+        dyf[rows, :] = ref[...]
     lora, half, heads = c_ref.shape[1], cos_ref.shape[0], lse_ref.shape[0]
     per = lambda ref, h: ref.at[pl.ds(h * (ref.shape[0] // heads), ref.shape[0] // heads), :]
 
@@ -566,7 +573,7 @@
         for h in range(heads):
             attn_fwd_body(per(q_ref, h), per(kn_ref, h), kp_ref, per(v_ref, h), cos_ref, sin_ref, per(o_ref, h), lse_ref.at[pl.ds(h, 1)])
 
-    ex.all_gather([dyf], scratch, arrive)
+    ex.all_gather([dyf], scratch, arrive, known=True)
     for cp in save:
         cp.wait()
 
@@ -582,7 +589,8 @@
     wg, wu, wd = (wall.at[pl.ds(k * ffn, ffn), :] for k in range(3))
     dfull = wall.at[pl.ds(0, part.shape[0]), :]
     loads = [pltpu.make_async_copy(a, b, wsem.at[k]) for k, (a, b) in enumerate(((wg_hbm, wg), (wu_hbm, wu), (wd_hbm, wd)))]
-    dy_in = [pltpu.make_async_copy(dy_hbm.at[ex.chip[j], :], dyb.at[j % 2], dsem.at[j % 2]) for j in range(4)]
+    turns = (0, 1, 3, 2)
+    dy_in = [pltpu.make_async_copy(dy_hbm.at[ex.chip[j], :], dyb.at[k % 2], dsem.at[k % 2]) for k, j in enumerate(turns)]
     for cp in loads + dy_in[:2]:
         cp.start()
     rs = 2 * NRS
@@ -598,27 +606,27 @@
     h_ref[...] = h
     z[ex.mine[0], :] = norm_rows(h.astype(F32), gain[...]).astype(BF16)
     save_z, save_d = ex.saver(z, z_out, zsem), ex.saver(dfull, dfull_out, fsem)
-    save_a = [[pltpu.make_async_copy(act.at[j % 2, k], dst.at[ex.chip[j], :], asem.at[j % 2, k]) for k, dst in enumerate((hid_out, dgate_out, dup_out))]
-              for j in range(4)]
-
-    def mlp(j):
+    save_a = [[pltpu.make_async_copy(act.at[t % 2, k], dst.at[ex.chip[j], :], asem.at[t % 2, k]) for k, dst in enumerate((hid_out, dgate_out, dup_out))]
+              for t, j in enumerate(turns)]
+
+    def mlp(j, t):
         rows = ex.chip[j]
         gate, up = nt(z[rows, :], wg[...]), nt(z[rows, :], wu[...])
         sig = jax.nn.sigmoid(gate)
         hid = (gate * sig * up).astype(BF16)
-        dh = nt(dyb[j % 2], wd[...])
+        dh = nt(dyb[t % 2], wd[...])
         dup = (dh * gate * sig).astype(BF16)
         dgate = (dh * up * sig * (1.0 + gate * (1.0 - sig))).astype(BF16)
-        if j > 1:
-            for cp in save_a[j - 2]:
+        if t > 1:
+            for cp in save_a[t - 2]:
                 cp.wait()
         for k, value in enumerate((hid, dgate, dup)):
-            act[j % 2, k] = value
+            act[t % 2, k] = value
         for c in range(0, width, COLS):
             cols = slice(c, c + COLS)
             part[rows, cols] = (nn(dgate, wg[:, cols]) + nn(dup, wu[:, cols])).astype(BF16)
             ypart[rows, cols] = nn(hid, wd[:, cols]).astype(BF16)
-        for cp in save_a[j]:
+        for cp in save_a[t]:
             cp.start()
 
     def arrive_z(j):
@@ -627,25 +635,25 @@
             for cp in loads:
                 cp.wait()
         save_z[j].start()
-        dy_in[j].wait()
-        mlp(j)
-        if j < 2:
-            dy_in[j + 2].start()
-        ex.ready(j)
-        ey.ready(j)
-        if j == 2:
-            ex.push(1)
-            ey.push(1)
-        if j == 3:
-            ex.push(2)
-            ex.push(3)
-
-    ex.all_gather([z], scratch[rs:rs + NAG], arrive_z, slow=True)
-    ex.relay()
-    ey.push(2)
-    ey.push(3)
+        for e in (ex, ey):
+            if j == 3:
+                e.push(1)
+            if j == 2:
+                e.push(3)
+        k = turns.index(j)
+        dy_in[k].wait()
+        mlp(j, k)
+        if k < 2:
+            dy_in[k + 2].start()
+        for e in (ex, ey):
+            e.ready(j)
+
+    ex.all_gather([z], scratch[rs:rs + NAG], arrive_z, blocks=turns[1:])
+    for e in (ex, ey):
+        e.relay((1,))
+        e.push(2)
+        e.relay((0,))
     ex.land([acc])
-    ey.relay()
     dx, dgain_ref[...] = norm_rows_vjp(h_ref[...].astype(F32), gain[...], acc[...])
     dres = dyl_ref[...].astype(F32) + dx
     dres_ref[...] = dres
@@ -696,14 +704,15 @@
     saved = partb + [dma((4,))]
     loc, fullb = shape((local, width), BF16), shape((seq, width), BF16)
     ga, gm = g_attn[None, :], g_mlp[None, :]
+    rows, dy_near = lax.optimization_barrier((rows, [shift(d_out, XBIT), shift(d_out, YBIT)]))
     embedded, query, latent, x_attn = exchange_call(
         embed_body, 'embed_exchange', 1, [rows, ga, w_q, w_dkv], [loc, shape((w_q.shape[0], seq), BF16), shape((seq, latw), F32), fullb], saved + main, out=1)
     cos_t, sin_t = (t.T for t in rope_tables(seq, latw - lora))
     nq, nk, nv = w_q.shape[0], w_uk.shape[0], w_uv.shape[0]
     c_kv, k_nope, k_pe_t, value, attn_out, lse, dy_full = exchange_call(
-        attn_body, 'attend_fwd', 2, [latent, g_kv[None, :], w_uk, w_uv, query, cos_t, sin_t, d_out],
+        attn_body, 'attend_fwd', 2, [latent, g_kv[None, :], w_uk, w_uv, query, cos_t, sin_t, d_out, *dy_near],
         [shape((seq, lora), BF16), shape((nk, seq), BF16), shape((latw - lora, seq), BF16), shape((nv, seq), BF16), shape((nv, seq), BF16),
-         shape((heads, 1, seq), F32), fullb], saved + one.ag_scratch(), out=1)
+         shape((heads, 1, seq), F32), fullb], saved + one.ag_scratch(), out=1, limit=ALL)
     kv_pull = jax.vjp(kv_prep, latent, g_kv)[1]
     ffn = w_gate.shape[0]
     act = shape((seq, ffn), BF16)
@@ -712,7 +721,7 @@
         [loc, loc, shape((local, width), F32), shape((1, width), F32), shape((w_o.shape[0], seq), BF16), fullb, act, act, act, fullb],
         [VM((3 * ffn, width), BF16), VM((2, seq // 4, width), BF16), VM((2, 3, seq // 4, ffn), BF16)] + partb * 3
         + [VM((local, width), F32), dma((3,)), dma((2,)), dma((2, 3)), dma((4,)), dma((4,))]
-        + one.rs_scratch(local) * 2 + one.ag_scratch() * 2, far=4, out=5, limit=63)
+        + one.rs_scratch(local) * 2 + one.ag_scratch() * 2, far=4, out=5, limit=ALL)
     d_query, d_knope, d_value, d_kpe, table0 = attend_bwd(query, k_nope, k_pe_t, value, cos_t, sin_t, lse, d_attn_out, heads, (vocab, width))
     d_ckv = (tn(d_knope, w_uk) + tn(d_value, w_uv)).astype(BF16)
     d_latent, dg_kv = kv_pull((d_ckv, d_kpe.T.astype(BF16)))

time: 396 us -> 374 us (0.944)
  local copies, waits for them, and re-layouts: 24.7 us -> 11.9 us
  matrix products: 49.3 us -> 40.2 us
  Pallas kernels: 297 us -> 290 us
  starting transfers between devices: 6.59 us -> 11 us
    pallas_call x4, Pallas kernels: 268 us -> 251 us  [exchange_call(): pl.pallas_call(body, out_shape=out_shape, in_specs=[vmem] * (len(ins) - f...]
    unnamed x118 -> x64, local copies, waits for them, and re-layouts: 19 us -> 6.19 us
    pallas_call x1, Pallas kernels: 15.3 us -> 26.1 us  [attend_bwd(): pl.pallas_call(attn_bwd_body, grid=(heads,), in_specs=ins + [lse_spec, pe...]
    dot_general x10, matrix products: 49.3 us -> 40.2 us  [mm(): lax.dot_general(lhs, rhs, (((lc,), (rc,)), ((), ())), preferred_element_t...]
    ppermute x10 -> x12, starting transfers between devices: 6.59 us -> 11 us  [shift(): return lax.ppermute(x, 'tp', [(d, d ^ bit) for d in range(8)])]
  transfers between devices with their start and end apart: 10 -> 12, of which waited for: 1 -> 1; matrix products, arithmetic and copies ran while one was open for 11% -> 12% of each run, Pallas kernels for 0% -> 2%
where the time goes in v6:
time: 374 us; the launch traced here: 369 us
  Pallas kernels  290 us (78%)
  matrix products  40.2 us (11%)
  local copies, waits for them, and re-layouts  11.9 us (3%)
  starting transfers between devices  11 us (3%)
  other arithmetic  10.8 us (3%)
  waiting for transfers between devices  3.76 us (1%)
    pallas_call x4, Pallas kernels, exchange_call(): pl.pallas_call(body, out_shape=out_shape, in_specs=[vmem] * (len(ins) - f...  251 us
    dot_general x10, matrix products, mm(): lax.dot_general(lhs, rhs, (((lc,), (rc,)), ((), ())), preferred_element_t...  40.2 us
    pallas_call x1, Pallas kernels, attend_bwd(): pl.pallas_call(attn_bwd_body, grid=(heads,), in_specs=ins + [lse_spec, pe...  26.1 us
    ppermute x12, starting transfers between devices, shift(): return lax.ppermute(x, 'tp', [(d, d ^ bit) for d in range(8)])  11 us
  transfers between devices with their start and end apart: 12, of which 1 were waited for; matrix products, arithmetic and copies ran while one was open for 12% of the time, Pallas kernels for 2%

profile of v6, /device:TPU:0, one launch (start us, length us, event | category | flops | bytes accessed | tf_op | source)
XLA Modules:
  0.0 368.6 jit_solution(18069703719347661259)
XLA Ops:
  0.6 3.4 collective-permute-start.1
  4.0 1.5 collective-permute-start
  5.5 0.7 broadcast_in_dim.71.gain
  6.3 1.3 broadcast_in_dim.73.gain
  7.6 0.7 broadcast_select_fusion
  8.3 0.8 select_reduce_fusion.1
  9.1 0.8 convert_reduce_fusion
  10.0 0.9 select_reduce_fusion.blocks_ref
  10.9 0.6 add_select_fusion.1
  11.5 0.8 slice.21
  12.3 0.3 copy.45
  13.4 6.7 %gather_rows.1.part = bf16[1024,2560]{1,0:T(8,128)(2,1)S(1)} custom-call(s32[1]{0:T(128)} %bitcast.2.count_ref, s32[1024]{0:T(1024)S(1)} %select_reduce_fusion.blocks_ref, s32[1024,1]{1,0:T(8,128)S(1)} %add_select_fusion.key_ref, bf16[8,2560]{1,0:T(8,128)(2,1)S(1)} %pad.20.tail_ref, bf16[9181,2560]{1,0:T(8,128)(2,1)} %table_ref.1), custom_call_target="tpu_custom_call" | custom-call | tf_op jit(solution)/shard_map/gather_rows/pallas_call | solution.py:134
  20.1 2.3 copy-done
  22.7 1.0 fusion.11
  23.7 57.0 %embed_exchange.1 = (bf16[128,2560]{1,0:T(8,128)(2,1)S(1)}, bf16[480,1024]{1,0:T(8,128)(2,1)S(1)}, f32[1024,288]{1,0:T(8,128)}, bf16[1024,2560]{1,0:T(8,128)(2,1)}) custom-call(bf16[1024,2560]{1,0:T(8,128)(2,1)} %copy-done, f32[1,2560]{1,0:T(1,128)S(1)} %broadcast_in_dim.71.gain, bf16[480,2560]{1,0:T(8,128)(2,1)} %bitcast.61, bf16[288,2560]{1,0:T(8,128)(2,1)S(1)} %bitcast.59), custom_call_target="tpu_custom_call" | custom-call | tf_op jit(solution)/shard_map/embed_exchange/pallas_call | solution.py:515
  80.8 0.9 copy-done.2
  81.8 0.8 copy-done.3
  82.6 1.4 multiply_reduce_fusion
  84.0 19.1 %attend_fwd.1 = (bf16[1024,256]{1,0:T(8,128)(2,1)}, bf16[320,1024]{1,0:T(8,128)(2,1)}, bf16[32,1024]{1,0:T(8,128)(2,1)}, bf16[320,1024]{1,0:T(8,128)(2,1)}, bf16...) custom-call(f32[1024,288]{1,0:T(8,128)} %get-tuple-element.70.lat, f32[1,256]{1,0:T(1,128)} %bitcast.85, ...), custom_call_target="tpu_custom_call" | custom-call | tf_op jit(solution)/shard_map/attend_fwd/pallas_call | solution.py:515
  103.2 140.3 %middle.1 = (bf16[128,2560]{1,0:T(8,128)(2,1)}, bf16[128,2560]{1,0:T(8,128)(2,1)}, f32[128,2560]{1,0:T(8,128)}, f32[1,2560]{1,0:T(1,128)}, bf16[320,1024]{1,0:T(...) custom-call(bf16[320,1024]{1,0:T(8,128)(2,1)} %get-tuple-element.107, ...), custom_call_target="tpu_custom_call" | custom-call | tf_op jit(solution)/shard_map/middle/pallas_call | solution.py:515
  243.5 26.1 %attend_bwd.1 = (bf16[480,1024]{1,0:T(8,128)(2,1)}, bf16[320,1024]{1,0:T(8,128)(2,1)}, bf16[320,1024]{1,0:T(8,128)(2,1)}, f32[32,1024]{1,0:T(8,128)}, bf16[9181,2560]{1,0:T(8,128)(2,1)}) custom-call(bf16[480,1024]{1,0:T(8,128)(2,1)} %copy-done.2, bf16[320,1024]{1,0:T(8,128)(2,1)} %get-tuple-element.78.kn_ref, bf16[32,1024]{1,0:T(8,128)(2,1)} %get-tuple-element.79.kp_ref, ...), custom_call_target="tpu_custom_call" | custom-call | tf_op jit(solution)/shard_map/attend_bwd/pallas_call | solution.py:293
  269.6 1.0 convert_element_type.33
  270.9 2.6 multiply_add_fusion.1
  273.5 1.6 fusion.16
  275.1 0.7 fusion.6
  276.0 0.3 add_add_fusion
  276.9 0.3 copy-done.5
  277.2 34.7 %back_exchange.1 = (bf16[128,2944]{1,0:T(8,128)(2,1)S(1)}, f32[1,2560]{1,0:T(1,128)S(1)}) custom-call(bf16[480,1024]{1,0:T(8,128)(2,1)S(1)} %copy-done.5, bf16[1024,384]{1,0:T(8,128)(2,1)S(1)} %pad.25.lat, bf16[480,2560]{1,0:T(8,128)(2,1)} %bitcast.62, bf16[288,2560]{1,0:T(8,128)(2,1)} %bitcast.58, bf16[128,2560]{1,0:T(8,128)(2,1)S(1)} %copy-done.4, ...), custom_call_target="tpu_custom_call" | custom-call | tf_op jit(solution)/shard_map/back_exchange/pallas_call | solution.py:515
  312.0 1.5 collective-permute-start.4
  313.5 0.9 collective-permute-start.3
  314.4 1.1 collective-permute-start.2
  315.5 11.0 %fusion.17 = f32[800,2560]{1,0:T(8,128)} fusion(bf16[1024,800]{1,0:T(8,128)(2,1)} %get-tuple-element.96, bf16[1024,2560]{1,0:T(8,128)(2,1)} %get-tuple-element.76.dy_hbm), kind=kOutput, calls=%fused_computation.59 | convolution fusion | flops 4194304000 | bytes 15073280 | tf_op jit(solution)/shard_map/dot_general | solution.py:24
  326.6 6.7 %fusion.18 = f32[800,2560]{1,0:T(8,128)} fusion(bf16[1024,800]{1,0:T(8,128)(2,1)S(1)} %copy-done.21, bf16[1024,2560]{1,0:T(8,128)(2,1)S(1)} %bitcast.91), kind=kOutput, calls=%fused_computation.60 | convolution fusion | flops 4194304000 | bytes 15073280 | tf_op jit(solution)/shard_map/dot_general | solution.py:24
  333.3 6.7 %fusion.19 = f32[800,2560]{1,0:T(8,128)} fusion(bf16[1024,800]{1,0:T(8,128)(2,1)S(1)} %copy-done.20, bf16[1024,2560]{1,0:T(8,128)(2,1)S(1)} %bitcast.91), kind=kOutput, calls=%fused_computation.61 | convolution fusion | flops 4194304000 | bytes 15073280 | tf_op jit(solution)/shard_map/dot_general | solution.py:24
  340.1 4.4 %fusion.20 = f32[480,2560]{1,0:T(8,128)} fusion(bf16[480,1024]{1,0:T(8,128)(2,1)S(1)} %copy-done.5, bf16[1024,2560]{1,0:T(8,128)(2,1)S(1)} %bitcast.87), kind=kOutput, calls=%fused_computation.62 | convolution fusion | flops 2516582400 | bytes 11141120 | tf_op jit(solution)/shard_map/dot_general | solution.py:24
  344.5 3.7 %collective-permute-done.3.refs_2_ = bf16[128,2944]{1,0:T(8,128)(2,1)S(1)} collective-permute-done((bf16[128,2944]{1,0:T(8,128)(2,1)S(1)}, bf16[128,2944]{1,0:T(8,128)(2,1)S(1)}, u32[]{:S(2)}, u32[]{:S(2)}) %collective-permute-start.3) | collective-permute-done | bytes 753696 | tf_op jit(solution)/shard_map/ppermute | solution.py:302
  348.2 0.5 collective-permute-start.8
  348.9 0.9 collective-permute-start.10
  349.8 3.6 fusion.21
  353.4 5.6 %table_grad.1 = (bf16[9181,2560]{1,0:T(8,128)(2,1)}, bf16[8,2560]{1,0:T(8,128)(2,1)S(1)}, bf16[1024,384]{1,0:T(8,128)(2,1)S(1)}) custom-call(s32[1]{0:T(128)} %bitcast.2.count_ref, s32[1024]{0:T(1024)S(1)} %select_reduce_fusion.blocks_ref, s32[1,1024]{1,0:T(1,128)S(1)} %bitcast.60, ...), custom_call_target="tpu_custom_call", output_to_operand_aliasing={{0}: (3, {})} | custom-call | tf_op jit(solution)/shard_map/table_grad/pallas_call | solution.py:194
  359.1 3.4 fusion.7
  362.5 1.1 collective-permute-start.11
  363.6 0.6 slice_dynamic-update-slice_fusion
  364.2 1.1 fusion.22
  365.3 1.1 fusion.23
  366.4 0.6 slice.28
  366.9 0.6 fusion.15
  367.5 0.8 copy.63
  (100 shorter events, 2.4 us)
Async XLA Ops:
  0.6 23.1 %collective-permute-start.1 = (bf16[128,2560]{1,0:T(8,128)(2,1)}, bf16[128,2560]{1,0:T(8,128)(2,1)S(1)}, u32[]{:S(2)}, u32[]{:S(2)}) collective-permute-start(bf16[128,2560]{1,0:T(8,128)(2,1)} %bitcast.65), channel_id=1, source_target_pairs={{0,4},{1,5},{2,6},{3,7},{4,0},{5,1},{6,2},{7,3}} | collective-permute-start | bytes 1966088 | tf_op jit(solution)/shard_map/ppermute | solution.py:302
  4.0 19.7 %collective-permute-start = (bf16[128,2560]{1,0:T(8,128)(2,1)}, bf16[128,2560]{1,0:T(8,128)(2,1)S(1)}, u32[]{:S(2)}, u32[]{:S(2)}) collective-permute-start(bf16[128,2560]{1,0:T(8,128)(2,1)} %bitcast.66), channel_id=1, source_target_pairs={{0,2},{1,3},{2,0},{3,1},{4,6},{5,7},{6,4},{7,5}} | collective-permute-start | bytes 1966088 | tf_op jit(solution)/shard_map/ppermute | solution.py:302
  13.3 10.4 %copy-start.1 = (bf16[2560,288]{0,1:T(8,128)(2,1)S(1)}, bf16[2560,288]{0,1:T(8,128)(2,1)}, u32[]{:S(2)}) copy-start(bf16[2560,288]{0,1:T(8,128)(2,1)} %param.17) | copy-start | bytes 4423684
  20.1 2.4 copy-start
  23.7 57.1 %copy-start.15 = (bf16[128,2560]{1,0:T(8,128)(2,1)}, bf16[128,2560]{1,0:T(8,128)(2,1)S(1)}, u32[]{:S(2)}) copy-start(bf16[128,2560]{1,0:T(8,128)(2,1)S(1)} %collective-permute-done.1.dyy_ref) | copy-start | bytes 1966084
  23.7 57.1 %copy-start.16 = (bf16[128,2560]{1,0:T(8,128)(2,1)}, bf16[128,2560]{1,0:T(8,128)(2,1)S(1)}, u32[]{:S(2)}) copy-start(bf16[128,2560]{1,0:T(8,128)(2,1)S(1)} %collective-permute-done.dyx_ref) | copy-start | bytes 1966084
  80.8 0.9 copy-start.2
  81.8 0.8 copy-start.3
  243.5 30.0 %copy-start.11 = (bf16[256,5,64]{0,2,1:T(8,128)(2,1)S(1)}, bf16[256,5,64]{0,2,1:T(8,128)(2,1)}, u32[]{:S(2)}) copy-start(bf16[256,5,64]{0,2,1:T(8,128)(2,1)} %param.19) | copy-start | bytes 491524
  243.5 31.6 %copy-start.17 = (bf16[256,5,64]{0,2,1:T(8,128)(2,1)S(1)}, bf16[256,5,64]{0,2,1:T(8,128)(2,1)}, u32[]{:S(2)}) copy-start(bf16[256,5,64]{0,2,1:T(8,128)(2,1)} %param.20) | copy-start | bytes 491524
  243.5 31.6 %copy-start.19 = (f32[256]{0:T(256)S(1)}, f32[256]{0:T(256)}, u32[]{:S(2)}) copy-start(f32[256]{0:T(256)} %param.18) | copy-start | bytes 3076
  269.6 5.4 %copy-start.6 = (f32[1024,288]{1,0:T(8,128)S(1)}, f32[1024,288]{1,0:T(8,128)}, u32[]{:S(2)}) copy-start(f32[1024,288]{1,0:T(8,128)} %get-tuple-element.70.lat) | copy-start | bytes 3538948
  270.8 4.2 %copy-start.13 = (bf16[320,1024]{1,0:T(8,128)(2,1)S(1)}, bf16[320,1024]{1,0:T(8,128)(2,1)}, u32[]{:S(2)}) copy-start(bf16[320,1024]{1,0:T(8,128)(2,1)} %get-tuple-element.120) | copy-start | bytes 1966084
  270.9 5.1 %copy-start.7 = (f32[1024,288]{1,0:T(8,128)S(1)}, f32[1024,288]{1,0:T(8,128)}, u32[]{:S(2)}) copy-start(f32[1024,288]{1,0:T(8,128)} %get-tuple-element.70.lat) | copy-start | bytes 3538948
  275.8 0.8 copy-start.18
  275.8 1.1 copy-start.4
  275.8 1.4 copy-start.5
  311.9 14.6 %slice-start.4 = ((s8[5242880]{0:T(1024)(128)(4,1)}), s8[4194304]{0:T(1024)(128)(4,1)S(1)}, s32[]{:S(2)}) async-start(s8[5242880]{0:T(1024)(128)(4,1)} %bitcast.90), calls=%async_computation.4 | async-start | bytes 8388608
  312.0 14.6 %slice-start.5 = ((s8[5242880]{0:T(1024)(128)(4,1)}), s8[1048576]{0:T(1024)(128)(4,1)S(1)}, s32[]{:S(2)}) async-start(s8[5242880]{0:T(1024)(128)(4,1)} %bitcast.90), calls=%async_computation.5 | async-start | bytes 2097152
  312.0 14.6 %copy-start.21 = (bf16[1024,800]{1,0:T(8,128)(2,1)S(1)}, bf16[1024,800]{1,0:T(8,128)(2,1)}, u32[]{:S(2)}) copy-start(bf16[1024,800]{1,0:T(8,128)(2,1)} %get-tuple-element.97) | copy-start | bytes 4915204
  312.0 32.5 %collective-permute-start.5 = (bf16[128,2944]{1,0:T(8,128)(2,1)S(1)}, bf16[128,2944]{1,0:T(8,128)(2,1)S(1)}, u32[]{:S(2)}, u32[]{:S(2)}) collective-permute-start(bf16[128,2944]{1,0:T(8,128)(2,1)S(1)} %get-tuple-element.95.refs_0_), channel_id=1, source_target_pairs={{0,1},{1,0},{2,3},{3,2},{4,5},{5,4},{6,7},{7,6}} | collective-permute-start | bytes 2261000 | tf_op jit(solution)/shard_map/ppermute | solution.py:302
  312.0 32.5 %collective-permute-start.4 = (bf16[128,2944]{1,0:T(8,128)(2,1)S(1)}, bf16[128,2944]{1,0:T(8,128)(2,1)S(1)}, u32[]{:S(2)}, u32[]{:S(2)}) collective-permute-start(bf16[128,2944]{1,0:T(8,128)(2,1)S(1)} %get-tuple-element.95.refs_0_), channel_id=1, source_target_pairs={{0,6},{1,7},{2,4},{3,5},{4,2},{5,3},{6,0},{7,1}} | collective-permute-start | bytes 2261000 | tf_op jit(solution)/shard_map/ppermute | solution.py:302
  313.5 34.7 %collective-permute-start.3 = (bf16[128,2944]{1,0:T(8,128)(2,1)S(1)}, bf16[128,2944]{1,0:T(8,128)(2,1)S(1)}, u32[]{:S(2)}, u32[]{:S(2)}) collective-permute-start(bf16[128,2944]{1,0:T(8,128)(2,1)S(1)} %get-tuple-element.95.refs_0_), channel_id=1, source_target_pairs={{0,4},{1,5},{2,6},{3,7},{4,0},{5,1},{6,2},{7,3}} | collective-permute-start | bytes 2261000 | tf_op jit(solution)/shard_map/ppermute | solution.py:302
  314.4 33.8 %collective-permute-start.2 = (bf16[128,2944]{1,0:T(8,128)(2,1)S(1)}, bf16[128,2944]{1,0:T(8,128)(2,1)S(1)}, u32[]{:S(2)}, u32[]{:S(2)}) collective-permute-start(bf16[128,2944]{1,0:T(8,128)(2,1)S(1)} %get-tuple-element.95.refs_0_), channel_id=1, source_target_pairs={{0,2},{1,3},{2,0},{3,1},{4,6},{5,7},{6,4},{7,5}} | collective-permute-start | bytes 2261000 | tf_op jit(solution)/shard_map/ppermute | solution.py:302
  315.5 28.9 %collective-permute-start.6 = (f32[5376]{0:T(1024)S(1)}, f32[5376]{0:T(1024)S(1)}, u32[]{:S(2)}, u32[]{:S(2)}) collective-permute-start(f32[5376]{0:T(1024)S(1)} %pad_maximum_fusion), channel_id=1, source_target_pairs={{0,1},{1,0},{2,3},{3,2},{4,5},{5,4},{6,7},{7,6}} | collective-permute-start | bytes 64520 | tf_op jit(solution)/shard_map/ppermute | solution.py:302
  326.6 6.8 %copy-start.20 = (bf16[1024,800]{1,0:T(8,128)(2,1)S(1)}, bf16[1024,800]{1,0:T(8,128)(2,1)}, u32[]{:S(2)}) copy-start(bf16[1024,800]{1,0:T(8,128)(2,1)} %get-tuple-element.99) | copy-start | bytes 4915204
  326.6 13.5 %slice-start = ((s8[5242880]{0:T(1024)(128)(4,1)}), s8[4194304]{0:T(1024)(128)(4,1)S(1)}, s32[]{:S(2)}) async-start(s8[5242880]{0:T(1024)(128)(4,1)} %bitcast.86), calls=%async_computation | async-start | bytes 8388608
  333.3 6.7 %slice-start.1 = ((s8[5242880]{0:T(1024)(128)(4,1)}), s8[1048576]{0:T(1024)(128)(4,1)S(1)}, s32[]{:S(2)}) async-start(s8[5242880]{0:T(1024)(128)(4,1)} %bitcast.86), calls=%async_computation.1 | async-start | bytes 2097152
  333.3 16.4 %slice-start.2 = ((s8[5242880]{0:T(1024)(128)(4,1)}), s8[4194304]{0:T(1024)(128)(4,1)S(1)}, s32[]{:S(2)}) async-start(s8[5242880]{0:T(1024)(128)(4,1)} %bitcast.88), calls=%async_computation.2 | async-start | bytes 8388608
  340.1 9.7 %copy-start.10 = (bf16[320,1024]{1,0:T(8,128)(2,1)S(1)}, bf16[320,1024]{1,0:T(8,128)(2,1)}, u32[]{:S(2)}) copy-start(bf16[320,1024]{1,0:T(8,128)(2,1)} %get-tuple-element.107.o_ref) | copy-start | bytes 1966084
  340.1 9.7 %slice-start.3 = ((s8[5242880]{0:T(1024)(128)(4,1)}), s8[1048576]{0:T(1024)(128)(4,1)S(1)}, s32[]{:S(2)}) async-start(s8[5242880]{0:T(1024)(128)(4,1)} %bitcast.88), calls=%async_computation.3 | async-start | bytes 2097152
  348.2 5.2 %collective-permute-start.7 = (bf16[128,2944]{1,0:T(8,128)(2,1)S(1)}, bf16[128,2944]{1,0:T(8,128)(2,1)S(1)}, u32[]{:S(2)}, u32[]{:S(2)}) collective-permute-start(bf16[128,2944]{1,0:T(8,128)(2,1)S(1)} %collective-permute-done.2.refs_1_), channel_id=1, source_target_pairs={{0,1},{1,0},{2,3},{3,2},{4,5},{5,4},{6,7},{7,6}} | collective-permute-start | bytes 2261000 | tf_op jit(solution)/shard_map/ppermute | solution.py:302
  348.2 5.2 %collective-permute-start.8 = (bf16[128,2944]{1,0:T(8,128)(2,1)S(1)}, bf16[128,2944]{1,0:T(8,128)(2,1)S(1)}, u32[]{:S(2)}, u32[]{:S(2)}) collective-permute-start(bf16[128,2944]{1,0:T(8,128)(2,1)S(1)} %collective-permute-done.3.refs_2_), channel_id=1, source_target_pairs={{0,1},{1,0},{2,3},{3,2},{4,5},{5,4},{6,7},{7,6}} | collective-permute-start | bytes 2261000 | tf_op jit(solution)/shard_map/ppermute | solution.py:302
  348.7 4.7 %collective-permute-start.9 = (bf16[128,2944]{1,0:T(8,128)(2,1)S(1)}, bf16[128,2944]{1,0:T(8,128)(2,1)S(1)}, u32[]{:S(2)}, u32[]{:S(2)}) collective-permute-start(bf16[128,2944]{1,0:T(8,128)(2,1)S(1)} %collective-permute-done.4.refs_3_), channel_id=1, source_target_pairs={{0,1},{1,0},{2,3},{3,2},{4,5},{5,4},{6,7},{7,6}} | collective-permute-start | bytes 2261000 | tf_op jit(solution)/shard_map/ppermute | solution.py:302
  348.9 4.5 %collective-permute-start.10 = (f32[5376]{0:T(1024)S(1)}, f32[5376]{0:T(1024)S(1)}, u32[]{:S(2)}, u32[]{:S(2)}) collective-permute-start(f32[5376]{0:T(1024)S(1)} %add.152), channel_id=1, source_target_pairs={{0,2},{1,3},{2,0},{3,1},{4,6},{5,7},{6,4},{7,5}} | collective-permute-start | bytes 64520 | tf_op jit(solution)/shard_map/ppermute | solution.py:302
  359.0 5.2 %copy-start.8 = (bf16[320,1024]{1,0:T(8,128)(2,1)S(1)}, bf16[320,1024]{1,0:T(8,128)(2,1)}, u32[]{:S(2)}) copy-start(bf16[320,1024]{1,0:T(8,128)(2,1)} %get-tuple-element.118) | copy-start | bytes 1966084
  359.1 5.2 %copy-start.9 = (bf16[1024,256]{1,0:T(8,128)(2,1)S(1)}, bf16[1024,256]{1,0:T(8,128)(2,1)}, u32[]{:S(2)}) copy-start(bf16[1024,256]{1,0:T(8,128)(2,1)} %get-tuple-element.119) | copy-start | bytes 1572868
  359.1 6.2 %copy-start.14 = (bf16[320,1024]{1,0:T(8,128)(2,1)S(1)}, bf16[320,1024]{1,0:T(8,128)(2,1)}, u32[]{:S(2)}) copy-start(bf16[320,1024]{1,0:T(8,128)(2,1)} %get-tuple-element.120) | copy-start | bytes 1966084
  359.1 8.5 %copy-start.12 = (bf16[128,2560]{1,0:T(8,128)(2,1)S(1)}, bf16[128,2560]{1,0:T(8,128)(2,1)}, u32[]{:S(2)}) copy-start(bf16[128,2560]{1,0:T(8,128)(2,1)} %get-tuple-element.77) | copy-start | bytes 1966084
  362.5 3.9 %collective-permute-start.11 = (f32[5376]{0:T(1024)S(1)}, f32[5376]{0:T(1024)S(1)}, u32[]{:S(2)}, u32[]{:S(2)}) collective-permute-start(f32[5376]{0:T(1024)S(1)} %add.153), channel_id=1, source_target_pairs={{0,4},{1,5},{2,6},{3,7},{4,0},{5,1},{6,2},{7,3}} | collective-permute-start | bytes 64520 | tf_op jit(solution)/shard_map/ppermute | solution.py:302

commit v7 on v6

--- a/solution.py
+++ b/solution.py
@@ -232,16 +232,22 @@
         lse_ref[0, :, lanes] = top + jnp.log2(total)
 
 
-def attn_bwd_body(q_ref, kn_ref, kp_ref, v_ref, cos_ref, sin_ref, lse_ref, do_ref, dq_ref, dkn_ref, dv_ref, dkp_ref, table_ref, dk_acc, dv_acc, zero, zsem):
+def attn_bwd_body(heads, q_ref, kn_ref, kp_ref, v_ref, cos_ref, sin_ref, lse_ref, do_ref, dq_ref, dkn_ref, dv_ref, dkp_ref, table_ref, dk_acc, dv_acc, zero, zsem):
     full = table_ref.shape[0] // 8 * 8
     fills = [pltpu.make_async_copy(zero.at[pl.ds(0, n), :], table_ref.at[pl.ds(r, n), :], zsem.at[k])
              for k, (r, n) in enumerate((r, min(ZR, full - r)) for r in range(0, full, ZR))]
 
-    @pl.when(pl.program_id(0) == 0)
+    head = pl.program_id(0)
+    share = -(-len(fills) // heads)
+
+    @pl.when(head == 0)
     def _():
         zero[...] = jnp.zeros_like(zero)
-        for cp in fills:
-            cp.start()
+    for h in range(heads):
+        @pl.when(head == h)
+        def _():
+            for cp in fills[h * share:(h + 1) * share]:
+                cp.start()
 
     nope, half = kn_ref.shape[0], cos_ref.shape[0]
     raw = q_ref.shape[0] ** -0.5
@@ -270,12 +276,12 @@
     dkn_ref[...] = dk_acc[:nope, :].astype(BF16)
     dv_ref[...] = dv_acc[...].astype(BF16)
 
-    @pl.when(pl.program_id(0) == 0)
+    @pl.when(head == 0)
     def _():
         dkp_ref[...] = jnp.zeros_like(dkp_ref)
     dkp_ref[...] += dk_acc[nope:, :]
 
-    @pl.when(pl.program_id(0) == pl.num_programs(0) - 1)
+    @pl.when(head == heads - 1)
     def _():
         for cp in fills:
             cp.wait()
@@ -291,7 +297,7 @@
     seq, qd, nope, vd, rope = q.shape[1], q.shape[0] // heads, kn.shape[0] // heads, v.shape[0] // heads, kp.shape[0]
     ins, per, one, lse_spec = attn_specs(heads, qd, nope, rope, vd, seq)
     return pl.pallas_call(
-        attn_bwd_body, grid=(heads,), in_specs=ins + [lse_spec, per(vd)], out_specs=[per(qd), per(nope), per(vd), one(rope), pl.BlockSpec(memory_space=pl.ANY)],
+        functools.partial(attn_bwd_body, heads), grid=(heads,), in_specs=ins + [lse_spec, per(vd)], out_specs=[per(qd), per(nope), per(vd), one(rope), pl.BlockSpec(memory_space=pl.ANY)],
         out_shape=[jax.ShapeDtypeStruct(q.shape, BF16), jax.ShapeDtypeStruct(kn.shape, BF16), jax.ShapeDtypeStruct(v.shape, BF16), jax.ShapeDtypeStruct(kp.shape, F32), jax.ShapeDtypeStruct(table, BF16)],
         scratch_shapes=[VM((qd, seq), F32), VM((vd, seq), F32), VM((ZR, table[1]), BF16), pltpu.SemaphoreType.DMA((-(-table[0] // ZR),))],
         compiler_params=pltpu.CompilerParams(vmem_limit_bytes=ALL << 20), name='attend_bwd',
@@ -706,7 +712,7 @@
     ga, gm = g_attn[None, :], g_mlp[None, :]
     rows, dy_near = lax.optimization_barrier((rows, [shift(d_out, XBIT), shift(d_out, YBIT)]))
     embedded, query, latent, x_attn = exchange_call(
-        embed_body, 'embed_exchange', 1, [rows, ga, w_q, w_dkv], [loc, shape((w_q.shape[0], seq), BF16), shape((seq, latw), F32), fullb], saved + main, out=1)
+        embed_body, 'embed_exchange', 1, [rows, ga, w_q, w_dkv], [loc, shape((w_q.shape[0], seq), BF16), shape((seq, latw), F32), fullb], saved + main, out=1, limit=36)
     cos_t, sin_t = (t.T for t in rope_tables(seq, latw - lora))
     nq, nk, nv = w_q.shape[0], w_uk.shape[0], w_uv.shape[0]
     c_kv, k_nope, k_pe_t, value, attn_out, lse, dy_full = exchange_call(
@@ -734,18 +740,17 @@
         partb + [VM((local, width), F32), VM((local, padw), F32)] + two.rs_scratch(local))
     later = lax.optimization_barrier
     dg = jnp.concatenate([dg_attn[0], dg_mlp[0], dg_kv])
-    hidden, d_gate, d_up, d_query, de, dg = later((hidden, d_gate, d_up, d_query, de, dg))
+    hidden, d_gate, d_up, d_query, attn_out, de, dg = later((hidden, d_gate, d_up, d_query, attn_out, de, dg))
     near = [shift(de, XBIT), shift(de, YBIT), shift(de, XBIT + YBIT)]
     pair = shift(de, PAIR)
     dg = dg + shift(dg, PAIR)
-    dw_down, dw_gate, dw_up, dw_q = tn(hidden, dy_full), tn(d_gate, x_mlp), tn(d_up, x_mlp), nn(d_query, x_attn)
-    dw_down, dw_gate, dw_up, dw_q, near, pair, dg, attn_out = later((dw_down, dw_gate, dw_up, dw_q, near, pair, dg, attn_out))
+    dw_down, dw_gate, dw_up, dw_q, dw_o = tn(hidden, dy_full), tn(d_gate, x_mlp), tn(d_up, x_mlp), nn(d_query, x_attn), nn(attn_out, d_attn_full)
+    dw_down, dw_gate, dw_up, dw_q, dw_o, near, pair, dg, d_knope, d_value = later((dw_down, dw_gate, dw_up, dw_q, dw_o, near, pair, dg, d_knope, d_value))
     far = [shift(b, PAIR) for b in near]
     dg = dg + shift(dg, XBIT)
-    dw_o = nn(attn_out, d_attn_full)
-    dw_o, far, dg, d_knope, d_value = later((dw_o, far, dg, d_knope, d_value))
+    dw_uk, dw_uv = nn(d_knope, c_kv), nn(d_value, c_kv)
+    dw_uk, dw_uv, far, dg = later((dw_uk, dw_uv, far, dg))
     dg = dg + shift(dg, YBIT)
-    dw_uk, dw_uv = nn(d_knope, c_kv), nn(d_value, c_kv)
     d_table, lat_full = table_grad(to_hop_order(key, 0), blocks, count, [de, *near, pair, *far], table0)
     dw_dkv = tn(lat_full[:, :latw], x_attn)
     dg_attn, dg_mlp, dg_kv = dg[:width], dg[width:2 * width], dg[2 * width:]

time: 374 us -> 362 us (0.968)
  Pallas kernels: 290 us -> 279 us
    pallas_call x1, Pallas kernels: 26.1 us -> 19.8 us  [attend_bwd(): pl.pallas_call(functools.partial(attn_bwd_body, heads), grid=(heads,), in...]
    pallas_call x4, Pallas kernels: 251 us -> 246 us  [exchange_call(): pl.pallas_call(body, out_shape=out_shape, in_specs=[vmem] * (len(ins) - f...]
  transfers between devices with their start and end apart: 12 -> 12, of which waited for: 1 -> 1; matrix products, arithmetic and copies ran while one was open for 12% -> 14% of each run, Pallas kernels for 2% -> 4%
where the time goes in v7:
time: 362 us; the launch traced here: 357 us
  Pallas kernels  279 us (77%)
  matrix products  42.8 us (12%)
  local copies, waits for them, and re-layouts  12.2 us (3%)
  starting transfers between devices  11.4 us (3%)
  other arithmetic  9.35 us (3%)
    pallas_call x4, Pallas kernels, exchange_call(): pl.pallas_call(body, out_shape=out_shape, in_specs=[vmem] * (len(ins) - f...  246 us
    dot_general x10, matrix products, mm(): lax.dot_general(lhs, rhs, (((lc,), (rc,)), ((), ())), preferred_element_t...  42.8 us
    pallas_call x1, Pallas kernels, attend_bwd(): pl.pallas_call(functools.partial(attn_bwd_body, heads), grid=(heads,), in...  19.8 us
    ppermute x12, starting transfers between devices, shift(): return lax.ppermute(x, 'tp', [(d, d ^ bit) for d in range(8)])  11.4 us
  transfers between devices with their start and end apart: 12, of which 1 were waited for; matrix products, arithmetic and copies ran while one was open for 14% of the time, Pallas kernels for 4%

profile of v7, /device:TPU:0, one launch (start us, length us, event | category | flops | bytes accessed | tf_op | source)
XLA Modules:
  0.0 356.8 jit_solution(13667574087411778768)
XLA Ops:
  0.6 3.4 collective-permute-start.1
  4.0 1.5 collective-permute-start
  5.5 0.7 broadcast_in_dim.71.gain
  6.3 1.3 broadcast_in_dim.73.gain
  7.6 0.7 broadcast_select_fusion
  8.3 0.8 select_reduce_fusion.1
  9.1 0.8 convert_reduce_fusion
  10.0 0.9 select_reduce_fusion.blocks_ref
  10.9 0.6 add_select_fusion.1
  11.5 0.8 slice.21
  12.3 0.3 copy.45
  13.3 6.8 %gather_rows.1.part = bf16[1024,2560]{1,0:T(8,128)(2,1)S(1)} custom-call(s32[1]{0:T(128)} %bitcast.2.count_ref, s32[1024]{0:T(1024)S(1)} %select_reduce_fusion.blocks_ref, s32[1024,1]{1,0:T(8,128)S(1)} %add_select_fusion.key_ref, bf16[8,2560]{1,0:T(8,128)(2,1)S(1)} %pad.20.tail_ref, bf16[9181,2560]{1,0:T(8,128)(2,1)} %table_ref.1), custom_call_target="tpu_custom_call" | custom-call | tf_op jit(solution)/shard_map/gather_rows/pallas_call | solution.py:134
  20.4 1.0 fusion.11
  21.4 51.7 %embed_exchange.1 = (bf16[128,2560]{1,0:T(8,128)(2,1)S(1)}, bf16[480,1024]{1,0:T(8,128)(2,1)S(1)}, f32[1024,288]{1,0:T(8,128)S(1)}, bf16[1024,2560]{1,0:T(8,128)(2,1)S(1)}) custom-call(bf16[1024,2560]{1,0:T(8,128)(2,1)S(1)} %gather_rows.1.part, f32[1,2560]{1,0:T(1,128)S(1)} %broadcast_in_dim.71.gain, bf16[480,2560]{1,0:T(8,128)(2,1)S(1)} %bitcast.59, ...), custom_call_target="tpu_custom_call" | custom-call | tf_op jit(solution)/shard_map/embed_exchange/pallas_call | solution.py:521
  73.2 0.8 copy-done.5
  74.0 2.3 copy-done.8
  76.4 1.1 copy-done.1
  77.8 19.0 %attend_fwd.1 = (bf16[1024,256]{1,0:T(8,128)(2,1)}, bf16[320,1024]{1,0:T(8,128)(2,1)}, bf16[32,1024]{1,0:T(8,128)(2,1)}, bf16[320,1024]{1,0:T(8,128)(2,1)}, bf16...) custom-call(f32[1024,288]{1,0:T(8,128)} %copy-done.1, f32[1,256]{1,0:T(1,128)} %bitcast.89, ...), custom_call_target="tpu_custom_call" | custom-call | tf_op jit(solution)/shard_map/attend_fwd/pallas_call | solution.py:521
  96.9 140.3 %middle.1 = (bf16[128,2560]{1,0:T(8,128)(2,1)}, bf16[128,2560]{1,0:T(8,128)(2,1)}, f32[128,2560]{1,0:T(8,128)}, f32[1,2560]{1,0:T(1,128)}, bf16[320,1024]{1,0:T(...) custom-call(bf16[320,1024]{1,0:T(8,128)(2,1)} %get-tuple-element.104, ...), custom_call_target="tpu_custom_call" | custom-call | tf_op jit(solution)/shard_map/middle/pallas_call | solution.py:521
  237.2 19.8 %attend_bwd.1 = (bf16[480,1024]{1,0:T(8,128)(2,1)}, bf16[320,1024]{1,0:T(8,128)(2,1)}, bf16[320,1024]{1,0:T(8,128)(2,1)}, f32[32,1024]{1,0:T(8,128)}, bf16[9181,2560]{1,0:T(8,128)(2,1)}) custom-call(bf16[480,1024]{1,0:T(8,128)(2,1)} %copy-done.4, bf16[320,1024]{1,0:T(8,128)(2,1)} %get-tuple-element.80.kn_ref, bf16[32,1024]{1,0:T(8,128)(2,1)} %get-tuple-element.81.kp_ref, ...), custom_call_target="tpu_custom_call" | custom-call | tf_op jit(solution)/shard_map/attend_bwd/pallas_call | solution.py:299
  257.0 1.0 convert_element_type.33
  258.3 2.4 multiply_add_fusion.1
  260.6 1.6 fusion.16
  262.3 0.7 fusion.6
  263.2 0.3 add_add_fusion
  263.8 0.3 copy-done.6
  264.0 0.3 copy-done.7
  264.4 34.7 %back_exchange.1 = (bf16[128,2944]{1,0:T(8,128)(2,1)S(1)}, f32[1,2560]{1,0:T(1,128)S(1)}) custom-call(bf16[480,1024]{1,0:T(8,128)(2,1)S(1)} %copy-done.7, bf16[1024,384]{1,0:T(8,128)(2,1)S(1)} %pad.25.lat, bf16[480,2560]{1,0:T(8,128)(2,1)} %bitcast.58, bf16[288,2560]{1,0:T(8,128)(2,1)} %bitcast.60, bf16[128,2560]{1,0:T(8,128)(2,1)S(1)} %copy-done.6, ...), custom_call_target="tpu_custom_call" | custom-call | tf_op jit(solution)/shard_map/back_exchange/pallas_call | solution.py:521
  299.2 1.5 collective-permute-start.4
  300.7 0.8 collective-permute-start.3
  301.5 1.3 collective-permute-start.2
  302.7 11.1 %fusion.17 = f32[800,2560]{1,0:T(8,128)} fusion(bf16[1024,800]{1,0:T(8,128)(2,1)} %get-tuple-element.98, bf16[1024,2560]{1,0:T(8,128)(2,1)} %get-tuple-element.78.dy_hbm), kind=kOutput, calls=%fused_computation.59 | convolution fusion | flops 4194304000 | bytes 15073280 | tf_op jit(solution)/shard_map/dot_general | solution.py:24
  313.9 6.7 %fusion.18 = f32[800,2560]{1,0:T(8,128)} fusion(bf16[1024,800]{1,0:T(8,128)(2,1)S(1)} %copy-done.19, bf16[1024,2560]{1,0:T(8,128)(2,1)S(1)} %bitcast.93), kind=kOutput, calls=%fused_computation.60 | convolution fusion | flops 4194304000 | bytes 15073280 | tf_op jit(solution)/shard_map/dot_general | solution.py:24
  320.6 6.7 %fusion.19 = f32[800,2560]{1,0:T(8,128)} fusion(bf16[1024,800]{1,0:T(8,128)(2,1)S(1)} %copy-done.18, bf16[1024,2560]{1,0:T(8,128)(2,1)S(1)} %bitcast.93), kind=kOutput, calls=%fused_computation.61 | convolution fusion | flops 4194304000 | bytes 15073280 | tf_op jit(solution)/shard_map/dot_general | solution.py:24
  327.3 4.4 %fusion.20 = f32[480,2560]{1,0:T(8,128)} fusion(bf16[480,1024]{1,0:T(8,128)(2,1)S(1)} %copy-done.7, bf16[1024,2560]{1,0:T(8,128)(2,1)S(1)} %bitcast.64), kind=kOutput, calls=%fused_computation.62 | convolution fusion | flops 2516582400 | bytes 11141120 | tf_op jit(solution)/shard_map/dot_general | solution.py:24
  331.7 3.6 %fusion.21 = f32[320,2560]{1,0:T(8,128)} fusion(bf16[320,1024]{1,0:T(8,128)(2,1)S(1)} %copy-done.9, bf16[1024,2560]{1,0:T(8,128)(2,1)S(1)} %bitcast.91), kind=kOutput, calls=%fused_computation.63 | convolution fusion | flops 1677721600 | bytes 9175040 | tf_op jit(solution)/shard_map/dot_general | solution.py:24
  335.4 0.4 collective-permute-start.7
  335.9 0.4 collective-permute-start.9
  336.6 0.8 collective-permute-start.10
  337.4 2.4 fusion.22
  339.8 2.3 fusion.23
  342.1 1.3 collective-permute-start.11
  343.4 6.9 %table_grad.1 = (bf16[9181,2560]{1,0:T(8,128)(2,1)}, bf16[8,2560]{1,0:T(8,128)(2,1)S(1)}, bf16[1024,384]{1,0:T(8,128)(2,1)S(1)}) custom-call(s32[1]{0:T(128)} %bitcast.2.count_ref, s32[1024]{0:T(1024)S(1)} %select_reduce_fusion.blocks_ref, s32[1,1024]{1,0:T(1,128)S(1)} %bitcast.62, ...), custom_call_target="tpu_custom_call", output_to_operand_aliasing={{0}: (3, {})} | custom-call | tf_op jit(solution)/shard_map/table_grad/pallas_call | solution.py:194
  350.4 0.6 slice_dynamic-update-slice_fusion
  351.0 3.4 fusion.7
  354.4 0.6 slice.28
  355.0 0.6 fusion.15
  355.6 0.8 copy.63
  (101 shorter events, 2.6 us)
Async XLA Ops:
  0.6 20.7 %collective-permute-start.1 = (bf16[128,2560]{1,0:T(8,128)(2,1)}, bf16[128,2560]{1,0:T(8,128)(2,1)S(1)}, u32[]{:S(2)}, u32[]{:S(2)}) collective-permute-start(bf16[128,2560]{1,0:T(8,128)(2,1)} %bitcast.69), channel_id=1, source_target_pairs={{0,4},{1,5},{2,6},{3,7},{4,0},{5,1},{6,2},{7,3}} | collective-permute-start | bytes 1966088 | tf_op jit(solution)/shard_map/ppermute | solution.py:308
  4.0 17.3 %collective-permute-start = (bf16[128,2560]{1,0:T(8,128)(2,1)}, bf16[128,2560]{1,0:T(8,128)(2,1)S(1)}, u32[]{:S(2)}, u32[]{:S(2)}) collective-permute-start(bf16[128,2560]{1,0:T(8,128)(2,1)} %bitcast.70), channel_id=1, source_target_pairs={{0,2},{1,3},{2,0},{3,1},{4,6},{5,7},{6,4},{7,5}} | collective-permute-start | bytes 1966088 | tf_op jit(solution)/shard_map/ppermute | solution.py:308
  13.3 8.1 %copy-start = (bf16[2560,5,96]{0,2,1:T(8,128)(2,1)S(1)}, bf16[2560,5,96]{0,2,1:T(8,128)(2,1)}, u32[]{:S(2)}) copy-start(bf16[2560,5,96]{0,2,1:T(8,128)(2,1)} %param.16) | copy-start | bytes 7372804
  13.3 8.1 %copy-start.3 = (bf16[2560,288]{0,1:T(8,128)(2,1)S(1)}, bf16[2560,288]{0,1:T(8,128)(2,1)}, u32[]{:S(2)}) copy-start(bf16[2560,288]{0,1:T(8,128)(2,1)} %param.17) | copy-start | bytes 4423684
  21.4 51.8 %copy-start.13 = (bf16[128,2560]{1,0:T(8,128)(2,1)}, bf16[128,2560]{1,0:T(8,128)(2,1)S(1)}, u32[]{:S(2)}) copy-start(bf16[128,2560]{1,0:T(8,128)(2,1)S(1)} %collective-permute-done.1.dyy_ref) | copy-start | bytes 1966084
  21.4 51.8 %copy-start.14 = (bf16[128,2560]{1,0:T(8,128)(2,1)}, bf16[128,2560]{1,0:T(8,128)(2,1)S(1)}, u32[]{:S(2)}) copy-start(bf16[128,2560]{1,0:T(8,128)(2,1)S(1)} %collective-permute-done.dyx_ref) | copy-start | bytes 1966084
  73.2 0.8 copy-start.5
  74.0 2.3 copy-start.8
  76.3 1.1 copy-start.1
  76.4 1.5 copy-start.4
  237.2 23.4 %copy-start.10 = (bf16[256,5,64]{0,2,1:T(8,128)(2,1)S(1)}, bf16[256,5,64]{0,2,1:T(8,128)(2,1)}, u32[]{:S(2)}) copy-start(bf16[256,5,64]{0,2,1:T(8,128)(2,1)} %param.19) | copy-start | bytes 491524
  237.2 25.0 %copy-start.15 = (bf16[256,5,64]{0,2,1:T(8,128)(2,1)S(1)}, bf16[256,5,64]{0,2,1:T(8,128)(2,1)}, u32[]{:S(2)}) copy-start(bf16[256,5,64]{0,2,1:T(8,128)(2,1)} %param.20) | copy-start | bytes 491524
  237.2 25.0 %copy-start.17 = (f32[256]{0:T(256)S(1)}, f32[256]{0:T(256)}, u32[]{:S(2)}) copy-start(f32[256]{0:T(256)} %param.18) | copy-start | bytes 3076
  257.0 5.2 %copy-start.2 = (f32[1024,288]{1,0:T(8,128)S(1)}, f32[1024,288]{1,0:T(8,128)}, u32[]{:S(2)}) copy-start(f32[1024,288]{1,0:T(8,128)} %copy-done.1) | copy-start | bytes 3538948
  258.2 4.0 %copy-start.12 = (bf16[320,1024]{1,0:T(8,128)(2,1)S(1)}, bf16[320,1024]{1,0:T(8,128)(2,1)}, u32[]{:S(2)}) copy-start(bf16[320,1024]{1,0:T(8,128)(2,1)} %get-tuple-element.113) | copy-start | bytes 1966084
  262.9 0.8 copy-start.16
  262.9 1.1 copy-start.6
  263.0 1.4 copy-start.7
  299.1 14.7 %slice-start.6 = ((s8[5242880]{0:T(1024)(128)(4,1)}), s8[4194304]{0:T(1024)(128)(4,1)S(1)}, s32[]{:S(2)}) async-start(s8[5242880]{0:T(1024)(128)(4,1)} %bitcast.92), calls=%async_computation.6 | async-start | bytes 8388608
  299.2 14.7 %slice-start.7 = ((s8[5242880]{0:T(1024)(128)(4,1)}), s8[1048576]{0:T(1024)(128)(4,1)S(1)}, s32[]{:S(2)}) async-start(s8[5242880]{0:T(1024)(128)(4,1)} %bitcast.92), calls=%async_computation.7 | async-start | bytes 2097152
  299.2 14.7 %copy-start.19 = (bf16[1024,800]{1,0:T(8,128)(2,1)S(1)}, bf16[1024,800]{1,0:T(8,128)(2,1)}, u32[]{:S(2)}) copy-start(bf16[1024,800]{1,0:T(8,128)(2,1)} %get-tuple-element.99) | copy-start | bytes 4915204
  299.2 36.1 %collective-permute-start.5 = (bf16[128,2944]{1,0:T(8,128)(2,1)S(1)}, bf16[128,2944]{1,0:T(8,128)(2,1)S(1)}, u32[]{:S(2)}, u32[]{:S(2)}) collective-permute-start(bf16[128,2944]{1,0:T(8,128)(2,1)S(1)} %get-tuple-element.97.refs_0_), channel_id=1, source_target_pairs={{0,1},{1,0},{2,3},{3,2},{4,5},{5,4},{6,7},{7,6}} | collective-permute-start | bytes 2261000 | tf_op jit(solution)/shard_map/ppermute | solution.py:308
  299.2 36.1 %collective-permute-start.4 = (bf16[128,2944]{1,0:T(8,128)(2,1)S(1)}, bf16[128,2944]{1,0:T(8,128)(2,1)}, u32[]{:S(2)}, u32[]{:S(2)}) collective-permute-start(bf16[128,2944]{1,0:T(8,128)(2,1)S(1)} %get-tuple-element.97.refs_0_), channel_id=1, source_target_pairs={{0,6},{1,7},{2,4},{3,5},{4,2},{5,3},{6,0},{7,1}} | collective-permute-start | bytes 2261000 | tf_op jit(solution)/shard_map/ppermute | solution.py:308
  300.7 34.7 %collective-permute-start.3 = (bf16[128,2944]{1,0:T(8,128)(2,1)S(1)}, bf16[128,2944]{1,0:T(8,128)(2,1)}, u32[]{:S(2)}, u32[]{:S(2)}) collective-permute-start(bf16[128,2944]{1,0:T(8,128)(2,1)S(1)} %get-tuple-element.97.refs_0_), channel_id=1, source_target_pairs={{0,4},{1,5},{2,6},{3,7},{4,0},{5,1},{6,2},{7,3}} | collective-permute-start | bytes 2261000 | tf_op jit(solution)/shard_map/ppermute | solution.py:308
  301.5 33.9 %collective-permute-start.2 = (bf16[128,2944]{1,0:T(8,128)(2,1)S(1)}, bf16[128,2944]{1,0:T(8,128)(2,1)}, u32[]{:S(2)}, u32[]{:S(2)}) collective-permute-start(bf16[128,2944]{1,0:T(8,128)(2,1)S(1)} %get-tuple-element.97.refs_0_), channel_id=1, source_target_pairs={{0,2},{1,3},{2,0},{3,1},{4,6},{5,7},{6,4},{7,5}} | collective-permute-start | bytes 2261000 | tf_op jit(solution)/shard_map/ppermute | solution.py:308
  302.7 32.6 %collective-permute-start.6 = (f32[5376]{0:T(1024)S(1)}, f32[5376]{0:T(1024)S(1)}, u32[]{:S(2)}, u32[]{:S(2)}) collective-permute-start(f32[5376]{0:T(1024)S(1)} %pad_maximum_fusion), channel_id=1, source_target_pairs={{0,1},{1,0},{2,3},{3,2},{4,5},{5,4},{6,7},{7,6}} | collective-permute-start | bytes 64520 | tf_op jit(solution)/shard_map/ppermute | solution.py:308
  313.8 6.7 %copy-start.18 = (bf16[1024,800]{1,0:T(8,128)(2,1)S(1)}, bf16[1024,800]{1,0:T(8,128)(2,1)}, u32[]{:S(2)}) copy-start(bf16[1024,800]{1,0:T(8,128)(2,1)} %get-tuple-element.101) | copy-start | bytes 4915204
  313.9 13.4 %slice-start = ((s8[5242880]{0:T(1024)(128)(4,1)}), s8[4194304]{0:T(1024)(128)(4,1)S(1)}, s32[]{:S(2)}) async-start(s8[5242880]{0:T(1024)(128)(4,1)} %bitcast.63), calls=%async_computation | async-start | bytes 8388608
  320.6 6.7 %slice-start.1 = ((s8[5242880]{0:T(1024)(128)(4,1)}), s8[1048576]{0:T(1024)(128)(4,1)S(1)}, s32[]{:S(2)}) async-start(s8[5242880]{0:T(1024)(128)(4,1)} %bitcast.63), calls=%async_computation.1 | async-start | bytes 2097152
  320.6 11.1 %slice-start.4 = ((s8[5242880]{0:T(1024)(128)(4,1)}), s8[4194304]{0:T(1024)(128)(4,1)S(1)}, s32[]{:S(2)}) async-start(s8[5242880]{0:T(1024)(128)(4,1)} %bitcast.90), calls=%async_computation.4 | async-start | bytes 8388608
  327.3 4.4 %copy-start.9 = (bf16[320,1024]{1,0:T(8,128)(2,1)S(1)}, bf16[320,1024]{1,0:T(8,128)(2,1)}, u32[]{:S(2)}) copy-start(bf16[320,1024]{1,0:T(8,128)(2,1)} %get-tuple-element.104.o_ref) | copy-start | bytes 1966084
  327.3 4.4 %slice-start.5 = ((s8[5242880]{0:T(1024)(128)(4,1)}), s8[1048576]{0:T(1024)(128)(4,1)S(1)}, s32[]{:S(2)}) async-start(s8[5242880]{0:T(1024)(128)(4,1)} %bitcast.90), calls=%async_computation.5 | async-start | bytes 2097152
  335.4 6.7 %collective-permute-start.7 = (bf16[128,2944]{1,0:T(8,128)(2,1)}, bf16[128,2944]{1,0:T(8,128)(2,1)S(1)}, u32[]{:S(2)}, u32[]{:S(2)}) collective-permute-start(bf16[128,2944]{1,0:T(8,128)(2,1)} %collective-permute-done.2.refs_1_), channel_id=1, source_target_pairs={{0,1},{1,0},{2,3},{3,2},{4,5},{5,4},{6,7},{7,6}} | collective-permute-start | bytes 2261000 | tf_op jit(solution)/shard_map/ppermute | solution.py:308
  335.8 6.3 %collective-permute-start.8 = (bf16[128,2944]{1,0:T(8,128)(2,1)}, bf16[128,2944]{1,0:T(8,128)(2,1)S(1)}, u32[]{:S(2)}, u32[]{:S(2)}) collective-permute-start(bf16[128,2944]{1,0:T(8,128)(2,1)} %collective-permute-done.3.refs_2_), channel_id=1, source_target_pairs={{0,1},{1,0},{2,3},{3,2},{4,5},{5,4},{6,7},{7,6}} | collective-permute-start | bytes 2261000 | tf_op jit(solution)/shard_map/ppermute | solution.py:308
  335.9 6.2 %collective-permute-start.9 = (bf16[128,2944]{1,0:T(8,128)(2,1)}, bf16[128,2944]{1,0:T(8,128)(2,1)}, u32[]{:S(2)}, u32[]{:S(2)}) collective-permute-start(bf16[128,2944]{1,0:T(8,128)(2,1)} %collective-permute-done.4.refs_3_), channel_id=1, source_target_pairs={{0,1},{1,0},{2,3},{3,2},{4,5},{5,4},{6,7},{7,6}} | collective-permute-start | bytes 2261000 | tf_op jit(solution)/shard_map/ppermute | solution.py:308
  336.6 5.5 %collective-permute-start.10 = (f32[5376]{0:T(1024)S(1)}, f32[5376]{0:T(1024)S(1)}, u32[]{:S(2)}, u32[]{:S(2)}) collective-permute-start(f32[5376]{0:T(1024)S(1)} %add.152), channel_id=1, source_target_pairs={{0,2},{1,3},{2,0},{3,1},{4,6},{5,7},{6,4},{7,5}} | collective-permute-start | bytes 64520 | tf_op jit(solution)/shard_map/ppermute | solution.py:308
  337.4 13.6 %slice-start.2 = ((s8[5242880]{0:T(1024)(128)(4,1)}), s8[4194304]{0:T(1024)(128)(4,1)S(1)}, s32[]{:S(2)}) async-start(s8[5242880]{0:T(1024)(128)(4,1)} %bitcast.65), calls=%async_computation.2 | async-start | bytes 8388608
  342.1 12.2 %collective-permute-start.11 = (f32[5376]{0:T(1024)S(1)}, f32[5376]{0:T(1024)S(1)}, u32[]{:S(2)}, u32[]{:S(2)}) collective-permute-start(f32[5376]{0:T(1024)S(1)} %add.153), channel_id=1, source_target_pairs={{0,4},{1,5},{2,6},{3,7},{4,0},{5,1},{6,2},{7,3}} | collective-permute-start | bytes 64520 | tf_op jit(solution)/shard_map/ppermute | solution.py:308
  343.4 7.6 %slice-start.3 = ((s8[5242880]{0:T(1024)(128)(4,1)}), s8[1048576]{0:T(1024)(128)(4,1)S(1)}, s32[]{:S(2)}) async-start(s8[5242880]{0:T(1024)(128)(4,1)} %bitcast.65), calls=%async_computation.3 | async-start | bytes 2097152
  351.0 4.6 %copy-start.11 = (bf16[128,2560]{1,0:T(8,128)(2,1)S(1)}, bf16[128,2560]{1,0:T(8,128)(2,1)}, u32[]{:S(2)}) copy-start(bf16[128,2560]{1,0:T(8,128)(2,1)} %get-tuple-element.79) | copy-start | bytes 1966084

commit v8 on v7

--- a/solution.py
+++ b/solution.py
@@ -744,7 +744,9 @@
     near = [shift(de, XBIT), shift(de, YBIT), shift(de, XBIT + YBIT)]
     pair = shift(de, PAIR)
     dg = dg + shift(dg, PAIR)
-    dw_down, dw_gate, dw_up, dw_q, dw_o = tn(hidden, dy_full), tn(d_gate, x_mlp), tn(d_up, x_mlp), nn(d_query, x_attn), nn(attn_out, d_attn_full)
+    dw_q, dw_o = nn(d_query, x_attn), nn(attn_out, d_attn_full)
+    dw_q, dw_o, hidden, d_gate, d_up = later((dw_q, dw_o, hidden, d_gate, d_up))
+    dw_down, dw_gate, dw_up = tn(hidden, dy_full), tn(d_gate, x_mlp), tn(d_up, x_mlp)
     dw_down, dw_gate, dw_up, dw_q, dw_o, near, pair, dg, d_knope, d_value = later((dw_down, dw_gate, dw_up, dw_q, dw_o, near, pair, dg, d_knope, d_value))
     far = [shift(b, PAIR) for b in near]
     dg = dg + shift(dg, XBIT)

time: 362 us -> 362 us (level)
  transfers between devices with their start and end apart: 12 -> 12, of which waited for: 1 -> 0; matrix products, arithmetic and copies ran while one was open for 14% -> 14% of each run, Pallas kernels for 4% -> 4%
where the time goes in v8:
time: 362 us; the launch traced here: 357 us
  Pallas kernels  279 us (77%)
  matrix products  44.1 us (12%)
  starting transfers between devices  11.5 us (3%)
  local copies, waits for them, and re-layouts  11.5 us (3%)
  other arithmetic  9.35 us (3%)
    pallas_call x4, Pallas kernels, exchange_call(): pl.pallas_call(body, out_shape=out_shape, in_specs=[vmem] * (len(ins) - f...  246 us
    dot_general x10, matrix products, mm(): lax.dot_general(lhs, rhs, (((lc,), (rc,)), ((), ())), preferred_element_t...  44.1 us
    pallas_call x1, Pallas kernels, attend_bwd(): pl.pallas_call(functools.partial(attn_bwd_body, heads), grid=(heads,), in...  19.8 us
    ppermute x12, starting transfers between devices, shift(): return lax.ppermute(x, 'tp', [(d, d ^ bit) for d in range(8)])  11.5 us
  transfers between devices with their start and end apart: 12, of which 0 were waited for; matrix products, arithmetic and copies ran while one was open for 14% of the time, Pallas kernels for 4%

profile of v8, /device:TPU:0, one launch (start us, length us, event | category | flops | bytes accessed | tf_op | source)
XLA Modules:
  0.0 357.4 jit_solution(7320536625306497922)
XLA Ops:
  0.6 3.4 collective-permute-start.1
  4.0 1.5 collective-permute-start
  5.5 0.7 broadcast_in_dim.71.gain
  6.3 1.3 broadcast_in_dim.73.gain
  7.6 0.7 broadcast_select_fusion
  8.3 0.8 select_reduce_fusion.1
  9.1 0.8 convert_reduce_fusion
  10.0 0.9 select_reduce_fusion.blocks_ref
  10.9 0.6 add_select_fusion.1
  11.5 0.8 slice.21
  12.3 0.3 copy.45
  13.3 6.9 %gather_rows.1.part = bf16[1024,2560]{1,0:T(8,128)(2,1)S(1)} custom-call(s32[1]{0:T(128)} %bitcast.2.count_ref, s32[1024]{0:T(1024)S(1)} %select_reduce_fusion.blocks_ref, s32[1024,1]{1,0:T(8,128)S(1)} %add_select_fusion.key_ref, bf16[8,2560]{1,0:T(8,128)(2,1)S(1)} %pad.20.tail_ref, bf16[9181,2560]{1,0:T(8,128)(2,1)} %table_ref.1), custom_call_target="tpu_custom_call" | custom-call | tf_op jit(solution)/shard_map/gather_rows/pallas_call | solution.py:134
  20.5 1.0 fusion.11
  21.5 51.7 %embed_exchange.1 = (bf16[128,2560]{1,0:T(8,128)(2,1)S(1)}, bf16[480,1024]{1,0:T(8,128)(2,1)S(1)}, f32[1024,288]{1,0:T(8,128)S(1)}, bf16[1024,2560]{1,0:T(8,128)(2,1)S(1)}) custom-call(bf16[1024,2560]{1,0:T(8,128)(2,1)S(1)} %gather_rows.1.part, f32[1,2560]{1,0:T(1,128)S(1)} %broadcast_in_dim.71.gain, bf16[480,2560]{1,0:T(8,128)(2,1)S(1)} %bitcast.59, ...), custom_call_target="tpu_custom_call" | custom-call | tf_op jit(solution)/shard_map/embed_exchange/pallas_call | solution.py:521
  73.2 0.8 copy-done.5
  74.1 1.1 copy-done.1
  75.5 1.7 copy-done.8
  77.2 19.1 %attend_fwd.1 = (bf16[1024,256]{1,0:T(8,128)(2,1)}, bf16[320,1024]{1,0:T(8,128)(2,1)}, bf16[32,1024]{1,0:T(8,128)(2,1)}, bf16[320,1024]{1,0:T(8,128)(2,1)}, bf16...) custom-call(f32[1024,288]{1,0:T(8,128)} %copy-done.1, f32[1,256]{1,0:T(1,128)} %bitcast.89, ...), custom_call_target="tpu_custom_call" | custom-call | tf_op jit(solution)/shard_map/attend_fwd/pallas_call | solution.py:521
  96.3 140.2 %middle.1 = (bf16[128,2560]{1,0:T(8,128)(2,1)}, bf16[128,2560]{1,0:T(8,128)(2,1)}, f32[128,2560]{1,0:T(8,128)}, f32[1,2560]{1,0:T(1,128)}, bf16[320,1024]{1,0:T(...) custom-call(bf16[320,1024]{1,0:T(8,128)(2,1)} %get-tuple-element.105, ...), custom_call_target="tpu_custom_call" | custom-call | tf_op jit(solution)/shard_map/middle/pallas_call | solution.py:521
  236.6 19.8 %attend_bwd.1 = (bf16[480,1024]{1,0:T(8,128)(2,1)}, bf16[320,1024]{1,0:T(8,128)(2,1)}, bf16[320,1024]{1,0:T(8,128)(2,1)}, f32[32,1024]{1,0:T(8,128)}, bf16[9181,2560]{1,0:T(8,128)(2,1)}) custom-call(bf16[480,1024]{1,0:T(8,128)(2,1)} %copy-done.4, bf16[320,1024]{1,0:T(8,128)(2,1)} %get-tuple-element.85.kn_ref, bf16[32,1024]{1,0:T(8,128)(2,1)} %get-tuple-element.86.kp_ref, ...), custom_call_target="tpu_custom_call" | custom-call | tf_op jit(solution)/shard_map/attend_bwd/pallas_call | solution.py:299
  256.4 1.0 convert_element_type.33
  257.6 2.4 multiply_add_fusion.1
  260.0 1.6 fusion.16
  261.6 0.7 fusion.6
  262.6 0.3 add_add_fusion
  263.1 0.3 copy-done.6
  263.4 0.3 copy-done.7
  263.7 34.7 %back_exchange.1 = (bf16[128,2944]{1,0:T(8,128)(2,1)S(1)}, f32[1,2560]{1,0:T(1,128)S(1)}) custom-call(bf16[480,1024]{1,0:T(8,128)(2,1)S(1)} %copy-done.7, bf16[1024,384]{1,0:T(8,128)(2,1)S(1)} %pad.25.lat, bf16[480,2560]{1,0:T(8,128)(2,1)} %bitcast.58, bf16[288,2560]{1,0:T(8,128)(2,1)} %bitcast.60, bf16[128,2560]{1,0:T(8,128)(2,1)S(1)} %copy-done.6, ...), custom_call_target="tpu_custom_call" | custom-call | tf_op jit(solution)/shard_map/back_exchange/pallas_call | solution.py:521
  298.5 1.5 collective-permute-start.4
  300.0 0.9 collective-permute-start.3
  300.9 1.1 collective-permute-start.2
  302.0 6.4 %fusion.18 = f32[320,2560]{1,0:T(8,128)} fusion(bf16[320,1024]{1,0:T(8,128)(2,1)} %get-tuple-element.105.o_ref, bf16[1024,2560]{1,0:T(8,128)(2,1)} %get-tuple-element.106), kind=kOutput, calls=%fused_computation.60 | convolution fusion | flops 1677721600 | bytes 9175040 | tf_op jit(solution)/shard_map/dot_general | solution.py:24
  308.4 7.0 %fusion.17 = f32[480,2560]{1,0:T(8,128)} fusion(bf16[480,1024]{1,0:T(8,128)(2,1)S(1)} %copy-done.7, bf16[1024,2560]{1,0:T(8,128)(2,1)} %copy-done.8), kind=kOutput, calls=%fused_computation.59 | convolution fusion | flops 2516582400 | bytes 11141120 | tf_op jit(solution)/shard_map/dot_general | solution.py:24
  315.5 7.0 %fusion.19 = f32[800,2560]{1,0:T(8,128)} fusion(bf16[1024,800]{1,0:T(8,128)(2,1)S(1)} %copy-done.19, bf16[1024,2560]{1,0:T(8,128)(2,1)S(1)} %bitcast.66), kind=kOutput, calls=%fused_computation.61 | convolution fusion | flops 4194304000 | bytes 15073280 | tf_op jit(solution)/shard_map/dot_general | solution.py:24
  322.4 6.7 %fusion.20 = f32[800,2560]{1,0:T(8,128)} fusion(bf16[1024,800]{1,0:T(8,128)(2,1)S(1)} %copy-done.18, bf16[1024,2560]{1,0:T(8,128)(2,1)S(1)} %bitcast.91), kind=kOutput, calls=%fused_computation.62 | convolution fusion | flops 4194304000 | bytes 15073280 | tf_op jit(solution)/shard_map/dot_general | solution.py:24
  329.2 6.7 %fusion.21 = f32[800,2560]{1,0:T(8,128)} fusion(bf16[1024,800]{1,0:T(8,128)(2,1)S(1)} %copy-done.17, bf16[1024,2560]{1,0:T(8,128)(2,1)S(1)} %bitcast.91), kind=kOutput, calls=%fused_computation.63 | convolution fusion | flops 4194304000 | bytes 15073280 | tf_op jit(solution)/shard_map/dot_general | solution.py:24
  335.9 0.5 collective-permute-start.7
  336.5 0.5 collective-permute-start.9
  337.2 0.9 collective-permute-start.10
  338.1 2.4 fusion.22
  340.5 2.3 fusion.23
  342.9 1.1 collective-permute-start.11
  344.0 6.9 %table_grad.1 = (bf16[9181,2560]{1,0:T(8,128)(2,1)}, bf16[8,2560]{1,0:T(8,128)(2,1)S(1)}, bf16[1024,384]{1,0:T(8,128)(2,1)S(1)}) custom-call(s32[1]{0:T(128)} %bitcast.2.count_ref, s32[1024]{0:T(1024)S(1)} %select_reduce_fusion.blocks_ref, s32[1,1024]{1,0:T(1,128)S(1)} %bitcast.62, ...), custom_call_target="tpu_custom_call", output_to_operand_aliasing={{0}: (3, {})} | custom-call | tf_op jit(solution)/shard_map/table_grad/pallas_call | solution.py:194
  351.0 0.6 slice_dynamic-update-slice_fusion
  351.6 3.4 fusion.7
  355.0 0.6 slice.28
  355.6 0.6 fusion.15
  356.2 0.8 copy.63
  (96 shorter events, 2.5 us)
Async XLA Ops:
  0.6 20.8 %collective-permute-start.1 = (bf16[128,2560]{1,0:T(8,128)(2,1)}, bf16[128,2560]{1,0:T(8,128)(2,1)S(1)}, u32[]{:S(2)}, u32[]{:S(2)}) collective-permute-start(bf16[128,2560]{1,0:T(8,128)(2,1)} %bitcast.69), channel_id=1, source_target_pairs={{0,4},{1,5},{2,6},{3,7},{4,0},{5,1},{6,2},{7,3}} | collective-permute-start | bytes 1966088 | tf_op jit(solution)/shard_map/ppermute | solution.py:308
  4.0 17.4 %collective-permute-start = (bf16[128,2560]{1,0:T(8,128)(2,1)}, bf16[128,2560]{1,0:T(8,128)(2,1)S(1)}, u32[]{:S(2)}, u32[]{:S(2)}) collective-permute-start(bf16[128,2560]{1,0:T(8,128)(2,1)} %bitcast.70), channel_id=1, source_target_pairs={{0,2},{1,3},{2,0},{3,1},{4,6},{5,7},{6,4},{7,5}} | collective-permute-start | bytes 1966088 | tf_op jit(solution)/shard_map/ppermute | solution.py:308
  13.3 8.2 %copy-start = (bf16[2560,5,96]{0,2,1:T(8,128)(2,1)S(1)}, bf16[2560,5,96]{0,2,1:T(8,128)(2,1)}, u32[]{:S(2)}) copy-start(bf16[2560,5,96]{0,2,1:T(8,128)(2,1)} %param.16) | copy-start | bytes 7372804
  13.3 8.2 %copy-start.3 = (bf16[2560,288]{0,1:T(8,128)(2,1)S(1)}, bf16[2560,288]{0,1:T(8,128)(2,1)}, u32[]{:S(2)}) copy-start(bf16[2560,288]{0,1:T(8,128)(2,1)} %param.17) | copy-start | bytes 4423684
  21.4 51.8 %copy-start.12 = (bf16[128,2560]{1,0:T(8,128)(2,1)}, bf16[128,2560]{1,0:T(8,128)(2,1)S(1)}, u32[]{:S(2)}) copy-start(bf16[128,2560]{1,0:T(8,128)(2,1)S(1)} %collective-permute-done.1.dyy_ref) | copy-start | bytes 1966084
  21.4 51.8 %copy-start.13 = (bf16[128,2560]{1,0:T(8,128)(2,1)}, bf16[128,2560]{1,0:T(8,128)(2,1)S(1)}, u32[]{:S(2)}) copy-start(bf16[128,2560]{1,0:T(8,128)(2,1)S(1)} %collective-permute-done.dyx_ref) | copy-start | bytes 1966084
  73.2 0.8 copy-start.5
  74.1 1.1 copy-start.1
  74.1 1.5 copy-start.4
  74.1 3.2 copy-start.8
  236.6 23.4 %copy-start.9 = (bf16[256,5,64]{0,2,1:T(8,128)(2,1)S(1)}, bf16[256,5,64]{0,2,1:T(8,128)(2,1)}, u32[]{:S(2)}) copy-start(bf16[256,5,64]{0,2,1:T(8,128)(2,1)} %param.19) | copy-start | bytes 491524
  236.6 25.0 %copy-start.14 = (bf16[256,5,64]{0,2,1:T(8,128)(2,1)S(1)}, bf16[256,5,64]{0,2,1:T(8,128)(2,1)}, u32[]{:S(2)}) copy-start(bf16[256,5,64]{0,2,1:T(8,128)(2,1)} %param.20) | copy-start | bytes 491524
  236.6 25.0 %copy-start.16 = (f32[256]{0:T(256)S(1)}, f32[256]{0:T(256)}, u32[]{:S(2)}) copy-start(f32[256]{0:T(256)} %param.18) | copy-start | bytes 3076
  256.4 5.2 %copy-start.2 = (f32[1024,288]{1,0:T(8,128)S(1)}, f32[1024,288]{1,0:T(8,128)}, u32[]{:S(2)}) copy-start(f32[1024,288]{1,0:T(8,128)} %copy-done.1) | copy-start | bytes 3538948
  257.6 4.0 %copy-start.11 = (bf16[320,1024]{1,0:T(8,128)(2,1)S(1)}, bf16[320,1024]{1,0:T(8,128)(2,1)}, u32[]{:S(2)}) copy-start(bf16[320,1024]{1,0:T(8,128)(2,1)} %get-tuple-element.123) | copy-start | bytes 1966084
  262.3 0.8 copy-start.15
  262.3 1.1 copy-start.6
  262.3 1.4 copy-start.7
  298.5 37.4 %collective-permute-start.5 = (bf16[128,2944]{1,0:T(8,128)(2,1)S(1)}, bf16[128,2944]{1,0:T(8,128)(2,1)S(1)}, u32[]{:S(2)}, u32[]{:S(2)}) collective-permute-start(bf16[128,2944]{1,0:T(8,128)(2,1)S(1)} %get-tuple-element.102.refs_0_), channel_id=1, source_target_pairs={{0,1},{1,0},{2,3},{3,2},{4,5},{5,4},{6,7},{7,6}} | collective-permute-start | bytes 2261000 | tf_op jit(solution)/shard_map/ppermute | solution.py:308
  298.5 37.4 %collective-permute-start.4 = (bf16[128,2944]{1,0:T(8,128)(2,1)S(1)}, bf16[128,2944]{1,0:T(8,128)(2,1)}, u32[]{:S(2)}, u32[]{:S(2)}) collective-permute-start(bf16[128,2944]{1,0:T(8,128)(2,1)S(1)} %get-tuple-element.102.refs_0_), channel_id=1, source_target_pairs={{0,6},{1,7},{2,4},{3,5},{4,2},{5,3},{6,0},{7,1}} | collective-permute-start | bytes 2261000 | tf_op jit(solution)/shard_map/ppermute | solution.py:308
  300.0 35.9 %collective-permute-start.3 = (bf16[128,2944]{1,0:T(8,128)(2,1)S(1)}, bf16[128,2944]{1,0:T(8,128)(2,1)}, u32[]{:S(2)}, u32[]{:S(2)}) collective-permute-start(bf16[128,2944]{1,0:T(8,128)(2,1)S(1)} %get-tuple-element.102.refs_0_), channel_id=1, source_target_pairs={{0,4},{1,5},{2,6},{3,7},{4,0},{5,1},{6,2},{7,3}} | collective-permute-start | bytes 2261000 | tf_op jit(solution)/shard_map/ppermute | solution.py:308
  300.9 35.0 %collective-permute-start.2 = (bf16[128,2944]{1,0:T(8,128)(2,1)S(1)}, bf16[128,2944]{1,0:T(8,128)(2,1)}, u32[]{:S(2)}, u32[]{:S(2)}) collective-permute-start(bf16[128,2944]{1,0:T(8,128)(2,1)S(1)} %get-tuple-element.102.refs_0_), channel_id=1, source_target_pairs={{0,2},{1,3},{2,0},{3,1},{4,6},{5,7},{6,4},{7,5}} | collective-permute-start | bytes 2261000 | tf_op jit(solution)/shard_map/ppermute | solution.py:308
  302.0 33.8 %collective-permute-start.6 = (f32[5376]{0:T(1024)S(1)}, f32[5376]{0:T(1024)S(1)}, u32[]{:S(2)}, u32[]{:S(2)}) collective-permute-start(f32[5376]{0:T(1024)S(1)} %pad_maximum_fusion), channel_id=1, source_target_pairs={{0,1},{1,0},{2,3},{3,2},{4,5},{5,4},{6,7},{7,6}} | collective-permute-start | bytes 64520 | tf_op jit(solution)/shard_map/ppermute | solution.py:308
  302.0 13.4 %slice-start.2 = ((s8[5242880]{0:T(1024)(128)(4,1)}), s8[4194304]{0:T(1024)(128)(4,1)S(1)}, s32[]{:S(2)}) async-start(s8[5242880]{0:T(1024)(128)(4,1)} %bitcast.65), calls=%async_computation.2 | async-start | bytes 8388608
  302.0 20.4 %slice-start.4 = ((s8[5242880]{0:T(1024)(128)(4,1)}), s8[4194304]{0:T(1024)(128)(4,1)S(1)}, s32[]{:S(2)}) async-start(s8[5242880]{0:T(1024)(128)(4,1)} %bitcast.90), calls=%async_computation.4 | async-start | bytes 8388608
  308.4 7.0 %slice-start.3 = ((s8[5242880]{0:T(1024)(128)(4,1)}), s8[1048576]{0:T(1024)(128)(4,1)S(1)}, s32[]{:S(2)}) async-start(s8[5242880]{0:T(1024)(128)(4,1)} %bitcast.65), calls=%async_computation.3 | async-start | bytes 2097152
  308.4 7.0 %copy-start.19 = (bf16[1024,800]{1,0:T(8,128)(2,1)S(1)}, bf16[1024,800]{1,0:T(8,128)(2,1)}, u32[]{:S(2)}) copy-start(bf16[1024,800]{1,0:T(8,128)(2,1)} %get-tuple-element.110) | copy-start | bytes 4915204
  308.4 14.0 %slice-start.5 = ((s8[5242880]{0:T(1024)(128)(4,1)}), s8[1048576]{0:T(1024)(128)(4,1)S(1)}, s32[]{:S(2)}) async-start(s8[5242880]{0:T(1024)(128)(4,1)} %bitcast.90), calls=%async_computation.5 | async-start | bytes 2097152
  315.4 7.0 %copy-start.18 = (bf16[1024,800]{1,0:T(8,128)(2,1)S(1)}, bf16[1024,800]{1,0:T(8,128)(2,1)}, u32[]{:S(2)}) copy-start(bf16[1024,800]{1,0:T(8,128)(2,1)} %get-tuple-element.111) | copy-start | bytes 4915204
  322.4 6.7 %copy-start.17 = (bf16[1024,800]{1,0:T(8,128)(2,1)S(1)}, bf16[1024,800]{1,0:T(8,128)(2,1)}, u32[]{:S(2)}) copy-start(bf16[1024,800]{1,0:T(8,128)(2,1)} %get-tuple-element.113) | copy-start | bytes 4915204
  335.9 7.0 %collective-permute-start.7 = (bf16[128,2944]{1,0:T(8,128)(2,1)}, bf16[128,2944]{1,0:T(8,128)(2,1)S(1)}, u32[]{:S(2)}, u32[]{:S(2)}) collective-permute-start(bf16[128,2944]{1,0:T(8,128)(2,1)} %collective-permute-done.2.refs_1_), channel_id=1, source_target_pairs={{0,1},{1,0},{2,3},{3,2},{4,5},{5,4},{6,7},{7,6}} | collective-permute-start | bytes 2261000 | tf_op jit(solution)/shard_map/ppermute | solution.py:308
  336.4 6.4 %collective-permute-start.8 = (bf16[128,2944]{1,0:T(8,128)(2,1)}, bf16[128,2944]{1,0:T(8,128)(2,1)S(1)}, u32[]{:S(2)}, u32[]{:S(2)}) collective-permute-start(bf16[128,2944]{1,0:T(8,128)(2,1)} %collective-permute-done.3.refs_2_), channel_id=1, source_target_pairs={{0,1},{1,0},{2,3},{3,2},{4,5},{5,4},{6,7},{7,6}} | collective-permute-start | bytes 2261000 | tf_op jit(solution)/shard_map/ppermute | solution.py:308
  336.5 6.4 %collective-permute-start.9 = (bf16[128,2944]{1,0:T(8,128)(2,1)}, bf16[128,2944]{1,0:T(8,128)(2,1)}, u32[]{:S(2)}, u32[]{:S(2)}) collective-permute-start(bf16[128,2944]{1,0:T(8,128)(2,1)} %collective-permute-done.4.refs_3_), channel_id=1, source_target_pairs={{0,1},{1,0},{2,3},{3,2},{4,5},{5,4},{6,7},{7,6}} | collective-permute-start | bytes 2261000 | tf_op jit(solution)/shard_map/ppermute | solution.py:308
  337.2 5.7 %collective-permute-start.10 = (f32[5376]{0:T(1024)S(1)}, f32[5376]{0:T(1024)S(1)}, u32[]{:S(2)}, u32[]{:S(2)}) collective-permute-start(f32[5376]{0:T(1024)S(1)} %add.152), channel_id=1, source_target_pairs={{0,2},{1,3},{2,0},{3,1},{4,6},{5,7},{6,4},{7,5}} | collective-permute-start | bytes 64520 | tf_op jit(solution)/shard_map/ppermute | solution.py:308
  338.1 13.5 %slice-start = ((s8[5242880]{0:T(1024)(128)(4,1)}), s8[4194304]{0:T(1024)(128)(4,1)S(1)}, s32[]{:S(2)}) async-start(s8[5242880]{0:T(1024)(128)(4,1)} %bitcast.63), calls=%async_computation | async-start | bytes 8388608
  342.9 12.1 %collective-permute-start.11 = (f32[5376]{0:T(1024)S(1)}, f32[5376]{0:T(1024)S(1)}, u32[]{:S(2)}, u32[]{:S(2)}) collective-permute-start(f32[5376]{0:T(1024)S(1)} %add.153), channel_id=1, source_target_pairs={{0,4},{1,5},{2,6},{3,7},{4,0},{5,1},{6,2},{7,3}} | collective-permute-start | bytes 64520 | tf_op jit(solution)/shard_map/ppermute | solution.py:308
  344.0 7.6 %slice-start.1 = ((s8[5242880]{0:T(1024)(128)(4,1)}), s8[1048576]{0:T(1024)(128)(4,1)S(1)}, s32[]{:S(2)}) async-start(s8[5242880]{0:T(1024)(128)(4,1)} %bitcast.63), calls=%async_computation.1 | async-start | bytes 2097152
  351.6 4.6 %copy-start.10 = (bf16[128,2560]{1,0:T(8,128)(2,1)S(1)}, bf16[128,2560]{1,0:T(8,128)(2,1)}, u32[]{:S(2)}) copy-start(bf16[128,2560]{1,0:T(8,128)(2,1)} %get-tuple-element.84) | copy-start | bytes 1966084
